TPU v7x, 32 devices: a whole 2x2x4 slice. The times are simulated.
32 devices in a mesh: ctx: 8 (over z, y), fsdp: 4 (over x, core).
Axes of the slice: x: 2, y: 2, z: 4, core: 2. Of those that a mesh axis runs over, the one named last changes fastest.
Arguments:
- tokens: bfloat16 [4, 1024, 1600], P('fsdp', 'ctx'), may hold values from -6 to 6
- block_order: int32 [4, 16], P('fsdp'), may hold values from 0 to 15, each once within a row
- qkv_weight: bfloat16 [1600, 4800], P('fsdp'), may hold values from -0.15625 to 0.15625
- query_bias: float32 [1600], replicated, may hold values from -3 to 3
- value_bias: float32 [1600], replicated, may hold values from -0.18 to 0.18
- out_weight: bfloat16 [1600, 1600], P('fsdp'), may hold values from -2.5 to 2.5
- out_bias: float32 [1600], replicated, may hold values from -1.8 to 1.8
- expand_weight: bfloat16 [1600, 6400], P('fsdp'), may hold values from -0.15625 to 0.15625
- expand_bias: float32 [6400], replicated, may hold values from -3 to 3
- shrink_weight: bfloat16 [6400, 1600], P('fsdp'), may hold values from -0.078125 to 0.078125
- shrink_bias: float32 [1600], replicated, may hold values from -1.8 to 1.8
- first_gain: float32 [1600], replicated, may hold values from 0.5 to 1.5
- first_shift: float32 [1600], replicated, may hold values from -1.8 to 1.8
- second_gain: float32 [1600], replicated, may hold values from 0.5 to 1.5
- second_shift: float32 [1600], replicated, may hold values from -1.8 to 1.8
- cotangent: bfloat16 [4, 1024, 1600], P('fsdp', 'ctx'), may hold values from -6 to 6
Outputs:
- result: bfloat16 [4, 1024, 1600], P('fsdp', 'ctx')
- grad_tokens: float32 [4, 1024, 1600], P('fsdp', 'ctx')
- grad_qkv: float32 [1600, 4800], P('fsdp', 'ctx')
- grad_outw: float32 [1600, 1600], P('fsdp', 'ctx')
- grad_expand: float32 [1600, 6400], P('fsdp', 'ctx')
- grad_shrink: float32 [6400, 1600], P('fsdp', 'ctx')
- grad_query_bias: float32 [1600], replicated
- grad_value_bias: float32 [1600], replicated
- grad_out_bias: float32 [1600], replicated
- grad_expand_bias: float32 [6400], replicated
- grad_shrink_bias: float32 [1600], replicated
- grad_first_gain: float32 [1600], replicated
- grad_first_shift: float32 [1600], replicated
- grad_second_gain: float32 [1600], replicated
- grad_second_shift: float32 [1600], replicated
Inputs may be any that keep to these rules, and one draw needn't show every extreme that they name: Each row of block_order names every block of its sequence once.
All inputs are finite; a program needn't handle non-finite values.
Results may differ from a plain program's by a relative error of at most 0.015.
Values may be sent and summed in bfloat16 or wider, within the bound.
A program may use at most 384 MiB of HBM per device.

v0:
```python
import jax
import jax.numpy as jnp
from jax import lax
from jax.sharding import PartitionSpec as P

HEADS = 25
HEAD_DIM = 64


EPSILON = 1e-05


def layer_norm(values, gain, shift):
    center = jnp.mean(values, axis=-1, keepdims=True)
    centred = values - center
    spread = jnp.mean(centred * centred, axis=-1, keepdims=True)
    return centred * lax.rsqrt(spread + EPSILON) * gain + shift


def smooth_gelu(values):
    return (
        0.5
        * values
        * (1.0 + jnp.tanh(0.7978845608028654 * (values + 0.044715 * values * values * values)))
    )


def fetch(weight):
    return lax.all_gather(weight, "fsdp", axis=0, tiled=True)


def against(left, weight):
    return lax.dot_general(
        left, weight, (((1,), (1,)), ((), ())), preferred_element_type=jnp.float32
    )


def shard_rows(local):
    return lax.psum_scatter(
        local.astype(jnp.bfloat16), "fsdp", scatter_dimension=0, tiled=True
    ).astype(jnp.float32)


def column_grad(left, right):
    whole_left = lax.all_gather(left, "ctx", axis=0, tiled=True)
    right_columns = lax.all_to_all(right, "ctx", split_axis=1, concat_axis=0, tiled=True)
    local = lax.dot_general(
        whole_left, right_columns, (((0,), (0,)), ((), ())), preferred_element_type=jnp.float32
    )
    return shard_rows(local)


def shared_grad(left, right):
    return column_grad(left, right)


def masked_scores(queries, query_pos, keys, key_pos, factor):
    scores = jnp.einsum("qhd,khd->hqk", queries, keys, preferred_element_type=jnp.float32) * factor
    allowed = (key_pos[None, :] <= query_pos[:, None])[None]
    return jnp.where(allowed, scores, -jnp.inf)


def body(
    tokens,
    block_order,
    qkv_weight,
    query_bias,
    value_bias,
    out_weight,
    out_bias,
    expand_weight,
    expand_bias,
    shrink_weight,
    shrink_bias,
    first_gain,
    first_shift,
    second_gain,
    second_shift,
    cotangent,
):
    inputs = tokens[0].astype(jnp.float32)
    rows = inputs.shape[0]
    width = inputs.shape[1]
    half = rows // 2
    factor = HEAD_DIM ** (-0.5)
    place = lax.axis_index("ctx")
    key_pos = (block_order[0][:, None] * half + jnp.arange(half, dtype=jnp.int32)[None, :]).reshape(
        -1
    )
    length = key_pos.shape[0]
    query_pos = lax.dynamic_slice_in_dim(key_pos, place * rows, rows)
    block = min(512, length)
    count = length // block
    normed_one = layer_norm(inputs, first_gain, first_shift)
    lowered_one = normed_one.astype(jnp.bfloat16)
    project = jnp.dot(lowered_one, fetch(qkv_weight), preferred_element_type=jnp.float32)
    query = (project[:, :width] + query_bias).astype(jnp.bfloat16)
    keys_own = project[:, width : 2 * width].astype(jnp.bfloat16)
    values_own = (project[:, 2 * width :] + value_bias).astype(jnp.bfloat16)
    all_keys, all_values = (
        lax.all_gather(keys_own, "ctx", axis=0, tiled=True),
        lax.all_gather(values_own, "ctx", axis=0, tiled=True),
    )
    query_heads = query.reshape(rows, HEADS, HEAD_DIM)
    key_blocks = all_keys.reshape(count, block, HEADS, HEAD_DIM)
    value_blocks = all_values.reshape(count, block, HEADS, HEAD_DIM)
    pos_blocks = key_pos.reshape(count, block)

    def running(carry, pieces):
        highest, total = carry
        key_piece, pos_piece = pieces
        scores = masked_scores(query_heads, query_pos, key_piece, pos_piece, factor)
        fresh = jnp.maximum(highest, jnp.max(scores, axis=-1))
        total = total * jnp.exp(highest - fresh) + jnp.sum(
            jnp.exp(scores - fresh[..., None]), axis=-1
        )
        return ((fresh, total), None)

    start = (jnp.full((HEADS, rows), -1e30, jnp.float32), jnp.zeros((HEADS, rows), jnp.float32))
    (highest, total), unused = lax.scan(running, start, (key_blocks, pos_blocks))
    log_sum = highest + jnp.log(total)

    def weighted(acc, pieces):
        key_piece, value_piece, pos_piece = pieces
        scores = masked_scores(query_heads, query_pos, key_piece, pos_piece, factor)
        probs = jnp.exp(scores - log_sum[..., None]).astype(jnp.bfloat16)
        return (
            acc
            + jnp.einsum("hqk,khd->qhd", probs, value_piece, preferred_element_type=jnp.float32),
            None,
        )

    attended_heads, unused = lax.scan(
        weighted,
        jnp.zeros((rows, HEADS, HEAD_DIM), jnp.float32),
        (key_blocks, value_blocks, pos_blocks),
    )
    attended = attended_heads.reshape(rows, width)
    attended_low = attended.astype(jnp.bfloat16)
    middle = (
        inputs
        + jnp.dot(attended_low, fetch(out_weight), preferred_element_type=jnp.float32)
        + out_bias
    )
    normed_two = layer_norm(middle, second_gain, second_shift)
    lowered_two = normed_two.astype(jnp.bfloat16)
    expanded = (
        jnp.dot(lowered_two, fetch(expand_weight), preferred_element_type=jnp.float32) + expand_bias
    )
    hidden_low = smooth_gelu(expanded).astype(jnp.bfloat16)
    shrink_full = fetch(shrink_weight)
    result = (
        middle + jnp.dot(hidden_low, shrink_full, preferred_element_type=jnp.float32) + shrink_bias
    )
    grad_low = cotangent[0]
    grad_result = grad_low.astype(jnp.float32)
    grad_shrink = shared_grad(hidden_low, grad_low)
    grad_shrink_bias = jnp.sum(grad_result, axis=0)
    grad_hidden = against(grad_low, shrink_full)
    unused, gelu_back = jax.vjp(smooth_gelu, expanded)
    (grad_expanded,) = gelu_back(grad_hidden)
    expanded_low = grad_expanded.astype(jnp.bfloat16)
    grad_expand_bias = jnp.sum(expanded_low.astype(jnp.float32), axis=0)
    grad_expand = shared_grad(lowered_two, expanded_low)
    grad_normed_two = against(expanded_low, fetch(expand_weight))
    unused, second_back = jax.vjp(layer_norm, middle, second_gain, second_shift)
    grad_middle_norm, grad_second_gain, grad_second_shift = second_back(grad_normed_two)
    grad_middle = grad_result + grad_middle_norm
    middle_low = grad_middle.astype(jnp.bfloat16)
    grad_out_bias = jnp.sum(middle_low.astype(jnp.float32), axis=0)
    grad_outw = shared_grad(attended_low, middle_low)
    grad_att_low = against(middle_low, fetch(out_weight)).astype(jnp.bfloat16)
    grad_att_heads = grad_att_low.reshape(rows, HEADS, HEAD_DIM)
    delta = jnp.sum(grad_att_heads.astype(jnp.float32) * attended_heads, axis=-1).T

    def key_step(acc, pieces):
        key_piece, value_piece, pos_piece = pieces
        scores = masked_scores(query_heads, query_pos, key_piece, pos_piece, factor)
        probs = jnp.exp(scores - log_sum[..., None])
        slopes = jnp.einsum(
            "qhd,khd->hqk", grad_att_heads, value_piece, preferred_element_type=jnp.float32
        )
        score_grad = (probs * (slopes - delta[..., None])).astype(jnp.bfloat16)
        acc = acc + jnp.einsum(
            "hqk,khd->qhd", score_grad, key_piece, preferred_element_type=jnp.float32
        )
        return (acc, (probs.astype(jnp.bfloat16), score_grad))

    empty_heads = jnp.zeros((rows, HEADS, HEAD_DIM), jnp.float32)

    def query_step(acc, pieces):
        acc, unused_pair = key_step(acc, pieces)
        return (acc, None)

    query_acc, unused = lax.scan(query_step, empty_heads, (key_blocks, value_blocks, pos_blocks))
    all_queries, all_grads = (
        lax.all_gather(query, "ctx", axis=0, tiled=True),
        lax.all_gather(grad_att_low, "ctx", axis=0, tiled=True),
    )
    all_sums, all_deltas = (
        lax.all_gather(log_sum.T, "ctx", axis=0, tiled=True),
        lax.all_gather(delta.T, "ctx", axis=0, tiled=True),
    )
    own_keys = keys_own.reshape(rows, HEADS, HEAD_DIM)
    own_values = values_own.reshape(rows, HEADS, HEAD_DIM)

    def owner_step(carry, pieces):
        key_acc, value_acc = carry
        query_piece, grad_piece, sum_piece, delta_piece, pos_piece = pieces
        scores = masked_scores(query_piece, pos_piece, own_keys, query_pos, factor)
        probs = jnp.exp(scores - sum_piece.T[..., None])
        slopes = jnp.einsum(
            "qhd,khd->hqk", grad_piece, own_values, preferred_element_type=jnp.float32
        )
        score_grad = (probs * (slopes - delta_piece.T[..., None])).astype(jnp.bfloat16)
        key_acc = key_acc + jnp.einsum(
            "hqk,qhd->khd", score_grad, query_piece, preferred_element_type=jnp.float32
        )
        value_acc = value_acc + jnp.einsum(
            "hqk,qhd->khd",
            probs.astype(jnp.bfloat16),
            grad_piece,
            preferred_element_type=jnp.float32,
        )
        return ((key_acc, value_acc), None)

    (key_acc, value_acc), unused = lax.scan(
        owner_step,
        (empty_heads, empty_heads),
        (
            all_queries.reshape(count, block, HEADS, HEAD_DIM),
            all_grads.reshape(count, block, HEADS, HEAD_DIM),
            all_sums.reshape(count, block, HEADS),
            all_deltas.reshape(count, block, HEADS),
            pos_blocks,
        ),
    )
    grad_keys = key_acc.reshape(rows, width)
    grad_values = value_acc.reshape(rows, width)
    grad_query_low = (query_acc.reshape(rows, width) * factor).astype(jnp.bfloat16)
    grad_key_low = (grad_keys * factor).astype(jnp.bfloat16)
    grad_value_low = grad_values.astype(jnp.bfloat16)
    project_grad = jnp.concatenate([grad_query_low, grad_key_low, grad_value_low], axis=1)
    grad_query_bias = jnp.sum(grad_query_low.astype(jnp.float32), axis=0)
    grad_value_bias = jnp.sum(grad_value_low.astype(jnp.float32), axis=0)
    grad_qkv = shared_grad(lowered_one, project_grad)
    grad_normed_one = against(project_grad, fetch(qkv_weight))
    unused, first_back = jax.vjp(layer_norm, inputs, first_gain, first_shift)
    grad_first_input, grad_first_gain, grad_first_shift = first_back(grad_normed_one)
    grad_inputs = grad_middle + grad_first_input
    summed = lax.psum(
        (
            grad_query_bias,
            grad_value_bias,
            grad_out_bias,
            grad_expand_bias,
            grad_shrink_bias,
            grad_first_gain,
            grad_first_shift,
            grad_second_gain,
            grad_second_shift,
        ),
        ("ctx", "fsdp"),
    )
    return (
        result.astype(jnp.bfloat16)[None],
        grad_inputs[None],
        grad_qkv,
        grad_outw,
        grad_expand,
        grad_shrink,
        summed[0],
        summed[1],
        summed[2],
        summed[3],
        summed[4],
        summed[5],
        summed[6],
        summed[7],
        summed[8],
    )


def solution(mesh):
    placed = (
        P("fsdp", "ctx", None),
        P("fsdp", None),
        P("fsdp", None),
        P(),
        P(),
        P("fsdp", None),
        P(),
        P("fsdp", None),
        P(),
        P("fsdp", None),
        P(),
        P(),
        P(),
        P(),
        P(),
        P("fsdp", "ctx", None),
    )
    return jax.shard_map(
        body,
        mesh=mesh,
        in_specs=placed,
        out_specs=(
            P("fsdp", "ctx", None),
            P("fsdp", "ctx", None),
            P("fsdp", "ctx"),
            P("fsdp", "ctx"),
            P("fsdp", "ctx"),
            P("fsdp", "ctx"),
            P(),
            P(),
            P(),
            P(),
            P(),
            P(),
            P(),
            P(),
            P(),
        ),
        check_vma=False,
    )
```

profile of v0, /device:TPU:23, one launch (start us, length us, event | category | flops | bytes accessed | tf_op | source)
XLA Modules:
  0.0 1410.5 jit_solution(10884619457395824276)
XLA Ops:
  9.8 99.3 %all-gather.13.cloned.1.call-done = bf16[1600,4800]{1,0:T(8,128)(2,1)} async-done(((bf16[400,4800]{1,0:T(8,128)(2,1)}), bf16[1600,4800]{1,0:T(8,128)(2,1)}) %all-gather.13.cloned.1.call-update) | async-done | bytes 15360016 | tf_op jit(solution)/shard_map/all_gather | solution.py:29
  109.1 9.6 fusion.172
  124.4 57.4 %all-gather.17.cloned.1.call-done = bf16[1024,1600]{0,1:T(8,128)(2,1)} async-done(((bf16[128,1600]{0,1:T(8,128)(2,1)}), bf16[1024,1600]{0,1:T(8,128)(2,1)}) %all-gather.17.cloned.1.call-update) | async-done | bytes 3276816 | tf_op jit(solution)/shard_map/all_gather | solution.py:101
  181.8 8.5 reshape.298
  193.0 53.8 %all-gather.15.cloned.1.call-done = bf16[1024,1600]{0,1:T(8,128)(2,1)} async-done(((bf16[128,1600]{0,1:T(8,128)(2,1)}), bf16[1024,1600]{0,1:T(8,128)(2,1)}) %all-gather.15.cloned.1.call-update) | async-done | bytes 3276816 | tf_op jit(solution)/shard_map/all_gather | solution.py:102
  246.8 8.5 reshape.297
  255.3 4.9 copy.78
  260.2 19.4 %while.48 = (s32[]{:T(128)}, f32[25,128]{1,0:T(8,128)S(1)}, f32[25,128]{1,0:T(8,128)S(1)}, s32[2,512]{1,0:T(2,128)S(1)}, s32[128]{0:T(128)S(1)}, /*index=5*/bf16...) while((s32[]{:T(128)}, f32[25,128]{1,0:T(8,128)S(1)}, ...), condition=%wide.region_5.6_spmd.clone, body=%wide.region_2.5_spmd.clone.sunk | while | flops 221265536 | bytes 15524976 | solution.py:120
  260.4 5.2 fusion.228
  270.0 5.2 fusion.228
  279.6 9.9 while.49
  284.6 4.9 fusion.234
  291.7 5.0 fusion.171
  299.3 120.4 %all-gather.21.cloned.1.call-done = bf16[1600,6400]{1,0:T(8,128)(2,1)} async-done(((bf16[400,6400]{1,0:T(8,128)(2,1)}), bf16[1600,6400]{1,0:T(8,128)(2,1)}) %all-gather.21.cloned.1.call-update) | async-done | bytes 20480016 | tf_op jit(solution)/shard_map/all_gather | solution.py:29
  419.7 14.1 multiply_convert_fusion.6
  433.8 120.8 %all-gather.23.cloned.1.call-done = bf16[6400,1600]{1,0:T(8,128)(2,1)} async-done(((bf16[1600,1600]{1,0:T(8,128)(2,1)}), bf16[6400,1600]{1,0:T(8,128)(2,1)}) %all-gather.23.cloned.1.call-update) | async-done | bytes 20480016 | tf_op jit(solution)/shard_map/all_gather | solution.py:29
  554.5 12.3 convert_reduce_fusion
  566.8 12.8 multiply_reduce_fusion
  586.3 5.5 all-to-all-start.1
  591.7 38.5 %all_gather.52 = f32[1024,25]{0,1:T(8,128)S(1)} all-gather(f32[128,25]{0,1:T(8,128)S(1)} %bitcast.354), channel_id=1, replica_groups=mesh['ctx'=8,'fsdp'=4] {'ctx'}, dimensions={0}, use_global_device_ids=true | all-gather | bytes 115200 | tf_op jit(solution)/shard_map/all_gather | solution.py:201
  631.0 8.5 reshape.301
  649.1 6.3 all-to-all-start.2
  655.5 60.7 %all-gather.31.cloned.1.call-done = bf16[1024,1600]{0,1:T(8,128)(2,1)} async-done(((bf16[128,1600]{0,1:T(8,128)(2,1)}), bf16[1024,1600]{0,1:T(8,128)(2,1)}) %all-gather.31.cloned.1.call-update) | async-done | bytes 3276816 | tf_op jit(solution)/shard_map/all_gather | solution.py:45
  720.1 24.5 %while.50 = (s32[]{:T(128)}, f32[128,25,64]{0,2,1:T(8,128)}, bf16[2,512,25,64]{1,3,2,0:T(8,128)(2,1)S(1)}, s32[2,512]{1,0:T(2,128)S(1)}, s32[128]{0:T(128)S(1)},...) while((s32[]{:T(128)}, f32[128,25,64]{0,2,1:T(8,128)}, ...), condition=%wide.region_14.15_spmd.clone, body=%wide.region_13.14_spmd.clone.sunk | while | flops 639451136 | bytes 20651656 | solution.py:195
  725.0 7.2 fusion.242
  737.2 7.4 fusion.242
  744.6 26.5 %all_gather.54 = f32[1024,25]{0,1:T(8,128)S(1)} all-gather(f32[128,25]{0,1:T(8,128)S(1)} %bitcast.353), channel_id=1, replica_groups=mesh['ctx'=8,'fsdp'=4] {'ctx'}, dimensions={0}, use_global_device_ids=true | all-gather | bytes 115200 | tf_op jit(solution)/shard_map/all_gather | solution.py:202
  773.9 10.9 all-gather.33.cloned.1.call-done
  784.8 7.6 convolution_convert_fusion.1
  792.4 56.6 %all-gather.27.cloned.1.call-done = bf16[1024,1600]{0,1:T(8,128)(2,1)} async-done(((bf16[128,1600]{0,1:T(8,128)(2,1)}), bf16[1024,1600]{0,1:T(8,128)(2,1)}) %all-gather.27.cloned.1.call-update) | async-done | bytes 3276816 | tf_op jit(solution)/shard_map/all_gather | solution.py:198
  849.0 8.7 reshape.304
  862.4 41.6 %while.51 = (s32[]{:T(128)}, f32[128,25,64]{0,2,1:T(8,128)}, f32[128,25,64]{0,2,1:T(8,128)}, bf16[2,512,25,64]{1,3,2,0:T(8,128)(2,1)S(1)}, s32[128]{0:T(128)S(1)...) while((s32[]{:T(128)}, f32[128,25,64]{0,2,1:T(8,128)}, ...), condition=%wide.region_16.17_spmd.clone, body=%wide.region_15.16_spmd.clone.sunk | while | flops 856129536 | bytes 31107220 | solution.py:227
  868.4 9.1 fusion.251
  877.5 5.6 fusion.252
  889.0 9.2 fusion.251
  898.2 5.8 fusion.252
  907.9 5.7 all-to-all-start
  913.6 43.1 %all-to-all-done = bf16[128,8,600]{0,2,1:T(8,128)(2,1)S(1)} async-done(((bf16[128,8,600]{0,2,1:T(8,128)(2,1)}), bf16[128,8,600]{0,2,1:T(8,128)(2,1)S(1)}, u32[]{:S(2)}, u32[]{:S(2)}) %all-to-all-start) | async-done | bytes 1228832 | tf_op jit(solution)/shard_map/all_to_all | solution.py:46
  956.7 6.0 convolution_convert_fusion.2
  962.7 31.1 %all_to_all.76 = bf16[128,8,200]{0,2,1:T(8,128)(2,1)S(1)} all-to-all(bf16[128,8,200]{0,2,1:T(8,128)(2,1)S(1)} %bitcast.332), channel_id=1, replica_groups=mesh['ctx'=8,'fsdp'=4] {'ctx'}, dimensions={1} | all-to-all | bytes 819200 | tf_op jit(solution)/shard_map/all_to_all | solution.py:46
  993.9 124.3 %all-gather.35.cloned.1.call-done = bf16[1024,6400]{1,0:T(8,128)(2,1)} async-done(((bf16[128,6400]{1,0:T(8,128)(2,1)}), bf16[1024,6400]{1,0:T(8,128)(2,1)}) %all-gather.35.cloned.1.call-update) | async-done | bytes 13107216 | tf_op jit(solution)/shard_map/all_gather | solution.py:45
  1118.2 9.0 convolution_convert_fusion
  1133.4 9.7 fusion.168
  1146.3 13.3 fusion.136
  1161.3 21.0 %reduce-scatter.11.cloned.1.call-done = bf16[400,800]{1,0:T(8,128)(2,1)} async-done(((bf16[1600,800]{1,0:T(8,128)(2,1)}), bf16[400,800]{1,0:T(8,128)(2,1)}) %reduce-scatter.11.cloned.1.call-update) | async-done | bytes 640016 | tf_op jit(solution)/shard_map/reduce_scatter | solution.py:39
  1184.7 31.1 %reduce-scatter.7.cloned.1.call-done = bf16[400,600]{1,0:T(8,128)(2,1)} async-done(((bf16[1600,600]{1,0:T(8,128)(2,1)}), bf16[400,600]{1,0:T(8,128)(2,1)}) %reduce-scatter.7.cloned.1.call-update) | async-done | bytes 480016 | tf_op jit(solution)/shard_map/reduce_scatter | solution.py:39
  1217.8 39.1 %reduce-scatter.13.cloned.1.call-done = bf16[1600,200]{1,0:T(8,128)(2,1)} async-done(((bf16[6400,200]{1,0:T(8,128)(2,1)}), bf16[1600,200]{1,0:T(8,128)(2,1)}) %reduce-scatter.13.cloned.1.call-update) | async-done | bytes 640016
  1259.5 132.3 %all-reduce.3.cloned.1.call-done = (f32[1600]{0:T(1024)}, f32[1600]{0:T(1024)}, f32[1600]{0:T(1024)}, f32[6400]{0:T(1024)}, f32[1600]{0:T(1024)}, /*index=5*/f32...) async-done(((f32[1600]{0:T(1024)}, f32[1600]{0:T(1024)}, f32[1600]{0:T(1024)}, f32[6400]{0:T(1024)}, f32[1600]{0:T(1024)}, /*index=5*/f32[1600]{0:T(1024)}, ...) | async-done | bytes 76816 | tf_op jit(solution)/shard_map/psum | solution.py:251
  (210 shorter events, 112.9 us)
Async XLA Ops:
  7.2 2.0 copy-start.16
  7.2 2.0 copy-start.21
  7.2 101.9 %all-gather.13.cloned.1.call-start = ((), (), s32[]{:S(2)}) async-start(), calls=%async_computation.8 | async-start | bytes 19456000 | tf_op jit(solution)/shard_map/all_gather | solution.py:29
  7.9 173.9 %all-gather.17.cloned.1.call-start = ((), (), s32[]{:S(2)}) async-start(), calls=%async_computation.10 | async-start | bytes 3686400 | tf_op jit(solution)/shard_map/all_gather | solution.py:101
  8.4 1.3 copy-start.19
  9.7 109.0 %copy-start.12 = (bf16[128,1600]{0,1:T(8,128)(2,1)}, bf16[128,1600]{0,1:T(8,128)(2,1)S(1)}, u32[]{:S(2)}) copy-start(bf16[128,1600]{0,1:T(8,128)(2,1)S(1)} %fusion.149) | copy-start | bytes 1228804
  9.8 109.8 %copy-start.22 = (f32[1600]{0:T(1024)S(1)}, f32[1600]{0:T(1024)}, u32[]{:S(2)}) copy-start(f32[1600]{0:T(1024)} %param.27) | copy-start | bytes 19204
  9.8 109.8 %copy-start.23 = (f32[1600]{0:T(1024)S(1)}, f32[1600]{0:T(1024)}, u32[]{:S(2)}) copy-start(f32[1600]{0:T(1024)} %param.28) | copy-start | bytes 19204
  119.6 127.2 %all-gather.15.cloned.1.call-start = ((), (), s32[]{:S(2)}) async-start(), calls=%async_computation.9 | async-start | bytes 3686400 | tf_op jit(solution)/shard_map/all_gather | solution.py:102
  121.0 170.6 %all-gather.19.cloned.1.call-start = ((), (), s32[]{:S(2)}) async-start(), calls=%async_computation.11 | async-start | bytes 6656000 | tf_op jit(solution)/shard_map/all_gather | solution.py:29
  121.6 298.1 %all-gather.21.cloned.1.call-start = ((), (), s32[]{:S(2)}) async-start(), calls=%async_computation.12 | async-start | bytes 25600000 | tf_op jit(solution)/shard_map/all_gather | solution.py:29
  122.2 1.6 copy-start.31
  122.2 432.3 %all-gather.23.cloned.1.call-start = ((), (), s32[]{:S(2)}) async-start(), calls=%async_computation.13 | async-start | bytes 26624000 | tf_op jit(solution)/shard_map/all_gather | solution.py:29
  122.8 508.2 %all-gather.25.cloned.1.call-start = ((), (), s32[]{:S(2)}) async-start(), calls=%async_computation.14 | async-start | bytes 3686400 | tf_op jit(solution)/shard_map/all_gather | solution.py:197
  123.5 592.6 %all-gather.31.cloned.1.call-start = ((), (), s32[]{:S(2)}) async-start(), calls=%async_computation.18 | async-start | bytes 3686400 | tf_op jit(solution)/shard_map/all_gather | solution.py:45
  279.6 12.1 copy-start.24
  291.5 6.0 copy-start.15
  291.5 6.0 copy-start.25
  291.6 128.1 %copy-start.18 = (f32[6400]{0:T(1024)S(1)}, f32[6400]{0:T(1024)}, u32[]{:S(2)}) copy-start(f32[6400]{0:T(1024)} %param.32) | copy-start | bytes 76804
  291.6 493.3 %all-gather.33.cloned.1.call-start = ((), (), s32[]{:S(2)}) async-start(), calls=%async_computation.20 | async-start | bytes 3686400 | tf_op jit(solution)/shard_map/all_gather | solution.py:45
  298.8 550.2 %all-gather.27.cloned.1.call-start = ((), (), s32[]{:S(2)}) async-start(), calls=%async_computation.15 | async-start | bytes 3686400 | tf_op jit(solution)/shard_map/all_gather | solution.py:198
  554.5 12.3 copy-start.2
  566.8 12.8 copy-start.7
  566.8 15.8 %slice-start = ((s8[5324800]{0:T(1024)(128)(4,1)}), s8[4194304]{0:T(1024)(128)(4,1)S(1)}, s32[]{:S(2)}) async-start(s8[5324800]{0:T(1024)(128)(4,1)} %bitcast.330), calls=%async_computation.25 | async-start | bytes 8388608
  566.8 14.1 %copy-start.10 = (bf16[1,128,1600]{1,2,0:T(8,128)(2,1)S(1)}, bf16[1,128,1600]{1,2,0:T(8,128)(2,1)}, u32[]{:S(2)}) copy-start(bf16[1,128,1600]{1,2,0:T(8,128)(2,1)} %param.39) | copy-start | bytes 1228804
  566.8 15.8 %slice-start.1 = ((s8[5324800]{0:T(1024)(128)(4,1)}), s8[1130496]{0:T(1024)(128)(4,1)S(1)}, s32[]{:S(2)}) async-start(s8[5324800]{0:T(1024)(128)(4,1)} %bitcast.330), calls=%async_computation.26 | async-start | bytes 2260992
  584.9 328.6 %all-gather.29.cloned.1.call-start = ((), (), s32[]{:S(2)}) async-start(), calls=%async_computation.16 | async-start | bytes 3686400 | tf_op jit(solution)/shard_map/all_gather | solution.py:45
  585.7 532.5 %all-gather.35.cloned.1.call-start = ((), (), s32[]{:S(2)}) async-start(), calls=%async_computation.22 | async-start | bytes 14745600 | tf_op jit(solution)/shard_map/all_gather | solution.py:45
  586.3 62.8 %all-to-all-start.1 = ((bf16[128,8,200]{0,2,1:T(8,128)(2,1)}), bf16[128,8,200]{0,2,1:T(8,128)(2,1)}, u32[]{:S(2)}, u32[]{:S(2)}) async-start(bf16[128,8,200]{0,2,1:T(8,128)(2,1)} %bitcast.347), calls=%async_computation.2 | async-start | bytes 819200 | tf_op jit(solution)/shard_map/all_to_all | solution.py:46
  649.1 124.8 %all-to-all-start.2 = ((bf16[128,8,800]{0,2,1:T(8,128)(2,1)}), bf16[128,8,800]{0,2,1:T(8,128)(2,1)}, u32[]{:S(2)}, u32[]{:S(2)}) async-start(bf16[128,8,800]{0,2,1:T(8,128)(2,1)} %bitcast.329), calls=%async_computation.4 | async-start | bytes 3276800 | tf_op jit(solution)/shard_map/all_to_all | solution.py:46
  655.5 504.2 %reduce-scatter.9.cloned.1.call-start = ((), (), s32[]{:S(2)}) async-start(), calls=%async_computation.19 | async-start | bytes 1024000 | tf_op jit(solution)/shard_map/reduce_scatter | solution.py:39
  720.1 462.3 %reduce-scatter.11.cloned.1.call-start = ((), (), s32[]{:S(2)}) async-start(), calls=%async_computation.21 | async-start | bytes 3584000 | tf_op jit(solution)/shard_map/reduce_scatter | solution.py:39
  857.7 4.7 copy-start
  907.9 48.8 %all-to-all-start = ((bf16[128,8,600]{0,2,1:T(8,128)(2,1)}), bf16[128,8,600]{0,2,1:T(8,128)(2,1)S(1)}, u32[]{:S(2)}, u32[]{:S(2)}) async-start(bf16[128,8,600]{0,2,1:T(8,128)(2,1)} %bitcast.15), calls=%async_computation | async-start | bytes 2457600 | tf_op jit(solution)/shard_map/all_to_all | solution.py:46
  913.6 49.2 %copy-start.11 = (bf16[1,128,1600]{1,2,0:T(8,128)(2,1)S(1)}, bf16[1,128,1600]{1,2,0:T(8,128)(2,1)}, u32[]{:S(2)}) copy-start(bf16[1,128,1600]{1,2,0:T(8,128)(2,1)} %param.39) | copy-start | bytes 1228804
  913.6 302.2 %reduce-scatter.7.cloned.1.call-start = ((), (), s32[]{:S(2)}) async-start(), calls=%async_computation.17 | async-start | bytes 2560000 | tf_op jit(solution)/shard_map/reduce_scatter | solution.py:39
  962.7 294.2 %reduce-scatter.13.cloned.1.call-start = ((), (), s32[]{:S(2)}) async-start(), calls=%async_computation.23 | async-start | bytes 4096000
  1127.2 6.2 copy-start.5
  1127.2 6.2 copy-start.13
  1127.3 6.2 copy-start.17
  1127.3 6.2 copy-start.20
  1132.0 259.9 %all-reduce.3.cloned.1.call-start = ((), (), s32[]{:S(2)}) async-start(), calls=%async_computation.24 | async-start | bytes 188416 | tf_op jit(solution)/shard_map/psum | solution.py:251
  1133.4 9.7 copy-start.30
  1133.4 9.7 copy-start.28
  1133.4 10.9 copy-start.9
  1143.1 3.2 copy-start.3
  1143.1 3.2 copy-start.6
  1143.1 3.2 copy-start.26
  (6 other events, 4.7 us)
Sparse Core Ops, SparseCore 0:
  9.6 99.5 all-gather.12
  119.7 62.0 all-gather.16
  184.4 62.3 all-gather.14
  248.2 41.0 all-gather.18
  290.8 128.8 all-gather.20
  421.1 133.3 all-gather.22
  557.2 71.9 all-gather.24
  631.2 84.8 all-gather.30
  718.2 66.5 all-gather.32
  786.7 62.2 all-gather.26
  851.1 62.3 all-gather.28
  915.5 202.6 all-gather.34
  1120.7 23.0 reduce-scatter.8
  1146.2 36.1 reduce-scatter.10
  1184.8 30.8 reduce-scatter.6
  1218.2 38.6 reduce-scatter.12
  1264.3 127.4 all-reduce.2
where the time goes:
time: 1420 us; the launch traced here: 1410 us
  waiting for transfers between devices  975 us (69%)
  matrix products  189 us (13%)
  blocking collectives  96.2 us (7%)
  local copies, waits for them, and re-layouts  82 us (6%)
  other arithmetic  34.4 us (2%)
  starting transfers between devices  18.7 us (1%)
  between operations  14.8 us (1%)
    all_gather x4, waiting for transfers between devices, fetch(): return lax.all_gather(weight, 'fsdp', axis=0, tiled=True)  341 us
    all_gather x4, waiting for transfers between devices, column_grad(): whole_left = lax.all_gather(left, 'ctx', axis=0, tiled=True)  196 us
    psum x1, waiting for transfers between devices, body(): lax.psum((grad_query_bias, grad_value_bias, grad_out_bias, grad_expand_bi...  132 us
    all_gather x1, waiting for transfers between devices, body(): lax.all_gather(keys_own, 'ctx', axis=0, tiled=True)  57.4 us
    all_gather x1, waiting for transfers between devices, body(): lax.all_gather(grad_att_low, 'ctx', axis=0, tiled=True)  56.6 us
    all_gather x1, waiting for transfers between devices, body(): lax.all_gather(values_own, 'ctx', axis=0, tiled=True)  53.8 us
    reduce_scatter x3, waiting for transfers between devices, shard_rows(): lax.psum_scatter(local.astype(jnp.bfloat16), 'fsdp', scatter_dimension=0,...  52.1 us
    unnamed x18, waiting for transfers between devices  43.4 us
  transfers between devices with their start and end apart: 20, of which 14 were waited for; matrix products, arithmetic and copies ran while one was open for 20% of the time, Pallas kernels for 0%

commit v1 on v0

v1 whole, which is shorter than its diff:
```python
import functools
import itertools

import jax
import jax.numpy as jnp
from jax import lax
from jax.experimental import pallas as pl
from jax.experimental.pallas import tpu as pltpu
from jax.sharding import Mesh
from jax.sharding import PartitionSpec as P

HEADS = 25
HEAD_DIM = 64
EPSILON = 1e-05
MESH = pl.DeviceIdType.MESH
F32 = jnp.float32
BF16 = jnp.bfloat16
ANY = pl.BlockSpec(memory_space=pl.ANY)
VMEM = pl.BlockSpec(memory_space=pltpu.VMEM)


def offsets(sizes):
    return [o for o in itertools.product(*(range(s) for s in sizes)) if any(o)]


def moved(axes, sizes, offset, sign=1):
    return {
        a: lax.rem(lax.axis_index(a) + (o if sign > 0 else s - o), s)
        for a, s, o in zip(axes, sizes, offset)
    }


def flat(place, axes, sizes):
    index = 0
    for a, s in zip(axes, sizes):
        index = index * s + place[a]
    return index


def own_place(axes):
    return {a: lax.axis_index(a) for a in axes}


def greet(peers):
    barrier = pltpu.get_barrier_semaphore()
    for peer in peers:
        pl.semaphore_signal(barrier, inc=1, device_id=peer, device_id_type=MESH)
    pl.semaphore_wait(barrier, len(peers))


def remote(src, dst, send, recv, peer):
    return pltpu.make_async_remote_copy(
        src_ref=src,
        dst_ref=dst,
        send_sem=send,
        recv_sem=recv,
        device_id=peer,
        device_id_type=MESH,
    )


def gather_kernel(specs, *refs):
    count = len(specs)
    ins, outs = refs[:count], refs[count : 2 * count]
    scratch = refs[2 * count :]
    plans = []
    peers = []
    for index, (axes, sizes, pair) in enumerate(specs):
        offs = offsets(sizes)
        send, recv, local = scratch[3 * index : 3 * index + 3]
        side = lax.axis_index(pair)
        mate = {pair: 1 - side}
        plans.append((axes, sizes, offs, side, mate, ins[index], outs[index], send, recv, local))
        peers += [moved(axes, sizes, o) for o in offs] + [mate]
    greet(peers)
    started = []
    for axes, sizes, offs, side, mate, source, out, send, recv, local in plans:
        me = flat(own_place(axes), axes, sizes)
        here = pltpu.make_async_copy(source, out.at[me, side], local)
        here.start()
        for t, off in enumerate(offs):
            copy = remote(
                source, out.at[me, side], send.at[t], recv.at[t], moved(axes, sizes, off)
            )
            copy.start()
            started.append(copy)
        last = len(offs)
        copy = remote(source, out.at[me, side], send.at[last], recv.at[last], mate)
        copy.start()
        started.append(copy)
    for axes, sizes, offs, side, mate, source, out, send, recv, local in plans:
        last = len(offs)
        for t, off in enumerate(offs):
            came = flat(moved(axes, sizes, off, -1), axes, sizes)
            block = out.at[came, side]
            remote(source, block, send.at[t], recv.at[t], mate).wait_recv()
            copy = remote(block, block, send.at[last + 1 + t], recv.at[last + 1 + t], mate)
            copy.start()
            started.append(copy)
    for axes, sizes, offs, side, mate, source, out, send, recv, local in plans:
        last = len(offs)
        me = flat(own_place(axes), axes, sizes)
        pltpu.make_async_copy(source, out.at[me, side], local).wait()
        remote(source, out.at[me, 1 - side], send.at[last], recv.at[last], mate).wait_recv()
        for t, off in enumerate(offs):
            came = flat(moved(axes, sizes, off, -1), axes, sizes)
            remote(
                source, out.at[came, 1 - side], send.at[last + 1 + t], recv.at[last + 1 + t], mate
            ).wait_recv()
    for copy in started:
        copy.wait_send()


def gather(blocks, specs, ident):
    shapes, scratch, moved_bytes = [], [], 0
    for block, (axes, sizes, pair) in zip(blocks, specs):
        group = 1
        for s in sizes:
            group *= s
        shapes.append(jax.ShapeDtypeStruct((group, 2) + block.shape, block.dtype))
        scratch += [
            pltpu.SemaphoreType.DMA((2 * group,)),
            pltpu.SemaphoreType.DMA((2 * group,)),
            pltpu.SemaphoreType.DMA,
        ]
        moved_bytes += 2 * group * block.size * 2
    return pl.pallas_call(
        functools.partial(gather_kernel, specs),
        out_shape=shapes,
        in_specs=[VMEM] * len(blocks),
        out_specs=[ANY] * len(blocks),
        scratch_shapes=scratch,
        name="gather%d" % ident,
        compiler_params=pltpu.CompilerParams(collective_id=ident, has_side_effects=True),
        cost_estimate=pl.CostEstimate(
            flops=0, bytes_accessed=10 * moved_bytes, transcendentals=0
        ),
    )(*blocks)


def exchange_kernel(axes, sizes, source, out, send, recv, local):
    offs = offsets(sizes)
    greet([moved(axes, sizes, o) for o in offs])
    me = flat(own_place(axes), axes, sizes)
    here = pltpu.make_async_copy(source.at[me], out.at[me], local)
    here.start()
    started = []
    for t, off in enumerate(offs):
        peer = moved(axes, sizes, off)
        copy = remote(
            source.at[flat(peer, axes, sizes)], out.at[me], send.at[t], recv.at[t], peer
        )
        copy.start()
        started.append(copy)
    here.wait()
    for t, off in enumerate(offs):
        peer = moved(axes, sizes, off, -1)
        came = flat(peer, axes, sizes)
        remote(source.at[came], out.at[came], send.at[t], recv.at[t], peer).wait_recv()
    for copy in started:
        copy.wait_send()


def exchange(pieces, axes, sizes, ident):
    group = pieces.shape[0]
    return pl.pallas_call(
        functools.partial(exchange_kernel, axes, sizes),
        out_shape=jax.ShapeDtypeStruct(pieces.shape, pieces.dtype),
        in_specs=[VMEM],
        out_specs=VMEM,
        scratch_shapes=[
            pltpu.SemaphoreType.DMA((group,)),
            pltpu.SemaphoreType.DMA((group,)),
            pltpu.SemaphoreType.DMA,
        ],
        name="exchange%d" % ident,
        compiler_params=pltpu.CompilerParams(collective_id=ident, has_side_effects=True),
        cost_estimate=pl.CostEstimate(
            flops=0, bytes_accessed=20 * pieces.size, transcendentals=0
        ),
    )(pieces)


def scatter_kernel(axes, sizes, pair, source, out, first, summed, last, send, recv):
    offs = offsets(sizes)
    side = lax.axis_index(pair)
    mate = {pair: 1 - side}
    greet([moved(axes, sizes, o) for o in offs] + [mate])
    me = flat(own_place(axes), axes, sizes)
    count = len(offs)
    started = []
    for t, off in enumerate(offs + [(0,) * len(sizes)]):
        there = flat(moved(axes, sizes, off), axes, sizes)
        copy = remote(source.at[there, 1 - side], first.at[t], send.at[t], recv.at[t], mate)
        copy.start()
        started.append(copy)
    for t, off in enumerate(offs):
        peer = moved(axes, sizes, off)
        there = flat(peer, axes, sizes)
        started[t].wait_recv()
        summed[t] = (source[there, side].astype(F32) + first[t].astype(F32)).astype(BF16)
        slot = count + 1 + t
        copy = remote(summed.at[t], last.at[t], send.at[slot], recv.at[slot], peer)
        copy.start()
        started.append(copy)
    started[count].wait_recv()
    out[...] = source[me, side].astype(F32) + first[count].astype(F32)
    for t in range(count):
        started[count + 1 + t].wait_recv()
        out[...] += last[t].astype(F32)
    for copy in started:
        copy.wait_send()


def scatter(partial, axes, sizes, pair, ident):
    group = partial.shape[0]
    block = partial.shape[2:]
    return pl.pallas_call(
        functools.partial(scatter_kernel, axes, sizes, pair),
        out_shape=jax.ShapeDtypeStruct(block, F32),
        in_specs=[VMEM],
        out_specs=VMEM,
        scratch_shapes=[
            pltpu.VMEM((group,) + block, BF16),
            pltpu.VMEM((group - 1,) + block, BF16),
            pltpu.VMEM((group - 1,) + block, BF16),
            pltpu.SemaphoreType.DMA((2 * group,)),
            pltpu.SemaphoreType.DMA((2 * group,)),
        ],
        name="scatter%d" % ident,
        compiler_params=pltpu.CompilerParams(collective_id=ident, has_side_effects=True),
        cost_estimate=pl.CostEstimate(
            flops=0, bytes_accessed=20 * partial.size, transcendentals=0
        ),
    )(partial)


def total_kernel(axes, sizes, source, out, came, send, recv):
    offs = offsets(sizes)
    greet([moved(axes, sizes, o) for o in offs])
    me = flat(own_place(axes), axes, sizes)
    count = len(offs)
    started = []
    for t, off in enumerate(offs):
        peer = moved(axes, sizes, off)
        copy = remote(
            source.at[flat(peer, axes, sizes)], came.at[t], send.at[t], recv.at[t], peer
        )
        copy.start()
        started.append(copy)
    for copy in started:
        copy.wait_recv()
    out[me] = source[me] + jnp.sum(came[...], axis=0)
    second = []
    for t, off in enumerate(offs):
        peer = moved(axes, sizes, off)
        copy = remote(out.at[me], out.at[me], send.at[count + t], recv.at[count + t], peer)
        copy.start()
        second.append(copy)
    for t, off in enumerate(offs):
        peer = moved(axes, sizes, off, -1)
        block = out.at[flat(peer, axes, sizes)]
        remote(block, block, send.at[count + t], recv.at[count + t], peer).wait_recv()
    for copy in started + second:
        copy.wait_send()


def total(parts, axes, sizes, ident):
    group = parts.shape[0]
    return pl.pallas_call(
        functools.partial(total_kernel, axes, sizes),
        out_shape=jax.ShapeDtypeStruct(parts.shape, F32),
        in_specs=[VMEM],
        out_specs=VMEM,
        scratch_shapes=[
            pltpu.VMEM((group - 1,) + parts.shape[1:], F32),
            pltpu.SemaphoreType.DMA((2 * group,)),
            pltpu.SemaphoreType.DMA((2 * group,)),
        ],
        name="total%d" % ident,
        compiler_params=pltpu.CompilerParams(collective_id=ident, has_side_effects=True),
    )(parts)


def nt(left, right):
    return lax.dot_general(left, right, (((1,), (1,)), ((), ())), preferred_element_type=F32)


def nn(left, right):
    return lax.dot_general(left, right, (((1,), (0,)), ((), ())), preferred_element_type=F32)


def rows_of(inv, ref, pair, low, high):
    first = pl.multiple_of(inv[2 * pair] * HEAD_DIM, HEAD_DIM)
    second = pl.multiple_of(inv[2 * pair + 1] * HEAD_DIM, HEAD_DIM)
    return jnp.concatenate(
        [ref[pl.ds(first, 64), low:high], ref[pl.ds(second, 64), low:high]], axis=0
    )


def put_rows(inv, ref, pair, low, high, values):
    first = pl.multiple_of(inv[2 * pair] * HEAD_DIM, HEAD_DIM)
    second = pl.multiple_of(inv[2 * pair + 1] * HEAD_DIM, HEAD_DIM)
    ref[pl.ds(first, 64), low:high] = values[:64]
    ref[pl.ds(second, 64), low:high] = values[64:]


def head_slice(values, part, heads, head):
    low = (part * heads + head) * HEAD_DIM
    return values[:, low : low + HEAD_DIM]


def diagonal(block):
    return lax.broadcasted_iota(jnp.int32, (block, block), 0) <= lax.broadcasted_iota(
        jnp.int32, (block, block), 1
    )


def attend_kernel(heads, block, inv, qkv, out, lse, qs, ks, vt, ot):
    length = qkv.shape[0]
    width = heads * HEAD_DIM

    def sort(pair, unused):
        at = pl.multiple_of(pair * 128, 128)
        values = rows_of(inv, qkv, pair, 0, 3 * width)
        for h in range(heads):
            qs[h, pl.ds(at, 128), :] = head_slice(values, 0, heads, h) * BF16(0.125)
            ks[h, pl.ds(at, 128), :] = head_slice(values, 1, heads, h)
            vt[h, :, pl.ds(at, 128)] = head_slice(values, 2, heads, h).astype(F32).T.astype(BF16)
        return unused

    lax.fori_loop(0, length // 128, sort, 0)
    allowed = diagonal(block)

    def row(qi, unused):
        q_at = pl.multiple_of(qi * block, block)

        def first(h):
            scores = nt(ks[h, pl.ds(q_at, block), :], qs[h, pl.ds(q_at, block), :])
            scores = jnp.where(allowed, scores, -1e30)
            high = jnp.max(scores, axis=0, keepdims=True)
            probs = jnp.exp(scores - high)
            return (
                high,
                jnp.sum(probs, axis=0, keepdims=True),
                nn(vt[h, :, pl.ds(q_at, block)], probs.astype(BF16)),
            )

        def column(kj, state):
            k_at = pl.multiple_of(kj * block, block)
            fresh_state = []
            for h in range(heads):
                high, weight, acc = state[h]
                scores = nt(ks[h, pl.ds(k_at, block), :], qs[h, pl.ds(q_at, block), :])
                fresh = jnp.maximum(high, jnp.max(scores, axis=0, keepdims=True))
                probs = jnp.exp(scores - fresh)
                fade = jnp.exp(high - fresh)
                fresh_state.append(
                    (
                        fresh,
                        weight * fade + jnp.sum(probs, axis=0, keepdims=True),
                        acc * fade + nn(vt[h, :, pl.ds(k_at, block)], probs.astype(BF16)),
                    )
                )
            return tuple(fresh_state)

        state = lax.fori_loop(0, qi, column, tuple(first(h) for h in range(heads)))
        for h in range(heads):
            high, weight, acc = state[h]
            ot[h, :, pl.ds(q_at, block)] = acc / weight
            lse[h : h + 1, pl.ds(q_at, block)] = high + jnp.log(weight)
        return unused

    lax.fori_loop(0, length // block, row, 0)

    def unsort(pair, unused):
        at = pl.multiple_of(pair * 128, 128)
        values = [ot[h, :, pl.ds(at, 128)].T for h in range(heads)]
        put_rows(inv, out, pair, 0, width, jnp.concatenate(values, axis=1))
        return unused

    lax.fori_loop(0, length // 128, unsort, 0)


def attend(inv, qkv, heads):
    length = qkv.shape[0]
    width = heads * HEAD_DIM
    block = min(256, length)
    pairs = length * (length + block) // 2
    return pl.pallas_call(
        functools.partial(attend_kernel, heads, block),
        out_shape=(
            jax.ShapeDtypeStruct((length, width), F32),
            jax.ShapeDtypeStruct((heads, length), F32),
        ),
        grid_spec=pltpu.PrefetchScalarGridSpec(
            num_scalar_prefetch=1,
            grid=(1,),
            in_specs=[pl.BlockSpec((length, 3 * width), lambda i, inv: (0, 0))],
            out_specs=(
                pl.BlockSpec((length, width), lambda i, inv: (0, 0)),
                pl.BlockSpec((heads, length), lambda i, inv: (0, 0)),
            ),
            scratch_shapes=[
                pltpu.VMEM((heads, length, HEAD_DIM), BF16),
                pltpu.VMEM((heads, length, HEAD_DIM), BF16),
                pltpu.VMEM((heads, HEAD_DIM, length), BF16),
                pltpu.VMEM((heads, HEAD_DIM, length), F32),
            ],
        ),
        name="attend",
        cost_estimate=pl.CostEstimate(
            flops=4 * heads * pairs * HEAD_DIM * 4,
            bytes_accessed=length * width * 10,
            transcendentals=heads * pairs,
        ),
    )(inv, qkv)


def attend_back_kernel(
    heads, block, inv, qkv, grads, outs, lse, dqkv, qs, ks, vs, gs, kt, delta, dqt, dks, dvs
):
    length = qkv.shape[0]
    width = heads * HEAD_DIM
    count = length // block

    def sort(pair, unused):
        at = pl.multiple_of(pair * 128, 128)
        values = rows_of(inv, qkv, pair, 0, 3 * width)
        grad = rows_of(inv, grads, pair, 0, width)
        value = rows_of(inv, outs, pair, 0, width)
        product = (grad.astype(F32) * value).T
        for h in range(heads):
            qs[h, pl.ds(at, 128), :] = head_slice(values, 0, heads, h) * BF16(0.125)
            key = head_slice(values, 1, heads, h)
            ks[h, pl.ds(at, 128), :] = key
            kt[h, :, pl.ds(at, 128)] = key.astype(F32).T.astype(BF16)
            vs[h, pl.ds(at, 128), :] = head_slice(values, 2, heads, h)
            gs[h, pl.ds(at, 128), :] = head_slice(grad, 0, heads, h)
            delta[h : h + 1, pl.ds(at, 128)] = jnp.sum(
                product[h * HEAD_DIM : (h + 1) * HEAD_DIM], axis=0, keepdims=True
            )
            dqt[h, :, pl.ds(at, 128)] = jnp.zeros((HEAD_DIM, 128), F32)
        return unused

    lax.fori_loop(0, length // 128, sort, 0)
    allowed = diagonal(block)

    def column(kj, unused):
        k_at = pl.multiple_of(kj * block, block)

        def tile(h, q_at, masked):
            q = qs[h, pl.ds(q_at, block), :]
            g = gs[h, pl.ds(q_at, block), :]
            scores = nt(ks[h, pl.ds(k_at, block), :], q)
            probs = jnp.exp(scores - lse[h : h + 1, pl.ds(q_at, block)])
            if masked:
                probs = jnp.where(allowed, probs, 0.0)
            slopes = nt(vs[h, pl.ds(k_at, block), :], g)
            low = (probs * (slopes - delta[h : h + 1, pl.ds(q_at, block)])).astype(BF16)
            dqt[h, :, pl.ds(q_at, block)] += nn(kt[h, :, pl.ds(k_at, block)], low)
            return nn(low, q), nn(probs.astype(BF16), g)

        def row(qi, state):
            q_at = pl.multiple_of(qi * block, block)
            fresh = []
            for h in range(heads):
                dk, dv = tile(h, q_at, False)
                fresh.append((state[h][0] + dk, state[h][1] + dv))
            return tuple(fresh)

        state = tuple(tile(h, k_at, True) for h in range(heads))
        state = lax.fori_loop(kj + 1, count, row, state)
        for h in range(heads):
            dks[h, pl.ds(k_at, block), :] = state[h][0].astype(BF16)
            dvs[h, pl.ds(k_at, block), :] = state[h][1].astype(BF16)
        return unused

    lax.fori_loop(0, count, column, 0)

    def unsort(pair, unused):
        at = pl.multiple_of(pair * 128, 128)
        values = [(dqt[h, :, pl.ds(at, 128)].T * 0.125).astype(BF16) for h in range(heads)]
        values += [dks[h, pl.ds(at, 128), :] for h in range(heads)]
        values += [dvs[h, pl.ds(at, 128), :] for h in range(heads)]
        put_rows(inv, dqkv, pair, 0, 3 * width, jnp.concatenate(values, axis=1))
        return unused

    lax.fori_loop(0, length // 128, unsort, 0)


def attend_back(inv, qkv, grads, outs, lse, heads):
    length = qkv.shape[0]
    width = heads * HEAD_DIM
    block = min(256, length)
    pairs = length * (length + block) // 2
    row_shape = (heads, length, HEAD_DIM)
    return pl.pallas_call(
        functools.partial(attend_back_kernel, heads, block),
        out_shape=jax.ShapeDtypeStruct((length, 3 * width), BF16),
        grid_spec=pltpu.PrefetchScalarGridSpec(
            num_scalar_prefetch=1,
            grid=(1,),
            in_specs=[
                pl.BlockSpec((length, 3 * width), lambda i, inv: (0, 0)),
                pl.BlockSpec((length, width), lambda i, inv: (0, 0)),
                pl.BlockSpec((length, width), lambda i, inv: (0, 0)),
                pl.BlockSpec((heads, length), lambda i, inv: (0, 0)),
            ],
            out_specs=pl.BlockSpec((length, 3 * width), lambda i, inv: (0, 0)),
            scratch_shapes=[
                pltpu.VMEM(row_shape, BF16),
                pltpu.VMEM(row_shape, BF16),
                pltpu.VMEM(row_shape, BF16),
                pltpu.VMEM(row_shape, BF16),
                pltpu.VMEM((heads, HEAD_DIM, length), BF16),
                pltpu.VMEM((heads, length), F32),
                pltpu.VMEM((heads, HEAD_DIM, length), F32),
                pltpu.VMEM(row_shape, BF16),
                pltpu.VMEM(row_shape, BF16),
            ],
        ),
        name="attend_back",
        cost_estimate=pl.CostEstimate(
            flops=10 * heads * pairs * HEAD_DIM * 4,
            bytes_accessed=length * width * 20,
            transcendentals=heads * pairs,
        ),
    )(inv, qkv, grads, outs, lse)


def layer_norm(values, gain, shift):
    center = jnp.mean(values, axis=-1, keepdims=True)
    centred = values - center
    spread = jnp.mean(centred * centred, axis=-1, keepdims=True)
    return centred * lax.rsqrt(spread + EPSILON) * gain + shift


def smooth_gelu(values):
    return (
        0.5
        * values
        * (1.0 + jnp.tanh(0.7978845608028654 * (values + 0.044715 * values * values * values)))
    )


def matmul(left, right):
    return jnp.dot(left, right, preferred_element_type=F32)


def against(left, weight):
    return lax.dot_general(left, weight, (((1,), (1,)), ((), ())), preferred_element_type=F32)


def onto(left, right):
    return lax.dot_general(left, right, (((0,), (0,)), ((), ())), preferred_element_type=F32)


def body(
    sizes,
    tokens,
    block_order,
    qkv_weight,
    query_bias,
    value_bias,
    out_weight,
    out_bias,
    expand_weight,
    expand_bias,
    shrink_weight,
    shrink_bias,
    first_gain,
    first_shift,
    second_gain,
    second_shift,
    cotangent,
):
    outer, inner, xs, ks = (sizes[a] for a in ("o", "i", "x", "k"))
    spots = outer * inner
    shards = xs * ks
    rows, width = tokens.shape[1:]
    o, i = lax.axis_index("o"), lax.axis_index("i")
    shard = lax.axis_index("x") * ks + lax.axis_index("k")
    place = o * inner + i
    heads = -(-HEADS // spots)
    span = heads * HEAD_DIM
    padded = spots * span
    part = qkv_weight.shape[0]
    hidden = expand_weight.shape[1]
    piece = hidden // (shards * inner)
    ctx = (("o",), (outer,), "i")
    group = (("i", "x"), (inner, xs), "k")
    pair = (("x",), (xs,), "k")
    own = tokens[0]
    own_grad = cotangent[0]

    def columns(values, count):
        wide = values.reshape(values.shape[:-1] + (count, width))
        wide = jnp.pad(wide, [(0, 0)] * (wide.ndim - 1) + [(0, padded - width)])
        return lax.dynamic_slice_in_dim(wide, place * span, span, axis=wide.ndim - 1)

    qkv_own = columns(qkv_weight, 3).reshape(part, 3 * span)
    qkv_bias = jnp.concatenate(
        [columns(query_bias, 1)[0], jnp.zeros((span,), F32), columns(value_bias, 1)[0]]
    )
    gathered, qkv_columns = gather([own, qkv_own], [ctx, pair], 0)
    sequence = gathered.reshape(spots * rows, width)
    qkv_columns = qkv_columns.reshape(width, 3 * span)

    later = lax.optimization_barrier((out_weight, own_grad, gathered[0, 0, :8, :128]))
    out_full = lax.all_gather(later[0], ("x", "k"), axis=0, tiled=True)
    group_grad = lax.all_gather(later[1], ("i", "x", "k"), axis=0, tiled=True)

    expand_pieces = expand_weight.reshape(part, shards, inner, piece)
    expand_pieces = lax.dynamic_index_in_dim(expand_pieces, i, axis=2, keepdims=False)
    expand_pieces = expand_pieces.transpose(1, 0, 2)
    came = [lax.dynamic_index_in_dim(expand_pieces, shard, axis=0, keepdims=False)]
    for step in range(1, shards):
        there = lax.rem(shard + step, shards)
        sent = lax.dynamic_index_in_dim(expand_pieces, there, axis=0, keepdims=False)
        came.append(
            lax.ppermute(sent, ("x", "k"), [(f, (f + step) % shards) for f in range(shards)])
        )
    stacked = jnp.stack(came)
    order = lax.rem(shard - jnp.arange(shards) + shards, shards)
    expand_columns = jnp.take(stacked, order, axis=0).reshape(width, piece)
    shrink_rows = lax.dynamic_slice_in_dim(shrink_weight, i * piece, piece, axis=0)
    expand_own_bias = lax.dynamic_slice_in_dim(
        expand_bias, (shard * inner + i) * piece, piece, axis=0
    )

    order_row = block_order[0]
    blocks = order_row.shape[0]
    inv = jnp.sum(
        jnp.where(
            order_row[:, None] == jnp.arange(blocks, dtype=jnp.int32)[None, :],
            jnp.arange(blocks, dtype=jnp.int32)[:, None],
            0,
        ),
        axis=0,
    ).astype(jnp.int32)
    normed_low = layer_norm(sequence.astype(F32), first_gain, first_shift).astype(BF16)
    qkv = (matmul(normed_low, qkv_columns) + qkv_bias).astype(BF16)
    attended, log_sum = attend(inv, qkv, heads)
    came_out = exchange(
        attended.astype(BF16).reshape(spots, rows, span), ("o", "i"), (outer, inner), 1
    )
    attended_low = came_out.transpose(1, 0, 2).reshape(rows, padded)[:, :width]

    inputs = own.astype(F32)
    middle = inputs + matmul(attended_low, out_full) + out_bias
    lowered_two = layer_norm(middle, second_gain, second_shift).astype(BF16)

    (group_low,) = gather([lowered_two], [group], 2)
    group_low = group_low.reshape(-1, width)
    expanded = matmul(group_low, expand_columns) + expand_own_bias
    hidden_low = smooth_gelu(expanded).astype(BF16)
    grad_hidden = against(group_grad, shrink_rows)
    unused, gelu_back = jax.vjp(smooth_gelu, expanded)
    (grad_expanded,) = gelu_back(grad_hidden)
    expanded_low = grad_expanded.astype(BF16)
    grad_partial = against(expanded_low, expand_columns).astype(BF16)
    shape = (inner * xs, ks, rows, width)
    grad_normed_two = scatter(grad_partial.reshape(shape), *group, 3)
    result_partial = matmul(hidden_low, shrink_rows).astype(BF16)
    shrunk = scatter(result_partial.reshape(shape), *group, 4)
    result = middle + shrunk + shrink_bias

    grad_result = own_grad.astype(F32)
    unused, second_back = jax.vjp(layer_norm, middle, second_gain, second_shift)
    grad_middle_norm, grad_second_gain, grad_second_shift = second_back(grad_normed_two)
    grad_middle = grad_result + grad_middle_norm
    middle_low = grad_middle.astype(BF16)
    grad_att_low = against(middle_low, out_full).astype(BF16)
    grad_att_padded = jnp.pad(grad_att_low, ((0, 0), (0, padded - width)))
    grad_heads = exchange(
        grad_att_padded.reshape(rows, spots, span).transpose(1, 0, 2),
        ("o", "i"),
        (outer, inner),
        5,
    ).reshape(spots * rows, span)

    dqkv = attend_back(inv, qkv, grad_heads, attended, log_sum, heads)
    norm_partial = against(dqkv, qkv_columns).astype(BF16)
    grad_normed_one = scatter(norm_partial.reshape(outer, inner, rows, width), *ctx, 6)
    unused, first_back = jax.vjp(layer_norm, inputs, first_gain, first_shift)
    grad_first_input, grad_first_gain, grad_first_shift = first_back(grad_normed_one)
    grad_inputs = grad_middle + grad_first_input

    axes = ("o", "i", "x", "k")
    out_rows = width // (shards * inner)
    att_pieces = attended_low.reshape(rows, shards, inner, out_rows).transpose(2, 1, 0, 3)
    att_group = lax.all_to_all(
        att_pieces.reshape(inner * shards, rows, out_rows),
        ("i", "x", "k"),
        split_axis=0,
        concat_axis=0,
        tiled=True,
    ).reshape(-1, out_rows)
    middle_group = lax.all_gather(middle_low, ("i", "x", "k"), axis=0, tiled=True)
    both = jnp.concatenate(
        [onto(hidden_low, group_grad).astype(BF16), onto(att_group, middle_group).astype(BF16)],
        axis=0,
    )
    both = lax.psum_scatter(both, "o", scatter_dimension=1, tiled=True)
    cell = both.shape[1] // inner
    both = lax.all_to_all(
        both.reshape(piece + out_rows, inner, cell), "i", split_axis=1, concat_axis=1
    )
    grad_shrink = both[:piece].transpose(1, 0, 2).reshape(inner * piece, cell).astype(F32)
    grad_outw = both[piece:].transpose(1, 0, 2).reshape(inner * out_rows, cell).astype(F32)

    cuts = outer // shards
    expand_partial = onto(group_low, expanded_low).astype(BF16)
    expand_partial = expand_partial.reshape(shards, part, cuts, piece // cuts).transpose(0, 2, 1, 3)
    expand_partial = lax.psum_scatter(
        expand_partial.reshape(outer, part, piece // cuts), "o", scatter_dimension=0, tiled=True
    )[0]
    routes = []
    for so in range(outer):
        for si in range(inner):
            for sf in range(shards):
                spot = sf * (spots // shards) + si * (spots // (shards * inner)) + so % cuts
                routes.append(
                    (
                        (so * inner + si) * shards + sf,
                        spot * shards + so // cuts,
                    )
                )
    grad_expand = lax.ppermute(expand_partial, axes, routes).astype(F32)

    qkv_partial = onto(normed_low, dqkv).astype(BF16)
    qkv_partial = lax.psum_scatter(qkv_partial, ("x", "k"), scatter_dimension=0, tiled=True)
    qkv_all = lax.all_gather(qkv_partial, ("o", "i"), axis=0, tiled=False)
    qkv_all = qkv_all.reshape(spots, part, 3, span).transpose(1, 2, 0, 3)
    qkv_all = qkv_all.reshape(part, 3, padded)[:, :, :width].reshape(part, 3 * width)
    share = 3 * width // spots
    grad_qkv = lax.dynamic_slice_in_dim(qkv_all, place * share, share, axis=1).astype(F32)

    def placed(values, start, size):
        return lax.dynamic_update_slice_in_dim(jnp.zeros((size,), F32), values, start, axis=0)

    dqkv_sums = jnp.sum(dqkv.astype(F32), axis=0)
    small = [
        placed(dqkv_sums[:span], place * span, padded),
        placed(dqkv_sums[2 * span :], place * span, padded),
        jnp.sum(middle_low.astype(F32), axis=0),
        placed(
            jnp.sum(expanded_low.astype(F32), axis=0), (shard * inner + i) * piece, hidden
        ),
        jnp.sum(grad_result, axis=0),
        grad_first_gain,
        grad_first_shift,
        grad_second_gain,
        grad_second_shift,
    ]
    lengths = [s.shape[0] for s in small]
    devices = spots * shards
    lanes = 128 * (-(-sum(lengths) // (devices * 1024)))
    line = jnp.concatenate(small)
    line = jnp.pad(line, (0, devices * 8 * lanes - line.shape[0])).reshape(devices, 8, lanes)
    line = total(line, axes, (outer, inner, xs, ks), 7).reshape(-1)
    summed = []
    start = 0
    for length in lengths:
        summed.append(line[start : start + length])
        start += length
    summed[0] = summed[0][:width]
    summed[1] = summed[1][:width]
    return (
        result.astype(BF16)[None],
        grad_inputs[None],
        grad_qkv,
        grad_outw,
        grad_expand,
        grad_shrink,
        *summed,
    )


def solution(mesh):
    spots, shards = mesh.shape["ctx"], mesh.shape["fsdp"]
    sizes = {"o": spots // 2, "i": 2, "x": shards // 2, "k": 2}
    fine = Mesh(mesh.devices.reshape(tuple(sizes.values())), tuple(sizes))
    seq, pos = ("x", "k"), ("o", "i")
    weight = P(seq, None)
    placed = (
        P(seq, pos, None),
        P(seq, None),
        weight,
        P(),
        P(),
        weight,
        P(),
        weight,
        P(),
        weight,
        P(),
        P(),
        P(),
        P(),
        P(),
        P(seq, pos, None),
    )
    given = (P(seq, pos, None),) * 2 + (P(seq, pos),) * 4 + (P(),) * 9
    return jax.shard_map(
        functools.partial(body, sizes),
        mesh=fine,
        in_specs=placed,
        out_specs=given,
        check_vma=False,
    )
```

time: 1420 us -> 763 us (0.54)
  waiting for transfers between devices: 975 us -> 75.7 us
  Pallas kernels: 0 us -> 387 us
  matrix products: 189 us -> 69.2 us
  blocking collectives: 96.2 us -> 0 us
  local copies, waits for them, and re-layouts: 82 us -> 153 us
    all_gather x12 -> x4, waiting for transfers between devices: 704 us -> 63.1 us  [the longest x1 63 us: body(): qkv_all = lax.all_gather(qkv_partial, ('o', 'i'), axis=0, tiled=False)]
    pallas_call x0 -> x10, Pallas kernels: none -> 387 us  [the longest x3 138 us: scatter(): pl.pallas_call(functools.partial(scatter_kernel, axes, sizes, pair), out_...]
    psum x1 -> x0, waiting for transfers between devices: 132 us -> none  [body(): lax.psum((grad_query_bias, grad_value_bias, grad_out_bias, grad_expand_bi...]
    dot_general x22 -> x8, matrix products: 152 us -> 45.6 us  [the longest x4 24.2 us: onto(): lax.dot_general(left, right, (((0,), (0,)), ((), ())), preferred_element_...]
    all_gather x2 -> x0, blocking collectives: 65.1 us -> none  [the longest x1 38.5 us: body(): lax.all_gather(log_sum.T, 'ctx', axis=0, tiled=True)]
    reduce_scatter x3 -> x2, waiting for transfers between devices: 52.1 us -> 4.81 us  [the longest x1 4.79 us: body(): lax.psum_scatter(qkv_partial, ('x', 'k'), scatter_dimension=0, tiled=True)]
    unnamed x18 -> x8, waiting for transfers between devices: 43.4 us -> 1.41 us
    all_to_all x3 -> x2, waiting for transfers between devices: 43.1 us -> 6.35 us  [the longest x1 6.35 us: body(): lax.all_to_all(both.reshape(piece + out_rows, inner, cell), 'i', split_ax...]
  transfers between devices with their start and end apart: 20 -> 13, of which waited for: 14 -> 4; matrix products, arithmetic and copies ran while one was open for 20% -> 22% of each run, Pallas kernels for 0% -> 48%
where the time goes in v1:
time: 763 us; the launch traced here: 752 us
  Pallas kernels  387 us (51%)
  local copies, waits for them, and re-layouts  153 us (20%)
  waiting for transfers between devices  75.7 us (10%)
  matrix products  69.2 us (9%)
  other arithmetic  35.4 us (5%)
  starting transfers between devices  16.5 us (2%)
  between operations  15 us (2%)
    pallas_call x3, Pallas kernels, scatter(): pl.pallas_call(functools.partial(scatter_kernel, axes, sizes, pair), out_...  138 us
    pallas_call x1, Pallas kernels, total(): pl.pallas_call(functools.partial(total_kernel, axes, sizes), out_shape=ja...  81.1 us
    pallas_call x2, Pallas kernels, gather(): pl.pallas_call(functools.partial(gather_kernel, specs), out_shape=shapes,...  77.9 us
    all_gather x1, waiting for transfers between devices, body(): qkv_all = lax.all_gather(qkv_partial, ('o', 'i'), axis=0, tiled=False)  63 us
    pallas_call x2, Pallas kernels, exchange(): pl.pallas_call(functools.partial(exchange_kernel, axes, sizes), out_shape...  46.7 us
    dot_general x4, matrix products, onto(): lax.dot_general(left, right, (((0,), (0,)), ((), ())), preferred_element_...  24.2 us
    pallas_call x1, Pallas kernels, attend_back(): pl.pallas_call(functools.partial(attend_back_kernel, heads, block), out_s...  23.8 us
    dot_general x4, matrix products, against(): lax.dot_general(left, weight, (((1,), (1,)), ((), ())), preferred_element...  23.6 us
  transfers between devices with their start and end apart: 13, of which 4 were waited for; matrix products, arithmetic and copies ran while one was open for 22% of the time, Pallas kernels for 48%

profile of v1, /device:TPU:23, one launch (start us, length us, event | category | flops | bytes accessed | tf_op | source)
XLA Modules:
  0.0 752.0 jit_solution(10987783767483467108)
XLA Ops:
  9.3 11.9 %reshape.330 = bf16[400,4,2,800]{3,2,1,0:T(2,128)(2,1)} reshape(bf16[400,6400]{1,0:T(8,128)(2,1)} %param.23) | data formatting | bytes 10240000 | tf_op jit(solution)/shard_map/reshape | solution.py:614
  21.2 8.4 %constant_dynamic-slice_fusion.3 = (bf16[400,1,1,800]{3,2,1,0:T(2,128)(2,1)}, bf16[400,1,1,800]{3,2,1,0:T(2,128)(2,1)S(1)}, bf16[400,1,1,800]{3,2,1,0:T(2,128)(2,1)S(1)}, bf16[400,1,1,800]{3,2,1,0:T(2,128)(2,1)S(1)}) fusion(bf16[400,4,2,800]{3,2,1,0:T(2,128)(2,1)} %reshape.330, s32[]{:T(128)S(6)} %select_n.84, s32[]{:T(128)S(6)} %select_n.86, ...), kind=kLoop, calls=%fused_computation.89 | loop fusion | bytes 5120020 | tf_op jit(solution)/shard_map/dynamic-slice.4
  36.0 11.4 %reshape.322 = bf16[400,3,1600]{2,1,0:T(4,128)(2,1)} reshape(bf16[400,4800]{1,0:T(8,128)(2,1)} %param.18) | data formatting | bytes 7680000 | tf_op jit(solution)/shard_map/reshape | solution.py:598
  50.0 52.7 %gather0.1 = (bf16[4,2,128,1600]{3,2,1,0:T(8,128)(2,1)}, bf16[2,2,400,768]{3,2,1,0:T(8,128)(2,1)}) custom-call(bf16[128,1600]{1,0:T(8,128)(2,1)} %bitcast.128, bf16[400,768]{1,0:T(8,128)(2,1)} %bitcast.143), custom_call_target="tpu_custom_call" | custom-call | bytes 57344000 | tf_op jit(solution)/shard_map/gather0/pallas_call | solution.py:127
  102.8 2.6 convert_reduce_fusion
  108.6 4.1 add_convert_fusion.1.qkv
  113.5 19.8 %attend.1 = (f32[1024,256]{1,0:T(8,128)}, f32[4,1024]{1,0:T(4,128)}) custom-call(s32[16]{0:T(128)} %select_reduce_fusion.inv, bf16[1024,768]{1,0:T(8,128)(2,1)} %add_convert_fusion.1.qkv), custom_call_target="tpu_custom_call" | custom-call | flops 2684354560 | bytes 2621440 | tf_op jit(solution)/shard_map/attend/pallas_call | solution.py:390
  135.4 30.2 %exchange1.1 = bf16[8,128,256]{2,1,0:T(8,128)(2,1)} custom-call(bf16[8,128,256]{2,1,0:T(8,128)(2,1)} %bitcast.144), custom_call_target="tpu_custom_call" | custom-call | bytes 5242880 | tf_op jit(solution)/shard_map/exchange1/pallas_call | solution.py:166
  170.7 3.1 pad_maximum_fusion.1
  173.9 4.3 gather_fusion
  178.1 3.9 broadcast_select_fusion
  184.3 3.8 fusion.41
  190.1 25.1 %gather2.1 = bf16[4,2,128,1600]{3,2,1,0:T(8,128)(2,1)} custom-call(bf16[128,1600]{1,0:T(8,128)(2,1)} %add_convert_fusion.3.refs_0_), custom_call_target="tpu_custom_call" | custom-call | bytes 32768000 | tf_op jit(solution)/shard_map/gather2/pallas_call | solution.py:127
  215.2 6.1 fusion.42
  223.0 7.4 convolution_convert_fusion.2
  230.4 5.6 copy.100
  236.0 27.0 %scatter4.1 = f32[128,1600]{1,0:T(8,128)} custom-call(bf16[4,2,128,1600]{3,2,1,0:T(8,128)(2,1)} %bitcast.129), custom_call_target="tpu_custom_call" | custom-call | bytes 32768000 | tf_op jit(solution)/shard_map/scatter4/pallas_call | solution.py:218
  263.1 8.7 %convert_reduce_fusion.1 = (f32[800]{0:T(1024)S(1)}, bf16[1024,800]{0,1:T(8,128)(2,1)S(1)}) fusion(bf16[1024,1600]{1,0:T(8,128)(2,1)} %all-gather.8.cloned.1.call-done, bf16[1600,1600]{1,0:T(8,128)(2,1)} %param.25, s32[]{:T(128)S(6)} %select_n.97, f32[1024,800]{0,1:T(8,128)} %copy-done.27, f32[800]{0:T(1024)S(1)} %dynamic_slice.31), kind=kOutput, calls=%fused_computation.27 | convolution fusion | flops 2643557632 | bytes 10991876 | tf_op jit(solution)/shard_map/dot_general | solution.py:552
  273.0 4.9 convolution_convert_fusion
  277.9 5.4 copy.101
  283.3 26.8 %scatter3.1 = f32[128,1600]{1,0:T(8,128)} custom-call(bf16[4,2,128,1600]{3,2,1,0:T(8,128)(2,1)} %bitcast.130), custom_call_target="tpu_custom_call" | custom-call | bytes 32768000 | tf_op jit(solution)/shard_map/scatter3/pallas_call | solution.py:218
  312.0 2.7 fusion.39
  316.7 3.2 fusion.3
  319.9 4.1 convolution_convert_fusion.7
  325.0 16.6 %exchange5.1 = bf16[8,128,256]{2,1,0:T(8,128)(2,1)} custom-call(bf16[8,128,256]{2,1,0:T(8,128)(2,1)} %bitcast.147), custom_call_target="tpu_custom_call" | custom-call | bytes 5242880 | tf_op jit(solution)/shard_map/exchange5/pallas_call | solution.py:166
  341.6 23.8 %attend_back.1 = bf16[1024,768]{1,0:T(8,128)(2,1)} custom-call(s32[16]{0:T(128)} %select_reduce_fusion.inv, bf16[1024,768]{1,0:T(8,128)(2,1)} %add_convert_fusion.1.qkv, bf16[1024,256]{1,0:T(8,128)(2,1)} %bitcast.150, f32[1024,256]{1,0:T(8,128)} %get-tuple-element.23.outs, f32[4,1024]{1,0:T(4,128)} %get-tuple-element.26.lse), custom_call_target="tpu_custom_call" | custom-call | flops 6710886400 | bytes 5242880 | tf_op jit(solution)/shard_map/attend_back/pallas_call | solution.py:498
  365.4 6.8 convolution_convert_fusion.5
  372.3 6.1 convolution_convert_fusion.3
  378.4 5.3 copy.111
  384.5 5.1 all-to-all-start
  389.8 8.4 %convolution_convert_fusion.4 = bf16[800,1600]{1,0:T(8,128)(2,1)} fusion(bf16[1024,1600]{1,0:T(8,128)(2,1)} %all-gather.8.cloned.1.call-done, f32[1024,800]{0,1:T(8,128)} %copy-done.27, f32[800]{0:T(1024)S(1)} %dynamic_slice.31), kind=kOutput, calls=%fused_computation.18 | convolution fusion | flops 2630912000 | bytes 9116800 | tf_op jit(solution)/shard_map/dot_general | solution.py:556
  398.2 3.0 convolution_convert_fusion.6
  401.5 3.7 copy.116
  405.2 4.8 reduce-scatter.6.cloned.1.call-done
  410.2 5.9 convolution_convert_fusion.1
  416.1 5.4 copy.103
  421.6 83.8 %scatter6.1 = f32[128,1600]{1,0:T(8,128)} custom-call(bf16[4,2,128,1600]{3,2,1,0:T(8,128)(2,1)} %bitcast.131), custom_call_target="tpu_custom_call" | custom-call | bytes 32768000 | tf_op jit(solution)/shard_map/scatter6/pallas_call | solution.py:218
  509.8 4.6 collective-permute-start.3
  517.5 81.1 %total7.1 = f32[32,8,128]{2,1,0:T(8,128)} custom-call(f32[32,8,128]{2,1,0:T(8,128)} %pad_bitcast_fusion.source), custom_call_target="tpu_custom_call" | custom-call | tf_op jit(solution)/shard_map/total7/pallas_call | solution.py:270
  601.4 4.0 all-to-all-start.1
  609.4 6.3 all-to-all-done.1
  619.7 63.0 %all-gather.12.cloned.1.call-done = bf16[3200,768]{1,0:T(8,128)(2,1)} async-done(((bf16[400,768]{1,0:T(8,128)(2,1)}), bf16[3200,768]{1,0:T(8,128)(2,1)}) %all-gather.12.cloned.1.call-update) | async-done | bytes 4915216 | tf_op jit(solution)/shard_map/all_gather | solution.py:734
  682.7 7.4 copy.104
  690.2 17.0 %reshape.336 = bf16[8,400,3,256]{1,0,3,2:T(8,128)(2,1)} reshape(bf16[3200,768]{0,1:T(8,128)(2,1)} %copy.104) | data formatting | bytes 9830400 | tf_op jit(solution)/shard_map/reshape | solution.py:735
  707.2 9.4 %copy.105 = bf16[400,3,8,256]{3,2,0,1:T(8,128)(2,1)} copy(bf16[400,3,8,256]{0,2,3,1:T(8,128)(2,1)} %bitcast.127) | data formatting | bytes 9830400 | tf_op jit(solution)/shard_map/transpose | solution.py:735
  716.5 8.6 %reshape.337 = bf16[400,3,2048]{2,0,1:T(8,128)(2,1)} reshape(bf16[400,3,8,256]{3,2,0,1:T(8,128)(2,1)} %copy.105) | data formatting | bytes 9830400 | tf_op jit(solution)/shard_map/reshape | solution.py:736
  727.2 4.4 copy.106
  731.6 11.1 %reshape.338 = bf16[400,4800]{1,0:T(8,128)(2,1)} reshape(bf16[400,3,1600]{2,1,0:T(4,128)(2,1)} %copy.106) | data formatting | bytes 7680000 | tf_op jit(solution)/shard_map/reshape | solution.py:736
  (155 shorter events, 58.2 us)
Async XLA Ops:
  7.2 177.1 %all-gather.6.cloned.1.call-start = ((), (), s32[]{:S(2)}) async-start(), calls=%async_computation.5 | async-start | bytes 6656000 | tf_op jit(solution)/shard_map/all_gather | solution.py:611
  9.2 253.8 %all-gather.8.cloned.1.call-start = ((), (), s32[]{:S(2)}) async-start(), calls=%async_computation.6 | async-start | bytes 3833856 | tf_op jit(solution)/shard_map/all_gather | solution.py:612
  29.6 5.4 copy-start.23
  29.6 5.4 copy-start.24
  29.6 5.4 copy-start.16
  30.6 140.2 %collective-permute-start = (bf16[400,800]{1,0:T(8,128)(2,1)}, bf16[400,800]{1,0:T(8,128)(2,1)}, u32[]{:S(2)}, u32[]{:S(2)}) collective-permute-start(bf16[400,800]{1,0:T(8,128)(2,1)} %bitcast.123), channel_id=1, source_target_pairs={{0,1},{1,2},{2,3},{3,0},{4,5},{5,6},{6,7},{7,4},{8,9},{9,10},{10,1... | collective-permute-start | bytes 1920008 | tf_op jit(solution)/shard_map/ppermute | solution.py:622
  32.2 138.5 %collective-permute-start.1 = (bf16[400,800]{1,0:T(8,128)(2,1)}, bf16[400,800]{1,0:T(8,128)(2,1)}, u32[]{:S(2)}, u32[]{:S(2)}) collective-permute-start(bf16[400,800]{1,0:T(8,128)(2,1)} %bitcast.122), channel_id=1, source_target_pairs={{0,2},{1,3},{2,0},{3,1},{4,6},{5,7},{6,4},{7,5},{8,10},{9,11},{10,... | collective-permute-start | bytes 1920008 | tf_op jit(solution)/shard_map/ppermute | solution.py:622
  34.4 136.4 %collective-permute-start.2 = (bf16[400,800]{1,0:T(8,128)(2,1)}, bf16[400,800]{1,0:T(8,128)(2,1)}, u32[]{:S(2)}, u32[]{:S(2)}) collective-permute-start(bf16[400,800]{1,0:T(8,128)(2,1)} %bitcast.121), channel_id=1, source_target_pairs={{0,3},{1,0},{2,1},{3,2},{4,7},{5,4},{6,5},{7,6},{8,11},{9,8},{10,9... | collective-permute-start | bytes 1920008 | tf_op jit(solution)/shard_map/ppermute | solution.py:622
  34.4 363.8 %all-gather.10.cloned.1.call-start = ((), (), s32[]{:S(2)}) async-start(), calls=%async_computation.8 | async-start | bytes 3833856 | tf_op jit(solution)/shard_map/all_gather | solution.py:700
  102.8 3.0 copy-start
  102.8 4.1 copy-start.17
  102.8 4.1 copy-start.19
  106.9 1.7 copy-start.25
  108.6 4.3 copy-start.26
  178.1 3.9 copy-start.1
  182.0 2.3 copy-start.20
  184.3 4.8 copy-start.18
  184.3 4.8 copy-start.21
  188.2 0.9 copy-start.2
  221.3 1.7 copy-start.27
  263.1 9.9 %copy-start.12 = (bf16[1600,800]{1,0:T(8,128)(2,1)S(1)}, bf16[1600,800]{1,0:T(8,128)(2,1)}, u32[]{:S(2)}) copy-start(bf16[1600,800]{1,0:T(8,128)(2,1)} %bitcast_select_fusion) | copy-start | bytes 7680004
  271.7 1.2 copy-start.28
  283.3 28.6 %copy-start.22 = (f32[1600]{0:T(1024)S(1)}, f32[1600]{0:T(1024)}, u32[]{:S(2)}) copy-start(f32[1600]{0:T(1024)} %param.26) | copy-start | bytes 19204
  310.1 5.5 copy-start.7
  314.7 0.9 copy-start.5
  316.7 93.4 %reduce-scatter.6.cloned.1.call-start = ((), (), s32[]{:S(2)}) async-start(), calls=%async_computation.7 | async-start | bytes 3072000 | tf_op jit(solution)/shard_map/reduce_scatter | solution.py:733
  316.7 3.2 copy-start.9
  365.4 6.9 copy-start.11
  372.2 137.5 %reduce-scatter.8.cloned.1.call-start = ((), (), s32[]{:S(2)}) async-start(), calls=%async_computation.9 | async-start | bytes 3584000 | tf_op jit(solution)/shard_map/reduce_scatter | solution.py:716
  378.4 5.3 copy-start.10
  384.5 13.6 %all-to-all-start = ((bf16[8,128,200]{1,2,0:T(8,128)(2,1)}), bf16[8,128,200]{1,2,0:T(8,128)(2,1)S(1)}, u32[]{:S(2)}, u32[]{:S(2)}) async-start(bf16[8,128,200]{1,2,0:T(8,128)(2,1)} %bitcast.31), calls=%async_computation.1 | async-start | bytes 819200 | tf_op jit(solution)/shard_map/all_to_all | solution.py:693
  389.6 211.8 %reduce-scatter.10.cloned.1.call-start = ((), (), s32[]{:S(2)}) async-start(), calls=%async_computation.11 | async-start | bytes 4096000
  398.2 3.0 copy-start.13
  405.2 4.9 copy-start.3
  405.2 5.1 copy-start.15
  405.2 277.6 %all-gather.12.cloned.1.call-start = ((), (), s32[]{:S(2)}) async-start(), calls=%async_computation.10 | async-start | bytes 5529600 | tf_op jit(solution)/shard_map/all_gather | solution.py:734
  421.5 87.8 %copy-start.6 = (f32[128,1600]{1,0:T(8,128)S(1)}, f32[128,1600]{1,0:T(8,128)}, u32[]{:S(2)}) copy-start(f32[128,1600]{1,0:T(8,128)} %copy-done.5) | copy-start | bytes 2457604
  421.6 87.8 %copy-start.8 = (bf16[1,128,1600]{2,1,0:T(8,128)(2,1)S(1)}, bf16[1,128,1600]{2,1,0:T(8,128)(2,1)}, u32[]{:S(2)}) copy-start(bf16[1,128,1600]{2,1,0:T(8,128)(2,1)} %copy.98) | copy-start | bytes 1228804
  505.4 3.4 copy-start.4
  506.9 7.5 %copy-start.14 = (bf16[1,128,1600]{2,1,0:T(8,128)(2,1)S(1)}, bf16[1,128,1600]{2,1,0:T(8,128)(2,1)}, u32[]{:S(2)}) copy-start(bf16[1,128,1600]{2,1,0:T(8,128)(2,1)} %get-tuple-element.118) | copy-start | bytes 1228804
  509.8 98.5 %collective-permute-start.3 = (bf16[400,800]{1,0:T(8,128)(2,1)}, bf16[400,800]{1,0:T(8,128)(2,1)S(1)}, u32[]{:S(2)}, u32[]{:S(2)}) collective-permute-start(bf16[400,800]{1,0:T(8,128)(2,1)} %bitcast.162), channel_id=1, source_target_pairs={{0,0},{1,8},{2,16},{3,24},{4,4},{5,12},{6,20},{7,28},{8,1},{9,9},{... | collective-permute-start | bytes 1920008 | tf_op jit(solution)/shard_map/ppermute | solution.py:730
  601.4 14.3 %all-to-all-start.1 = ((bf16[1000,2,200]{0,2,1:T(8,128)(2,1)}), bf16[1000,2,200]{0,2,1:T(8,128)(2,1)S(1)}, u32[]{:S(2)}, u32[]{:S(2)}) async-start(bf16[1000,2,200]{0,2,1:T(8,128)(2,1)} %bitcast.149), calls=%async_computation.2 | async-start | bytes 1638400 | tf_op jit(solution)/shard_map/all_to_all | solution.py:707
  725.1 2.1 slice-start
Sparse Core Ops, SparseCore 0:
  9.5 56.3 all-gather.5
  67.8 43.2 all-gather.7
  316.8 37.8 all-gather.9
  372.4 37.6 reduce-scatter.5
  412.2 89.0 reduce-scatter.7
  503.4 97.9 reduce-scatter.9
  603.6 79.0 all-gather.11

commit v2 on v1

--- a/solution.py
+++ b/solution.py
@@ -59,101 +59,199 @@
     )
 
 
+class Gather:
+    def __init__(self, axes, sizes, pair, source, out, send, recv, local):
+        self.axes, self.sizes = axes, sizes
+        self.offs = offsets(sizes)
+        self.side = lax.axis_index(pair)
+        self.mate = {pair: 1 - self.side}
+        self.source, self.out, self.send, self.recv, self.local = source, out, send, recv, local
+        self.started = []
+
+    def peers(self):
+        return [moved(self.axes, self.sizes, o) for o in self.offs] + [self.mate]
+
+    def mine(self):
+        return self.out.at[flat(own_place(self.axes), self.axes, self.sizes), self.side]
+
+    def start(self):
+        pltpu.make_async_copy(self.source, self.mine(), self.local).start()
+        last = len(self.offs)
+        for t, peer in enumerate(self.peers()):
+            copy = remote(self.source, self.mine(), self.send.at[t], self.recv.at[t], peer)
+            copy.start()
+            self.started.append(copy)
+
+    def hand_on(self):
+        last = len(self.offs)
+        for t, off in enumerate(self.offs):
+            came = flat(moved(self.axes, self.sizes, off, -1), self.axes, self.sizes)
+            block = self.out.at[came, self.side]
+            remote(self.source, block, self.send.at[t], self.recv.at[t], self.mate).wait_recv()
+            slot = last + 1 + t
+            copy = remote(block, block, self.send.at[slot], self.recv.at[slot], self.mate)
+            copy.start()
+            self.started.append(copy)
+
+    def finish(self):
+        last = len(self.offs)
+        me = flat(own_place(self.axes), self.axes, self.sizes)
+        pltpu.make_async_copy(self.source, self.mine(), self.local).wait()
+        block = self.out.at[me, 1 - self.side]
+        remote(self.source, block, self.send.at[last], self.recv.at[last], self.mate).wait_recv()
+        for t, off in enumerate(self.offs):
+            came = flat(moved(self.axes, self.sizes, off, -1), self.axes, self.sizes)
+            slot = last + 1 + t
+            block = self.out.at[came, 1 - self.side]
+            remote(
+                self.source, block, self.send.at[slot], self.recv.at[slot], self.mate
+            ).wait_recv()
+        for copy in self.started:
+            copy.wait_send()
+
+
+def gather_shape(block, spec):
+    group = 1
+    for s in spec[1]:
+        group *= s
+    return jax.ShapeDtypeStruct((group, 2) + block.shape, block.dtype)
+
+
+def gather_scratch(spec):
+    group = 1
+    for s in spec[1]:
+        group *= s
+    return [
+        pltpu.SemaphoreType.DMA((2 * group,)),
+        pltpu.SemaphoreType.DMA((2 * group,)),
+        pltpu.SemaphoreType.DMA,
+    ]
+
+
+def sent_estimate(size):
+    return pl.CostEstimate(flops=0, bytes_accessed=20 * size, transcendentals=0)
+
+
 def gather_kernel(specs, *refs):
     count = len(specs)
-    ins, outs = refs[:count], refs[count : 2 * count]
-    scratch = refs[2 * count :]
-    plans = []
-    peers = []
-    for index, (axes, sizes, pair) in enumerate(specs):
-        offs = offsets(sizes)
-        send, recv, local = scratch[3 * index : 3 * index + 3]
-        side = lax.axis_index(pair)
-        mate = {pair: 1 - side}
-        plans.append((axes, sizes, offs, side, mate, ins[index], outs[index], send, recv, local))
-        peers += [moved(axes, sizes, o) for o in offs] + [mate]
-    greet(peers)
-    started = []
-    for axes, sizes, offs, side, mate, source, out, send, recv, local in plans:
-        me = flat(own_place(axes), axes, sizes)
-        here = pltpu.make_async_copy(source, out.at[me, side], local)
-        here.start()
-        for t, off in enumerate(offs):
-            copy = remote(
-                source, out.at[me, side], send.at[t], recv.at[t], moved(axes, sizes, off)
-            )
-            copy.start()
-            started.append(copy)
-        last = len(offs)
-        copy = remote(source, out.at[me, side], send.at[last], recv.at[last], mate)
-        copy.start()
-        started.append(copy)
-    for axes, sizes, offs, side, mate, source, out, send, recv, local in plans:
-        last = len(offs)
-        for t, off in enumerate(offs):
-            came = flat(moved(axes, sizes, off, -1), axes, sizes)
-            block = out.at[came, side]
-            remote(source, block, send.at[t], recv.at[t], mate).wait_recv()
-            copy = remote(block, block, send.at[last + 1 + t], recv.at[last + 1 + t], mate)
-            copy.start()
-            started.append(copy)
-    for axes, sizes, offs, side, mate, source, out, send, recv, local in plans:
-        last = len(offs)
-        me = flat(own_place(axes), axes, sizes)
-        pltpu.make_async_copy(source, out.at[me, side], local).wait()
-        remote(source, out.at[me, 1 - side], send.at[last], recv.at[last], mate).wait_recv()
-        for t, off in enumerate(offs):
-            came = flat(moved(axes, sizes, off, -1), axes, sizes)
-            remote(
-                source, out.at[came, 1 - side], send.at[last + 1 + t], recv.at[last + 1 + t], mate
-            ).wait_recv()
-    for copy in started:
-        copy.wait_send()
+    gathers = [
+        Gather(*spec, refs[n], refs[count + n], *refs[2 * count + 3 * n : 2 * count + 3 * n + 3])
+        for n, spec in enumerate(specs)
+    ]
+    greet([peer for g in gathers for peer in g.peers()])
+    for g in gathers:
+        g.start()
+    for g in gathers:
+        g.hand_on()
+    for g in gathers:
+        g.finish()
 
 
 def gather(blocks, specs, ident):
-    shapes, scratch, moved_bytes = [], [], 0
-    for block, (axes, sizes, pair) in zip(blocks, specs):
-        group = 1
-        for s in sizes:
-            group *= s
-        shapes.append(jax.ShapeDtypeStruct((group, 2) + block.shape, block.dtype))
-        scratch += [
-            pltpu.SemaphoreType.DMA((2 * group,)),
-            pltpu.SemaphoreType.DMA((2 * group,)),
-            pltpu.SemaphoreType.DMA,
-        ]
-        moved_bytes += 2 * group * block.size * 2
+    shapes = [gather_shape(block, spec) for block, spec in zip(blocks, specs)]
     return pl.pallas_call(
         functools.partial(gather_kernel, specs),
         out_shape=shapes,
         in_specs=[VMEM] * len(blocks),
         out_specs=[ANY] * len(blocks),
-        scratch_shapes=scratch,
+        scratch_shapes=[s for spec in specs for s in gather_scratch(spec)],
         name="gather%d" % ident,
         compiler_params=pltpu.CompilerParams(collective_id=ident, has_side_effects=True),
-        cost_estimate=pl.CostEstimate(
-            flops=0, bytes_accessed=10 * moved_bytes, transcendentals=0
-        ),
+        cost_estimate=sent_estimate(sum(s.size for s in shapes)),
     )(*blocks)
 
 
-def exchange_kernel(axes, sizes, source, out, send, recv, local):
-    offs = offsets(sizes)
-    greet([moved(axes, sizes, o) for o in offs])
-    me = flat(own_place(axes), axes, sizes)
-    here = pltpu.make_async_copy(source.at[me], out.at[me], local)
+def first_kernel(
+    specs, shard_sizes, own, columns, weight, all_tokens, all_columns, pieces, whole, cut, *sems
+):
+    axes = ("x", "k")
+    offs = offsets(shard_sizes)
+    tokens = Gather(*specs[0], own, all_tokens, *sems[0:3])
+    heads = Gather(*specs[1], columns, all_columns, *sems[3:6])
+    read, send, recv, local = sems[6:10]
+    fetch = pltpu.make_async_copy(weight, whole, read)
+    fetch.start()
+    greet(tokens.peers() + heads.peers() + [moved(axes, shard_sizes, o) for o in offs])
+    tokens.start()
+    heads.start()
+    fetch.wait()
+    width = cut.shape[2]
+    inner = lax.axis_index("i")
+    for half in range(2):
+
+        @pl.when(inner == half)
+        def _():
+            for f in range(cut.shape[0]):
+                low = (2 * f + half) * width
+                cut[f] = whole[:, low : low + width]
+
+    me = flat(own_place(axes), axes, shard_sizes)
+    here = pltpu.make_async_copy(cut.at[me], pieces.at[me], local)
     here.start()
     started = []
     for t, off in enumerate(offs):
+        peer = moved(axes, shard_sizes, off)
+        there = flat(peer, axes, shard_sizes)
+        copy = remote(cut.at[there], pieces.at[me], send.at[t], recv.at[t], peer)
+        copy.start()
+        started.append(copy)
+    heads.hand_on()
+    tokens.hand_on()
+    here.wait()
+    for t, off in enumerate(offs):
+        peer = moved(axes, shard_sizes, off, -1)
+        came = flat(peer, axes, shard_sizes)
+        remote(cut.at[came], pieces.at[came], send.at[t], recv.at[t], peer).wait_recv()
+    for copy in started:
+        copy.wait_send()
+    heads.finish()
+    tokens.finish()
+
+
+def first_gather(own, columns, weight, specs, shard_sizes, piece, ident):
+    shards = shard_sizes[0] * shard_sizes[1]
+    part = weight.shape[0]
+    shapes = [
+        gather_shape(own, specs[0]),
+        gather_shape(columns, specs[1]),
+        jax.ShapeDtypeStruct((shards, part, piece), BF16),
+    ]
+    return pl.pallas_call(
+        functools.partial(first_kernel, specs, shard_sizes),
+        out_shape=shapes,
+        in_specs=[VMEM, VMEM, ANY],
+        out_specs=[ANY] * 3,
+        scratch_shapes=[
+            pltpu.VMEM(weight.shape, BF16),
+            pltpu.VMEM((shards, part, piece), BF16),
+            *gather_scratch(specs[0]),
+            *gather_scratch(specs[1]),
+            pltpu.SemaphoreType.DMA,
+            pltpu.SemaphoreType.DMA((shards,)),
+            pltpu.SemaphoreType.DMA((shards,)),
+            pltpu.SemaphoreType.DMA,
+        ],
+        name="first%d" % ident,
+        compiler_params=pltpu.CompilerParams(collective_id=ident, has_side_effects=True),
+        cost_estimate=sent_estimate(sum(s.size for s in shapes)),
+    )(own, columns, weight)
+
+
+def pieces_out(axes, sizes, source, out, send, recv):
+    me = flat(own_place(axes), axes, sizes)
+    started = []
+    for t, off in enumerate(offsets(sizes)):
         peer = moved(axes, sizes, off)
         copy = remote(
             source.at[flat(peer, axes, sizes)], out.at[me], send.at[t], recv.at[t], peer
         )
         copy.start()
         started.append(copy)
-    here.wait()
-    for t, off in enumerate(offs):
+    return started
+
+
+def pieces_in(axes, sizes, source, out, send, recv, started):
+    for t, off in enumerate(offsets(sizes)):
         peer = moved(axes, sizes, off, -1)
         came = flat(peer, axes, sizes)
         remote(source.at[came], out.at[came], send.at[t], recv.at[t], peer).wait_recv()
@@ -161,81 +259,226 @@
         copy.wait_send()
 
 
-def exchange(pieces, axes, sizes, ident):
-    group = pieces.shape[0]
+def to_tokens_kernel(
+    axes, sizes, spec, source, block, out, everyone, came, send, recv, *gather_sems
+):
+    beside = Gather(*spec, block, everyone, *gather_sems)
+    greet([moved(axes, sizes, o) for o in offsets(sizes)] + beside.peers())
+    started = pieces_out(axes, sizes, source, came, send, recv)
+    beside.start()
+    me = flat(own_place(axes), axes, sizes)
+    came[me] = source[me]
+    pieces_in(axes, sizes, source, came, send, recv, started)
+    span, width = came.shape[2], out.shape[1]
+    for d in range(came.shape[0]):
+        low, high = d * span, min((d + 1) * span, width)
+        if low < high:
+            out[:, low:high] = came[d, :, : high - low]
+    beside.hand_on()
+    beside.finish()
+
+
+def to_tokens(pieces, block, width, axes, sizes, spec, ident):
+    group, rows, span = pieces.shape
     return pl.pallas_call(
-        functools.partial(exchange_kernel, axes, sizes),
-        out_shape=jax.ShapeDtypeStruct(pieces.shape, pieces.dtype),
-        in_specs=[VMEM],
-        out_specs=VMEM,
+        functools.partial(to_tokens_kernel, axes, sizes, spec),
+        out_shape=[
+            jax.ShapeDtypeStruct((rows, width), pieces.dtype),
+            gather_shape(block, spec),
+        ],
+        in_specs=[VMEM, VMEM],
+        out_specs=[VMEM, ANY],
         scratch_shapes=[
+            pltpu.VMEM(pieces.shape, pieces.dtype),
             pltpu.SemaphoreType.DMA((group,)),
             pltpu.SemaphoreType.DMA((group,)),
-            pltpu.SemaphoreType.DMA,
+            *gather_scratch(spec),
         ],
-        name="exchange%d" % ident,
+        name="to_tokens%d" % ident,
         compiler_params=pltpu.CompilerParams(collective_id=ident, has_side_effects=True),
-        cost_estimate=pl.CostEstimate(
-            flops=0, bytes_accessed=20 * pieces.size, transcendentals=0
-        ),
-    )(pieces)
-
-
-def scatter_kernel(axes, sizes, pair, source, out, first, summed, last, send, recv):
-    offs = offsets(sizes)
-    side = lax.axis_index(pair)
-    mate = {pair: 1 - side}
-    greet([moved(axes, sizes, o) for o in offs] + [mate])
+        cost_estimate=sent_estimate(3 * pieces.size),
+    )(pieces, block)
+
+
+def to_heads_kernel(
+    axes,
+    sizes,
+    spec,
+    group_axes,
+    group_sizes,
+    source,
+    block,
+    att,
+    out,
+    everyone,
+    att_out,
+    cut,
+    att_cut,
+    send,
+    recv,
+    att_send,
+    att_recv,
+    *gather_sems,
+):
+    beside = Gather(*spec, block, everyone, *gather_sems)
+    greet(
+        [moved(axes, sizes, o) for o in offsets(sizes)]
+        + [moved(group_axes, group_sizes, o) for o in offsets(group_sizes)]
+    )
+    span, width = cut.shape[2], source.shape[1]
+    for d in range(cut.shape[0]):
+        low, high = d * span, min((d + 1) * span, width)
+        if high - low < span:
+            cut[d] = jnp.zeros(cut.shape[1:], cut.dtype)
+        if low < high:
+            cut[d, :, : high - low] = source[:, low:high]
+    cell = att_cut.shape[2]
+    inner, shards = group_sizes[0], group_sizes[1] * group_sizes[2]
+    for half in range(inner):
+        for f in range(shards):
+            low = (f * inner + half) * cell
+            att_cut[half * shards + f] = att[:, low : low + cell]
+    started = pieces_out(axes, sizes, cut, out, send, recv)
+    att_started = pieces_out(group_axes, group_sizes, att_cut, att_out, att_send, att_recv)
+    beside.start()
     me = flat(own_place(axes), axes, sizes)
-    count = len(offs)
-    started = []
-    for t, off in enumerate(offs + [(0,) * len(sizes)]):
-        there = flat(moved(axes, sizes, off), axes, sizes)
-        copy = remote(source.at[there, 1 - side], first.at[t], send.at[t], recv.at[t], mate)
-        copy.start()
-        started.append(copy)
-    for t, off in enumerate(offs):
-        peer = moved(axes, sizes, off)
-        there = flat(peer, axes, sizes)
-        started[t].wait_recv()
-        summed[t] = (source[there, side].astype(F32) + first[t].astype(F32)).astype(BF16)
-        slot = count + 1 + t
-        copy = remote(summed.at[t], last.at[t], send.at[slot], recv.at[slot], peer)
-        copy.start()
-        started.append(copy)
-    started[count].wait_recv()
-    out[...] = source[me, side].astype(F32) + first[count].astype(F32)
-    for t in range(count):
-        started[count + 1 + t].wait_recv()
-        out[...] += last[t].astype(F32)
-    for copy in started:
-        copy.wait_send()
-
-
-def scatter(partial, axes, sizes, pair, ident):
-    group = partial.shape[0]
-    block = partial.shape[2:]
+    out[me] = cut[me]
+    me = flat(own_place(group_axes), group_axes, group_sizes)
+    att_out[me] = att_cut[me]
+    pieces_in(axes, sizes, cut, out, send, recv, started)
+    beside.hand_on()
+    pieces_in(group_axes, group_sizes, att_cut, att_out, att_send, att_recv, att_started)
+    beside.finish()
+
+
+def to_heads(source, block, att, span, axes, sizes, spec, group_axes, group_sizes, ident):
+    rows, width = source.shape
+    count, group = 1, 1
+    for s in sizes:
+        count *= s
+    for s in group_sizes:
+        group *= s
+    cell = width // group
     return pl.pallas_call(
-        functools.partial(scatter_kernel, axes, sizes, pair),
-        out_shape=jax.ShapeDtypeStruct(block, F32),
-        in_specs=[VMEM],
-        out_specs=VMEM,
+        functools.partial(to_heads_kernel, axes, sizes, spec, group_axes, group_sizes),
+        out_shape=[
+            jax.ShapeDtypeStruct((count, rows, span), source.dtype),
+            gather_shape(block, spec),
+            jax.ShapeDtypeStruct((group, rows, cell), att.dtype),
+        ],
+        in_specs=[VMEM, VMEM, VMEM],
+        out_specs=[VMEM, ANY, VMEM],
         scratch_shapes=[
+            pltpu.VMEM((count, rows, span), source.dtype),
+            pltpu.VMEM((group, rows, cell), att.dtype),
+            pltpu.SemaphoreType.DMA((count,)),
+            pltpu.SemaphoreType.DMA((count,)),
+            pltpu.SemaphoreType.DMA((group,)),
+            pltpu.SemaphoreType.DMA((group,)),
+            *gather_scratch(spec),
+        ],
+        name="to_heads%d" % ident,
+        compiler_params=pltpu.CompilerParams(collective_id=ident, has_side_effects=True),
+        cost_estimate=sent_estimate(8 * source.size),
+    )(source, block, att)
+
+
+class Scatter:
+    def __init__(self, axes, sizes, pair, source, out, first, summed, last, send, recv):
+        self.axes, self.sizes = axes, sizes
+        self.offs = offsets(sizes)
+        self.side = lax.axis_index(pair)
+        self.mate = {pair: 1 - self.side}
+        self.source, self.out = source, out
+        self.first, self.summed, self.last = first, summed, last
+        self.send, self.recv = send, recv
+        self.started = []
+
+    def peers(self):
+        return [moved(self.axes, self.sizes, o) for o in self.offs] + [self.mate]
+
+    def start(self):
+        for t, off in enumerate(self.offs + [(0,) * len(self.sizes)]):
+            there = flat(moved(self.axes, self.sizes, off), self.axes, self.sizes)
+            copy = remote(
+                self.source.at[there, 1 - self.side],
+                self.first.at[t],
+                self.send.at[t],
+                self.recv.at[t],
+                self.mate,
+            )
+            copy.start()
+            self.started.append(copy)
+
+    def add(self):
+        count = len(self.offs)
+        for t, off in enumerate(self.offs):
+            peer = moved(self.axes, self.sizes, off)
+            there = flat(peer, self.axes, self.sizes)
+            self.started[t].wait_recv()
+            self.summed[t] = (
+                self.source[there, self.side].astype(F32) + self.first[t].astype(F32)
+            ).astype(BF16)
+            slot = count + 1 + t
+            copy = remote(
+                self.summed.at[t], self.last.at[t], self.send.at[slot], self.recv.at[slot], peer
+            )
+            copy.start()
+            self.started.append(copy)
+
+    def finish(self):
+        count = len(self.offs)
+        me = flat(own_place(self.axes), self.axes, self.sizes)
+        self.started[count].wait_recv()
+        self.out[...] = self.source[me, self.side].astype(F32) + self.first[count].astype(F32)
+        for t in range(count):
+            self.started[count + 1 + t].wait_recv()
+            self.out[...] += self.last[t].astype(F32)
+        for copy in self.started:
+            copy.wait_send()
+
+
+def scatter_kernel(specs, *refs):
+    count = len(specs)
+    scatters = [
+        Scatter(*spec, refs[n], refs[count + n], *refs[2 * count + 5 * n : 2 * count + 5 * n + 5])
+        for n, spec in enumerate(specs)
+    ]
+    greet([peer for s in scatters for peer in s.peers()])
+    for s in scatters:
+        s.start()
+    for s in scatters:
+        s.add()
+    for s in scatters:
+        s.finish()
+
+
+def scatter(partials, specs, ident):
+    scratch = []
+    for partial in partials:
+        group, block = partial.shape[0], partial.shape[2:]
+        scratch += [
             pltpu.VMEM((group,) + block, BF16),
             pltpu.VMEM((group - 1,) + block, BF16),
             pltpu.VMEM((group - 1,) + block, BF16),
             pltpu.SemaphoreType.DMA((2 * group,)),
             pltpu.SemaphoreType.DMA((2 * group,)),
-        ],
+        ]
+    return pl.pallas_call(
+        functools.partial(scatter_kernel, specs),
+        out_shape=[jax.ShapeDtypeStruct(p.shape[2:], F32) for p in partials],
+        in_specs=[VMEM] * len(partials),
+        out_specs=[VMEM] * len(partials),
+        scratch_shapes=scratch,
         name="scatter%d" % ident,
         compiler_params=pltpu.CompilerParams(collective_id=ident, has_side_effects=True),
-        cost_estimate=pl.CostEstimate(
-            flops=0, bytes_accessed=20 * partial.size, transcendentals=0
-        ),
-    )(partial)
-
-
-def total_kernel(axes, sizes, source, out, came, send, recv):
+        cost_estimate=sent_estimate(sum(p.size for p in partials)),
+    )(*partials)
+
+
+def last_kernel(
+    axes, sizes, spots, heads, share, source, blocks, out, routed, came, send, recv, hop, land
+):
     offs = offsets(sizes)
     greet([moved(axes, sizes, o) for o in offs])
     me = flat(own_place(axes), axes, sizes)
@@ -248,6 +491,53 @@
         )
         copy.start()
         started.append(copy)
+
+    ctx_axes, ctx_sizes = axes[:3], sizes[:3]
+    place = flat(own_place(ctx_axes), ctx_axes, ctx_sizes)
+
+    def where(spot):
+        return {
+            ctx_axes[0]: spot // (ctx_sizes[1] * ctx_sizes[2]),
+            ctx_axes[1]: (spot // ctx_sizes[2]) % ctx_sizes[1],
+            ctx_axes[2]: spot % ctx_sizes[2],
+        }
+
+    def each_sent(act):
+        for part in range(3):
+            for h in range(heads):
+                head = place * heads + h
+                block = part * HEADS + head
+                low = (block * HEAD_DIM) // share
+                high = (block * HEAD_DIM + HEAD_DIM - 1) // share
+                index = part * heads + h
+                for which, owner, needed in (
+                    (0, low, head < HEADS),
+                    (1, high, (head < HEADS) & (high != low)),
+                ):
+
+                    @pl.when(needed)
+                    def _(which=which, owner=owner, block=block, index=index):
+                        act(index, 2 * index + which, owner, block - (share * owner) // HEAD_DIM)
+
+    def send_block(index, slot, owner, target):
+        @pl.when(owner != place)
+        def _():
+            remote(
+                blocks.at[index], routed.at[target], hop.at[slot], land.at[target], where(owner)
+            ).start()
+
+        @pl.when(owner == place)
+        def _():
+            routed[target] = blocks[index]
+
+    def sent_block(index, slot, owner, target):
+        @pl.when(owner != place)
+        def _():
+            remote(
+                blocks.at[index], routed.at[target], hop.at[slot], land.at[target], where(owner)
+            ).wait_send()
+
+    each_sent(send_block)
     for copy in started:
         copy.wait_recv()
     out[me] = source[me] + jnp.sum(came[...], axis=0)
@@ -257,6 +547,19 @@
         copy = remote(out.at[me], out.at[me], send.at[count + t], recv.at[count + t], peer)
         copy.start()
         second.append(copy)
+
+    base = (share * place) // HEAD_DIM
+    for slot in range(routed.shape[0]):
+        block = base + slot
+        owner = (block % HEADS) // heads
+
+        @pl.when((block * HEAD_DIM < share * (place + 1)) & (owner != place))
+        def _(slot=slot):
+            remote(
+                blocks.at[0], routed.at[slot], hop.at[0], land.at[slot], where(place)
+            ).wait_recv()
+
+    each_sent(sent_block)
     for t, off in enumerate(offs):
         peer = moved(axes, sizes, off, -1)
         block = out.at[flat(peer, axes, sizes)]
@@ -265,21 +568,29 @@
         copy.wait_send()
 
 
-def total(parts, axes, sizes, ident):
+def last_exchange(parts, blocks, axes, sizes, spots, heads, share, ident):
     group = parts.shape[0]
+    slots = max(
+        (share * (c + 1) - 1) // HEAD_DIM - (share * c) // HEAD_DIM + 1 for c in range(spots)
+    )
     return pl.pallas_call(
-        functools.partial(total_kernel, axes, sizes),
-        out_shape=jax.ShapeDtypeStruct(parts.shape, F32),
-        in_specs=[VMEM],
-        out_specs=VMEM,
+        functools.partial(last_kernel, axes, sizes, spots, heads, share),
+        out_shape=[
+            jax.ShapeDtypeStruct(parts.shape, F32),
+            jax.ShapeDtypeStruct((slots,) + blocks.shape[1:], BF16),
+        ],
+        in_specs=[VMEM, VMEM],
+        out_specs=[VMEM, VMEM],
         scratch_shapes=[
             pltpu.VMEM((group - 1,) + parts.shape[1:], F32),
             pltpu.SemaphoreType.DMA((2 * group,)),
             pltpu.SemaphoreType.DMA((2 * group,)),
+            pltpu.SemaphoreType.DMA((6 * heads,)),
+            pltpu.SemaphoreType.DMA((slots,)),
         ],
-        name="total%d" % ident,
+        name="last%d" % ident,
         compiler_params=pltpu.CompilerParams(collective_id=ident, has_side_effects=True),
-    )(parts)
+    )(parts, blocks)
 
 
 def nt(left, right):
@@ -316,7 +627,7 @@
     )
 
 
-def attend_kernel(heads, block, inv, qkv, out, lse, qs, ks, vt, ot):
+def attend_kernel(heads, block, inv, qkv, out, out_low, lse, qs, ks, vt, ot):
     length = qkv.shape[0]
     width = heads * HEAD_DIM
 
@@ -376,7 +687,9 @@
     def unsort(pair, unused):
         at = pl.multiple_of(pair * 128, 128)
         values = [ot[h, :, pl.ds(at, 128)].T for h in range(heads)]
-        put_rows(inv, out, pair, 0, width, jnp.concatenate(values, axis=1))
+        values = jnp.concatenate(values, axis=1)
+        put_rows(inv, out, pair, 0, width, values)
+        put_rows(inv, out_low, pair, 0, width, values.astype(BF16))
         return unused
 
     lax.fori_loop(0, length // 128, unsort, 0)
@@ -391,6 +704,7 @@
         functools.partial(attend_kernel, heads, block),
         out_shape=(
             jax.ShapeDtypeStruct((length, width), F32),
+            jax.ShapeDtypeStruct((length, width), BF16),
             jax.ShapeDtypeStruct((heads, length), F32),
         ),
         grid_spec=pltpu.PrefetchScalarGridSpec(
@@ -398,6 +712,7 @@
             grid=(1,),
             in_specs=[pl.BlockSpec((length, 3 * width), lambda i, inv: (0, 0))],
             out_specs=(
+                pl.BlockSpec((length, width), lambda i, inv: (0, 0)),
                 pl.BlockSpec((length, width), lambda i, inv: (0, 0)),
                 pl.BlockSpec((heads, length), lambda i, inv: (0, 0)),
             ),
@@ -575,20 +890,21 @@
     second_shift,
     cotangent,
 ):
-    outer, inner, xs, ks = (sizes[a] for a in ("o", "i", "x", "k"))
-    spots = outer * inner
+    outer, inner, ys, xs, ks = (sizes[a] for a in ("o", "i", "y", "x", "k"))
+    spots = outer * inner * ys
     shards = xs * ks
     rows, width = tokens.shape[1:]
-    o, i = lax.axis_index("o"), lax.axis_index("i")
+    o, i, y = lax.axis_index("o"), lax.axis_index("i"), lax.axis_index("y")
     shard = lax.axis_index("x") * ks + lax.axis_index("k")
-    place = o * inner + i
+    place = (o * inner + i) * ys + y
     heads = -(-HEADS // spots)
     span = heads * HEAD_DIM
     padded = spots * span
     part = qkv_weight.shape[0]
     hidden = expand_weight.shape[1]
     piece = hidden // (shards * inner)
-    ctx = (("o",), (outer,), "i")
+    every = (("o", "i", "y"), (outer, inner, ys))
+    ctx = (("o", "i"), (outer, inner), "y")
     group = (("i", "x"), (inner, xs), "k")
     pair = (("x",), (xs,), "k")
     own = tokens[0]
@@ -603,27 +919,17 @@
     qkv_bias = jnp.concatenate(
         [columns(query_bias, 1)[0], jnp.zeros((span,), F32), columns(value_bias, 1)[0]]
     )
-    gathered, qkv_columns = gather([own, qkv_own], [ctx, pair], 0)
+    gathered, qkv_columns, expand_columns = first_gather(
+        own, qkv_own, expand_weight, [ctx, pair], (xs, ks), piece, 0
+    )
     sequence = gathered.reshape(spots * rows, width)
     qkv_columns = qkv_columns.reshape(width, 3 * span)
-
-    later = lax.optimization_barrier((out_weight, own_grad, gathered[0, 0, :8, :128]))
-    out_full = lax.all_gather(later[0], ("x", "k"), axis=0, tiled=True)
-    group_grad = lax.all_gather(later[1], ("i", "x", "k"), axis=0, tiled=True)
-
-    expand_pieces = expand_weight.reshape(part, shards, inner, piece)
-    expand_pieces = lax.dynamic_index_in_dim(expand_pieces, i, axis=2, keepdims=False)
-    expand_pieces = expand_pieces.transpose(1, 0, 2)
-    came = [lax.dynamic_index_in_dim(expand_pieces, shard, axis=0, keepdims=False)]
-    for step in range(1, shards):
-        there = lax.rem(shard + step, shards)
-        sent = lax.dynamic_index_in_dim(expand_pieces, there, axis=0, keepdims=False)
-        came.append(
-            lax.ppermute(sent, ("x", "k"), [(f, (f + step) % shards) for f in range(shards)])
-        )
-    stacked = jnp.stack(came)
-    order = lax.rem(shard - jnp.arange(shards) + shards, shards)
-    expand_columns = jnp.take(stacked, order, axis=0).reshape(width, piece)
+    expand_columns = expand_columns.reshape(width, piece)
+
+    out_own = lax.optimization_barrier((out_weight, gathered[0, 0, :8, :128]))[0]
+    x_swap, k_swap, y_swap = ([(0, 1), (1, 0)],) * 3
+    out_pair = jnp.stack([out_own, lax.ppermute(out_own, "x", x_swap)])
+    out_mate = lax.ppermute(out_pair, "k", k_swap)
     shrink_rows = lax.dynamic_slice_in_dim(shrink_weight, i * piece, piece, axis=0)
     expand_own_bias = lax.dynamic_slice_in_dim(
         expand_bias, (shard * inner + i) * piece, piece, axis=0
@@ -641,14 +947,24 @@
     ).astype(jnp.int32)
     normed_low = layer_norm(sequence.astype(F32), first_gain, first_shift).astype(BF16)
     qkv = (matmul(normed_low, qkv_columns) + qkv_bias).astype(BF16)
-    attended, log_sum = attend(inv, qkv, heads)
-    came_out = exchange(
-        attended.astype(BF16).reshape(spots, rows, span), ("o", "i"), (outer, inner), 1
-    )
-    attended_low = came_out.transpose(1, 0, 2).reshape(rows, padded)[:, :width]
+    attended, attended_bf, log_sum = attend(inv, qkv, heads)
+    attended_low, group_grad = to_tokens(
+        attended_bf.reshape(spots, rows, span), own_grad, width, *every, group, 1
+    )
+    group_grad = group_grad.reshape(-1, width)
+
+    out_parts = [out_pair[0], out_mate[0], out_pair[1], out_mate[1]]
+    out_spots = [shard, shard ^ 1, shard ^ 2, shard ^ 3]
+
+    def out_project(low):
+        terms = [
+            matmul(lax.dynamic_slice_in_dim(low, spot * part, part, axis=1), weight)
+            for spot, weight in zip(out_spots, out_parts)
+        ]
+        return terms[0] + terms[1] + terms[2] + terms[3]
 
     inputs = own.astype(F32)
-    middle = inputs + matmul(attended_low, out_full) + out_bias
+    middle = inputs + out_project(attended_low) + out_bias
     lowered_two = layer_norm(middle, second_gain, second_shift).astype(BF16)
 
     (group_low,) = gather([lowered_two], [group], 2)
@@ -661,81 +977,96 @@
     expanded_low = grad_expanded.astype(BF16)
     grad_partial = against(expanded_low, expand_columns).astype(BF16)
     shape = (inner * xs, ks, rows, width)
-    grad_normed_two = scatter(grad_partial.reshape(shape), *group, 3)
-    result_partial = matmul(hidden_low, shrink_rows).astype(BF16)
-    shrunk = scatter(result_partial.reshape(shape), *group, 4)
-    result = middle + shrunk + shrink_bias
+    (grad_normed_two,) = scatter([grad_partial.reshape(shape)], [group], 3)
 
     grad_result = own_grad.astype(F32)
     unused, second_back = jax.vjp(layer_norm, middle, second_gain, second_shift)
     grad_middle_norm, grad_second_gain, grad_second_shift = second_back(grad_normed_two)
     grad_middle = grad_result + grad_middle_norm
     middle_low = grad_middle.astype(BF16)
-    grad_att_low = against(middle_low, out_full).astype(BF16)
-    grad_att_padded = jnp.pad(grad_att_low, ((0, 0), (0, padded - width)))
-    grad_heads = exchange(
-        grad_att_padded.reshape(rows, spots, span).transpose(1, 0, 2),
-        ("o", "i"),
-        (outer, inner),
-        5,
-    ).reshape(spots * rows, span)
+    turned = jnp.stack([against(middle_low, weight) for weight in out_parts])
+    turned = turned.reshape(2, 2, rows, part)
+    turned = jnp.where(lax.axis_index("x") == 0, turned, turned[::-1])
+    turned = jnp.where(lax.axis_index("k") == 0, turned, turned[:, ::-1])
+    grad_att_low = turned.reshape(shards, rows, part).transpose(1, 0, 2).reshape(rows, width)
+    grad_att_low = grad_att_low.astype(BF16)
+    grad_heads, middle_group, att_group = to_heads(
+        grad_att_low,
+        middle_low,
+        attended_low,
+        span,
+        *every,
+        group,
+        ("i", "x", "k"),
+        (inner, xs, ks),
+        4,
+    )
+    grad_heads = grad_heads.reshape(spots * rows, span)
+    middle_group = middle_group.reshape(-1, width)
+    att_group = att_group.reshape(middle_group.shape[0], -1)
 
     dqkv = attend_back(inv, qkv, grad_heads, attended, log_sum, heads)
     norm_partial = against(dqkv, qkv_columns).astype(BF16)
-    grad_normed_one = scatter(norm_partial.reshape(outer, inner, rows, width), *ctx, 6)
+    qkv_partial = onto(normed_low, dqkv).astype(BF16)
+    result_partial = matmul(hidden_low, shrink_rows).astype(BF16)
+    grad_normed_one, qkv_cells, shrunk = scatter(
+        [
+            norm_partial.reshape(outer * inner, ys, rows, width),
+            qkv_partial.reshape(xs, ks, part, 3 * span),
+            result_partial.reshape(shape),
+        ],
+        [ctx, pair, group],
+        5,
+    )
+    result = middle + shrunk + shrink_bias
     unused, first_back = jax.vjp(layer_norm, inputs, first_gain, first_shift)
     grad_first_input, grad_first_gain, grad_first_shift = first_back(grad_normed_one)
     grad_inputs = grad_middle + grad_first_input
 
-    axes = ("o", "i", "x", "k")
-    out_rows = width // (shards * inner)
-    att_pieces = attended_low.reshape(rows, shards, inner, out_rows).transpose(2, 1, 0, 3)
-    att_group = lax.all_to_all(
-        att_pieces.reshape(inner * shards, rows, out_rows),
-        ("i", "x", "k"),
-        split_axis=0,
-        concat_axis=0,
-        tiled=True,
-    ).reshape(-1, out_rows)
-    middle_group = lax.all_gather(middle_low, ("i", "x", "k"), axis=0, tiled=True)
-    both = jnp.concatenate(
-        [onto(hidden_low, group_grad).astype(BF16), onto(att_group, middle_group).astype(BF16)],
-        axis=0,
-    )
-    both = lax.psum_scatter(both, "o", scatter_dimension=1, tiled=True)
-    cell = both.shape[1] // inner
-    both = lax.all_to_all(
-        both.reshape(piece + out_rows, inner, cell), "i", split_axis=1, concat_axis=1
-    )
-    grad_shrink = both[:piece].transpose(1, 0, 2).reshape(inner * piece, cell).astype(F32)
-    grad_outw = both[piece:].transpose(1, 0, 2).reshape(inner * out_rows, cell).astype(F32)
-
-    cuts = outer // shards
-    expand_partial = onto(group_low, expanded_low).astype(BF16)
-    expand_partial = expand_partial.reshape(shards, part, cuts, piece // cuts).transpose(0, 2, 1, 3)
-    expand_partial = lax.psum_scatter(
-        expand_partial.reshape(outer, part, piece // cuts), "o", scatter_dimension=0, tiled=True
-    )[0]
+    def kept_and_sent(values, axis_name, dim):
+        index = lax.axis_index(axis_name)
+        size = sizes[axis_name]
+        kept = lax.dynamic_index_in_dim(values, index, axis=dim, keepdims=False)
+        total = kept.astype(F32)
+        for step in range(1, size):
+            sent = lax.dynamic_index_in_dim(
+                values, lax.rem(index + step, size), axis=dim, keepdims=False
+            )
+            ring = [(d, (d + step) % size) for d in range(size)]
+            total = total + lax.ppermute(sent, axis_name, ring).astype(F32)
+        return total.astype(BF16)
+
+    def swapped(values, axis_name):
+        index = lax.axis_index(axis_name)
+        kept = lax.dynamic_index_in_dim(values, index, axis=0, keepdims=False)
+        sent = lax.dynamic_index_in_dim(values, 1 - index, axis=0, keepdims=False)
+        came = lax.ppermute(sent, axis_name, [(0, 1), (1, 0)])
+        return jnp.where(index == 0, jnp.stack([kept, came]), jnp.stack([came, kept]))
+
+    def owned(left, right):
+        cell = width // spots
+        local = onto(left, right).astype(BF16)
+        local = local.reshape(outer, inner, ys, cell, right.shape[1])
+        local = kept_and_sent(local, "y", 2)
+        local = kept_and_sent(local, "o", 0)
+        local = swapped(local, "i")
+        return local.transpose(0, 2, 1).reshape(inner * right.shape[1], cell).astype(F32)
+
+    grad_shrink = owned(group_grad, hidden_low)
+    grad_outw = owned(middle_group, att_group)
+
+    cuts = spots // (2 * shards)
+    local = onto(group_low, expanded_low).astype(BF16)
+    local = local.reshape(shards, part, cuts, piece // cuts).transpose(0, 2, 1, 3)
+    local = local.reshape(outer, ys, part, piece // cuts)
+    local = kept_and_sent(kept_and_sent(local, "y", 1), "o", 0)
+    axes = ("o", "i", "y", "x", "k")
     routes = []
-    for so in range(outer):
-        for si in range(inner):
-            for sf in range(shards):
-                spot = sf * (spots // shards) + si * (spots // (shards * inner)) + so % cuts
-                routes.append(
-                    (
-                        (so * inner + si) * shards + sf,
-                        spot * shards + so // cuts,
-                    )
-                )
-    grad_expand = lax.ppermute(expand_partial, axes, routes).astype(F32)
-
-    qkv_partial = onto(normed_low, dqkv).astype(BF16)
-    qkv_partial = lax.psum_scatter(qkv_partial, ("x", "k"), scatter_dimension=0, tiled=True)
-    qkv_all = lax.all_gather(qkv_partial, ("o", "i"), axis=0, tiled=False)
-    qkv_all = qkv_all.reshape(spots, part, 3, span).transpose(1, 2, 0, 3)
-    qkv_all = qkv_all.reshape(part, 3, padded)[:, :, :width].reshape(part, 3 * width)
-    share = 3 * width // spots
-    grad_qkv = lax.dynamic_slice_in_dim(qkv_all, place * share, share, axis=1).astype(F32)
+    for so, si, sy, sf in itertools.product(*map(range, (outer, inner, ys, shards))):
+        index = so * ys + sy
+        spot = sf * (spots // shards) + si * cuts + index % cuts
+        routes.append((((so * inner + si) * ys + sy) * shards + sf, spot * shards + index // cuts))
+    grad_expand = lax.ppermute(local, axes, routes).astype(F32)
 
     def placed(values, start, size):
         return lax.dynamic_update_slice_in_dim(jnp.zeros((size,), F32), values, start, axis=0)
@@ -759,7 +1090,15 @@
     lanes = 128 * (-(-sum(lengths) // (devices * 1024)))
     line = jnp.concatenate(small)
     line = jnp.pad(line, (0, devices * 8 * lanes - line.shape[0])).reshape(devices, 8, lanes)
-    line = total(line, axes, (outer, inner, xs, ks), 7).reshape(-1)
+    share = 3 * width // spots
+    qkv_blocks = qkv_cells.astype(BF16).T.reshape(3 * heads, HEAD_DIM, part)
+    line, routed = last_exchange(
+        line, qkv_blocks, axes, (outer, inner, ys, xs, ks), spots, heads, share, 6
+    )
+    line = line.reshape(-1)
+    start = share * place - HEAD_DIM * ((share * place) // HEAD_DIM)
+    grad_qkv = lax.dynamic_slice_in_dim(routed.reshape(-1, part), start, share, axis=0)
+    grad_qkv = grad_qkv.T.astype(F32)
     summed = []
     start = 0
     for length in lengths:
@@ -780,9 +1119,9 @@
 
 def solution(mesh):
     spots, shards = mesh.shape["ctx"], mesh.shape["fsdp"]
-    sizes = {"o": spots // 2, "i": 2, "x": shards // 2, "k": 2}
+    sizes = {"o": spots // 4, "i": 2, "y": 2, "x": shards // 2, "k": 2}
     fine = Mesh(mesh.devices.reshape(tuple(sizes.values())), tuple(sizes))
-    seq, pos = ("x", "k"), ("o", "i")
+    seq, pos = ("x", "k"), ("o", "i", "y")
     weight = P(seq, None)
     placed = (
         P(seq, pos, None),

time: 763 us -> 676 us (0.89)
  local copies, waits for them, and re-layouts: 153 us -> 78.2 us
  starting transfers between devices: 16.5 us -> 35.2 us
  waiting for transfers between devices: 75.7 us -> 61.2 us
  between operations: 15 us -> 1.66 us
    all_gather x4 -> x0, waiting for transfers between devices: 63.1 us -> none  [the longest x1 63 us: body(): qkv_all = lax.all_gather(qkv_partial, ('o', 'i'), axis=0, tiled=False)]
    ppermute x4 -> x11, waiting for transfers between devices: 0.01 us -> 61.2 us  [the longest x6 51.2 us: kept_and_sent(): total = total + lax.ppermute(sent, axis_name, ring).astype(F32)]
    pallas_call x2 -> x1, Pallas kernels: 77.9 us -> 25.1 us  [gather(): pl.pallas_call(functools.partial(gather_kernel, specs), out_shape=shapes,...]
    pallas_call x6, Pallas kernels: 265 us -> 315 us  [the longest x2 142 us: scatter(): pl.pallas_call(functools.partial(scatter_kernel, specs), out_shape=[jax.S...]
    reshape x5 -> x1, local copies, waits for them, and re-layouts: 49.6 us -> 4.07 us  [owned(): local = local.reshape(outer, inner, ys, cell, right.shape[1])]
    ppermute x4 -> x11, starting transfers between devices: 6.51 us -> 35.2 us  [the longest x2 23.6 us: swapped(): came = lax.ppermute(sent, axis_name, [(0, 1), (1, 0)])]
    transpose x3 -> x1, local copies, waits for them, and re-layouts: 12.2 us -> 1.15 us  [body(): qkv_blocks = qkv_cells.astype(BF16).T.reshape(3 * heads, HEAD_DIM, part)]
    all_to_all x2 -> x0, starting transfers between devices: 9.08 us -> none  [the longest x1 5.09 us: body(): lax.all_to_all(att_pieces.reshape(inner * shards, rows, out_rows), ('i',...]
  transfers between devices with their start and end apart: 13 -> 11, of which waited for: 4 -> 4; matrix products, arithmetic and copies ran while one was open for 22% -> 14% of each run, Pallas kernels for 48% -> 40%
where the time goes in v2:
time: 676 us; the launch traced here: 666 us
  Pallas kernels  384 us (57%)
  local copies, waits for them, and re-layouts  78.2 us (12%)
  matrix products  67.5 us (10%)
  waiting for transfers between devices  61.2 us (9%)
  other arithmetic  38.8 us (6%)
  starting transfers between devices  35.2 us (5%)
    pallas_call x2, Pallas kernels, scatter(): pl.pallas_call(functools.partial(scatter_kernel, specs), out_shape=[jax.S...  142 us
    pallas_call x1, Pallas kernels, first_gather(): pl.pallas_call(functools.partial(first_kernel, specs, shard_sizes), out_s...  59.3 us
    ppermute x6, waiting for transfers between devices, kept_and_sent(): total = total + lax.ppermute(sent, axis_name, ring).astype(F32)  51.2 us
    pallas_call x1, Pallas kernels, to_heads(): pl.pallas_call(functools.partial(to_heads_kernel, axes, sizes, spec, grou...  42.8 us
    pallas_call x1, Pallas kernels, last_exchange(): pl.pallas_call(functools.partial(last_kernel, axes, sizes, spots, heads,...  36.4 us
    pallas_call x1, Pallas kernels, to_tokens(): pl.pallas_call(functools.partial(to_tokens_kernel, axes, sizes, spec), ou...  34.8 us
    dot_general x7, matrix products, matmul(): return jnp.dot(left, right, preferred_element_type=F32)  26.1 us
    pallas_call x1, Pallas kernels, gather(): pl.pallas_call(functools.partial(gather_kernel, specs), out_shape=shapes,...  25.1 us
  transfers between devices with their start and end apart: 11, of which 4 were waited for; matrix products, arithmetic and copies ran while one was open for 14% of the time, Pallas kernels for 40%

profile of v2, /device:TPU:23, one launch (start us, length us, event | category | flops | bytes accessed | tf_op | source)
XLA Modules:
  0.0 666.2 jit_solution(17252934852286101086)
XLA Ops:
  1.0 2.0 copy.87
  2.9 11.4 %reshape.248 = bf16[400,3,1600]{2,1,0:T(4,128)(2,1)} reshape(bf16[400,4800]{1,0:T(8,128)(2,1)} %param.18) | data formatting | bytes 7680000 | tf_op jit(solution)/shard_map/reshape | solution.py:914
  16.9 59.3 %first0.1 = (bf16[4,2,128,1600]{3,2,1,0:T(8,128)(2,1)}, bf16[2,2,400,768]{3,2,1,0:T(8,128)(2,1)}, bf16[4,400,800]{2,1,0:T(8,128)(2,1)}) custom-call(bf16[128,1600]{1,0:T(8,128)(2,1)} %bitcast.163, bf16[400,768]{1,0:T(8,128)(2,1)} %bitcast.179, bf16[400,6400]{1,0:T(8,128)(2,1)} %weight.1), custom_call_target="tpu_custom_call" | custom-call | bytes 82944000 | tf_op jit(solution)/shard_map/first0/pallas_call | solution.py:219
  76.3 2.6 convert_reduce_fusion
  80.3 2.8 add_convert_fusion
  83.1 3.2 pad_maximum_fusion
  86.4 2.0 copy.88
  89.7 6.9 %add_convert_fusion.1.qkv = bf16[1024,768]{1,0:T(8,128)(2,1)} fusion(bf16[1024,1600]{1,0:T(8,128)(2,1)} %bitcast.173, bf16[1600,768]{1,0:T(8,128)(2,1)} %bitcast.200, f32[768]{0:T(1024)S(1)} %pad_maximum_fusion.2), kind=kOutput, calls=%fused_computation.28 | convolution fusion | flops 2518155264 | bytes 7310336 | tf_op jit(solution)/shard_map/dot_general | solution.py:863
  96.6 20.0 %attend.1 = (f32[1024,256]{1,0:T(8,128)}, bf16[1024,256]{1,0:T(8,128)(2,1)}, f32[4,1024]{1,0:T(4,128)}) custom-call(s32[16]{0:T(128)} %select_reduce_fusion.inv, bf16[1024,768]{1,0:T(8,128)(2,1)} %add_convert_fusion.1.qkv), custom_call_target="tpu_custom_call" | custom-call | flops 2684354560 | bytes 2621440 | tf_op jit(solution)/shard_map/attend/pallas_call | solution.py:703
  116.6 34.8 %to_tokens1.1 = (bf16[128,1600]{1,0:T(8,128)(2,1)}, bf16[4,2,128,1600]{3,2,1,0:T(8,128)(2,1)}) custom-call(bf16[8,128,256]{2,1,0:T(8,128)(2,1)} %bitcast.182, bf16[128,1600]{1,0:T(8,128)(2,1)} %bitcast.172), custom_call_target="tpu_custom_call" | custom-call | bytes 15728640 | tf_op jit(solution)/shard_map/to_tokens1/pallas_call | solution.py:283
  154.4 2.8 fusion.3
  160.9 1.9 fusion.58
  164.0 25.1 %gather2.1 = bf16[4,2,128,1600]{3,2,1,0:T(8,128)(2,1)} custom-call(bf16[128,1600]{1,0:T(8,128)(2,1)} %add_convert_fusion.3.refs_0_), custom_call_target="tpu_custom_call" | custom-call | bytes 32768000 | tf_op jit(solution)/shard_map/gather2/pallas_call | solution.py:152
  189.2 6.2 fusion.59
  195.5 5.8 convolution_convert_fusion.3
  201.3 5.5 convert_reduce_fusion.1
  206.8 5.7 convolution_convert_fusion.1
  212.5 4.4 convolution_convert_fusion.4
  216.9 5.0 convolution_convert_fusion
  221.8 5.6 copy.93
  227.4 27.1 %scatter3.1 = f32[128,1600]{1,0:T(8,128)} custom-call(bf16[4,2,128,1600]{3,2,1,0:T(8,128)(2,1)} %bitcast.166), custom_call_target="tpu_custom_call" | custom-call | bytes 32768000 | tf_op jit(solution)/shard_map/scatter3/pallas_call | solution.py:467
  265.3 42.8 %to_heads4.1 = (bf16[8,128,256]{2,1,0:T(8,128)(2,1)}, bf16[4,2,128,1600]{3,2,1,0:T(8,128)(2,1)}, bf16[8,128,200]{2,1,0:T(8,128)(2,1)}) custom-call(bf16[128,1600]{1,0:T(8,128)(2,1)} %copy.94.source, bf16[128,1600]{1,0:T(8,128)(2,1)} %copy-done.7, bf16[128,1600]{1,0:T(8,128)(2,1)} %get-tuple-element.34.att), custom_call_target="tpu_custom_call" | custom-call | bytes 32768000 | tf_op jit(solution)/shard_map/to_heads4/pallas_call | solution.py:362
  308.2 23.4 %attend_back.1 = bf16[1024,768]{1,0:T(8,128)(2,1)} custom-call(s32[16]{0:T(128)} %select_reduce_fusion.inv, bf16[1024,768]{1,0:T(8,128)(2,1)} %add_convert_fusion.1.qkv, bf16[1024,256]{1,0:T(8,128)(2,1)} %bitcast.203, f32[1024,256]{1,0:T(8,128)} %get-tuple-element.38.outs, f32[4,1024]{1,0:T(4,128)} %get-tuple-element.39.lse), custom_call_target="tpu_custom_call" | custom-call | flops 6710886400 | bytes 5242880 | tf_op jit(solution)/shard_map/attend_back/pallas_call | solution.py:813
  333.2 6.6 convolution_convert_fusion.2
  339.8 5.5 copy.96
  345.3 5.2 copy.102
  350.5 5.2 copy.103
  355.7 2.8 dynamic-slice_bitcast_fusion
  361.2 6.2 convolution_convert_fusion.5
  369.5 5.6 copy.95
  375.1 114.7 %scatter5.1 = (f32[128,1600]{1,0:T(8,128)}, f32[400,768]{1,0:T(8,128)}, f32[128,1600]{1,0:T(8,128)}) custom-call(bf16[4,2,128,1600]{3,2,1,0:T(8,128)(2,1)} %bitcast.165, bf16[2,2,400,768]{3,2,1,0:T(8,128)(2,1)} %bitcast.178, bf16[4,2,128,1600]{3,2,1,0:T(8,128)(2,1)} %bitcast.164), custom_call_target="tpu_custom_call" | custom-call | bytes 90112000 | tf_op jit(solution)/shard_map/scatter5/pallas_call | solution.py:467
  491.5 2.2 fusion.34
  493.7 2.5 add_bitcast_fusion
  498.0 4.1 reshape.268
  503.4 2.6 constant_dynamic-slice_fusion.3
  505.9 1.9 copy.113
  510.7 36.4 %last6.1 = (f32[32,8,128]{2,1,0:T(8,128)}, bf16[11,64,400]{2,1,0:T(8,128)(2,1)}) custom-call(f32[32,8,128]{2,1,0:T(8,128)} %pad_bitcast_fusion.source, bf16[12,64,400]{2,1,0:T(8,128)(2,1)} %bitcast.177), custom_call_target="tpu_custom_call" | custom-call | tf_op jit(solution)/shard_map/last6/pallas_call | solution.py:576
  549.4 2.5 copy.112
  551.9 2.1 convert_bitcast_fusion.1
  557.2 2.2 collective-permute-start.6
  562.2 32.4 %collective-permute-done.3 = bf16[2,200,200]{2,1,0:T(8,128)(2,1)S(1)} collective-permute-done((bf16[2,200,200]{2,1,0:T(8,128)(2,1)S(1)}, bf16[2,200,200]{2,1,0:T(8,128)(2,1)S(1)}, u32[]{:S(2)}, u32[]{:S(2)}) %collective-permute-start.3) | collective-permute-done | bytes 160032 | tf_op jit(solution)/shard_map/ppermute | solution.py:1036
  595.4 4.0 collective-permute-start.4
  599.4 10.6 %collective-permute-done.6 = bf16[400,800]{1,0:T(8,128)(2,1)S(1)} collective-permute-done((bf16[400,800]{1,0:T(8,128)(2,1)S(1)}, bf16[400,800]{1,0:T(8,128)(2,1)S(1)}, u32[]{:S(2)}, u32[]{:S(2)}) %collective-permute-start.6) | collective-permute-done | bytes 640032 | tf_op jit(solution)/shard_map/ppermute | solution.py:1036
  610.2 7.0 %collective-permute-start.7 = (bf16[400,800]{1,0:T(8,128)(2,1)S(1)}, bf16[400,800]{1,0:T(8,128)(2,1)S(1)}, u32[]{:S(2)}, u32[]{:S(2)}) collective-permute-start(bf16[400,800]{1,0:T(8,128)(2,1)S(1)} %fusion.21), channel_id=1, source_target_pairs={{0,0},{1,8},{2,16},{3,24},{4,1},{5,9},{6,17},{7,25},{8,4},{9,12},{... | collective-permute-start | bytes 1920008 | tf_op jit(solution)/shard_map/ppermute | solution.py:1069
  617.3 8.1 %collective-permute-done.9 = bf16[2,200,800]{2,1,0:T(8,128)(2,1)S(1)} collective-permute-done((bf16[2,200,800]{2,1,0:T(8,128)(2,1)S(1)}, bf16[2,200,800]{2,1,0:T(8,128)(2,1)S(1)}, u32[]{:S(2)}, u32[]{:S(2)}) %collective-permute-start.9) | collective-permute-done | bytes 640032 | tf_op jit(solution)/shard_map/ppermute | solution.py:1036
  625.7 19.5 %collective-permute-start.10 = (bf16[200,800]{1,0:T(8,128)(2,1)S(1)}, bf16[200,800]{1,0:T(8,128)(2,1)}, u32[]{:S(2)}, u32[]{:S(2)}) collective-permute-start(bf16[200,800]{1,0:T(8,128)(2,1)S(1)} %get-tuple-element.122), channel_id=1, source_target_pairs={{0,8},{8,0},{1,9},{9,1},{2,10},{10,2},{3,11},{11,3},{4,12},{12,4},... | collective-permute-start | bytes 960008 | tf_op jit(solution)/shard_map/ppermute | solution.py:1043
  650.6 10.0 %collective-permute-done.10 = bf16[200,800]{1,0:T(8,128)(2,1)} collective-permute-done((bf16[200,800]{1,0:T(8,128)(2,1)S(1)}, bf16[200,800]{1,0:T(8,128)(2,1)}, u32[]{:S(2)}, u32[]{:S(2)}) %collective-permute-start.10) | collective-permute-done | bytes 320032 | tf_op jit(solution)/shard_map/ppermute | solution.py:1043
  662.7 2.0 reshape.279
  (161 shorter events, 56.3 us)
Async XLA Ops:
  0.6 82.5 %collective-permute-start = (bf16[400,1600]{1,0:T(8,128)(2,1)}, bf16[400,1600]{1,0:T(8,128)(2,1)}, u32[]{:S(2)}, u32[]{:S(2)}) collective-permute-start(bf16[400,1600]{1,0:T(8,128)(2,1)} %param.21), channel_id=1, source_target_pairs={{0,2},{2,0},{1,3},{3,1},{4,6},{6,4},{5,7},{7,5},{8,10},{10,8},{9,1... | collective-permute-start | bytes 3840008 | tf_op jit(solution)/shard_map/ppermute | solution.py:931
  16.9 62.0 %copy-start.26 = (f32[1600]{0:T(1024)S(1)}, f32[1600]{0:T(1024)}, u32[]{:S(2)}) copy-start(f32[1600]{0:T(1024)} %param.19) | copy-start | bytes 19204
  16.9 62.0 %copy-start.27 = (f32[1600]{0:T(1024)S(1)}, f32[1600]{0:T(1024)}, u32[]{:S(2)}) copy-start(f32[1600]{0:T(1024)} %param.20) | copy-start | bytes 19204
  76.2 3.0 copy-start
  76.2 4.1 copy-start.16
  76.2 4.0 copy-start.19
  80.3 2.8 copy-start.2
  83.1 6.0 copy-start.33
  86.3 70.9 %collective-permute-start.1 = (bf16[2,400,1600]{2,1,0:T(8,128)(2,1)}, bf16[2,400,1600]{2,1,0:T(8,128)(2,1)}, u32[]{:S(2)}, u32[]{:S(2)}) collective-permute-start(bf16[2,400,1600]{2,1,0:T(8,128)(2,1)} %pad_maximum_fusion), channel_id=1, source_target_pairs={{0,1},{1,0},{2,3},{3,2},{4,5},{5,4},{6,7},{7,6},{8,9},{9,8},{10,11... | collective-permute-start | bytes 7680008 | tf_op jit(solution)/shard_map/ppermute | solution.py:932
  154.4 2.8 copy-start.11
  157.2 3.6 copy-start.1
  157.2 3.6 copy-start.23
  160.9 2.2 copy-start.17
  160.9 2.2 copy-start.24
  189.2 6.3 copy-start.30
  189.2 12.1 %slice-start = ((s8[5324800]{0:T(1024)(128)(4,1)}), s8[4194304]{0:T(1024)(128)(4,1)S(1)}, s32[]{:S(2)}) async-start(s8[5324800]{0:T(1024)(128)(4,1)} %bitcast.193), calls=%async_computation | async-start | bytes 8388608
  195.5 5.8 slice-start.1
  206.8 5.7 copy-start.10
  212.5 4.4 copy-start.31
  227.4 30.3 %copy-start.8 = (bf16[1,128,1600]{2,1,0:T(8,128)(2,1)S(1)}, bf16[1,128,1600]{2,1,0:T(8,128)(2,1)}, u32[]{:S(2)}) copy-start(bf16[1,128,1600]{2,1,0:T(8,128)(2,1)} %copy.88) | copy-start | bytes 1228804
  254.6 3.4 copy-start.3
  258.0 6.1 copy-start.7
  355.7 2.8 copy-start.5
  355.7 5.5 copy-start.13
  359.7 195.5 %collective-permute-start.5 = (bf16[2,400,800]{2,1,0:T(8,128)(2,1)}, bf16[2,400,800]{2,1,0:T(8,128)(2,1)}, u32[]{:S(2)}, u32[]{:S(2)}) collective-permute-start(bf16[2,400,800]{2,1,0:T(8,128)(2,1)} %dynamic-slice_bitcast_fusion.1), channel_id=1, source_target_pairs={{0,4},{4,0},{1,5},{5,1},{2,6},{6,2},{3,7},{7,3},{8,12},{12,8},{9,1... | collective-permute-start | bytes 3840008 | tf_op jit(solution)/shard_map/ppermute | solution.py:1036
  360.0 199.4 %collective-permute-start.8 = (bf16[2,2,200,800]{3,2,1,0:T(8,128)(2,1)}, bf16[2,2,200,800]{3,2,1,0:T(8,128)(2,1)}, u32[]{:S(2)}, u32[]{:S(2)}) collective-permute-start(bf16[2,2,200,800]{3,2,1,0:T(8,128)(2,1)} %dynamic-slice_bitcast_fusion), channel_id=1, source_target_pairs={{0,4},{4,0},{1,5},{5,1},{2,6},{6,2},{3,7},{7,3},{8,12},{12,8},{9,1... | collective-permute-start | bytes 3840008 | tf_op jit(solution)/shard_map/ppermute | solution.py:1036
  369.5 5.6 copy-start.21
  489.8 6.4 copy-start.29
  489.8 6.4 copy-start.32
  496.2 5.9 copy-start.14
  502.1 5.9 copy-start.28
  502.2 6.2 copy-start.20
  502.2 6.2 copy-start.22
  502.2 7.0 %copy-start.15 = (f32[128,1600]{1,0:T(8,128)S(1)}, f32[128,1600]{1,0:T(8,128)}, u32[]{:S(2)}) copy-start(f32[128,1600]{1,0:T(8,128)} %get-tuple-element.40) | copy-start | bytes 2457604
  502.2 7.0 %copy-start.25 = (f32[1600]{0:T(1024)S(1)}, f32[1600]{0:T(1024)}, u32[]{:S(2)}) copy-start(f32[1600]{0:T(1024)} %param.26) | copy-start | bytes 19204
  507.8 46.2 %collective-permute-start.2 = (bf16[2,2,200,200]{3,2,1,0:T(8,128)(2,1)}, bf16[2,2,200,200]{3,2,1,0:T(8,128)(2,1)}, u32[]{:S(2)}, u32[]{:S(2)}) collective-permute-start(bf16[2,2,200,200]{3,2,1,0:T(8,128)(2,1)} %bitcast.41), channel_id=1, source_target_pairs={{0,4},{4,0},{1,5},{5,1},{2,6},{6,2},{3,7},{7,3},{8,12},{12,8},{9,1... | collective-permute-start | bytes 960008 | tf_op jit(solution)/shard_map/ppermute | solution.py:1036
  547.1 8.1 %copy-start.6 = (bf16[1600,800]{1,0:T(8,128)(2,1)S(1)}, bf16[1600,800]{1,0:T(8,128)(2,1)}, u32[]{:S(2)}) copy-start(bf16[1600,800]{1,0:T(8,128)(2,1)} %copy.102) | copy-start | bytes 7680004
  555.1 4.4 copy-start.4
  555.1 39.5 %collective-permute-start.3 = (bf16[2,200,200]{2,1,0:T(8,128)(2,1)S(1)}, bf16[2,200,200]{2,1,0:T(8,128)(2,1)S(1)}, u32[]{:S(2)}, u32[]{:S(2)}) collective-permute-start(bf16[2,200,200]{2,1,0:T(8,128)(2,1)S(1)} %dynamic-slice_bitcast_fusion.5), channel_id=1, source_target_pairs={{0,16},{16,0},{1,17},{17,1},{2,18},{18,2},{3,19},{19,3},{4,20},{20... | collective-permute-start | bytes 480008 | tf_op jit(solution)/shard_map/ppermute | solution.py:1036
  557.1 4.4 copy-start.18
  557.2 52.8 %collective-permute-start.6 = (bf16[400,800]{1,0:T(8,128)(2,1)S(1)}, bf16[400,800]{1,0:T(8,128)(2,1)S(1)}, u32[]{:S(2)}, u32[]{:S(2)}) collective-permute-start(bf16[400,800]{1,0:T(8,128)(2,1)S(1)} %dynamic-slice_bitcast_fusion.3), channel_id=1, source_target_pairs={{0,16},{16,0},{1,17},{17,1},{2,18},{18,2},{3,19},{19,3},{4,20},{20... | collective-permute-start | bytes 1920008 | tf_op jit(solution)/shard_map/ppermute | solution.py:1036
  561.3 64.1 %collective-permute-start.9 = (bf16[2,200,800]{2,1,0:T(8,128)(2,1)S(1)}, bf16[2,200,800]{2,1,0:T(8,128)(2,1)S(1)}, u32[]{:S(2)}, u32[]{:S(2)}) collective-permute-start(bf16[2,200,800]{2,1,0:T(8,128)(2,1)S(1)} %dynamic-slice_bitcast_fusion.2), channel_id=1, source_target_pairs={{0,16},{16,0},{1,17},{17,1},{2,18},{18,2},{3,19},{19,3},{4,20},{20... | collective-permute-start | bytes 1920008 | tf_op jit(solution)/shard_map/ppermute | solution.py:1036
  562.2 84.3 %copy-start.12 = (bf16[1,128,1600]{2,1,0:T(8,128)(2,1)S(1)}, bf16[1,128,1600]{2,1,0:T(8,128)(2,1)}, u32[]{:S(2)}) copy-start(bf16[1,128,1600]{2,1,0:T(8,128)(2,1)} %fusion.38) | copy-start | bytes 1228804
  595.4 52.0 %copy-start.9 = (f32[1,128,1600]{2,1,0:T(8,128)S(1)}, f32[1,128,1600]{2,1,0:T(8,128)}, u32[]{:S(2)}) copy-start(f32[1,128,1600]{2,1,0:T(8,128)} %add_bitcast_fusion) | copy-start | bytes 2457604
  595.4 53.2 %collective-permute-start.4 = (bf16[200,200]{1,0:T(8,128)(2,1)}, bf16[200,200]{1,0:T(8,128)(2,1)}, u32[]{:S(2)}, u32[]{:S(2)}) collective-permute-start(bf16[200,200]{1,0:T(8,128)(2,1)} %get-tuple-element.125), channel_id=1, source_target_pairs={{0,8},{8,0},{1,9},{9,1},{2,10},{10,2},{3,11},{11,3},{4,12},{12,4},... | collective-permute-start | bytes 240008 | tf_op jit(solution)/shard_map/ppermute | solution.py:1043
  610.2 54.5 %collective-permute-start.7 = (bf16[400,800]{1,0:T(8,128)(2,1)S(1)}, bf16[400,800]{1,0:T(8,128)(2,1)S(1)}, u32[]{:S(2)}, u32[]{:S(2)}) collective-permute-start(bf16[400,800]{1,0:T(8,128)(2,1)S(1)} %fusion.21), channel_id=1, source_target_pairs={{0,0},{1,8},{2,16},{3,24},{4,1},{5,9},{6,17},{7,25},{8,4},{9,12},{... | collective-permute-start | bytes 1920008 | tf_op jit(solution)/shard_map/ppermute | solution.py:1069
  625.7 34.9 %collective-permute-start.10 = (bf16[200,800]{1,0:T(8,128)(2,1)S(1)}, bf16[200,800]{1,0:T(8,128)(2,1)}, u32[]{:S(2)}, u32[]{:S(2)}) collective-permute-start(bf16[200,800]{1,0:T(8,128)(2,1)S(1)} %get-tuple-element.122), channel_id=1, source_target_pairs={{0,8},{8,0},{1,9},{9,1},{2,10},{10,2},{3,11},{11,3},{4,12},{12,4},... | collective-permute-start | bytes 960008 | tf_op jit(solution)/shard_map/ppermute | solution.py:1043

commit v3 on v2

--- a/solution.py
+++ b/solution.py
@@ -162,17 +162,54 @@
 
 
 def first_kernel(
-    specs, shard_sizes, own, columns, weight, all_tokens, all_columns, pieces, whole, cut, *sems
+    specs,
+    shard_sizes,
+    ctx_axes,
+    ctx_sizes,
+    own,
+    qkv_weight,
+    weight,
+    all_tokens,
+    all_columns,
+    pieces,
+    qkv_whole,
+    columns,
+    whole,
+    cut,
+    *sems,
 ):
     axes = ("x", "k")
     offs = offsets(shard_sizes)
     tokens = Gather(*specs[0], own, all_tokens, *sems[0:3])
     heads = Gather(*specs[1], columns, all_columns, *sems[3:6])
-    read, send, recv, local = sems[6:10]
+    read, qkv_read, send, recv, local = sems[6:11]
+    qkv_fetch = pltpu.make_async_copy(qkv_weight, qkv_whole, qkv_read)
+    qkv_fetch.start()
     fetch = pltpu.make_async_copy(weight, whole, read)
     fetch.start()
     greet(tokens.peers() + heads.peers() + [moved(axes, shard_sizes, o) for o in offs])
     tokens.start()
+    qkv_fetch.wait()
+    place = flat(own_place(ctx_axes), ctx_axes, ctx_sizes)
+    rows, span = columns.shape[0], columns.shape[1] // 3
+    width = qkv_whole.shape[1] // 3
+    for spot in range(-(-width // span)):
+
+        @pl.when(place == spot)
+        def _(spot=spot):
+            size = min(span, width - spot * span)
+            for section in range(3):
+                low = section * width + spot * span
+                if size < span:
+                    columns[:, section * span : (section + 1) * span] = jnp.zeros(
+                        (rows, span), BF16
+                    )
+                columns[:, section * span : section * span + size] = qkv_whole[:, low : low + size]
+
+    @pl.when(place * span >= width)
+    def _():
+        columns[...] = jnp.zeros(columns.shape, BF16)
+
     heads.start()
     fetch.wait()
     width = cut.shape[2]
@@ -208,24 +245,28 @@
     tokens.finish()
 
 
-def first_gather(own, columns, weight, specs, shard_sizes, piece, ident):
+def first_gather(own, qkv_weight, weight, span, specs, shard_sizes, every, piece, ident):
     shards = shard_sizes[0] * shard_sizes[1]
     part = weight.shape[0]
+    columns = jax.ShapeDtypeStruct((part, 3 * span), BF16)
     shapes = [
         gather_shape(own, specs[0]),
         gather_shape(columns, specs[1]),
         jax.ShapeDtypeStruct((shards, part, piece), BF16),
     ]
     return pl.pallas_call(
-        functools.partial(first_kernel, specs, shard_sizes),
+        functools.partial(first_kernel, specs, shard_sizes, *every),
         out_shape=shapes,
-        in_specs=[VMEM, VMEM, ANY],
+        in_specs=[VMEM, ANY, ANY],
         out_specs=[ANY] * 3,
         scratch_shapes=[
+            pltpu.VMEM(qkv_weight.shape, BF16),
+            pltpu.VMEM(columns.shape, BF16),
             pltpu.VMEM(weight.shape, BF16),
             pltpu.VMEM((shards, part, piece), BF16),
             *gather_scratch(specs[0]),
             *gather_scratch(specs[1]),
+            pltpu.SemaphoreType.DMA,
             pltpu.SemaphoreType.DMA,
             pltpu.SemaphoreType.DMA((shards,)),
             pltpu.SemaphoreType.DMA((shards,)),
@@ -234,7 +275,7 @@
         name="first%d" % ident,
         compiler_params=pltpu.CompilerParams(collective_id=ident, has_side_effects=True),
         cost_estimate=sent_estimate(sum(s.size for s in shapes)),
-    )(own, columns, weight)
+    )(own, qkv_weight, weight)
 
 
 def pieces_out(axes, sizes, source, out, send, recv):
@@ -259,13 +300,9 @@
         copy.wait_send()
 
 
-def to_tokens_kernel(
-    axes, sizes, spec, source, block, out, everyone, came, send, recv, *gather_sems
-):
-    beside = Gather(*spec, block, everyone, *gather_sems)
-    greet([moved(axes, sizes, o) for o in offsets(sizes)] + beside.peers())
+def to_tokens_kernel(axes, sizes, source, out, came, send, recv):
+    greet([moved(axes, sizes, o) for o in offsets(sizes)])
     started = pieces_out(axes, sizes, source, came, send, recv)
-    beside.start()
     me = flat(own_place(axes), axes, sizes)
     came[me] = source[me]
     pieces_in(axes, sizes, source, came, send, recv, started)
@@ -274,43 +311,34 @@
         low, high = d * span, min((d + 1) * span, width)
         if low < high:
             out[:, low:high] = came[d, :, : high - low]
-    beside.hand_on()
-    beside.finish()
-
-
-def to_tokens(pieces, block, width, axes, sizes, spec, ident):
+
+
+def to_tokens(pieces, width, axes, sizes, ident):
     group, rows, span = pieces.shape
     return pl.pallas_call(
-        functools.partial(to_tokens_kernel, axes, sizes, spec),
-        out_shape=[
-            jax.ShapeDtypeStruct((rows, width), pieces.dtype),
-            gather_shape(block, spec),
-        ],
-        in_specs=[VMEM, VMEM],
-        out_specs=[VMEM, ANY],
+        functools.partial(to_tokens_kernel, axes, sizes),
+        out_shape=jax.ShapeDtypeStruct((rows, width), pieces.dtype),
+        in_specs=[VMEM],
+        out_specs=VMEM,
         scratch_shapes=[
             pltpu.VMEM(pieces.shape, pieces.dtype),
             pltpu.SemaphoreType.DMA((group,)),
             pltpu.SemaphoreType.DMA((group,)),
-            *gather_scratch(spec),
         ],
         name="to_tokens%d" % ident,
         compiler_params=pltpu.CompilerParams(collective_id=ident, has_side_effects=True),
         cost_estimate=sent_estimate(3 * pieces.size),
-    )(pieces, block)
+    )(pieces)
 
 
 def to_heads_kernel(
     axes,
     sizes,
-    spec,
     group_axes,
     group_sizes,
     source,
-    block,
     att,
     out,
-    everyone,
     att_out,
     cut,
     att_cut,
@@ -318,9 +346,7 @@
     recv,
     att_send,
     att_recv,
-    *gather_sems,
 ):
-    beside = Gather(*spec, block, everyone, *gather_sems)
     greet(
         [moved(axes, sizes, o) for o in offsets(sizes)]
         + [moved(group_axes, group_sizes, o) for o in offsets(group_sizes)]
@@ -332,26 +358,23 @@
             cut[d] = jnp.zeros(cut.shape[1:], cut.dtype)
         if low < high:
             cut[d, :, : high - low] = source[:, low:high]
+    started = pieces_out(axes, sizes, cut, out, send, recv)
     cell = att_cut.shape[2]
     inner, shards = group_sizes[0], group_sizes[1] * group_sizes[2]
     for half in range(inner):
         for f in range(shards):
             low = (f * inner + half) * cell
             att_cut[half * shards + f] = att[:, low : low + cell]
-    started = pieces_out(axes, sizes, cut, out, send, recv)
     att_started = pieces_out(group_axes, group_sizes, att_cut, att_out, att_send, att_recv)
-    beside.start()
     me = flat(own_place(axes), axes, sizes)
     out[me] = cut[me]
     me = flat(own_place(group_axes), group_axes, group_sizes)
     att_out[me] = att_cut[me]
     pieces_in(axes, sizes, cut, out, send, recv, started)
-    beside.hand_on()
     pieces_in(group_axes, group_sizes, att_cut, att_out, att_send, att_recv, att_started)
-    beside.finish()
-
-
-def to_heads(source, block, att, span, axes, sizes, spec, group_axes, group_sizes, ident):
+
+
+def to_heads(source, att, span, axes, sizes, group_axes, group_sizes, ident):
     rows, width = source.shape
     count, group = 1, 1
     for s in sizes:
@@ -360,14 +383,13 @@
         group *= s
     cell = width // group
     return pl.pallas_call(
-        functools.partial(to_heads_kernel, axes, sizes, spec, group_axes, group_sizes),
+        functools.partial(to_heads_kernel, axes, sizes, group_axes, group_sizes),
         out_shape=[
             jax.ShapeDtypeStruct((count, rows, span), source.dtype),
-            gather_shape(block, spec),
             jax.ShapeDtypeStruct((group, rows, cell), att.dtype),
         ],
-        in_specs=[VMEM, VMEM, VMEM],
-        out_specs=[VMEM, ANY, VMEM],
+        in_specs=[VMEM, VMEM],
+        out_specs=[VMEM, VMEM],
         scratch_shapes=[
             pltpu.VMEM((count, rows, span), source.dtype),
             pltpu.VMEM((group, rows, cell), att.dtype),
@@ -375,12 +397,11 @@
             pltpu.SemaphoreType.DMA((count,)),
             pltpu.SemaphoreType.DMA((group,)),
             pltpu.SemaphoreType.DMA((group,)),
-            *gather_scratch(spec),
         ],
         name="to_heads%d" % ident,
         compiler_params=pltpu.CompilerParams(collective_id=ident, has_side_effects=True),
-        cost_estimate=sent_estimate(8 * source.size),
-    )(source, block, att)
+        cost_estimate=sent_estimate(3 * source.size),
+    )(source, att)
 
 
 class Scatter:
@@ -915,21 +936,35 @@
         wide = jnp.pad(wide, [(0, 0)] * (wide.ndim - 1) + [(0, padded - width)])
         return lax.dynamic_slice_in_dim(wide, place * span, span, axis=wide.ndim - 1)
 
-    qkv_own = columns(qkv_weight, 3).reshape(part, 3 * span)
     qkv_bias = jnp.concatenate(
         [columns(query_bias, 1)[0], jnp.zeros((span,), F32), columns(value_bias, 1)[0]]
     )
     gathered, qkv_columns, expand_columns = first_gather(
-        own, qkv_own, expand_weight, [ctx, pair], (xs, ks), piece, 0
+        own, qkv_weight, expand_weight, span, [ctx, pair], (xs, ks), every, piece, 0
     )
     sequence = gathered.reshape(spots * rows, width)
     qkv_columns = qkv_columns.reshape(width, 3 * span)
     expand_columns = expand_columns.reshape(width, piece)
 
-    out_own = lax.optimization_barrier((out_weight, gathered[0, 0, :8, :128]))[0]
-    x_swap, k_swap, y_swap = ([(0, 1), (1, 0)],) * 3
-    out_pair = jnp.stack([out_own, lax.ppermute(out_own, "x", x_swap)])
-    out_mate = lax.ppermute(out_pair, "k", k_swap)
+    def doubled(values, axis_name):
+        came = lax.ppermute(values, axis_name, [(0, 1), (1, 0)])
+        return jnp.where(
+            lax.axis_index(axis_name) == 0, jnp.stack([values, came]), jnp.stack([came, values])
+        )
+
+    def over_group(values):
+        near = doubled(values, "x")
+        near = doubled(near, "i")
+        far = lax.ppermute(near, "k", [(0, 1), (1, 0)])
+        first = lax.axis_index("k") == 0
+        both = jnp.stack([jnp.where(first, near, far), jnp.where(first, far, near)], axis=2)
+        return both.reshape(-1, width)
+
+    sequence, out_own, later_grad = lax.optimization_barrier((sequence, out_weight, own_grad))
+    swap = [(0, 1), (1, 0)]
+    out_pair = jnp.stack([out_own, lax.ppermute(out_own, "x", swap)])
+    out_mate = lax.ppermute(out_pair, "k", swap)
+    group_grad = over_group(later_grad)
     shrink_rows = lax.dynamic_slice_in_dim(shrink_weight, i * piece, piece, axis=0)
     expand_own_bias = lax.dynamic_slice_in_dim(
         expand_bias, (shard * inner + i) * piece, piece, axis=0
@@ -948,10 +983,7 @@
     normed_low = layer_norm(sequence.astype(F32), first_gain, first_shift).astype(BF16)
     qkv = (matmul(normed_low, qkv_columns) + qkv_bias).astype(BF16)
     attended, attended_bf, log_sum = attend(inv, qkv, heads)
-    attended_low, group_grad = to_tokens(
-        attended_bf.reshape(spots, rows, span), own_grad, width, *every, group, 1
-    )
-    group_grad = group_grad.reshape(-1, width)
+    attended_low = to_tokens(attended_bf.reshape(spots, rows, span), width, *every, 1)
 
     out_parts = [out_pair[0], out_mate[0], out_pair[1], out_mate[1]]
     out_spots = [shard, shard ^ 1, shard ^ 2, shard ^ 3]
@@ -966,6 +998,34 @@
     inputs = own.astype(F32)
     middle = inputs + out_project(attended_low) + out_bias
     lowered_two = layer_norm(middle, second_gain, second_shift).astype(BF16)
+
+    def cut(values, axis_name, dim):
+        index, size = lax.axis_index(axis_name), sizes[axis_name]
+        return [
+            lax.dynamic_index_in_dim(values, lax.rem(index + s, size), axis=dim, keepdims=False)
+            for s in range(size)
+        ]
+
+    def added(pieces, axis_name):
+        size = sizes[axis_name]
+        total = pieces[0].astype(F32)
+        for step in range(1, size):
+            ring = [(d, (d + step) % size) for d in range(size)]
+            total = total + lax.ppermute(pieces[step], axis_name, ring).astype(F32)
+        return total.astype(BF16)
+
+    cell = width // spots
+    cuts = spots // (2 * shards)
+
+    def cut_columns(left, right):
+        local = onto(left, right).astype(BF16)
+        return cut(local.reshape(outer, inner, ys, cell, right.shape[1]), "y", 2)
+
+    def owned(local):
+        kept, sent = cut(local, "i", 0)
+        came = lax.ppermute(sent, "i", [(0, 1), (1, 0)])
+        local = jnp.where(i == 0, jnp.stack([kept, came]), jnp.stack([came, kept]))
+        return local.transpose(0, 2, 1).reshape(-1, cell).astype(F32)
 
     (group_low,) = gather([lowered_two], [group], 2)
     group_low = group_low.reshape(-1, width)
@@ -977,6 +1037,13 @@
     expanded_low = grad_expanded.astype(BF16)
     grad_partial = against(expanded_low, expand_columns).astype(BF16)
     shape = (inner * xs, ks, rows, width)
+    shrink_cut = cut_columns(group_grad, hidden_low)
+    expand_cut = onto(group_low, expanded_low).astype(BF16)
+    expand_cut = expand_cut.reshape(shards, part, cuts, piece // cuts).transpose(0, 2, 1, 3)
+    expand_cut = cut(expand_cut.reshape(outer, ys, part, piece // cuts), "y", 1)
+    grad_partial, shrink_cut, expand_cut = lax.optimization_barrier(
+        (grad_partial, shrink_cut, expand_cut)
+    )
     (grad_normed_two,) = scatter([grad_partial.reshape(shape)], [group], 3)
 
     grad_result = own_grad.astype(F32)
@@ -990,25 +1057,27 @@
     turned = jnp.where(lax.axis_index("k") == 0, turned, turned[:, ::-1])
     grad_att_low = turned.reshape(shards, rows, part).transpose(1, 0, 2).reshape(rows, width)
     grad_att_low = grad_att_low.astype(BF16)
-    grad_heads, middle_group, att_group = to_heads(
-        grad_att_low,
-        middle_low,
-        attended_low,
-        span,
-        *every,
-        group,
-        ("i", "x", "k"),
-        (inner, xs, ks),
-        4,
+    grad_heads, att_group = to_heads(
+        grad_att_low, attended_low, span, *every, ("i", "x", "k"), (inner, xs, ks), 4
     )
     grad_heads = grad_heads.reshape(spots * rows, span)
-    middle_group = middle_group.reshape(-1, width)
+    middle_group = over_group(middle_low)
     att_group = att_group.reshape(middle_group.shape[0], -1)
+    shrink_half, expand_half = added(shrink_cut, "y"), added(expand_cut, "y")
+    shrink_cut, expand_cut = cut(shrink_half, "o", 0), cut(expand_half, "o", 0)
+    grad_heads, shrink_cut, expand_cut = lax.optimization_barrier(
+        (grad_heads, shrink_cut, expand_cut)
+    )
 
     dqkv = attend_back(inv, qkv, grad_heads, attended, log_sum, heads)
     norm_partial = against(dqkv, qkv_columns).astype(BF16)
     qkv_partial = onto(normed_low, dqkv).astype(BF16)
     result_partial = matmul(hidden_low, shrink_rows).astype(BF16)
+    outw_cut = cut_columns(middle_group, att_group)
+    shrink_whole, expand_whole = added(shrink_cut, "o"), added(expand_cut, "o")
+    norm_partial, shrink_whole, expand_whole, outw_cut = lax.optimization_barrier(
+        (norm_partial, shrink_whole, expand_whole, outw_cut)
+    )
     grad_normed_one, qkv_cells, shrunk = scatter(
         [
             norm_partial.reshape(outer * inner, ys, rows, width),
@@ -1023,50 +1092,15 @@
     grad_first_input, grad_first_gain, grad_first_shift = first_back(grad_normed_one)
     grad_inputs = grad_middle + grad_first_input
 
-    def kept_and_sent(values, axis_name, dim):
-        index = lax.axis_index(axis_name)
-        size = sizes[axis_name]
-        kept = lax.dynamic_index_in_dim(values, index, axis=dim, keepdims=False)
-        total = kept.astype(F32)
-        for step in range(1, size):
-            sent = lax.dynamic_index_in_dim(
-                values, lax.rem(index + step, size), axis=dim, keepdims=False
-            )
-            ring = [(d, (d + step) % size) for d in range(size)]
-            total = total + lax.ppermute(sent, axis_name, ring).astype(F32)
-        return total.astype(BF16)
-
-    def swapped(values, axis_name):
-        index = lax.axis_index(axis_name)
-        kept = lax.dynamic_index_in_dim(values, index, axis=0, keepdims=False)
-        sent = lax.dynamic_index_in_dim(values, 1 - index, axis=0, keepdims=False)
-        came = lax.ppermute(sent, axis_name, [(0, 1), (1, 0)])
-        return jnp.where(index == 0, jnp.stack([kept, came]), jnp.stack([came, kept]))
-
-    def owned(left, right):
-        cell = width // spots
-        local = onto(left, right).astype(BF16)
-        local = local.reshape(outer, inner, ys, cell, right.shape[1])
-        local = kept_and_sent(local, "y", 2)
-        local = kept_and_sent(local, "o", 0)
-        local = swapped(local, "i")
-        return local.transpose(0, 2, 1).reshape(inner * right.shape[1], cell).astype(F32)
-
-    grad_shrink = owned(group_grad, hidden_low)
-    grad_outw = owned(middle_group, att_group)
-
-    cuts = spots // (2 * shards)
-    local = onto(group_low, expanded_low).astype(BF16)
-    local = local.reshape(shards, part, cuts, piece // cuts).transpose(0, 2, 1, 3)
-    local = local.reshape(outer, ys, part, piece // cuts)
-    local = kept_and_sent(kept_and_sent(local, "y", 1), "o", 0)
+    grad_shrink = owned(shrink_whole)
     axes = ("o", "i", "y", "x", "k")
     routes = []
     for so, si, sy, sf in itertools.product(*map(range, (outer, inner, ys, shards))):
         index = so * ys + sy
         spot = sf * (spots // shards) + si * cuts + index % cuts
         routes.append((((so * inner + si) * ys + sy) * shards + sf, spot * shards + index // cuts))
-    grad_expand = lax.ppermute(local, axes, routes).astype(F32)
+    grad_expand = lax.ppermute(expand_whole, axes, routes).astype(F32)
+    grad_outw = owned(added(cut(added(outw_cut, "y"), "o", 0), "o"))
 
     def placed(values, start, size):
         return lax.dynamic_update_slice_in_dim(jnp.zeros((size,), F32), values, start, axis=0)

time: 676 us -> 694 us (1.027)
  Pallas kernels: 384 us -> 328 us
  waiting for transfers between devices: 61.2 us -> 86.9 us
  local copies, waits for them, and re-layouts: 78.2 us -> 97.7 us
  other arithmetic: 38.8 us -> 55.5 us
    pallas_call x2, Pallas kernels: 142 us -> 97.2 us  [scatter(): pl.pallas_call(functools.partial(scatter_kernel, specs), out_shape=[jax.S...]
    ppermute x11 -> x17, waiting for transfers between devices: 61.2 us -> 86.9 us  [the longest x4 46.4 us: doubled(): came = lax.ppermute(values, axis_name, [(0, 1), (1, 0)])]
    pallas_call x3, Pallas kernels: 137 us -> 123 us  [the longest x1 56.5 us: to_heads(): pl.pallas_call(functools.partial(to_heads_kernel, axes, sizes, group_axes...]
    select_n x0 -> x6, other arithmetic: none -> 13.2 us  [doubled(): jnp.where(lax.axis_index(axis_name) == 0, jnp.stack([values, came]), jnp....]
    ppermute x0 -> x4, local copies, waits for them, and re-layouts: none -> 12 us  [the longest x2 7.63 us: over_group(): far = lax.ppermute(near, 'k', [(0, 1), (1, 0)])]
    reshape x3 -> x2, local copies, waits for them, and re-layouts: 11.4 us -> 0.01 us  [columns(): wide = values.reshape(values.shape[:-1] + (count, width))]
    convert_element_type x7 -> x5, local copies, waits for them, and re-layouts: 25.4 us -> 14.2 us  [the longest x1 5.25 us: cut_columns(): local = onto(left, right).astype(BF16)]
    optimization_barrier x0 -> x2, local copies, waits for them, and re-layouts: none -> 10.9 us  [the longest x1 5.47 us: body(): lax.optimization_barrier((grad_partial, shrink_cut, expand_cut))]
  transfers between devices with their start and end apart: 11 -> 17, of which waited for: 4 -> 4; matrix products, arithmetic and copies ran while one was open for 14% -> 20% of each run, Pallas kernels for 40% -> 33%
where the time goes in v3:
time: 694 us; the launch traced here: 682 us
  Pallas kernels  328 us (47%)
  local copies, waits for them, and re-layouts  97.7 us (14%)
  waiting for transfers between devices  86.9 us (13%)
  matrix products  69.9 us (10%)
  other arithmetic  55.5 us (8%)
  starting transfers between devices  41.3 us (6%)
    pallas_call x2, Pallas kernels, scatter(): pl.pallas_call(functools.partial(scatter_kernel, specs), out_shape=[jax.S...  97.2 us
    pallas_call x1, Pallas kernels, to_heads(): pl.pallas_call(functools.partial(to_heads_kernel, axes, sizes, group_axes...  56.5 us
    pallas_call x1, Pallas kernels, first_gather(): pl.pallas_call(functools.partial(first_kernel, specs, shard_sizes, *every...  49.9 us
    ppermute x4, waiting for transfers between devices, doubled(): came = lax.ppermute(values, axis_name, [(0, 1), (1, 0)])  46.4 us
    ppermute x6, waiting for transfers between devices, added(): total = total + lax.ppermute(pieces[step], axis_name, ring).astype(F32)  40.5 us
    pallas_call x1, Pallas kernels, last_exchange(): pl.pallas_call(functools.partial(last_kernel, axes, sizes, spots, heads,...  38.1 us
    pallas_call x1, Pallas kernels, gather(): pl.pallas_call(functools.partial(gather_kernel, specs), out_shape=shapes,...  26.9 us
    dot_general x7, matrix products, matmul(): return jnp.dot(left, right, preferred_element_type=F32)  26.6 us
  transfers between devices with their start and end apart: 17, of which 4 were waited for; matrix products, arithmetic and copies ran while one was open for 20% of the time, Pallas kernels for 33%

profile of v3, /device:TPU:23, one launch (start us, length us, event | category | flops | bytes accessed | tf_op | source)
XLA Modules:
  0.0 681.6 jit_solution(2240808651076566942)
XLA Ops:
  4.6 49.9 %first0.1 = (bf16[4,2,128,1600]{3,2,1,0:T(8,128)(2,1)}, bf16[2,2,400,768]{3,2,1,0:T(8,128)(2,1)}, bf16[4,400,800]{2,1,0:T(8,128)(2,1)}) custom-call(bf16[128,1600]{1,0:T(8,128)(2,1)} %bitcast.159, bf16[400,4800]{1,0:T(8,128)(2,1)} %qkv_weight.1, bf16[400,6400]{1,0:T(8,128)(2,1)} %weight.1), custom_call_target="tpu_custom_call" | custom-call | bytes 82944000 | tf_op jit(solution)/shard_map/first0/pallas_call | solution.py:257
  56.1 2.6 convert_reduce_fusion
  59.4 33.3 %collective-permute-done.2 = bf16[128,1600]{1,0:T(8,128)(2,1)} collective-permute-done((bf16[128,1600]{1,0:T(8,128)(2,1)}, bf16[128,1600]{1,0:T(8,128)(2,1)}, u32[]{:S(2)}, u32[]{:S(2)}) %collective-permute-start.2) | collective-permute-done | bytes 409632 | tf_op jit(solution)/shard_map/ppermute | solution.py:950
  101.5 13.1 %collective-permute-done.3 = bf16[2,128,1600]{1,2,0:T(8,128)(2,1)} collective-permute-done((bf16[2,128,1600]{1,2,0:T(8,128)(2,1)}, bf16[2,128,1600]{1,2,0:T(8,128)(2,1)}, u32[]{:S(2)}, u32[]{:S(2)}) %collective-permute-start.3) | collective-permute-done | bytes 819232 | tf_op jit(solution)/shard_map/ppermute | solution.py:950
  116.7 3.6 maximum_select_fusion
  120.3 3.6 copy.129
  123.9 3.8 collective-permute-start.4
  127.8 3.5 pad_maximum_fusion.2
  131.5 4.6 add_convert_fusion.qkv
  136.1 20.1 %attend.1 = (f32[1024,256]{1,0:T(8,128)}, bf16[1024,256]{1,0:T(8,128)(2,1)}, f32[4,1024]{1,0:T(4,128)}) custom-call(s32[16]{0:T(128)} %select_reduce_fusion.inv, bf16[1024,768]{1,0:T(8,128)(2,1)} %add_convert_fusion.qkv), custom_call_target="tpu_custom_call" | custom-call | flops 2684354560 | bytes 2621440 | tf_op jit(solution)/shard_map/attend/pallas_call | solution.py:724
  156.3 16.2 %to_tokens1.1.att = bf16[128,1600]{1,0:T(8,128)(2,1)} custom-call(bf16[8,128,256]{2,1,0:T(8,128)(2,1)} %bitcast.187), custom_call_target="tpu_custom_call" | custom-call | bytes 15728640 | tf_op jit(solution)/shard_map/to_tokens1/pallas_call | solution.py:318
  174.0 2.8 fusion.40
  176.7 3.8 copy.130
  191.8 26.9 %gather2.1 = bf16[4,2,128,1600]{3,2,1,0:T(8,128)(2,1)} custom-call(bf16[128,1600]{1,0:T(8,128)(2,1)} %add_convert_fusion.6.refs_0_), custom_call_target="tpu_custom_call" | custom-call | bytes 32768000 | tf_op jit(solution)/shard_map/gather2/pallas_call | solution.py:152
  218.7 6.2 fusion.58
  225.0 5.5 convolution_convert_fusion.4
  230.5 5.5 convert_reduce_fusion.1
  236.0 4.8 convolution_convert_fusion.3
  240.8 5.0 convolution_convert_fusion
  245.7 5.2 copy.134
  251.0 5.3 copy.133
  256.2 3.8 dynamic-slice_bitcast_fusion
  261.8 5.5 copy.135
  267.2 27.0 %scatter3.1 = f32[128,1600]{1,0:T(8,128)} custom-call(bf16[4,2,128,1600]{3,2,1,0:T(8,128)(2,1)} %bitcast.162), custom_call_target="tpu_custom_call" | custom-call | bytes 32768000 | tf_op jit(solution)/shard_map/scatter3/pallas_call | solution.py:488
  300.9 7.5 %convolution_convert_fusion.1 = bf16[1024,1600]{0,1:T(8,128)(2,1)} fusion(bf16[1600,1600]{1,0:T(8,128)(2,1)} %param.25, s32[]{:T(128)S(6)} %select_n.183, f32[1024,800]{0,1:T(8,128)S(1)} %copy-done.47, f32[800]{0:T(1024)S(1)} %dynamic_slice.89), kind=kOutput, calls=%fused_computation.13 | convolution fusion | flops 2631270400 | bytes 9219204 | tf_op jit(solution)/shard_map/dot_general | solution.py:884
  309.9 2.5 fusion.28
  312.4 2.5 convolution_bitcast_fusion
  314.9 2.5 fusion.27
  321.9 56.5 %to_heads4.1 = (bf16[8,128,256]{2,1,0:T(8,128)(2,1)}, bf16[8,128,200]{2,1,0:T(8,128)(2,1)}) custom-call(bf16[128,1600]{1,0:T(8,128)(2,1)} %copy.136.source, bf16[128,1600]{1,0:T(8,128)(2,1)} %to_tokens1.1.att), custom_call_target="tpu_custom_call" | custom-call | bytes 12288000 | tf_op jit(solution)/shard_map/to_heads4/pallas_call | solution.py:385
  378.4 5.4 copy.146
  387.8 3.1 maximum_select_fusion.1
  390.9 3.8 copy.139
  403.7 23.5 %attend_back.1 = bf16[1024,768]{1,0:T(8,128)(2,1)} custom-call(s32[16]{0:T(128)} %select_reduce_fusion.inv, bf16[1024,768]{1,0:T(8,128)(2,1)} %add_convert_fusion.qkv, bf16[1024,256]{1,0:T(8,128)(2,1)} %bitcast.205, f32[1024,256]{1,0:T(8,128)} %get-tuple-element.60.outs, f32[4,1024]{1,0:T(4,128)} %get-tuple-element.61.lse), custom_call_target="tpu_custom_call" | custom-call | flops 6710886400 | bytes 5242880 | tf_op jit(solution)/shard_map/attend_back/pallas_call | solution.py:834
  427.1 7.3 %convolution_convert_fusion.5 = bf16[1600,768]{1,0:T(8,128)(2,1)} fusion(bf16[1024,768]{1,0:T(8,128)(2,1)} %attend_back.1, bf16[1024,1600]{1,0:T(8,128)(2,1)} %bitcast.164, f32[1600]{0:T(1024)S(1)} %copy-done.44, f32[1600]{0:T(1024)S(1)} %copy-done.22, f32[1024]{0:T(1024)S(1)} %copy-done.35, f32[1024]{0:T(1024)S(1)} %broadcast_multiply_fusion), kind=kOutput, calls=%fused_computation.19 | convolution fusion | flops 2527641600 | bytes 7328256 | tf_op jit(solution)/shard_map/dot_general | solution.py:892
  434.4 4.1 convolution_convert_fusion.2
  444.5 26.5 %collective-permute-done.7 = bf16[2,200,800]{2,1,0:T(8,128)(2,1)S(1)} collective-permute-done((bf16[2,200,800]{2,1,0:T(8,128)(2,1)S(1)}, bf16[2,200,800]{2,1,0:T(8,128)(2,1)S(1)}, u32[]{:S(2)}, u32[]{:S(2)}) %collective-permute-start.7) | collective-permute-done | bytes 640032 | tf_op jit(solution)/shard_map/ppermute | solution.py:1014
  472.0 3.8 copy.140
  475.8 2.6 select_bitcast_fusion.1
  481.6 4.1 reshape.323
  485.7 2.9 constant_dynamic-slice_fusion.3
  490.9 3.4 copy.158
  495.3 3.0 collective-permute-start.16
  499.5 5.5 copy.145
  505.0 70.2 %scatter5.1 = (f32[128,1600]{1,0:T(8,128)}, f32[400,768]{1,0:T(8,128)}, f32[128,1600]{1,0:T(8,128)}) custom-call(bf16[4,2,128,1600]{3,2,1,0:T(8,128)(2,1)} %bitcast.161, bf16[2,2,400,768]{3,2,1,0:T(8,128)(2,1)} %bitcast.181, bf16[4,2,128,1600]{3,2,1,0:T(8,128)(2,1)} %bitcast.160), custom_call_target="tpu_custom_call" | custom-call | bytes 90112000 | tf_op jit(solution)/shard_map/scatter5/pallas_call | solution.py:488
  584.9 38.1 %last6.1 = (f32[32,8,128]{2,1,0:T(8,128)}, bf16[11,64,400]{2,1,0:T(8,128)(2,1)}) custom-call(f32[32,8,128]{2,1,0:T(8,128)} %pad_bitcast_fusion.source, bf16[12,64,400]{2,1,0:T(8,128)(2,1)} %bitcast.180), custom_call_target="tpu_custom_call" | custom-call | tf_op jit(solution)/shard_map/last6/pallas_call | solution.py:597
  627.4 3.8 collective-permute-start.15
  640.6 14.0 %collective-permute-done.13 = bf16[2,200,200]{2,1,0:T(8,128)(2,1)S(1)} collective-permute-done((bf16[2,200,200]{2,1,0:T(8,128)(2,1)S(1)}, bf16[2,200,200]{2,1,0:T(8,128)(2,1)S(1)}, u32[]{:S(2)}, u32[]{:S(2)}) %collective-permute-start.13) | collective-permute-done | bytes 160032 | tf_op jit(solution)/shard_map/ppermute | solution.py:1014
  654.8 19.0 %collective-permute-start.14 = (bf16[200,200]{1,0:T(8,128)(2,1)S(1)}, bf16[200,200]{1,0:T(8,128)(2,1)S(1)}, u32[]{:S(2)}, u32[]{:S(2)}) collective-permute-start(bf16[200,200]{1,0:T(8,128)(2,1)S(1)} %get-tuple-element.182), channel_id=1, source_target_pairs={{0,8},{8,0},{1,9},{9,1},{2,10},{10,2},{3,11},{11,3},{4,12},{12,4},... | collective-permute-start | bytes 240008 | tf_op jit(solution)/shard_map/ppermute | solution.py:1026
  (216 shorter events, 102.7 us)
Async XLA Ops:
  4.6 51.5 %copy-start.27 = (f32[1600]{0:T(1024)S(1)}, f32[1600]{0:T(1024)}, u32[]{:S(2)}) copy-start(f32[1600]{0:T(1024)} %param.19) | copy-start | bytes 19204
  4.6 51.5 %copy-start.28 = (f32[1600]{0:T(1024)S(1)}, f32[1600]{0:T(1024)}, u32[]{:S(2)}) copy-start(f32[1600]{0:T(1024)} %param.20) | copy-start | bytes 19204
  54.5 73.3 %collective-permute-start = (bf16[400,1600]{1,0:T(8,128)(2,1)}, bf16[400,1600]{1,0:T(8,128)(2,1)}, u32[]{:S(2)}, u32[]{:S(2)}) collective-permute-start(bf16[400,1600]{1,0:T(8,128)(2,1)} %param.21), channel_id=1, source_target_pairs={{0,2},{2,0},{1,3},{3,1},{4,6},{6,4},{5,7},{7,5},{8,10},{10,8},{9,1... | collective-permute-start | bytes 3840008 | tf_op jit(solution)/shard_map/ppermute | solution.py:965
  55.0 37.7 %collective-permute-start.2 = (bf16[128,1600]{1,0:T(8,128)(2,1)}, bf16[128,1600]{1,0:T(8,128)(2,1)}, u32[]{:S(2)}, u32[]{:S(2)}) collective-permute-start(bf16[128,1600]{1,0:T(8,128)(2,1)} %bitcast.3), channel_id=1, source_target_pairs={{0,2},{2,0},{1,3},{3,1},{4,6},{6,4},{5,7},{7,5},{8,10},{10,8},{9,1... | collective-permute-start | bytes 1228808 | tf_op jit(solution)/shard_map/ppermute | solution.py:950
  56.1 41.8 %copy-start.1 = (bf16[4,2,128,1600]{3,2,1,0:T(8,128)(2,1)S(1)}, bf16[4,2,128,1600]{3,2,1,0:T(8,128)(2,1)}, u32[]{:S(2)}) copy-start(bf16[4,2,128,1600]{3,2,1,0:T(8,128)(2,1)} %get-tuple-element.46) | copy-start | bytes 9830404
  97.3 17.2 %collective-permute-start.3 = (bf16[2,128,1600]{1,2,0:T(8,128)(2,1)}, bf16[2,128,1600]{1,2,0:T(8,128)(2,1)}, u32[]{:S(2)}, u32[]{:S(2)}) collective-permute-start(bf16[2,128,1600]{1,2,0:T(8,128)(2,1)} %copy.127), channel_id=1, source_target_pairs={{0,8},{8,0},{1,9},{9,1},{2,10},{10,2},{3,11},{11,3},{4,12},{12,4},... | collective-permute-start | bytes 2457608 | tf_op jit(solution)/shard_map/ppermute | solution.py:950
  99.0 32.5 %copy-start.34 = (f32[1024]{0:T(1024)}, f32[1024]{0:T(1024)S(1)}, u32[]{:S(2)}) copy-start(f32[1024]{0:T(1024)S(1)} %add_rsqrt_fusion) | copy-start | bytes 12292
  123.9 7.5 %copy-start.22 = (f32[1600]{0:T(1024)S(1)}, f32[1600]{0:T(1024)}, u32[]{:S(2)}) copy-start(f32[1600]{0:T(1024)} %param.27) | copy-start | bytes 19204
  123.9 7.5 %copy-start.40 = (bf16[2,2,400,768]{3,2,1,0:T(8,128)(2,1)S(1)}, bf16[2,2,400,768]{3,2,1,0:T(8,128)(2,1)}, u32[]{:S(2)}) copy-start(bf16[2,2,400,768]{3,2,1,0:T(8,128)(2,1)} %get-tuple-element.48) | copy-start | bytes 7372804
  123.9 7.5 %copy-start.43 = (f32[1600]{0:T(1024)S(1)}, f32[1600]{0:T(1024)}, u32[]{:S(2)}) copy-start(f32[1600]{0:T(1024)} %param.28) | copy-start | bytes 19204
  123.9 52.8 %collective-permute-start.4 = (bf16[2,2,128,1600]{2,3,1,0:T(8,128)(2,1)}, bf16[2,2,128,1600]{2,3,1,0:T(8,128)(2,1)}, u32[]{:S(2)}, u32[]{:S(2)}) collective-permute-start(bf16[2,2,128,1600]{2,3,1,0:T(8,128)(2,1)} %copy.129), channel_id=1, source_target_pairs={{0,1},{1,0},{2,3},{3,2},{4,5},{5,4},{6,7},{7,6},{8,9},{9,8},{10,11... | collective-permute-start | bytes 4915208 | tf_op jit(solution)/shard_map/ppermute | solution.py:958
  131.3 53.7 %collective-permute-start.1 = (bf16[2,400,1600]{2,1,0:T(8,128)(2,1)}, bf16[2,400,1600]{2,1,0:T(8,128)(2,1)}, u32[]{:S(2)}, u32[]{:S(2)}) collective-permute-start(bf16[2,400,1600]{2,1,0:T(8,128)(2,1)} %pad_maximum_fusion.2), channel_id=1, source_target_pairs={{0,1},{1,0},{2,3},{3,2},{4,5},{5,4},{6,7},{7,6},{8,9},{9,8},{10,11... | collective-permute-start | bytes 7680008 | tf_op jit(solution)/shard_map/ppermute | solution.py:966
  136.1 37.2 %copy-start = (bf16[1,128,1600]{2,1,0:T(8,128)(2,1)S(1)}, bf16[1,128,1600]{2,1,0:T(8,128)(2,1)}, u32[]{:S(2)}) copy-start(bf16[1,128,1600]{2,1,0:T(8,128)(2,1)} %copy.121) | copy-start | bytes 1228804
  173.4 7.1 %copy-start.3 = (bf16[1,2,128,1600]{3,2,1,0:T(8,128)(2,1)S(1)}, bf16[1,2,128,1600]{3,2,1,0:T(8,128)(2,1)}, u32[]{:S(2)}) copy-start(bf16[1,2,128,1600]{3,2,1,0:T(8,128)(2,1)} %maximum_select_fusion.2) | copy-start | bytes 2457604
  173.4 7.1 %copy-start.4 = (bf16[2,128,1600]{2,1,0:T(8,128)(2,1)S(1)}, bf16[2,128,1600]{2,1,0:T(8,128)(2,1)}, u32[]{:S(2)}) copy-start(bf16[2,128,1600]{2,1,0:T(8,128)(2,1)} %copy.128) | copy-start | bytes 2457604
  218.7 6.3 copy-start.9
  218.7 11.8 %slice-start = ((s8[5324800]{0:T(1024)(128)(4,1)}), s8[4194304]{0:T(1024)(128)(4,1)S(1)}, s32[]{:S(2)}) async-start(s8[5324800]{0:T(1024)(128)(4,1)} %bitcast.198), calls=%async_computation | async-start | bytes 8388608
  225.0 5.5 copy-start.46
  225.0 5.5 slice-start.1
  297.5 11.0 %copy-start.37 = (f32[128]{0:T(128)}, f32[128]{0:T(128)S(1)}, u32[]{:S(2)}) copy-start(f32[128]{0:T(128)S(1)} %negate_multiply_fusion.1) | copy-start | bytes 1540
  298.7 18.7 %collective-permute-start.9 = (bf16[128,1600]{1,0:T(8,128)(2,1)S(1)}, bf16[128,1600]{1,0:T(8,128)(2,1)S(1)}, u32[]{:S(2)}, u32[]{:S(2)}) collective-permute-start(bf16[128,1600]{1,0:T(8,128)(2,1)S(1)} %get-tuple-element.161), channel_id=1, source_target_pairs={{0,2},{2,0},{1,3},{3,1},{4,6},{6,4},{5,7},{7,5},{8,10},{10,8},{9,1... | collective-permute-start | bytes 1228808 | tf_op jit(solution)/shard_map/ppermute | solution.py:950
  308.4 87.9 %collective-permute-start.6 = (bf16[2,400,800]{2,1,0:T(8,128)(2,1)}, bf16[2,400,800]{2,1,0:T(8,128)(2,1)}, u32[]{:S(2)}, u32[]{:S(2)}) collective-permute-start(bf16[2,400,800]{2,1,0:T(8,128)(2,1)} %get-tuple-element.58), channel_id=1, source_target_pairs={{0,4},{4,0},{1,5},{5,1},{2,6},{6,2},{3,7},{7,3},{8,12},{12,8},{9,1... | collective-permute-start | bytes 3840008 | tf_op jit(solution)/shard_map/ppermute | solution.py:1014
  309.6 90.1 %collective-permute-start.5 = (bf16[2,2,200,800]{3,2,1,0:T(8,128)(2,1)}, bf16[2,2,200,800]{3,2,1,0:T(8,128)(2,1)}, u32[]{:S(2)}, u32[]{:S(2)}) collective-permute-start(bf16[2,2,200,800]{3,2,1,0:T(8,128)(2,1)} %get-tuple-element.56), channel_id=1, source_target_pairs={{0,4},{4,0},{1,5},{5,1},{2,6},{6,2},{3,7},{7,3},{8,12},{12,8},{9,1... | collective-permute-start | bytes 3840008 | tf_op jit(solution)/shard_map/ppermute | solution.py:1014
  319.6 66.0 %collective-permute-start.10 = (bf16[2,128,1600]{1,2,0:T(8,128)(2,1)}, bf16[2,128,1600]{1,2,0:T(8,128)(2,1)}, u32[]{:S(2)}, u32[]{:S(2)}) collective-permute-start(bf16[2,128,1600]{1,2,0:T(8,128)(2,1)} %copy.137), channel_id=1, source_target_pairs={{0,8},{8,0},{1,9},{9,1},{2,10},{10,2},{3,11},{11,3},{4,12},{12,4},... | collective-permute-start | bytes 2457608 | tf_op jit(solution)/shard_map/ppermute | solution.py:950
  394.6 77.3 %collective-permute-start.11 = (bf16[2,2,128,1600]{2,3,1,0:T(8,128)(2,1)}, bf16[2,2,128,1600]{2,3,1,0:T(8,128)(2,1)}, u32[]{:S(2)}, u32[]{:S(2)}) collective-permute-start(bf16[2,2,128,1600]{2,3,1,0:T(8,128)(2,1)} %copy.139), channel_id=1, source_target_pairs={{0,1},{1,0},{2,3},{3,2},{4,5},{5,4},{6,7},{7,6},{8,9},{9,8},{10,11... | collective-permute-start | bytes 4915208 | tf_op jit(solution)/shard_map/ppermute | solution.py:958
  402.7 39.6 %collective-permute-start.8 = (bf16[400,800]{1,0:T(8,128)(2,1)}, bf16[400,800]{1,0:T(8,128)(2,1)}, u32[]{:S(2)}, u32[]{:S(2)}) collective-permute-start(bf16[400,800]{1,0:T(8,128)(2,1)} %get-tuple-element.65), channel_id=1, source_target_pairs={{0,16},{16,0},{1,17},{17,1},{2,18},{18,2},{3,19},{19,3},{4,20},{20... | collective-permute-start | bytes 1920008 | tf_op jit(solution)/shard_map/ppermute | solution.py:1014
  403.7 23.5 %copy-start.35 = (f32[1024]{0:T(1024)S(1)}, f32[1024]{0:T(1024)}, u32[]{:S(2)}) copy-start(f32[1024]{0:T(1024)} %copy-done.34) | copy-start | bytes 12292
  403.7 23.5 %copy-start.44 = (f32[1600]{0:T(1024)S(1)}, f32[1600]{0:T(1024)}, u32[]{:S(2)}) copy-start(f32[1600]{0:T(1024)} %param.28) | copy-start | bytes 19204
  427.1 7.3 %copy-start.16 = (bf16[1024,768]{1,0:T(8,128)(2,1)S(1)}, bf16[1024,768]{1,0:T(8,128)(2,1)}, u32[]{:S(2)}) copy-start(bf16[1024,768]{1,0:T(8,128)(2,1)} %attend_back.1) | copy-start | bytes 4718596
  427.1 7.3 %copy-start.41 = (bf16[2,2,400,768]{3,2,1,0:T(8,128)(2,1)S(1)}, bf16[2,2,400,768]{3,2,1,0:T(8,128)(2,1)}, u32[]{:S(2)}) copy-start(bf16[2,2,400,768]{3,2,1,0:T(8,128)(2,1)} %get-tuple-element.48) | copy-start | bytes 7372804
  434.4 7.9 %copy-start.13 = (bf16[400,800]{1,0:T(8,128)(2,1)S(1)}, bf16[400,800]{1,0:T(8,128)(2,1)}, u32[]{:S(2)}) copy-start(bf16[400,800]{1,0:T(8,128)(2,1)} %get-tuple-element.64) | copy-start | bytes 1920004
  438.6 32.4 %copy-start.14 = (bf16[2,200,800]{2,1,0:T(8,128)(2,1)S(1)}, bf16[2,200,800]{2,1,0:T(8,128)(2,1)}, u32[]{:S(2)}) copy-start(bf16[2,200,800]{2,1,0:T(8,128)(2,1)} %get-tuple-element.62) | copy-start | bytes 1920004
  438.6 32.4 %collective-permute-start.7 = (bf16[2,200,800]{2,1,0:T(8,128)(2,1)S(1)}, bf16[2,200,800]{2,1,0:T(8,128)(2,1)S(1)}, u32[]{:S(2)}, u32[]{:S(2)}) collective-permute-start(bf16[2,200,800]{2,1,0:T(8,128)(2,1)S(1)} %copy-done.19), channel_id=1, source_target_pairs={{0,16},{16,0},{1,17},{17,1},{2,18},{18,2},{3,19},{19,3},{4,20},{20... | collective-permute-start | bytes 1920008 | tf_op jit(solution)/shard_map/ppermute | solution.py:1014
  442.3 33.5 %copy-start.23 = (f32[2048]{0:T(1024)}, f32[2048]{0:T(1024)S(1)}, u32[]{:S(2)}) copy-start(f32[2048]{0:T(1024)S(1)} %slice_dynamic-update-slice_fusion.1) | copy-start | bytes 24580
  488.6 5.8 copy-start.12
  495.3 178.5 %collective-permute-start.16 = (bf16[200,800]{1,0:T(8,128)(2,1)}, bf16[200,800]{1,0:T(8,128)(2,1)}, u32[]{:S(2)}, u32[]{:S(2)}) collective-permute-start(bf16[200,800]{1,0:T(8,128)(2,1)} %get-tuple-element.179), channel_id=1, source_target_pairs={{0,8},{8,0},{1,9},{9,1},{2,10},{10,2},{3,11},{11,3},{4,12},{12,4},... | collective-permute-start | bytes 960008 | tf_op jit(solution)/shard_map/ppermute | solution.py:1026
  498.3 134.0 %collective-permute-start.12 = (bf16[2,2,200,200]{3,2,1,0:T(8,128)(2,1)}, bf16[2,2,200,200]{3,2,1,0:T(8,128)(2,1)}, u32[]{:S(2)}, u32[]{:S(2)}) collective-permute-start(bf16[2,2,200,200]{3,2,1,0:T(8,128)(2,1)} %bitcast.189), channel_id=1, source_target_pairs={{0,4},{4,0},{1,5},{5,1},{2,6},{6,2},{3,7},{7,3},{8,12},{12,8},{9,1... | collective-permute-start | bytes 960008 | tf_op jit(solution)/shard_map/ppermute | solution.py:1014
  505.0 70.2 %copy-start.29 = (f32[128]{0:T(128)S(1)}, f32[128]{0:T(128)}, u32[]{:S(2)}) copy-start(f32[128]{0:T(128)} %broadcast_multiply_fusion.1) | copy-start | bytes 1540
  576.7 47.9 %copy-start.5 = (f32[128,1600]{1,0:T(8,128)S(1)}, f32[128,1600]{1,0:T(8,128)}, u32[]{:S(2)}) copy-start(f32[128,1600]{1,0:T(8,128)} %get-tuple-element.69) | copy-start | bytes 2457604
  579.8 44.8 %copy-start.38 = (f32[128]{0:T(128)S(1)}, f32[128]{0:T(128)}, u32[]{:S(2)}) copy-start(f32[128]{0:T(128)} %get-tuple-element.155) | copy-start | bytes 1540
  579.8 44.8 %copy-start.31 = (f32[128]{0:T(128)S(1)}, f32[128]{0:T(128)}, u32[]{:S(2)}) copy-start(f32[128]{0:T(128)} %copy-done.30) | copy-start | bytes 1540
  579.8 44.8 %copy-start.33 = (f32[128]{0:T(128)S(1)}, f32[128]{0:T(128)}, u32[]{:S(2)}) copy-start(f32[128]{0:T(128)} %copy-done.32) | copy-start | bytes 1540
  582.7 44.3 %copy-start.26 = (f32[1600]{0:T(1024)S(1)}, f32[1600]{0:T(1024)}, u32[]{:S(2)}) copy-start(f32[1600]{0:T(1024)} %param.26) | copy-start | bytes 19204
  627.1 11.4 %copy-start.8 = (f32[1,128,1600]{2,1,0:T(8,128)S(1)}, f32[1,128,1600]{2,1,0:T(8,128)}, u32[]{:S(2)}) copy-start(f32[1,128,1600]{2,1,0:T(8,128)} %add_bitcast_fusion) | copy-start | bytes 2457604
  627.4 51.4 %collective-permute-start.15 = (bf16[400,800]{1,0:T(8,128)(2,1)}, bf16[400,800]{1,0:T(8,128)(2,1)}, u32[]{:S(2)}, u32[]{:S(2)}) collective-permute-start(bf16[400,800]{1,0:T(8,128)(2,1)} %add_convert_fusion.3), channel_id=1, source_target_pairs={{0,0},{1,8},{2,16},{3,24},{4,1},{5,9},{6,17},{7,25},{8,4},{9,12},{... | collective-permute-start | bytes 1920008 | tf_op jit(solution)/shard_map/ppermute | solution.py:1102
  632.3 41.5 %copy-start.17 = (bf16[1,200,800]{2,1,0:T(8,128)(2,1)S(1)}, bf16[1,200,800]{2,1,0:T(8,128)(2,1)}, u32[]{:S(2)}) copy-start(bf16[1,200,800]{2,1,0:T(8,128)(2,1)} %get-tuple-element.178) | copy-start | bytes 960004
  633.5 21.2 %collective-permute-start.13 = (bf16[2,200,200]{2,1,0:T(8,128)(2,1)S(1)}, bf16[2,200,200]{2,1,0:T(8,128)(2,1)S(1)}, u32[]{:S(2)}, u32[]{:S(2)}) collective-permute-start(bf16[2,200,200]{2,1,0:T(8,128)(2,1)S(1)} %dynamic-slice_bitcast_fusion.9), channel_id=1, source_target_pairs={{0,16},{16,0},{1,17},{17,1},{2,18},{18,2},{3,19},{19,3},{4,20},{20... | collective-permute-start | bytes 480008 | tf_op jit(solution)/shard_map/ppermute | solution.py:1014
  654.8 23.1 %collective-permute-start.14 = (bf16[200,200]{1,0:T(8,128)(2,1)S(1)}, bf16[200,200]{1,0:T(8,128)(2,1)S(1)}, u32[]{:S(2)}, u32[]{:S(2)}) collective-permute-start(bf16[200,200]{1,0:T(8,128)(2,1)S(1)} %get-tuple-element.182), channel_id=1, source_target_pairs={{0,8},{8,0},{1,9},{9,1},{2,10},{10,2},{3,11},{11,3},{4,12},{12,4},... | collective-permute-start | bytes 240008 | tf_op jit(solution)/shard_map/ppermute | solution.py:1026
  (19 other events, 66.6 us)

commit v4 on v3

--- a/solution.py
+++ b/solution.py
@@ -300,108 +300,48 @@
         copy.wait_send()
 
 
-def to_tokens_kernel(axes, sizes, source, out, came, send, recv):
+def side_kernel(
+    spec, axes, sizes, block, att, everyone, att_out, att_cut, send, recv, *gather_sems
+):
+    beside = Gather(*spec, block, everyone, *gather_sems)
     greet([moved(axes, sizes, o) for o in offsets(sizes)])
-    started = pieces_out(axes, sizes, source, came, send, recv)
-    me = flat(own_place(axes), axes, sizes)
-    came[me] = source[me]
-    pieces_in(axes, sizes, source, came, send, recv, started)
-    span, width = came.shape[2], out.shape[1]
-    for d in range(came.shape[0]):
-        low, high = d * span, min((d + 1) * span, width)
-        if low < high:
-            out[:, low:high] = came[d, :, : high - low]
-
-
-def to_tokens(pieces, width, axes, sizes, ident):
-    group, rows, span = pieces.shape
-    return pl.pallas_call(
-        functools.partial(to_tokens_kernel, axes, sizes),
-        out_shape=jax.ShapeDtypeStruct((rows, width), pieces.dtype),
-        in_specs=[VMEM],
-        out_specs=VMEM,
-        scratch_shapes=[
-            pltpu.VMEM(pieces.shape, pieces.dtype),
-            pltpu.SemaphoreType.DMA((group,)),
-            pltpu.SemaphoreType.DMA((group,)),
-        ],
-        name="to_tokens%d" % ident,
-        compiler_params=pltpu.CompilerParams(collective_id=ident, has_side_effects=True),
-        cost_estimate=sent_estimate(3 * pieces.size),
-    )(pieces)
-
-
-def to_heads_kernel(
-    axes,
-    sizes,
-    group_axes,
-    group_sizes,
-    source,
-    att,
-    out,
-    att_out,
-    cut,
-    att_cut,
-    send,
-    recv,
-    att_send,
-    att_recv,
-):
-    greet(
-        [moved(axes, sizes, o) for o in offsets(sizes)]
-        + [moved(group_axes, group_sizes, o) for o in offsets(group_sizes)]
-    )
-    span, width = cut.shape[2], source.shape[1]
-    for d in range(cut.shape[0]):
-        low, high = d * span, min((d + 1) * span, width)
-        if high - low < span:
-            cut[d] = jnp.zeros(cut.shape[1:], cut.dtype)
-        if low < high:
-            cut[d, :, : high - low] = source[:, low:high]
-    started = pieces_out(axes, sizes, cut, out, send, recv)
+    beside.start()
     cell = att_cut.shape[2]
-    inner, shards = group_sizes[0], group_sizes[1] * group_sizes[2]
+    inner, shards = sizes[0], sizes[1] * sizes[2]
     for half in range(inner):
         for f in range(shards):
             low = (f * inner + half) * cell
             att_cut[half * shards + f] = att[:, low : low + cell]
-    att_started = pieces_out(group_axes, group_sizes, att_cut, att_out, att_send, att_recv)
+    started = pieces_out(axes, sizes, att_cut, att_out, send, recv)
     me = flat(own_place(axes), axes, sizes)
-    out[me] = cut[me]
-    me = flat(own_place(group_axes), group_axes, group_sizes)
     att_out[me] = att_cut[me]
-    pieces_in(axes, sizes, cut, out, send, recv, started)
-    pieces_in(group_axes, group_sizes, att_cut, att_out, att_send, att_recv, att_started)
-
-
-def to_heads(source, att, span, axes, sizes, group_axes, group_sizes, ident):
-    rows, width = source.shape
-    count, group = 1, 1
-    for s in sizes:
-        count *= s
-    for s in group_sizes:
-        group *= s
+    beside.hand_on()
+    pieces_in(axes, sizes, att_cut, att_out, send, recv, started)
+    beside.finish()
+
+
+def side_gather(block, att, spec, axes, sizes, ident):
+    rows, width = block.shape
+    group = sizes[0] * sizes[1] * sizes[2]
     cell = width // group
     return pl.pallas_call(
-        functools.partial(to_heads_kernel, axes, sizes, group_axes, group_sizes),
+        functools.partial(side_kernel, spec, axes, sizes),
         out_shape=[
-            jax.ShapeDtypeStruct((count, rows, span), source.dtype),
+            gather_shape(block, spec),
             jax.ShapeDtypeStruct((group, rows, cell), att.dtype),
         ],
         in_specs=[VMEM, VMEM],
-        out_specs=[VMEM, VMEM],
+        out_specs=[ANY, VMEM],
         scratch_shapes=[
-            pltpu.VMEM((count, rows, span), source.dtype),
             pltpu.VMEM((group, rows, cell), att.dtype),
-            pltpu.SemaphoreType.DMA((count,)),
-            pltpu.SemaphoreType.DMA((count,)),
             pltpu.SemaphoreType.DMA((group,)),
             pltpu.SemaphoreType.DMA((group,)),
+            *gather_scratch(spec),
         ],
-        name="to_heads%d" % ident,
+        name="side%d" % ident,
         compiler_params=pltpu.CompilerParams(collective_id=ident, has_side_effects=True),
-        cost_estimate=sent_estimate(3 * source.size),
-    )(source, att)
+        cost_estimate=sent_estimate(8 * block.size),
+    )(block, att)
 
 
 class Scatter:
@@ -612,6 +552,382 @@
         name="last%d" % ident,
         compiler_params=pltpu.CompilerParams(collective_id=ident, has_side_effects=True),
     )(parts, blocks)
+
+
+def normed(values):
+    center = jnp.mean(values, axis=-1, keepdims=True)
+    centred = values - center
+    spread = jnp.mean(centred * centred, axis=-1, keepdims=True)
+    scale = lax.rsqrt(spread + EPSILON)
+    return centred * scale, scale
+
+
+def norm_back(grad, gain, plain, scale):
+    inner = grad * gain
+    return scale * (
+        inner
+        - jnp.mean(inner, axis=-1, keepdims=True)
+        - plain * jnp.mean(inner * plain, axis=-1, keepdims=True)
+    )
+
+
+def middle_kernel(
+    every,
+    spec,
+    pieces,
+    own,
+    own_grad,
+    out_own,
+    out_far,
+    expand,
+    shrink,
+    out_bias,
+    expand_bias,
+    shrink_bias,
+    gain,
+    shift,
+    att_out,
+    c_out,
+    e_out,
+    u_out,
+    gz_out,
+    result,
+    grad_middle,
+    low_middle,
+    sums,
+    hidden_sum,
+    to_heads,
+    came,
+    att,
+    out_w,
+    expand_w,
+    shrink_w,
+    mid,
+    c_own,
+    c_all,
+    e_all,
+    gh,
+    u_all,
+    gz_all,
+    part,
+    first,
+    summed,
+    last,
+    part_two,
+    first_two,
+    summed_two,
+    last_two,
+    cut,
+    send,
+    recv,
+    c_send,
+    c_recv,
+    c_local,
+    e_send,
+    e_recv,
+    e_local,
+    w_sem,
+    w_send,
+    w_recv,
+    r_send,
+    r_recv,
+    s_send,
+    s_recv,
+    h_send,
+    h_recv,
+    store,
+):
+    axes, sizes = every
+    x, k, inner = lax.axis_index("x"), lax.axis_index("k"), lax.axis_index("i")
+    mate = {"k": 1 - k}
+    shard = 2 * x + k
+    part_rows = out_own.shape[0]
+    width = own.shape[1]
+    rows = own.shape[0]
+    piece = expand.shape[2]
+
+    def chip(t):
+        ti, tx = lax.rem(inner + t // 2, 2), lax.rem(x + t % 2, 2)
+        return 2 * ti + tx, {"i": ti, "x": tx}
+
+    loads = [
+        pltpu.make_async_copy(out_own, out_w.at[pl.ds(shard * part_rows, part_rows)], w_sem.at[0]),
+        pltpu.make_async_copy(
+            out_far, out_w.at[pl.ds((shard ^ 2) * part_rows, part_rows)], w_sem.at[1]
+        ),
+        pltpu.make_async_copy(shrink.at[pl.ds(inner * piece, piece)], shrink_w, w_sem.at[2]),
+    ]
+    for f in range(expand.shape[0]):
+        loads.append(
+            pltpu.make_async_copy(
+                expand.at[f], expand_w.at[pl.ds(f * part_rows, part_rows)], w_sem.at[3 + f]
+            )
+        )
+    for copy in loads:
+        copy.start()
+    greet([moved(axes, sizes, o) for o in offsets(sizes)] + [chip(t)[1] for t in range(1, 4)] + [mate])
+
+    started = pieces_out(axes, sizes, pieces, came, send, recv)
+    out_sent = []
+    for n, (source, owner) in enumerate(((out_own, shard), (out_far, shard ^ 2))):
+        copy = remote(
+            source, out_w.at[pl.ds(owner * part_rows, part_rows)], w_send.at[n], w_recv.at[n], mate
+        )
+        copy.start()
+        out_sent.append(copy)
+    e_gather = Gather(*spec, own_grad, e_all, e_send, e_recv, e_local)
+    e_gather.start()
+    here = flat(own_place(axes), axes, sizes)
+    came[here] = pieces[here]
+    pieces_in(axes, sizes, pieces, came, send, recv, started)
+    span = came.shape[2]
+    for d in range(came.shape[0]):
+        low, high = d * span, min((d + 1) * span, width)
+        if low < high:
+            att[:, low:high] = came[d, :, : high - low]
+    for copy in loads[:2]:
+        copy.wait()
+    for n, owner in enumerate((shard ^ 1, shard ^ 3)):
+        remote(
+            out_own,
+            out_w.at[pl.ds(owner * part_rows, part_rows)],
+            w_send.at[n],
+            w_recv.at[n],
+            mate,
+        ).wait_recv()
+
+    mid[...] = (
+        own[...].astype(F32)
+        + jnp.dot(att[...], out_w[...], preferred_element_type=F32)
+        + out_bias[...]
+    )
+    plain, scale = normed(mid[...])
+    c_own[...] = (plain * gain[...] + shift[...]).astype(BF16)
+    c_gather = Gather(*spec, c_own, c_all, c_send, c_recv, c_local)
+    c_gather.start()
+    att_copy = pltpu.make_async_copy(att, att_out, store.at[0])
+    att_copy.start()
+    e_gather.hand_on()
+    e_gather.finish()
+    e_copy = pltpu.make_async_copy(e_all, e_out, store.at[1])
+    e_copy.start()
+    for copy in loads[2:]:
+        copy.wait()
+
+    def both(ref, place):
+        return ref[place].reshape(2 * rows, ref.shape[3])
+
+    def slopes(t, unused):
+        place, unused_peer = chip(t)
+        gh[place] = nt(both(e_all, place), shrink_w[...])
+        return unused
+
+    lax.fori_loop(0, 4, slopes, 0)
+    hidden_sum[...] = jnp.zeros(hidden_sum.shape, F32)
+
+    def c_wait(t):
+        place, peer = chip(t)
+        block = c_all.at[place, 1 - k]
+        remote(c_own, block, c_send.at[3 + t], c_recv.at[3 + t], mate).wait_recv()
+
+    def c_hand_on(t):
+        place, peer = chip(t)
+        block = c_all.at[place, k]
+        remote(c_own, block, c_send.at[t - 1], c_recv.at[t - 1], mate).wait_recv()
+        remote(block, block, c_send.at[3 + t], c_recv.at[3 + t], mate).start()
+
+    def to_mate(t, source, target, sends, recvs):
+        place, peer = chip(t)
+        return remote(source.at[place, 1 - k], target.at[t], sends.at[t], recvs.at[t], mate)
+
+    def to_chip(t, source, target, sends, recvs):
+        place, peer = chip(t)
+        return remote(
+            source.at[t - 1], target.at[t - 1], sends.at[3 + t], recvs.at[3 + t], peer
+        )
+
+    def add_and_send(t, parts, firsts, sums_of, lasts, sends, recvs):
+        place, peer = chip(t)
+        to_mate(t, parts, firsts, sends, recvs).wait_recv()
+        sums_of[t - 1] = (parts[place, k].astype(F32) + firsts[t].astype(F32)).astype(BF16)
+        to_chip(t, sums_of, lasts, sends, recvs).start()
+
+    pltpu.make_async_copy(c_own, c_gather.mine(), c_local).wait()
+
+    def feed(t, unused):
+        c_wait(t)
+        place, peer = chip(t)
+        expanded = jnp.dot(both(c_all, place), expand_w[...], preferred_element_type=F32)
+        expanded = expanded + expand_bias[...]
+        square = expanded * expanded
+        bent = jnp.tanh(0.7978845608028654 * (expanded + 0.044715 * square * expanded))
+        half = 0.5 * (1.0 + bent)
+        u_all[place] = (expanded * half).astype(BF16)
+        slope = half + 0.5 * expanded * (1.0 - bent * bent) * (
+            0.7978845608028654 * (1.0 + 3 * 0.044715 * square)
+        )
+        low = (slope * gh[place]).astype(BF16)
+        gz_all[place] = low
+        hidden_sum[...] += jnp.sum(low.astype(F32), axis=0, keepdims=True)
+        back = nt(low, expand_w[...]).astype(BF16)
+        part[place] = back.reshape(2, rows, width)
+        to_mate(t, part, first, r_send, r_recv).start()
+
+        @pl.when(t < 3)
+        def _():
+            c_hand_on(t + 1)
+
+        @pl.when(t > 1)
+        def _():
+            add_and_send(t - 1, part, first, summed, last, r_send, r_recv)
+
+        return unused
+
+    lax.fori_loop(0, 4, feed, 0)
+    add_and_send(3, part, first, summed, last, r_send, r_recv)
+    c_copy = pltpu.make_async_copy(c_all, c_out, store.at[2])
+    c_copy.start()
+    u_copy = pltpu.make_async_copy(u_all, u_out, store.at[3])
+    u_copy.start()
+    gz_copy = pltpu.make_async_copy(gz_all, gz_out, store.at[4])
+    gz_copy.start()
+
+    def shrunk(t, unused):
+        place, peer = chip(t)
+        terms = jnp.dot(u_all[place], shrink_w[...], preferred_element_type=F32).astype(BF16)
+        part_two[place] = terms.reshape(2, rows, width)
+        to_mate(t, part_two, first_two, s_send, s_recv).start()
+        return unused
+
+    lax.fori_loop(0, 4, shrunk, 0)
+
+    def gathered_sum(parts, firsts, lasts, sends, recvs):
+        place, unused_peer = chip(0)
+        to_mate(0, parts, firsts, sends, recvs).wait_recv()
+        total = parts[place, k].astype(F32) + firsts[0].astype(F32)
+        for t in range(1, 4):
+            to_chip(t, firsts, lasts, sends, recvs).wait_recv()
+            total = total + lasts[t - 1].astype(F32)
+        return total
+
+    grad = gathered_sum(part, first, last, r_send, r_recv)
+    plain, scale = normed(mid[...])
+    grad_mid = own_grad[...].astype(F32) + norm_back(grad, gain[...], plain, scale)
+    grad_middle[...] = grad_mid
+    low = grad_mid.astype(BF16)
+    low_middle[...] = low
+    sums[0:1, :] = jnp.sum(low.astype(F32), axis=0, keepdims=True)
+    sums[1:2, :] = jnp.sum(own_grad[...].astype(F32), axis=0, keepdims=True)
+    sums[2:3, :] = jnp.sum(grad * plain, axis=0, keepdims=True)
+    sums[3:4, :] = jnp.sum(grad, axis=0, keepdims=True)
+    back = nt(low, out_w[...]).astype(BF16)
+    for d in range(cut.shape[0]):
+        low_end, high = d * span, min((d + 1) * span, width)
+        if high - low_end < span:
+            cut[d] = jnp.zeros(cut.shape[1:], cut.dtype)
+        if low_end < high:
+            cut[d, :, : high - low_end] = back[:, low_end:high]
+    head_started = pieces_out(axes, sizes, cut, to_heads, h_send, h_recv)
+    for t in range(1, 4):
+        add_and_send(t, part_two, first_two, summed_two, last_two, s_send, s_recv)
+    to_heads[here] = cut[here]
+    result[...] = (
+        mid[...] + gathered_sum(part_two, first_two, last_two, s_send, s_recv) + shrink_bias[...]
+    ).astype(BF16)
+    pieces_in(axes, sizes, cut, to_heads, h_send, h_recv, head_started)
+
+    for copy in out_sent + c_gather.started:
+        copy.wait_send()
+    for t in range(1, 4):
+        place, peer = chip(t)
+        remote(c_own, c_own, c_send.at[3 + t], c_recv.at[3 + t], mate).wait_send()
+    for t in range(4):
+        to_mate(t, part, first, r_send, r_recv).wait_send()
+        to_mate(t, part_two, first_two, s_send, s_recv).wait_send()
+    for t in range(1, 4):
+        to_chip(t, summed, last, r_send, r_recv).wait_send()
+        to_chip(t, summed_two, last_two, s_send, s_recv).wait_send()
+    for copy in (att_copy, e_copy, c_copy, u_copy, gz_copy):
+        copy.wait()
+
+
+def middle_part(
+    pieces, own, own_grad, out_own, out_far, expand, shrink, vectors, every, spec, ident
+):
+    spots, rows, span = pieces.shape
+    width = own.shape[1]
+    piece = expand.shape[2]
+    everyone = jax.ShapeDtypeStruct((4, 2, rows, width), BF16)
+    hidden = jax.ShapeDtypeStruct((4, 2 * rows, piece), BF16)
+    flat_f32 = jax.ShapeDtypeStruct((rows, width), F32)
+    flat_low = jax.ShapeDtypeStruct((rows, width), BF16)
+
+    def scatter_buffers():
+        return [
+            pltpu.VMEM(everyone.shape, BF16),
+            pltpu.VMEM((4, rows, width), BF16),
+            pltpu.VMEM((3, rows, width), BF16),
+            pltpu.VMEM((3, rows, width), BF16),
+        ]
+
+    return pl.pallas_call(
+        functools.partial(middle_kernel, every, spec),
+        out_shape=[
+            flat_low,
+            everyone,
+            everyone,
+            hidden,
+            hidden,
+            flat_low,
+            flat_f32,
+            flat_low,
+            jax.ShapeDtypeStruct((4, width), F32),
+            jax.ShapeDtypeStruct((1, piece), F32),
+            jax.ShapeDtypeStruct(pieces.shape, BF16),
+        ],
+        in_specs=[VMEM] * 3 + [ANY] * 4 + [VMEM] * 5,
+        out_specs=[ANY] * 5 + [VMEM] * 6,
+        scratch_shapes=[
+            pltpu.VMEM(pieces.shape, BF16),
+            pltpu.VMEM((rows, width), BF16),
+            pltpu.VMEM((width, width), BF16),
+            pltpu.VMEM((width, piece), BF16),
+            pltpu.VMEM((piece, width), BF16),
+            pltpu.VMEM((rows, width), F32),
+            pltpu.VMEM((rows, width), BF16),
+            pltpu.VMEM(everyone.shape, BF16),
+            pltpu.VMEM(everyone.shape, BF16),
+            pltpu.VMEM(hidden.shape, F32),
+            pltpu.VMEM(hidden.shape, BF16),
+            pltpu.VMEM(hidden.shape, BF16),
+            *scatter_buffers(),
+            *scatter_buffers(),
+            pltpu.VMEM(pieces.shape, BF16),
+            pltpu.SemaphoreType.DMA((spots,)),
+            pltpu.SemaphoreType.DMA((spots,)),
+            *gather_scratch(spec),
+            *gather_scratch(spec),
+            pltpu.SemaphoreType.DMA((7,)),
+            pltpu.SemaphoreType.DMA((2,)),
+            pltpu.SemaphoreType.DMA((2,)),
+            pltpu.SemaphoreType.DMA((7,)),
+            pltpu.SemaphoreType.DMA((7,)),
+            pltpu.SemaphoreType.DMA((7,)),
+            pltpu.SemaphoreType.DMA((7,)),
+            pltpu.SemaphoreType.DMA((spots,)),
+            pltpu.SemaphoreType.DMA((spots,)),
+            pltpu.SemaphoreType.DMA((5,)),
+        ],
+        name="middle%d" % ident,
+        compiler_params=pltpu.CompilerParams(
+            collective_id=ident, has_side_effects=True, vmem_limit_bytes=60 * 2**20
+        ),
+        cost_estimate=pl.CostEstimate(
+            flops=8 * rows * 8 * width * piece,
+            bytes_accessed=100 * rows * width * 2,
+            transcendentals=8 * rows * piece,
+        ),
+    )(pieces, own, own_grad, out_own, out_far, expand, shrink, *vectors)
 
 
 def nt(left, right):
@@ -944,7 +1260,6 @@
     )
     sequence = gathered.reshape(spots * rows, width)
     qkv_columns = qkv_columns.reshape(width, 3 * span)
-    expand_columns = expand_columns.reshape(width, piece)
 
     def doubled(values, axis_name):
         came = lax.ppermute(values, axis_name, [(0, 1), (1, 0)])
@@ -960,12 +1275,8 @@
         both = jnp.stack([jnp.where(first, near, far), jnp.where(first, far, near)], axis=2)
         return both.reshape(-1, width)
 
-    sequence, out_own, later_grad = lax.optimization_barrier((sequence, out_weight, own_grad))
-    swap = [(0, 1), (1, 0)]
-    out_pair = jnp.stack([out_own, lax.ppermute(out_own, "x", swap)])
-    out_mate = lax.ppermute(out_pair, "k", swap)
-    group_grad = over_group(later_grad)
-    shrink_rows = lax.dynamic_slice_in_dim(shrink_weight, i * piece, piece, axis=0)
+    sequence, out_own = lax.optimization_barrier((sequence, out_weight))
+    out_far = lax.ppermute(out_own, "x", [(0, 1), (1, 0)])
     expand_own_bias = lax.dynamic_slice_in_dim(
         expand_bias, (shard * inner + i) * piece, piece, axis=0
     )
@@ -983,22 +1294,6 @@
     normed_low = layer_norm(sequence.astype(F32), first_gain, first_shift).astype(BF16)
     qkv = (matmul(normed_low, qkv_columns) + qkv_bias).astype(BF16)
     attended, attended_bf, log_sum = attend(inv, qkv, heads)
-    attended_low = to_tokens(attended_bf.reshape(spots, rows, span), width, *every, 1)
-
-    out_parts = [out_pair[0], out_mate[0], out_pair[1], out_mate[1]]
-    out_spots = [shard, shard ^ 1, shard ^ 2, shard ^ 3]
-
-    def out_project(low):
-        terms = [
-            matmul(lax.dynamic_slice_in_dim(low, spot * part, part, axis=1), weight)
-            for spot, weight in zip(out_spots, out_parts)
-        ]
-        return terms[0] + terms[1] + terms[2] + terms[3]
-
-    inputs = own.astype(F32)
-    middle = inputs + out_project(attended_low) + out_bias
-    lowered_two = layer_norm(middle, second_gain, second_shift).astype(BF16)
-
     def cut(values, axis_name, dim):
         index, size = lax.axis_index(axis_name), sizes[axis_name]
         return [
@@ -1027,67 +1322,66 @@
         local = jnp.where(i == 0, jnp.stack([kept, came]), jnp.stack([came, kept]))
         return local.transpose(0, 2, 1).reshape(-1, cell).astype(F32)
 
-    (group_low,) = gather([lowered_two], [group], 2)
-    group_low = group_low.reshape(-1, width)
-    expanded = matmul(group_low, expand_columns) + expand_own_bias
-    hidden_low = smooth_gelu(expanded).astype(BF16)
-    grad_hidden = against(group_grad, shrink_rows)
-    unused, gelu_back = jax.vjp(smooth_gelu, expanded)
-    (grad_expanded,) = gelu_back(grad_hidden)
-    expanded_low = grad_expanded.astype(BF16)
-    grad_partial = against(expanded_low, expand_columns).astype(BF16)
-    shape = (inner * xs, ks, rows, width)
+    (
+        attended_low,
+        group_low,
+        group_grad,
+        hidden_low,
+        expanded_low,
+        result,
+        grad_middle,
+        middle_low,
+        row_sums,
+        hidden_sums,
+        grad_heads,
+    ) = middle_part(
+        attended_bf.reshape(spots, rows, span),
+        own,
+        own_grad,
+        out_own,
+        out_far,
+        expand_columns,
+        shrink_weight,
+        [
+            v[None]
+            for v in (out_bias, expand_own_bias, shrink_bias, second_gain, second_shift)
+        ],
+        every,
+        group,
+        1,
+    )
+    group_low, group_grad = group_low.reshape(-1, width), group_grad.reshape(-1, width)
+    hidden_low, expanded_low = hidden_low.reshape(-1, piece), expanded_low.reshape(-1, piece)
+    inputs = own.astype(F32)
+    grad_heads = grad_heads.reshape(spots * rows, span)
     shrink_cut = cut_columns(group_grad, hidden_low)
     expand_cut = onto(group_low, expanded_low).astype(BF16)
     expand_cut = expand_cut.reshape(shards, part, cuts, piece // cuts).transpose(0, 2, 1, 3)
     expand_cut = cut(expand_cut.reshape(outer, ys, part, piece // cuts), "y", 1)
-    grad_partial, shrink_cut, expand_cut = lax.optimization_barrier(
-        (grad_partial, shrink_cut, expand_cut)
-    )
-    (grad_normed_two,) = scatter([grad_partial.reshape(shape)], [group], 3)
-
-    grad_result = own_grad.astype(F32)
-    unused, second_back = jax.vjp(layer_norm, middle, second_gain, second_shift)
-    grad_middle_norm, grad_second_gain, grad_second_shift = second_back(grad_normed_two)
-    grad_middle = grad_result + grad_middle_norm
-    middle_low = grad_middle.astype(BF16)
-    turned = jnp.stack([against(middle_low, weight) for weight in out_parts])
-    turned = turned.reshape(2, 2, rows, part)
-    turned = jnp.where(lax.axis_index("x") == 0, turned, turned[::-1])
-    turned = jnp.where(lax.axis_index("k") == 0, turned, turned[:, ::-1])
-    grad_att_low = turned.reshape(shards, rows, part).transpose(1, 0, 2).reshape(rows, width)
-    grad_att_low = grad_att_low.astype(BF16)
-    grad_heads, att_group = to_heads(
-        grad_att_low, attended_low, span, *every, ("i", "x", "k"), (inner, xs, ks), 4
-    )
-    grad_heads = grad_heads.reshape(spots * rows, span)
-    middle_group = over_group(middle_low)
-    att_group = att_group.reshape(middle_group.shape[0], -1)
+    grad_heads, shrink_cut, expand_cut = lax.optimization_barrier(
+        (grad_heads, shrink_cut, expand_cut)
+    )
+
+    dqkv = attend_back(inv, qkv, grad_heads, attended, log_sum, heads)
     shrink_half, expand_half = added(shrink_cut, "y"), added(expand_cut, "y")
     shrink_cut, expand_cut = cut(shrink_half, "o", 0), cut(expand_half, "o", 0)
-    grad_heads, shrink_cut, expand_cut = lax.optimization_barrier(
-        (grad_heads, shrink_cut, expand_cut)
-    )
-
-    dqkv = attend_back(inv, qkv, grad_heads, attended, log_sum, heads)
+    dqkv, shrink_cut, expand_cut = lax.optimization_barrier((dqkv, shrink_cut, expand_cut))
     norm_partial = against(dqkv, qkv_columns).astype(BF16)
     qkv_partial = onto(normed_low, dqkv).astype(BF16)
-    result_partial = matmul(hidden_low, shrink_rows).astype(BF16)
-    outw_cut = cut_columns(middle_group, att_group)
     shrink_whole, expand_whole = added(shrink_cut, "o"), added(expand_cut, "o")
-    norm_partial, shrink_whole, expand_whole, outw_cut = lax.optimization_barrier(
-        (norm_partial, shrink_whole, expand_whole, outw_cut)
-    )
-    grad_normed_one, qkv_cells, shrunk = scatter(
+    middle_group, att_group = side_gather(
+        middle_low, attended_low, group, ("i", "x", "k"), (inner, xs, ks), 4
+    )
+    middle_group = middle_group.reshape(-1, width)
+    outw_cut = cut_columns(middle_group, att_group.reshape(middle_group.shape[0], -1))
+    grad_normed_one, qkv_cells = scatter(
         [
             norm_partial.reshape(outer * inner, ys, rows, width),
             qkv_partial.reshape(xs, ks, part, 3 * span),
-            result_partial.reshape(shape),
         ],
-        [ctx, pair, group],
+        [ctx, pair],
         5,
     )
-    result = middle + shrunk + shrink_bias
     unused, first_back = jax.vjp(layer_norm, inputs, first_gain, first_shift)
     grad_first_input, grad_first_gain, grad_first_shift = first_back(grad_normed_one)
     grad_inputs = grad_middle + grad_first_input
@@ -1109,15 +1403,15 @@
     small = [
         placed(dqkv_sums[:span], place * span, padded),
         placed(dqkv_sums[2 * span :], place * span, padded),
-        jnp.sum(middle_low.astype(F32), axis=0),
+        row_sums[0],
         placed(
-            jnp.sum(expanded_low.astype(F32), axis=0), (shard * inner + i) * piece, hidden
+            hidden_sums[0], (shard * inner + i) * piece, hidden
         ),
-        jnp.sum(grad_result, axis=0),
+        row_sums[1],
         grad_first_gain,
         grad_first_shift,
-        grad_second_gain,
-        grad_second_shift,
+        row_sums[2],
+        row_sums[3],
     ]
     lengths = [s.shape[0] for s in small]
     devices = spots * shards
@@ -1141,7 +1435,7 @@
     summed[0] = summed[0][:width]
     summed[1] = summed[1][:width]
     return (
-        result.astype(BF16)[None],
+        result[None],
         grad_inputs[None],
         grad_qkv,
         grad_outw,

time: 694 us -> 551 us (0.79); the launches traced: 682 us -> 546 us
  Pallas kernels: 328 us -> 366 us
  matrix products: 69.9 us -> 32.3 us
  waiting for transfers between devices: 86.9 us -> 49.8 us
  local copies, waits for them, and re-layouts: 97.7 us -> 63.9 us
  other arithmetic: 55.5 us -> 22.9 us
  starting transfers between devices: 41.3 us -> 9.7 us
    ppermute x8 -> x1, waiting for transfers between devices: 46.4 us -> 0.01 us  [body(): out_far = lax.ppermute(out_own, 'x', [(0, 1), (1, 0)])]
    pallas_call x3 -> x2, Pallas kernels: 99.6 us -> 143 us  [the longest x1 113 us: middle_part(): pl.pallas_call(functools.partial(middle_kernel, every, spec), out_shape=[...]
    ppermute x2, waiting for transfers between devices: 0.01 us -> 27.9 us  [owned(): came = lax.ppermute(sent, 'i', [(0, 1), (1, 0)])]
    ppermute x2, starting transfers between devices: 22 us -> 0.84 us  [owned(): came = lax.ppermute(sent, 'i', [(0, 1), (1, 0)])]
    dot_general x7 -> x1, matrix products: 23.9 us -> 2.95 us  [against(): lax.dot_general(left, weight, (((1,), (1,)), ((), ())), preferred_element...]
    dot_general x7 -> x1, matrix products: 26.6 us -> 6.32 us  [matmul(): return jnp.dot(left, right, preferred_element_type=F32)]
    ppermute x6, waiting for transfers between devices: 40.5 us -> 21.9 us  [added(): total = total + lax.ppermute(pieces[step], axis_name, ring).astype(F32)]
    select_n x7 -> x0, other arithmetic: 13.3 us -> none  [the longest x6 13.2 us: doubled(): jnp.where(lax.axis_index(axis_name) == 0, jnp.stack([values, came]), jnp....]
  transfers between devices with their start and end apart: 17 -> 10, of which waited for: 4 -> 4; matrix products, arithmetic and copies ran while one was open for 20% -> 11% of each run, Pallas kernels for 33% -> 32%
where the time goes in v4:
time: 551 us; the launch traced here: 546 us
  Pallas kernels  366 us (66%)
  local copies, waits for them, and re-layouts  63.9 us (12%)
  waiting for transfers between devices  49.8 us (9%)
  matrix products  32.3 us (6%)
  other arithmetic  22.9 us (4%)
  starting transfers between devices  9.7 us (2%)
    pallas_call x1, Pallas kernels, middle_part(): pl.pallas_call(functools.partial(middle_kernel, every, spec), out_shape=[...  113 us
    pallas_call x1, Pallas kernels, scatter(): pl.pallas_call(functools.partial(scatter_kernel, specs), out_shape=[jax.S...  95.7 us
    pallas_call x1, Pallas kernels, first_gather(): pl.pallas_call(functools.partial(first_kernel, specs, shard_sizes, *every...  50 us
    pallas_call x1, Pallas kernels, last_exchange(): pl.pallas_call(functools.partial(last_kernel, axes, sizes, spots, heads,...  33.9 us
    pallas_call x1, Pallas kernels, side_gather(): pl.pallas_call(functools.partial(side_kernel, spec, axes, sizes), out_sha...  30.9 us
    ppermute x2, waiting for transfers between devices, owned(): came = lax.ppermute(sent, 'i', [(0, 1), (1, 0)])  27.9 us
    pallas_call x1, Pallas kernels, attend_back(): pl.pallas_call(functools.partial(attend_back_kernel, heads, block), out_s...  23.4 us
    dot_general x4, matrix products, onto(): lax.dot_general(left, right, (((0,), (0,)), ((), ())), preferred_element_...  23.1 us
  transfers between devices with their start and end apart: 10, of which 4 were waited for; matrix products, arithmetic and copies ran while one was open for 11% of the time, Pallas kernels for 32%

profile of v4, /device:TPU:23, one launch (start us, length us, event | category | flops | bytes accessed | tf_op | source)
XLA Modules:
  0.0 546.4 jit_solution(9631517869742609781)
XLA Ops:
  0.6 2.0 copy.65
  2.6 50.0 %first0.1 = (bf16[4,2,128,1600]{3,2,1,0:T(8,128)(2,1)}, bf16[2,2,400,768]{3,2,1,0:T(8,128)(2,1)}, bf16[4,400,800]{2,1,0:T(8,128)(2,1)}) custom-call(bf16[128,1600]{1,0:T(8,128)(2,1)} %bitcast.96, bf16[400,4800]{1,0:T(8,128)(2,1)} %qkv_weight.1, bf16[400,6400]{1,0:T(8,128)(2,1)} %weight.1), custom_call_target="tpu_custom_call" | custom-call | bytes 82944000 | tf_op jit(solution)/shard_map/first0/pallas_call | solution.py:257
  53.4 2.6 convert_reduce_fusion
  59.3 2.0 copy.66
  63.8 6.3 %add_convert_fusion.qkv = bf16[1024,768]{1,0:T(8,128)(2,1)} fusion(bf16[1600,768]{1,0:T(8,128)(2,1)} %bitcast.120, f32[768]{0:T(1024)S(1)} %pad_maximum_fusion, bf16[1024,1600]{1,0:T(8,128)(2,1)S(1)} %bitcast.101, f32[1600]{0:T(1024)S(1)} %copy-done.22, f32[1600]{0:T(1024)S(1)} %copy-done.12, f32[1024]{0:T(1024)S(1)} %add_rsqrt_fusion, ...), kind=kOutput, calls=%fused_computation.13 | convolution fusion | flops 2527985664 | bytes 7331328 | tf_op jit(solution)/shard_map/dot_general | solution.py:1200
  70.1 20.0 %attend.1 = (f32[1024,256]{1,0:T(8,128)}, bf16[1024,256]{1,0:T(8,128)(2,1)}, f32[4,1024]{1,0:T(4,128)}) custom-call(s32[16]{0:T(128)} %select_reduce_fusion.inv, bf16[1024,768]{1,0:T(8,128)(2,1)} %add_convert_fusion.qkv), custom_call_target="tpu_custom_call" | custom-call | flops 2684354560 | bytes 2621440 | tf_op jit(solution)/shard_map/attend/pallas_call | solution.py:1040
  90.1 112.5 %middle1.1 = (bf16[128,1600]{1,0:T(8,128)(2,1)}, bf16[4,2,128,1600]{3,2,1,0:T(8,128)(2,1)}, bf16[4,2,128,1600]{3,2,1,0:T(8,128)(2,1)}, bf16[4,256,800]{2,1,0:T(8...) custom-call(bf16[8,128,256]{2,1,0:T(8,128)(2,1)} %bitcast.129, ...), custom_call_target="tpu_custom_call" | custom-call | flops 10485760000 | bytes 40960000 | tf_op jit(solution)/shard_map/middle1/pallas_call | solution.py:873
  202.6 7.3 %convolution_convert_fusion.1 = bf16[1600,800]{0,1:T(8,128)(2,1)} fusion(bf16[1024,1600]{1,0:T(8,128)(2,1)} %bitcast.125, bf16[1024,800]{1,0:T(8,128)(2,1)} %bitcast.127), kind=kOutput, calls=%fused_computation.9 | convolution fusion | flops 2622720000 | bytes 7475200 | tf_op jit(solution)/shard_map/dot_general | solution.py:1208
  209.9 5.2 copy.68
  215.1 7.2 %convolution_convert_fusion.2 = bf16[1600,800]{0,1:T(8,128)(2,1)} fusion(bf16[1024,1600]{1,0:T(8,128)(2,1)} %bitcast.124, bf16[1024,800]{1,0:T(8,128)(2,1)} %bitcast.126), kind=kOutput, calls=%fused_computation.10 | convolution fusion | flops 2622720000 | bytes 7475200 | tf_op jit(solution)/shard_map/dot_general | solution.py:1208
  222.4 5.2 copy.67
  227.6 30.9 %side4.1 = (bf16[4,2,128,1600]{3,2,1,0:T(8,128)(2,1)}, bf16[8,128,200]{2,1,0:T(8,128)(2,1)}) custom-call(bf16[128,1600]{1,0:T(8,128)(2,1)} %get-tuple-element.76.block, bf16[128,1600]{1,0:T(8,128)(2,1)} %get-tuple-element.77.att), custom_call_target="tpu_custom_call" | custom-call | bytes 32768000 | tf_op jit(solution)/shard_map/side4/pallas_call | solution.py:327
  258.5 3.9 convolution_convert_fusion.4
  262.4 5.2 reshape.166
  267.6 4.3 constant_dynamic-slice_fusion.3
  271.9 3.4 copy.80
  275.7 3.7 dynamic-slice_bitcast_fusion
  279.4 1.8 dynamic-slice_bitcast_fusion.2
  282.7 3.4 copy.79
  286.5 1.2 fusion.14
  289.2 23.4 %attend_back.1 = bf16[1024,768]{1,0:T(8,128)(2,1)} custom-call(s32[16]{0:T(128)} %select_reduce_fusion.inv, bf16[1024,768]{1,0:T(8,128)(2,1)} %add_convert_fusion.qkv, bf16[1024,256]{1,0:T(8,128)(2,1)} %bitcast.128, f32[1024,256]{1,0:T(8,128)} %get-tuple-element.64.outs, f32[4,1024]{1,0:T(4,128)} %get-tuple-element.65.lse), custom_call_target="tpu_custom_call" | custom-call | flops 6710886400 | bytes 5242880 | tf_op jit(solution)/shard_map/attend_back/pallas_call | solution.py:1150
  312.6 1.9 copy.76
  317.1 3.1 collective-permute-done.5
  321.0 1.9 copy.74
  322.9 2.2 add_convert_fusion.1
  325.2 1.3 dynamic-slice_bitcast_fusion.4
  326.4 21.5 %collective-permute-done.1 = bf16[2,2,200,800]{3,2,1,0:T(8,128)(2,1)} collective-permute-done((bf16[2,2,200,800]{3,2,1,0:T(8,128)(2,1)}, bf16[2,2,200,800]{3,2,1,0:T(8,128)(2,1)}, u32[]{:S(2)}, u32[]{:S(2)}) %collective-permute-start.1) | collective-permute-done | bytes 1280032 | tf_op jit(solution)/shard_map/ppermute | solution.py:1309
  347.9 1.7 add_convert_fusion.2
  349.7 1.3 dynamic-slice_bitcast_fusion.6
  351.0 4.7 convolution_convert_fusion.3
  355.7 3.0 convolution_convert_fusion
  359.0 2.4 collective-permute-start.6
  361.3 3.7 copy.69
  365.0 95.7 %scatter5.1 = (f32[128,1600]{1,0:T(8,128)}, f32[400,768]{1,0:T(8,128)}) custom-call(bf16[4,2,128,1600]{3,2,1,0:T(8,128)(2,1)} %bitcast.98, bf16[2,2,400,768]{3,2,1,0:T(8,128)(2,1)} %bitcast.106), custom_call_target="tpu_custom_call" | custom-call | bytes 57344000 | tf_op jit(solution)/shard_map/scatter5/pallas_call | solution.py:428
  460.7 1.5 convert_bitcast_fusion.2
  462.2 1.5 fusion.20
  466.7 33.9 %last6.1 = (f32[32,8,128]{2,1,0:T(8,128)}, bf16[11,64,400]{2,1,0:T(8,128)(2,1)}) custom-call(f32[32,8,128]{2,1,0:T(8,128)} %pad_bitcast_fusion.source, bf16[12,64,400]{2,1,0:T(8,128)(2,1)} %bitcast.105), custom_call_target="tpu_custom_call" | custom-call | tf_op jit(solution)/shard_map/last6/pallas_call | solution.py:537
  500.7 1.3 slice_bitcast_fusion
  502.0 1.5 fusion.21
  503.5 1.3 add_convert_fusion.4
  504.8 4.0 collective-permute-start.7
  508.9 1.3 add_convert_fusion.3
  511.1 1.4 slice.79
  512.8 1.2 copy.77
  515.0 24.8 %collective-permute-done.9 = bf16[200,800]{1,0:T(8,128)(2,1)} collective-permute-done((bf16[200,800]{1,0:T(8,128)(2,1)}, bf16[200,800]{1,0:T(8,128)(2,1)}, u32[]{:S(2)}, u32[]{:S(2)}) %collective-permute-start.9) | collective-permute-done | bytes 320032 | tf_op jit(solution)/shard_map/ppermute | solution.py:1321
  539.8 1.3 convert_bitcast_fusion
  541.9 2.0 reshape.171
  543.9 2.3 convert_element_type.158
  (105 shorter events, 19.7 us)
Async XLA Ops:
  2.6 50.5 %copy-start = (bf16[1,128,1600]{2,1,0:T(8,128)(2,1)S(1)}, bf16[1,128,1600]{2,1,0:T(8,128)(2,1)}, u32[]{:S(2)}) copy-start(bf16[1,128,1600]{2,1,0:T(8,128)(2,1)} %copy.65) | copy-start | bytes 1228804
  2.6 50.7 %copy-start.14 = (f32[1600]{0:T(1024)S(1)}, f32[1600]{0:T(1024)}, u32[]{:S(2)}) copy-start(f32[1600]{0:T(1024)} %param.19) | copy-start | bytes 19204
  2.6 50.7 %copy-start.15 = (f32[1600]{0:T(1024)S(1)}, f32[1600]{0:T(1024)}, u32[]{:S(2)}) copy-start(f32[1600]{0:T(1024)} %param.20) | copy-start | bytes 19204
  52.6 37.5 %collective-permute-start = (bf16[400,1600]{1,0:T(8,128)(2,1)}, bf16[400,1600]{1,0:T(8,128)(2,1)}, u32[]{:S(2)}, u32[]{:S(2)}) collective-permute-start(bf16[400,1600]{1,0:T(8,128)(2,1)} %out_own), channel_id=1, source_target_pairs={{0,2},{2,0},{1,3},{3,1},{4,6},{6,4},{5,7},{7,5},{8,10},{10,8},{9,1... | collective-permute-start | bytes 3840008 | tf_op jit(solution)/shard_map/ppermute | solution.py:1279
  53.3 3.0 copy-start.2
  53.3 4.0 copy-start.23
  56.0 5.3 copy-start.16
  56.0 5.8 %copy-start.17 = (f32[1600]{0:T(1024)S(1)}, f32[1600]{0:T(1024)}, u32[]{:S(2)}) copy-start(f32[1600]{0:T(1024)} %param.26) | copy-start | bytes 19204
  56.0 6.4 %copy-start.18 = (f32[1600]{0:T(1024)S(1)}, f32[1600]{0:T(1024)}, u32[]{:S(2)}) copy-start(f32[1600]{0:T(1024)} %param.29) | copy-start | bytes 19204
  56.0 7.0 %copy-start.19 = (f32[1600]{0:T(1024)S(1)}, f32[1600]{0:T(1024)}, u32[]{:S(2)}) copy-start(f32[1600]{0:T(1024)} %param.30) | copy-start | bytes 19204
  56.0 7.7 %copy-start.12 = (f32[1600]{0:T(1024)S(1)}, f32[1600]{0:T(1024)}, u32[]{:S(2)}) copy-start(f32[1600]{0:T(1024)} %param.27) | copy-start | bytes 19204
  56.1 7.7 %copy-start.22 = (f32[1600]{0:T(1024)S(1)}, f32[1600]{0:T(1024)}, u32[]{:S(2)}) copy-start(f32[1600]{0:T(1024)} %param.28) | copy-start | bytes 19204
  275.3 11.2 %collective-permute-start.3 = (bf16[2,2,200,200]{3,2,1,0:T(8,128)(2,1)}, bf16[2,2,200,200]{3,2,1,0:T(8,128)(2,1)}, u32[]{:S(2)}, u32[]{:S(2)}) collective-permute-start(bf16[2,2,200,200]{3,2,1,0:T(8,128)(2,1)} %bitcast.111), channel_id=1, source_target_pairs={{0,4},{4,0},{1,5},{5,1},{2,6},{6,2},{3,7},{7,3},{8,12},{12,8},{9,1... | collective-permute-start | bytes 960008 | tf_op jit(solution)/shard_map/ppermute | solution.py:1309
  275.7 3.7 copy-start.3
  281.2 41.7 %collective-permute-start.2 = (bf16[2,400,800]{2,1,0:T(8,128)(2,1)}, bf16[2,400,800]{2,1,0:T(8,128)(2,1)}, u32[]{:S(2)}, u32[]{:S(2)}) collective-permute-start(bf16[2,400,800]{2,1,0:T(8,128)(2,1)} %get-tuple-element.69), channel_id=1, source_target_pairs={{0,4},{4,0},{1,5},{5,1},{2,6},{6,2},{3,7},{7,3},{8,12},{12,8},{9,1... | collective-permute-start | bytes 3840008 | tf_op jit(solution)/shard_map/ppermute | solution.py:1309
  282.3 65.6 %collective-permute-start.1 = (bf16[2,2,200,800]{3,2,1,0:T(8,128)(2,1)}, bf16[2,2,200,800]{3,2,1,0:T(8,128)(2,1)}, u32[]{:S(2)}, u32[]{:S(2)}) collective-permute-start(bf16[2,2,200,800]{3,2,1,0:T(8,128)(2,1)} %get-tuple-element.67), channel_id=1, source_target_pairs={{0,4},{4,0},{1,5},{5,1},{2,6},{6,2},{3,7},{7,3},{8,12},{12,8},{9,1... | collective-permute-start | bytes 3840008 | tf_op jit(solution)/shard_map/ppermute | solution.py:1309
  287.7 0.8 copy-start.8
  289.2 25.9 %collective-permute-start.4 = (bf16[2,200,200]{2,1,0:T(8,128)(2,1)}, bf16[2,200,200]{2,1,0:T(8,128)(2,1)}, u32[]{:S(2)}, u32[]{:S(2)}) collective-permute-start(bf16[2,200,200]{2,1,0:T(8,128)(2,1)} %dynamic-slice_bitcast_fusion.9), channel_id=1, source_target_pairs={{0,16},{16,0},{1,17},{17,1},{2,18},{18,2},{3,19},{19,3},{4,20},{20... | collective-permute-start | bytes 480008 | tf_op jit(solution)/shard_map/ppermute | solution.py:1309
  289.2 25.4 %copy-start.20 = (f32[1,800]{1,0:T(1,128)S(1)}, f32[1,800]{1,0:T(1,128)}, u32[]{:S(2)}) copy-start(f32[1,800]{1,0:T(1,128)} %get-tuple-element.73) | copy-start | bytes 9604
  289.2 27.8 %copy-start.13 = (f32[4,1600]{1,0:T(4,128)S(1)}, f32[4,1600]{1,0:T(4,128)}, u32[]{:S(2)}) copy-start(f32[4,1600]{1,0:T(4,128)} %get-tuple-element.72) | copy-start | bytes 76804
  316.2 4.0 collective-permute-start.5
  322.9 25.0 %copy-start.5 = (bf16[2,2,200,800]{3,2,1,0:T(8,128)(2,1)S(1)}, bf16[2,2,200,800]{3,2,1,0:T(8,128)(2,1)}, u32[]{:S(2)}) copy-start(bf16[2,2,200,800]{3,2,1,0:T(8,128)(2,1)} %get-tuple-element.66) | copy-start | bytes 3840004
  326.4 24.5 %copy-start.9 = (bf16[1024,768]{1,0:T(8,128)(2,1)S(1)}, bf16[1024,768]{1,0:T(8,128)(2,1)}, u32[]{:S(2)}) copy-start(bf16[1024,768]{1,0:T(8,128)(2,1)} %attend_back.1) | copy-start | bytes 4718596
  351.0 4.7 copy-start.21
  358.9 149.9 %collective-permute-start.8 = (bf16[2,200,800]{2,1,0:T(8,128)(2,1)}, bf16[2,200,800]{2,1,0:T(8,128)(2,1)}, u32[]{:S(2)}, u32[]{:S(2)}) collective-permute-start(bf16[2,200,800]{2,1,0:T(8,128)(2,1)} %get-tuple-element.83), channel_id=1, source_target_pairs={{0,16},{16,0},{1,17},{17,1},{2,18},{18,2},{3,19},{19,3},{4,20},{20... | collective-permute-start | bytes 1920008 | tf_op jit(solution)/shard_map/ppermute | solution.py:1309
  359.0 144.5 %collective-permute-start.6 = (bf16[400,800]{1,0:T(8,128)(2,1)}, bf16[400,800]{1,0:T(8,128)(2,1)}, u32[]{:S(2)}, u32[]{:S(2)}) collective-permute-start(bf16[400,800]{1,0:T(8,128)(2,1)} %get-tuple-element.81), channel_id=1, source_target_pairs={{0,16},{16,0},{1,17},{17,1},{2,18},{18,2},{3,19},{19,3},{4,20},{20... | collective-permute-start | bytes 1920008 | tf_op jit(solution)/shard_map/ppermute | solution.py:1309
  365.0 97.2 %copy-start.1 = (bf16[1,128,1600]{2,1,0:T(8,128)(2,1)S(1)}, bf16[1,128,1600]{2,1,0:T(8,128)(2,1)}, u32[]{:S(2)}) copy-start(bf16[1,128,1600]{2,1,0:T(8,128)(2,1)} %copy.65) | copy-start | bytes 1228804
  460.7 3.0 copy-start.4
  460.7 3.6 copy-start.10
  464.4 39.1 %copy-start.6 = (bf16[400,800]{1,0:T(8,128)(2,1)S(1)}, bf16[400,800]{1,0:T(8,128)(2,1)}, u32[]{:S(2)}) copy-start(bf16[400,800]{1,0:T(8,128)(2,1)} %get-tuple-element.80) | copy-start | bytes 1920004
  464.7 44.2 %copy-start.7 = (bf16[2,200,800]{2,1,0:T(8,128)(2,1)S(1)}, bf16[2,200,800]{2,1,0:T(8,128)(2,1)}, u32[]{:S(2)}) copy-start(bf16[2,200,800]{2,1,0:T(8,128)(2,1)} %get-tuple-element.82) | copy-start | bytes 1920004
  503.5 7.6 %copy-start.11 = (bf16[11,64,400]{2,1,0:T(8,128)(2,1)S(1)}, bf16[11,64,400]{2,1,0:T(8,128)(2,1)}, u32[]{:S(2)}) copy-start(bf16[11,64,400]{2,1,0:T(8,128)(2,1)} %get-tuple-element.75) | copy-start | bytes 1689604
  504.8 39.1 %collective-permute-start.7 = (bf16[400,800]{1,0:T(8,128)(2,1)S(1)}, bf16[400,800]{1,0:T(8,128)(2,1)}, u32[]{:S(2)}, u32[]{:S(2)}) collective-permute-start(bf16[400,800]{1,0:T(8,128)(2,1)S(1)} %add_convert_fusion.4), channel_id=1, source_target_pairs={{0,0},{1,8},{2,16},{3,24},{4,1},{5,9},{6,17},{7,25},{8,4},{9,12},{... | collective-permute-start | bytes 1920008 | tf_op jit(solution)/shard_map/ppermute | solution.py:1396
  511.0 28.8 %collective-permute-start.9 = (bf16[200,800]{1,0:T(8,128)(2,1)}, bf16[200,800]{1,0:T(8,128)(2,1)}, u32[]{:S(2)}, u32[]{:S(2)}) collective-permute-start(bf16[200,800]{1,0:T(8,128)(2,1)} %get-tuple-element.165), channel_id=1, source_target_pairs={{0,8},{8,0},{1,9},{9,1},{2,10},{10,2},{3,11},{11,3},{4,12},{12,4},... | collective-permute-start | bytes 960008 | tf_op jit(solution)/shard_map/ppermute | solution.py:1321

commit v5 on v4

--- a/solution.py
+++ b/solution.py
@@ -130,35 +130,6 @@
 
 def sent_estimate(size):
     return pl.CostEstimate(flops=0, bytes_accessed=20 * size, transcendentals=0)
-
-
-def gather_kernel(specs, *refs):
-    count = len(specs)
-    gathers = [
-        Gather(*spec, refs[n], refs[count + n], *refs[2 * count + 3 * n : 2 * count + 3 * n + 3])
-        for n, spec in enumerate(specs)
-    ]
-    greet([peer for g in gathers for peer in g.peers()])
-    for g in gathers:
-        g.start()
-    for g in gathers:
-        g.hand_on()
-    for g in gathers:
-        g.finish()
-
-
-def gather(blocks, specs, ident):
-    shapes = [gather_shape(block, spec) for block, spec in zip(blocks, specs)]
-    return pl.pallas_call(
-        functools.partial(gather_kernel, specs),
-        out_shape=shapes,
-        in_specs=[VMEM] * len(blocks),
-        out_specs=[ANY] * len(blocks),
-        scratch_shapes=[s for spec in specs for s in gather_scratch(spec)],
-        name="gather%d" % ident,
-        compiler_params=pltpu.CompilerParams(collective_id=ident, has_side_effects=True),
-        cost_estimate=sent_estimate(sum(s.size for s in shapes)),
-    )(*blocks)
 
 
 def first_kernel(
@@ -300,260 +271,6 @@
         copy.wait_send()
 
 
-def side_kernel(
-    spec, axes, sizes, block, att, everyone, att_out, att_cut, send, recv, *gather_sems
-):
-    beside = Gather(*spec, block, everyone, *gather_sems)
-    greet([moved(axes, sizes, o) for o in offsets(sizes)])
-    beside.start()
-    cell = att_cut.shape[2]
-    inner, shards = sizes[0], sizes[1] * sizes[2]
-    for half in range(inner):
-        for f in range(shards):
-            low = (f * inner + half) * cell
-            att_cut[half * shards + f] = att[:, low : low + cell]
-    started = pieces_out(axes, sizes, att_cut, att_out, send, recv)
-    me = flat(own_place(axes), axes, sizes)
-    att_out[me] = att_cut[me]
-    beside.hand_on()
-    pieces_in(axes, sizes, att_cut, att_out, send, recv, started)
-    beside.finish()
-
-
-def side_gather(block, att, spec, axes, sizes, ident):
-    rows, width = block.shape
-    group = sizes[0] * sizes[1] * sizes[2]
-    cell = width // group
-    return pl.pallas_call(
-        functools.partial(side_kernel, spec, axes, sizes),
-        out_shape=[
-            gather_shape(block, spec),
-            jax.ShapeDtypeStruct((group, rows, cell), att.dtype),
-        ],
-        in_specs=[VMEM, VMEM],
-        out_specs=[ANY, VMEM],
-        scratch_shapes=[
-            pltpu.VMEM((group, rows, cell), att.dtype),
-            pltpu.SemaphoreType.DMA((group,)),
-            pltpu.SemaphoreType.DMA((group,)),
-            *gather_scratch(spec),
-        ],
-        name="side%d" % ident,
-        compiler_params=pltpu.CompilerParams(collective_id=ident, has_side_effects=True),
-        cost_estimate=sent_estimate(8 * block.size),
-    )(block, att)
-
-
-class Scatter:
-    def __init__(self, axes, sizes, pair, source, out, first, summed, last, send, recv):
-        self.axes, self.sizes = axes, sizes
-        self.offs = offsets(sizes)
-        self.side = lax.axis_index(pair)
-        self.mate = {pair: 1 - self.side}
-        self.source, self.out = source, out
-        self.first, self.summed, self.last = first, summed, last
-        self.send, self.recv = send, recv
-        self.started = []
-
-    def peers(self):
-        return [moved(self.axes, self.sizes, o) for o in self.offs] + [self.mate]
-
-    def start(self):
-        for t, off in enumerate(self.offs + [(0,) * len(self.sizes)]):
-            there = flat(moved(self.axes, self.sizes, off), self.axes, self.sizes)
-            copy = remote(
-                self.source.at[there, 1 - self.side],
-                self.first.at[t],
-                self.send.at[t],
-                self.recv.at[t],
-                self.mate,
-            )
-            copy.start()
-            self.started.append(copy)
-
-    def add(self):
-        count = len(self.offs)
-        for t, off in enumerate(self.offs):
-            peer = moved(self.axes, self.sizes, off)
-            there = flat(peer, self.axes, self.sizes)
-            self.started[t].wait_recv()
-            self.summed[t] = (
-                self.source[there, self.side].astype(F32) + self.first[t].astype(F32)
-            ).astype(BF16)
-            slot = count + 1 + t
-            copy = remote(
-                self.summed.at[t], self.last.at[t], self.send.at[slot], self.recv.at[slot], peer
-            )
-            copy.start()
-            self.started.append(copy)
-
-    def finish(self):
-        count = len(self.offs)
-        me = flat(own_place(self.axes), self.axes, self.sizes)
-        self.started[count].wait_recv()
-        self.out[...] = self.source[me, self.side].astype(F32) + self.first[count].astype(F32)
-        for t in range(count):
-            self.started[count + 1 + t].wait_recv()
-            self.out[...] += self.last[t].astype(F32)
-        for copy in self.started:
-            copy.wait_send()
-
-
-def scatter_kernel(specs, *refs):
-    count = len(specs)
-    scatters = [
-        Scatter(*spec, refs[n], refs[count + n], *refs[2 * count + 5 * n : 2 * count + 5 * n + 5])
-        for n, spec in enumerate(specs)
-    ]
-    greet([peer for s in scatters for peer in s.peers()])
-    for s in scatters:
-        s.start()
-    for s in scatters:
-        s.add()
-    for s in scatters:
-        s.finish()
-
-
-def scatter(partials, specs, ident):
-    scratch = []
-    for partial in partials:
-        group, block = partial.shape[0], partial.shape[2:]
-        scratch += [
-            pltpu.VMEM((group,) + block, BF16),
-            pltpu.VMEM((group - 1,) + block, BF16),
-            pltpu.VMEM((group - 1,) + block, BF16),
-            pltpu.SemaphoreType.DMA((2 * group,)),
-            pltpu.SemaphoreType.DMA((2 * group,)),
-        ]
-    return pl.pallas_call(
-        functools.partial(scatter_kernel, specs),
-        out_shape=[jax.ShapeDtypeStruct(p.shape[2:], F32) for p in partials],
-        in_specs=[VMEM] * len(partials),
-        out_specs=[VMEM] * len(partials),
-        scratch_shapes=scratch,
-        name="scatter%d" % ident,
-        compiler_params=pltpu.CompilerParams(collective_id=ident, has_side_effects=True),
-        cost_estimate=sent_estimate(sum(p.size for p in partials)),
-    )(*partials)
-
-
-def last_kernel(
-    axes, sizes, spots, heads, share, source, blocks, out, routed, came, send, recv, hop, land
-):
-    offs = offsets(sizes)
-    greet([moved(axes, sizes, o) for o in offs])
-    me = flat(own_place(axes), axes, sizes)
-    count = len(offs)
-    started = []
-    for t, off in enumerate(offs):
-        peer = moved(axes, sizes, off)
-        copy = remote(
-            source.at[flat(peer, axes, sizes)], came.at[t], send.at[t], recv.at[t], peer
-        )
-        copy.start()
-        started.append(copy)
-
-    ctx_axes, ctx_sizes = axes[:3], sizes[:3]
-    place = flat(own_place(ctx_axes), ctx_axes, ctx_sizes)
-
-    def where(spot):
-        return {
-            ctx_axes[0]: spot // (ctx_sizes[1] * ctx_sizes[2]),
-            ctx_axes[1]: (spot // ctx_sizes[2]) % ctx_sizes[1],
-            ctx_axes[2]: spot % ctx_sizes[2],
-        }
-
-    def each_sent(act):
-        for part in range(3):
-            for h in range(heads):
-                head = place * heads + h
-                block = part * HEADS + head
-                low = (block * HEAD_DIM) // share
-                high = (block * HEAD_DIM + HEAD_DIM - 1) // share
-                index = part * heads + h
-                for which, owner, needed in (
-                    (0, low, head < HEADS),
-                    (1, high, (head < HEADS) & (high != low)),
-                ):
-
-                    @pl.when(needed)
-                    def _(which=which, owner=owner, block=block, index=index):
-                        act(index, 2 * index + which, owner, block - (share * owner) // HEAD_DIM)
-
-    def send_block(index, slot, owner, target):
-        @pl.when(owner != place)
-        def _():
-            remote(
-                blocks.at[index], routed.at[target], hop.at[slot], land.at[target], where(owner)
-            ).start()
-
-        @pl.when(owner == place)
-        def _():
-            routed[target] = blocks[index]
-
-    def sent_block(index, slot, owner, target):
-        @pl.when(owner != place)
-        def _():
-            remote(
-                blocks.at[index], routed.at[target], hop.at[slot], land.at[target], where(owner)
-            ).wait_send()
-
-    each_sent(send_block)
-    for copy in started:
-        copy.wait_recv()
-    out[me] = source[me] + jnp.sum(came[...], axis=0)
-    second = []
-    for t, off in enumerate(offs):
-        peer = moved(axes, sizes, off)
-        copy = remote(out.at[me], out.at[me], send.at[count + t], recv.at[count + t], peer)
-        copy.start()
-        second.append(copy)
-
-    base = (share * place) // HEAD_DIM
-    for slot in range(routed.shape[0]):
-        block = base + slot
-        owner = (block % HEADS) // heads
-
-        @pl.when((block * HEAD_DIM < share * (place + 1)) & (owner != place))
-        def _(slot=slot):
-            remote(
-                blocks.at[0], routed.at[slot], hop.at[0], land.at[slot], where(place)
-            ).wait_recv()
-
-    each_sent(sent_block)
-    for t, off in enumerate(offs):
-        peer = moved(axes, sizes, off, -1)
-        block = out.at[flat(peer, axes, sizes)]
-        remote(block, block, send.at[count + t], recv.at[count + t], peer).wait_recv()
-    for copy in started + second:
-        copy.wait_send()
-
-
-def last_exchange(parts, blocks, axes, sizes, spots, heads, share, ident):
-    group = parts.shape[0]
-    slots = max(
-        (share * (c + 1) - 1) // HEAD_DIM - (share * c) // HEAD_DIM + 1 for c in range(spots)
-    )
-    return pl.pallas_call(
-        functools.partial(last_kernel, axes, sizes, spots, heads, share),
-        out_shape=[
-            jax.ShapeDtypeStruct(parts.shape, F32),
-            jax.ShapeDtypeStruct((slots,) + blocks.shape[1:], BF16),
-        ],
-        in_specs=[VMEM, VMEM],
-        out_specs=[VMEM, VMEM],
-        scratch_shapes=[
-            pltpu.VMEM((group - 1,) + parts.shape[1:], F32),
-            pltpu.SemaphoreType.DMA((2 * group,)),
-            pltpu.SemaphoreType.DMA((2 * group,)),
-            pltpu.SemaphoreType.DMA((6 * heads,)),
-            pltpu.SemaphoreType.DMA((slots,)),
-        ],
-        name="last%d" % ident,
-        compiler_params=pltpu.CompilerParams(collective_id=ident, has_side_effects=True),
-    )(parts, blocks)
-
-
 def normed(values):
     center = jnp.mean(values, axis=-1, keepdims=True)
     centred = values - center
@@ -569,6 +286,17 @@
         - jnp.mean(inner, axis=-1, keepdims=True)
         - plain * jnp.mean(inner * plain, axis=-1, keepdims=True)
     )
+
+
+def by_columns(left, right, out):
+    tokens = left.shape[0] * left.shape[1] * left.shape[2]
+    cell = out.shape[1]
+    wide = 400 // cell
+    others = right[...].reshape(tokens, right.shape[-1])
+    for c in range(left.shape[3] // 400):
+        terms = tn(left[:, :, :, c * 400 : (c + 1) * 400].reshape(tokens, 400), others)
+        for n in range(wide):
+            out[c * wide + n] = terms[n * cell : (n + 1) * cell].astype(BF16)
 
 
 def middle_kernel(
@@ -586,19 +314,16 @@
     shrink_bias,
     gain,
     shift,
-    att_out,
-    c_out,
-    e_out,
-    u_out,
-    gz_out,
+    att,
     result,
     grad_middle,
     low_middle,
     sums,
     hidden_sum,
     to_heads,
+    expand_half,
+    shrink_terms,
     came,
-    att,
     out_w,
     expand_w,
     shrink_w,
@@ -618,6 +343,8 @@
     summed_two,
     last_two,
     cut,
+    expand_terms,
+    expand_came,
     send,
     recv,
     c_send,
@@ -635,9 +362,11 @@
     s_recv,
     h_send,
     h_recv,
-    store,
+    y_send,
+    y_recv,
 ):
     axes, sizes = every
+    y = lax.axis_index("y")
     x, k, inner = lax.axis_index("x"), lax.axis_index("k"), lax.axis_index("i")
     mate = {"k": 1 - k}
     shard = 2 * x + k
@@ -705,12 +434,8 @@
     c_own[...] = (plain * gain[...] + shift[...]).astype(BF16)
     c_gather = Gather(*spec, c_own, c_all, c_send, c_recv, c_local)
     c_gather.start()
-    att_copy = pltpu.make_async_copy(att, att_out, store.at[0])
-    att_copy.start()
     e_gather.hand_on()
     e_gather.finish()
-    e_copy = pltpu.make_async_copy(e_all, e_out, store.at[1])
-    e_copy.start()
     for copy in loads[2:]:
         copy.wait()
 
@@ -785,21 +510,28 @@
 
     lax.fori_loop(0, 4, feed, 0)
     add_and_send(3, part, first, summed, last, r_send, r_recv)
-    c_copy = pltpu.make_async_copy(c_all, c_out, store.at[2])
-    c_copy.start()
-    u_copy = pltpu.make_async_copy(u_all, u_out, store.at[3])
-    u_copy.start()
-    gz_copy = pltpu.make_async_copy(gz_all, gz_out, store.at[4])
-    gz_copy.start()
-
-    def shrunk(t, unused):
-        place, peer = chip(t)
-        terms = jnp.dot(u_all[place], shrink_w[...], preferred_element_type=F32).astype(BF16)
-        part_two[place] = terms.reshape(2, rows, width)
-        to_mate(t, part_two, first_two, s_send, s_recv).start()
-        return unused
-
-    lax.fori_loop(0, 4, shrunk, 0)
+
+    parts, cuts = expand.shape[0], expand_terms.shape[0] * 2 // expand.shape[0]
+    cut_width = expand_terms.shape[3]
+    for f in range(parts):
+        terms = tn(
+            c_all[:, :, :, f * part_rows : (f + 1) * part_rows].reshape(8 * rows, part_rows),
+            gz_all[...].reshape(8 * rows, piece),
+        )
+        for c in range(cuts):
+            index = f * cuts + c
+            expand_terms[index // 2, index % 2] = terms[
+                :, c * cut_width : (c + 1) * cut_width
+            ].astype(BF16)
+    y_mate = {"y": 1 - y}
+    y_copies = [
+        remote(
+            expand_terms.at[n, 1 - y], expand_came.at[n], y_send.at[n], y_recv.at[n], y_mate
+        )
+        for n in range(expand_terms.shape[0])
+    ]
+    for copy in y_copies:
+        copy.start()
 
     def gathered_sum(parts, firsts, lasts, sends, recvs):
         place, unused_peer = chip(0)
@@ -828,13 +560,28 @@
         if low_end < high:
             cut[d, :, : high - low_end] = back[:, low_end:high]
     head_started = pieces_out(axes, sizes, cut, to_heads, h_send, h_recv)
+
+    def shrunk(t, unused):
+        place, peer = chip(t)
+        terms = jnp.dot(u_all[place], shrink_w[...], preferred_element_type=F32).astype(BF16)
+        part_two[place] = terms.reshape(2, rows, width)
+        to_mate(t, part_two, first_two, s_send, s_recv).start()
+        return unused
+
+    lax.fori_loop(0, 4, shrunk, 0)
     for t in range(1, 4):
         add_and_send(t, part_two, first_two, summed_two, last_two, s_send, s_recv)
     to_heads[here] = cut[here]
+    by_columns(e_all, u_all, shrink_terms)
     result[...] = (
         mid[...] + gathered_sum(part_two, first_two, last_two, s_send, s_recv) + shrink_bias[...]
     ).astype(BF16)
     pieces_in(axes, sizes, cut, to_heads, h_send, h_recv, head_started)
+    for n, copy in enumerate(y_copies):
+        copy.wait_recv()
+        expand_half[n] = (
+            expand_terms[n, y].astype(F32) + expand_came[n].astype(F32)
+        ).astype(BF16)
 
     for copy in out_sent + c_gather.started:
         copy.wait_send()
@@ -847,8 +594,8 @@
     for t in range(1, 4):
         to_chip(t, summed, last, r_send, r_recv).wait_send()
         to_chip(t, summed_two, last_two, s_send, s_recv).wait_send()
-    for copy in (att_copy, e_copy, c_copy, u_copy, gz_copy):
-        copy.wait()
+    for copy in y_copies:
+        copy.wait_send()
 
 
 def middle_part(
@@ -857,6 +604,9 @@
     spots, rows, span = pieces.shape
     width = own.shape[1]
     piece = expand.shape[2]
+    outer = every[1][0]
+    cuts = outer * 2 // expand.shape[0]
+    expand_cut = (outer, 2, expand.shape[1], piece // cuts)
     everyone = jax.ShapeDtypeStruct((4, 2, rows, width), BF16)
     hidden = jax.ShapeDtypeStruct((4, 2 * rows, piece), BF16)
     flat_f32 = jax.ShapeDtypeStruct((rows, width), F32)
@@ -874,22 +624,19 @@
         functools.partial(middle_kernel, every, spec),
         out_shape=[
             flat_low,
-            everyone,
-            everyone,
-            hidden,
-            hidden,
             flat_low,
             flat_f32,
             flat_low,
             jax.ShapeDtypeStruct((4, width), F32),
             jax.ShapeDtypeStruct((1, piece), F32),
             jax.ShapeDtypeStruct(pieces.shape, BF16),
+            jax.ShapeDtypeStruct(expand_cut[:1] + expand_cut[2:], BF16),
+            jax.ShapeDtypeStruct((spots, width // spots, piece), BF16),
         ],
         in_specs=[VMEM] * 3 + [ANY] * 4 + [VMEM] * 5,
-        out_specs=[ANY] * 5 + [VMEM] * 6,
+        out_specs=[VMEM] * 9,
         scratch_shapes=[
             pltpu.VMEM(pieces.shape, BF16),
-            pltpu.VMEM((rows, width), BF16),
             pltpu.VMEM((width, width), BF16),
             pltpu.VMEM((width, piece), BF16),
             pltpu.VMEM((piece, width), BF16),
@@ -903,6 +650,8 @@
             *scatter_buffers(),
             *scatter_buffers(),
             pltpu.VMEM(pieces.shape, BF16),
+            pltpu.VMEM(expand_cut, BF16),
+            pltpu.VMEM(expand_cut[:1] + expand_cut[2:], BF16),
             pltpu.SemaphoreType.DMA((spots,)),
             pltpu.SemaphoreType.DMA((spots,)),
             *gather_scratch(spec),
@@ -916,11 +665,12 @@
             pltpu.SemaphoreType.DMA((7,)),
             pltpu.SemaphoreType.DMA((spots,)),
             pltpu.SemaphoreType.DMA((spots,)),
-            pltpu.SemaphoreType.DMA((5,)),
+            pltpu.SemaphoreType.DMA(expand_cut[:1]),
+            pltpu.SemaphoreType.DMA(expand_cut[:1]),
         ],
         name="middle%d" % ident,
         compiler_params=pltpu.CompilerParams(
-            collective_id=ident, has_side_effects=True, vmem_limit_bytes=60 * 2**20
+            collective_id=ident, has_side_effects=True, vmem_limit_bytes=67_000_000
         ),
         cost_estimate=pl.CostEstimate(
             flops=8 * rows * 8 * width * piece,
@@ -930,12 +680,524 @@
     )(pieces, own, own_grad, out_own, out_far, expand, shrink, *vectors)
 
 
+class Owned:
+    def __init__(self, outer, terms, out, came, half, last, whole, y_sems, o_sems, i_sems):
+        self.outer = outer
+        self.terms, self.out = terms, out
+        self.came, self.half, self.last, self.whole = came, half, last, whole
+        self.y_sems, self.o_sems, self.i_sems = y_sems, o_sems, i_sems
+        self.o, self.i, self.y = (lax.axis_index(a) for a in ("o", "i", "y"))
+
+    def start(self):
+        mate = {"y": 1 - self.y}
+        self.first = [
+            remote(
+                self.terms.at[2 * n + 1 - self.y],
+                self.came.at[n],
+                self.y_sems.at[0, n],
+                self.y_sems.at[1, n],
+                mate,
+            )
+            for n in range(2 * self.outer)
+        ]
+        for copy in self.first:
+            copy.start()
+
+    def over_o(self):
+        for n, copy in enumerate(self.first):
+            copy.wait_recv()
+            self.half[n // 2, n % 2] = (
+                self.terms[2 * n + self.y].astype(F32) + self.came[n].astype(F32)
+            ).astype(BF16)
+        self.second = []
+        for step in range(1, self.outer):
+            there = lax.rem(self.o + step, self.outer)
+            copy = remote(
+                self.half.at[there],
+                self.last.at[step - 1],
+                self.o_sems.at[0, step],
+                self.o_sems.at[1, step],
+                {"o": there},
+            )
+            copy.start()
+            self.second.append(copy)
+
+    def over_i(self):
+        total = self.half[self.o].astype(F32)
+        for step, copy in enumerate(self.second):
+            copy.wait_recv()
+            total = total + self.last[step].astype(F32)
+        self.whole[...] = total.astype(BF16)
+        self.third = remote(
+            self.whole.at[1 - self.i],
+            self.out.at[self.i],
+            self.i_sems.at[0],
+            self.i_sems.at[1],
+            {"i": 1 - self.i},
+        )
+        self.third.start()
+        self.out[self.i] = self.whole[self.i]
+
+    def finish(self):
+        self.third.wait_recv()
+        for copy in self.first + self.second + [self.third]:
+            copy.wait_send()
+
+
+def owned_scratch(outer, cell, rows):
+    return [
+        pltpu.VMEM((2 * outer, cell, rows), BF16),
+        pltpu.VMEM((outer, 2, cell, rows), BF16),
+        pltpu.VMEM((max(outer - 1, 1), 2, cell, rows), BF16),
+        pltpu.VMEM((2, cell, rows), BF16),
+        pltpu.SemaphoreType.DMA((2, 2 * outer)),
+        pltpu.SemaphoreType.DMA((2, outer)),
+        pltpu.SemaphoreType.DMA((2,)),
+    ]
+
+
+def final_kernel(
+    axes,
+    sizes,
+    heads,
+    share,
+    dqkv,
+    columns,
+    normed_low,
+    shrink_terms,
+    low_middle,
+    att,
+    own,
+    grad_middle,
+    gain,
+    row_sums,
+    hidden_sum,
+    grad_inputs,
+    routed,
+    shrink_out,
+    outw_out,
+    query_out,
+    value_out,
+    rows_out,
+    hidden_out,
+    part,
+    first,
+    last,
+    normed_part,
+    q_part,
+    q_first,
+    q_sum,
+    q_last,
+    blocks,
+    gy_all,
+    att_cut,
+    att_all,
+    outw_terms,
+    line,
+    line_came,
+    line_out,
+    r_send,
+    r_recv,
+    q_send,
+    q_recv,
+    hop,
+    land,
+    a_send,
+    a_recv,
+    l_send,
+    l_recv,
+    g_send,
+    g_recv,
+    g_local,
+    load_sem,
+    *owned,
+):
+    outer, inner, ys, xs, ks = sizes
+    o, i, y, x, k = (lax.axis_index(a) for a in axes)
+    offs = offsets(sizes)
+    chips = outer * inner
+    spots = chips * ys
+    place = (o * inner + i) * ys + y
+    shard = x * ks + k
+    me = place * xs * ks + shard
+    rows, width = own.shape
+    span = heads * HEAD_DIM
+    y_mate, k_mate, x_mate = {"y": 1 - y}, {"k": 1 - k}, {"x": 1 - x}
+    shrink = Owned(outer, shrink_terms, shrink_out, *owned[:7])
+    outw = Owned(outer, outw_terms, outw_out, *owned[7:])
+
+    def load_normed(n):
+        some = normed_part.shape[0]
+        return pltpu.make_async_copy(
+            normed_low.at[pl.ds(n * some, some)], normed_part, load_sem
+        )
+
+    load_normed(0).start()
+    greet([moved(axes, sizes, off) for off in offs])
+
+    group = (("i", "x", "k"), (inner, xs, ks))
+    side = Gather(("i", "x"), (inner, xs), "k", low_middle, gy_all, g_send, g_recv, g_local)
+    side.start()
+    cell = att_cut.shape[2]
+    for half in range(inner):
+        for f in range(xs * ks):
+            low = (f * inner + half) * cell
+            att_cut[half * xs * ks + f] = att[:, low : low + cell]
+    att_started = pieces_out(*group, att_cut, att_all, a_send, a_recv)
+    here = (i * xs + x) * ks + k
+    att_all[here] = att_cut[here]
+
+    def chip(t):
+        to, ti = lax.rem(o + t // inner, outer), lax.rem(i + t % inner, inner)
+        return to * inner + ti, {"o": to, "i": ti}
+
+    def back_chip(t):
+        to = lax.rem(o + outer - t // inner, outer)
+        ti = lax.rem(i + inner - t % inner, inner)
+        return to * inner + ti
+
+    def to_mate(t):
+        return remote(
+            part.at[chip(t)[0], 1 - y], first.at[t], r_send.at[t], r_recv.at[t], y_mate
+        )
+
+    def to_chip(t):
+        slot = chips + t - 1
+        return remote(
+            part.at[chip(t)[0], y], last.at[t - 1], r_send.at[slot], r_recv.at[slot], chip(t)[1]
+        )
+
+    def terms(step, unused):
+        t = lax.rem(step + 1, chips)
+        spot = chip(t)[0]
+        at = pl.multiple_of(spot * 2 * rows, 2 * rows)
+        values = nt(dqkv[pl.ds(at, 2 * rows), :], columns[...]).astype(BF16)
+        part[spot] = values.reshape(2, rows, width)
+        to_mate(t).start()
+        return unused
+
+    lax.fori_loop(0, chips, terms, 0)
+    shrink.start()
+
+    quarter = q_part.shape[3]
+    some = normed_part.shape[0]
+    pieces = dqkv.shape[0] // some
+    for section in range(3):
+        low = section * span
+        values = 0.0
+        for n in range(pieces):
+            if n or section == 0 or pieces > 1:
+                copy = load_normed(n)
+                if n or section:
+                    copy.start()
+                copy.wait()
+            values = values + tn(
+                dqkv[n * some : (n + 1) * some, low : low + span], normed_part[...]
+            )
+        for f in range(xs * ks):
+            q_part[f // ks, f % ks, low : low + span, :] = values[
+                :, f * quarter : (f + 1) * quarter
+            ].astype(BF16)
+    q_copies = [
+        remote(q_part.at[1 - x, 1 - k], q_first.at[1], q_send.at[1], q_recv.at[1], k_mate),
+        remote(q_part.at[x, 1 - k], q_first.at[0], q_send.at[0], q_recv.at[0], k_mate),
+    ]
+    for copy in q_copies:
+        copy.start()
+
+    def add_and_send(step, unused):
+        t = step + 1
+        to_mate(t).wait_recv()
+        spot = chip(t)[0]
+        part[spot, y] = (part[spot, y].astype(F32) + first[t].astype(F32)).astype(BF16)
+        to_chip(t).start()
+        return unused
+
+    lax.fori_loop(0, chips - 1, add_and_send, 0)
+    q_copies[0].wait_recv()
+    q_sum[...] = (q_part[1 - x, k].astype(F32) + q_first[1].astype(F32)).astype(BF16)
+    q_over = remote(q_sum, q_last, q_send.at[2], q_recv.at[2], x_mate)
+    q_over.start()
+
+    side.hand_on()
+    pieces_in(*group, att_cut, att_all, a_send, a_recv, att_started)
+    side.finish()
+    by_columns(gy_all, att_all, outw_terms)
+    outw.start()
+
+    q_copies[1].wait_recv()
+    q_over.wait_recv()
+    total = q_part[x, k].astype(F32) + q_first[0].astype(F32) + q_last[...].astype(F32)
+    blocks[...] = total.astype(BF16).reshape(blocks.shape)
+
+    def where(spot):
+        return {
+            "o": spot // (inner * ys),
+            "i": (spot // ys) % inner,
+            "y": spot % ys,
+        }
+
+    def each_sent(act):
+        for section in range(3):
+            for h in range(heads):
+                head = place * heads + h
+                block = section * HEADS + head
+                low = (block * HEAD_DIM) // share
+                high = (block * HEAD_DIM + HEAD_DIM - 1) // share
+                index = section * heads + h
+                for which, owner, needed in (
+                    (0, low, head < HEADS),
+                    (1, high, (head < HEADS) & (high != low)),
+                ):
+
+                    @pl.when(needed)
+                    def _(which=which, owner=owner, block=block, index=index):
+                        act(index, 2 * index + which, owner, block - (share * owner) // HEAD_DIM)
+
+    def block_copy(index, slot, owner, target):
+        return remote(
+            blocks.at[index], routed.at[target], hop.at[slot], land.at[target], where(owner)
+        )
+
+    def send_block(index, slot, owner, target):
+        @pl.when(owner != place)
+        def _():
+            block_copy(index, slot, owner, target).start()
+
+        @pl.when(owner == place)
+        def _():
+            routed[target] = blocks[index]
+
+    def sent_block(index, slot, owner, target):
+        @pl.when(owner != place)
+        def _():
+            block_copy(index, slot, owner, target).wait_send()
+
+    each_sent(send_block)
+
+    to_mate(0).wait_recv()
+    grad = part[chip(0)[0], y].astype(F32) + first[0].astype(F32)
+    for t in range(1, chips):
+        to_chip(t).wait_recv()
+        grad = grad + last[t - 1].astype(F32)
+    plain, scale = normed(own[...].astype(F32))
+    grad_inputs[...] = grad_middle[...] + norm_back(grad, gain[...], plain, scale)
+
+    def fill(base, values):
+        size = values.shape[1]
+        for n in range(-(-size // 128)):
+            low, high = n * 128, min(n * 128 + 128, size)
+            line[pl.ds(base + n, 1), 0 : high - low] = values[:, low:high]
+
+    q_rows, w_rows = -(-span // 128), -(-width // 128)
+    piece = hidden_sum.shape[1]
+    p_rows = -(-piece // 128)
+    value_base = spots * q_rows
+    rows_base = 2 * spots * q_rows
+    hidden_base = rows_base + 6 * w_rows
+    line[...] = jnp.zeros(line.shape, F32)
+    fill(place * q_rows, jnp.sum(dqkv[:, 0:span].astype(F32), axis=0, keepdims=True))
+    fill(
+        value_base + place * q_rows,
+        jnp.sum(dqkv[:, 2 * span : 3 * span].astype(F32), axis=0, keepdims=True),
+    )
+    for n in range(4):
+        fill(rows_base + n * w_rows, row_sums[n : n + 1, :])
+    fill(rows_base + 4 * w_rows, jnp.sum(grad * plain, axis=0, keepdims=True))
+    fill(rows_base + 5 * w_rows, jnp.sum(grad, axis=0, keepdims=True))
+    fill(hidden_base + (shard * inner + i) * p_rows, hidden_sum[...])
+    line_rows = line_came.shape[1]
+
+    def share_of(ref, device):
+        return ref.at[pl.ds(pl.multiple_of(device * line_rows, line_rows), line_rows)]
+
+    line_started = []
+    for t, off in enumerate(offs):
+        peer = moved(axes, sizes, off)
+        device = flat(peer, axes, sizes)
+        copy = remote(
+            share_of(line, device), line_came.at[t], l_send.at[t], l_recv.at[t], peer
+        )
+        copy.start()
+        line_started.append(copy)
+    shrink.over_o()
+    outw.over_o()
+    for copy in line_started:
+        copy.wait_recv()
+    mine = pl.ds(pl.multiple_of(me * line_rows, line_rows), line_rows)
+    line_out[mine, :] = line[mine, :] + jnp.sum(line_came[...], axis=0)
+    count = len(offs)
+    for t, off in enumerate(offs):
+        peer = moved(axes, sizes, off)
+        copy = remote(
+            share_of(line_out, me),
+            share_of(line_out, me),
+            l_send.at[count + t],
+            l_recv.at[count + t],
+            peer,
+        )
+        copy.start()
+        line_started.append(copy)
+    shrink.over_i()
+    outw.over_i()
+
+    base = (share * place) // HEAD_DIM
+    for slot in range(routed.shape[0]):
+        block = base + slot
+        owner = (block % HEADS) // heads
+
+        @pl.when((block * HEAD_DIM < share * (place + 1)) & (owner != place))
+        def _(slot=slot):
+            remote(
+                blocks.at[0], routed.at[slot], hop.at[0], land.at[slot], where(place)
+            ).wait_recv()
+
+    for t, off in enumerate(offs):
+        peer = moved(axes, sizes, off, -1)
+        block = share_of(line_out, flat(peer, axes, sizes))
+        remote(block, block, l_send.at[count + t], l_recv.at[count + t], peer).wait_recv()
+
+    def take(base, ref, row, start, size):
+        for n in range(-(-size // 128)):
+            low, high = n * 128, min(n * 128 + 128, size)
+            ref[row : row + 1, start + low : start + high] = line_out[
+                base + n : base + n + 1, 0 : high - low
+            ]
+
+    for c in range(spots):
+        take(c * q_rows, query_out, 0, c * span, span)
+        take(value_base + c * q_rows, value_out, 0, c * span, span)
+    for n in range(6):
+        take(rows_base + n * w_rows, rows_out, n, 0, width)
+    for n in range(xs * ks * inner):
+        take(hidden_base + n * p_rows, hidden_out, 0, n * piece, piece)
+    shrink.finish()
+    outw.finish()
+    each_sent(sent_block)
+    for copy in line_started + q_copies + [q_over]:
+        copy.wait_send()
+    for t in range(chips):
+        to_mate(t).wait_send()
+    for t in range(1, chips):
+        to_chip(t).wait_send()
+
+
+def final_part(
+    dqkv,
+    columns,
+    normed_low,
+    shrink_terms,
+    low_middle,
+    att,
+    own,
+    grad_middle,
+    gain,
+    row_sums,
+    hidden_sum,
+    axes,
+    sizes,
+    heads,
+    share,
+    ident,
+):
+    outer, inner, ys, xs, ks = sizes
+    spots, cell, piece = shrink_terms.shape
+    rows, width = own.shape
+    chips = outer * inner
+    devices = spots * xs * ks
+    group = inner * xs * ks
+    span = heads * HEAD_DIM
+    part_rows = width // (xs * ks)
+    slots = max(
+        (share * (c + 1) - 1) // HEAD_DIM - (share * c) // HEAD_DIM + 1 for c in range(spots)
+    )
+    line_rows = (
+        2 * spots * -(-span // 128) + 6 * -(-width // 128) + xs * ks * inner * -(-piece // 128)
+    )
+    line_rows = 8 * -(-line_rows // (8 * devices))
+    block = (rows, width)
+    q_block = (3 * span, part_rows)
+    out_rows = width // group
+    return pl.pallas_call(
+        functools.partial(final_kernel, axes, sizes, heads, share),
+        out_shape=[
+            jax.ShapeDtypeStruct(block, F32),
+            jax.ShapeDtypeStruct((slots, HEAD_DIM, part_rows), BF16),
+            jax.ShapeDtypeStruct((inner, cell, piece), BF16),
+            jax.ShapeDtypeStruct((inner, cell, out_rows), BF16),
+            jax.ShapeDtypeStruct((1, spots * span), F32),
+            jax.ShapeDtypeStruct((1, spots * span), F32),
+            jax.ShapeDtypeStruct((6, width), F32),
+            jax.ShapeDtypeStruct((1, group * piece), F32),
+        ],
+        in_specs=[VMEM] * 2 + [ANY] + [VMEM] * 8,
+        out_specs=[VMEM] * 8,
+        scratch_shapes=[
+            pltpu.VMEM((chips, ys) + block, BF16),
+            pltpu.VMEM((chips,) + block, BF16),
+            pltpu.VMEM((chips - 1,) + block, BF16),
+            pltpu.VMEM((min(1024, dqkv.shape[0]), width), BF16),
+            pltpu.VMEM((xs, ks) + q_block, BF16),
+            pltpu.VMEM((2,) + q_block, BF16),
+            pltpu.VMEM(q_block, BF16),
+            pltpu.VMEM(q_block, BF16),
+            pltpu.VMEM((3 * heads, HEAD_DIM, part_rows), BF16),
+            pltpu.VMEM((inner * xs, ks) + block, BF16),
+            pltpu.VMEM((group, rows, out_rows), BF16),
+            pltpu.VMEM((group, rows, out_rows), BF16),
+            pltpu.VMEM((spots, cell, out_rows), BF16),
+            pltpu.VMEM((devices * line_rows, 128), F32),
+            pltpu.VMEM((devices - 1, line_rows, 128), F32),
+            pltpu.VMEM((devices * line_rows, 128), F32),
+            pltpu.SemaphoreType.DMA((2 * chips,)),
+            pltpu.SemaphoreType.DMA((2 * chips,)),
+            pltpu.SemaphoreType.DMA((3,)),
+            pltpu.SemaphoreType.DMA((3,)),
+            pltpu.SemaphoreType.DMA((6 * heads,)),
+            pltpu.SemaphoreType.DMA((slots,)),
+            pltpu.SemaphoreType.DMA((group,)),
+            pltpu.SemaphoreType.DMA((group,)),
+            pltpu.SemaphoreType.DMA((2 * devices,)),
+            pltpu.SemaphoreType.DMA((2 * devices,)),
+            *gather_scratch((("i", "x"), (inner, xs), "k")),
+            pltpu.SemaphoreType.DMA,
+            *owned_scratch(outer, cell, piece),
+            *owned_scratch(outer, cell, out_rows),
+        ],
+        name="final%d" % ident,
+        compiler_params=pltpu.CompilerParams(
+            collective_id=ident, has_side_effects=True, vmem_limit_bytes=67_000_000
+        ),
+        cost_estimate=pl.CostEstimate(
+            flops=12 * rows * spots * width * span,
+            bytes_accessed=100 * rows * width * 2,
+            transcendentals=0,
+        ),
+    )(
+        dqkv,
+        columns,
+        normed_low,
+        shrink_terms,
+        low_middle,
+        att,
+        own,
+        grad_middle,
+        gain,
+        row_sums,
+        hidden_sum,
+    )
+
+
 def nt(left, right):
     return lax.dot_general(left, right, (((1,), (1,)), ((), ())), preferred_element_type=F32)
 
 
 def nn(left, right):
     return lax.dot_general(left, right, (((1,), (0,)), ((), ())), preferred_element_type=F32)
+
+
+def tn(left, right):
+    return lax.dot_general(left, right, (((0,), (0,)), ((), ())), preferred_element_type=F32)
 
 
 def rows_of(inv, ref, pair, low, high):
@@ -1188,24 +1450,8 @@
     return centred * lax.rsqrt(spread + EPSILON) * gain + shift
 
 
-def smooth_gelu(values):
-    return (
-        0.5
-        * values
-        * (1.0 + jnp.tanh(0.7978845608028654 * (values + 0.044715 * values * values * values)))
-    )
-
-
 def matmul(left, right):
     return jnp.dot(left, right, preferred_element_type=F32)
-
-
-def against(left, weight):
-    return lax.dot_general(left, weight, (((1,), (1,)), ((), ())), preferred_element_type=F32)
-
-
-def onto(left, right):
-    return lax.dot_general(left, right, (((0,), (0,)), ((), ())), preferred_element_type=F32)
 
 
 def body(
@@ -1261,20 +1507,6 @@
     sequence = gathered.reshape(spots * rows, width)
     qkv_columns = qkv_columns.reshape(width, 3 * span)
 
-    def doubled(values, axis_name):
-        came = lax.ppermute(values, axis_name, [(0, 1), (1, 0)])
-        return jnp.where(
-            lax.axis_index(axis_name) == 0, jnp.stack([values, came]), jnp.stack([came, values])
-        )
-
-    def over_group(values):
-        near = doubled(values, "x")
-        near = doubled(near, "i")
-        far = lax.ppermute(near, "k", [(0, 1), (1, 0)])
-        first = lax.axis_index("k") == 0
-        both = jnp.stack([jnp.where(first, near, far), jnp.where(first, far, near)], axis=2)
-        return both.reshape(-1, width)
-
     sequence, out_own = lax.optimization_barrier((sequence, out_weight))
     out_far = lax.ppermute(out_own, "x", [(0, 1), (1, 0)])
     expand_own_bias = lax.dynamic_slice_in_dim(
@@ -1309,31 +1541,17 @@
             total = total + lax.ppermute(pieces[step], axis_name, ring).astype(F32)
         return total.astype(BF16)
 
-    cell = width // spots
     cuts = spots // (2 * shards)
-
-    def cut_columns(left, right):
-        local = onto(left, right).astype(BF16)
-        return cut(local.reshape(outer, inner, ys, cell, right.shape[1]), "y", 2)
-
-    def owned(local):
-        kept, sent = cut(local, "i", 0)
-        came = lax.ppermute(sent, "i", [(0, 1), (1, 0)])
-        local = jnp.where(i == 0, jnp.stack([kept, came]), jnp.stack([came, kept]))
-        return local.transpose(0, 2, 1).reshape(-1, cell).astype(F32)
-
     (
         attended_low,
-        group_low,
-        group_grad,
-        hidden_low,
-        expanded_low,
         result,
         grad_middle,
         middle_low,
         row_sums,
         hidden_sums,
         grad_heads,
+        expand_half,
+        shrink_terms,
     ) = middle_part(
         attended_bf.reshape(spots, rows, span),
         own,
@@ -1350,43 +1568,10 @@
         group,
         1,
     )
-    group_low, group_grad = group_low.reshape(-1, width), group_grad.reshape(-1, width)
-    hidden_low, expanded_low = hidden_low.reshape(-1, piece), expanded_low.reshape(-1, piece)
-    inputs = own.astype(F32)
     grad_heads = grad_heads.reshape(spots * rows, span)
-    shrink_cut = cut_columns(group_grad, hidden_low)
-    expand_cut = onto(group_low, expanded_low).astype(BF16)
-    expand_cut = expand_cut.reshape(shards, part, cuts, piece // cuts).transpose(0, 2, 1, 3)
-    expand_cut = cut(expand_cut.reshape(outer, ys, part, piece // cuts), "y", 1)
-    grad_heads, shrink_cut, expand_cut = lax.optimization_barrier(
-        (grad_heads, shrink_cut, expand_cut)
-    )
-
     dqkv = attend_back(inv, qkv, grad_heads, attended, log_sum, heads)
-    shrink_half, expand_half = added(shrink_cut, "y"), added(expand_cut, "y")
-    shrink_cut, expand_cut = cut(shrink_half, "o", 0), cut(expand_half, "o", 0)
-    dqkv, shrink_cut, expand_cut = lax.optimization_barrier((dqkv, shrink_cut, expand_cut))
-    norm_partial = against(dqkv, qkv_columns).astype(BF16)
-    qkv_partial = onto(normed_low, dqkv).astype(BF16)
-    shrink_whole, expand_whole = added(shrink_cut, "o"), added(expand_cut, "o")
-    middle_group, att_group = side_gather(
-        middle_low, attended_low, group, ("i", "x", "k"), (inner, xs, ks), 4
-    )
-    middle_group = middle_group.reshape(-1, width)
-    outw_cut = cut_columns(middle_group, att_group.reshape(middle_group.shape[0], -1))
-    grad_normed_one, qkv_cells = scatter(
-        [
-            norm_partial.reshape(outer * inner, ys, rows, width),
-            qkv_partial.reshape(xs, ks, part, 3 * span),
-        ],
-        [ctx, pair],
-        5,
-    )
-    unused, first_back = jax.vjp(layer_norm, inputs, first_gain, first_shift)
-    grad_first_input, grad_first_gain, grad_first_shift = first_back(grad_normed_one)
-    grad_inputs = grad_middle + grad_first_input
-
-    grad_shrink = owned(shrink_whole)
+    expand_whole = added(cut(expand_half, "o", 0), "o")
+    dqkv, expand_whole = lax.optimization_barrier((dqkv, expand_whole))
     axes = ("o", "i", "y", "x", "k")
     routes = []
     for so, si, sy, sf in itertools.product(*map(range, (outer, inner, ys, shards))):
@@ -1394,54 +1579,56 @@
         spot = sf * (spots // shards) + si * cuts + index % cuts
         routes.append((((so * inner + si) * ys + sy) * shards + sf, spot * shards + index // cuts))
     grad_expand = lax.ppermute(expand_whole, axes, routes).astype(F32)
-    grad_outw = owned(added(cut(added(outw_cut, "y"), "o", 0), "o"))
-
-    def placed(values, start, size):
-        return lax.dynamic_update_slice_in_dim(jnp.zeros((size,), F32), values, start, axis=0)
-
-    dqkv_sums = jnp.sum(dqkv.astype(F32), axis=0)
-    small = [
-        placed(dqkv_sums[:span], place * span, padded),
-        placed(dqkv_sums[2 * span :], place * span, padded),
-        row_sums[0],
-        placed(
-            hidden_sums[0], (shard * inner + i) * piece, hidden
-        ),
-        row_sums[1],
-        grad_first_gain,
-        grad_first_shift,
-        row_sums[2],
-        row_sums[3],
-    ]
-    lengths = [s.shape[0] for s in small]
-    devices = spots * shards
-    lanes = 128 * (-(-sum(lengths) // (devices * 1024)))
-    line = jnp.concatenate(small)
-    line = jnp.pad(line, (0, devices * 8 * lanes - line.shape[0])).reshape(devices, 8, lanes)
     share = 3 * width // spots
-    qkv_blocks = qkv_cells.astype(BF16).T.reshape(3 * heads, HEAD_DIM, part)
-    line, routed = last_exchange(
-        line, qkv_blocks, axes, (outer, inner, ys, xs, ks), spots, heads, share, 6
+    (
+        grad_inputs,
+        routed,
+        shrink_cells,
+        outw_cells,
+        query_sums,
+        value_sums,
+        row_totals,
+        hidden_totals,
+    ) = final_part(
+        dqkv,
+        qkv_columns,
+        normed_low,
+        shrink_terms,
+        middle_low,
+        attended_low,
+        own,
+        grad_middle,
+        first_gain[None],
+        row_sums,
+        hidden_sums,
+        axes,
+        (outer, inner, ys, xs, ks),
+        heads,
+        share,
+        2,
     )
-    line = line.reshape(-1)
+
+    def upright(cells):
+        return cells.transpose(0, 2, 1).reshape(-1, cells.shape[1]).astype(F32)
+
     start = share * place - HEAD_DIM * ((share * place) // HEAD_DIM)
     grad_qkv = lax.dynamic_slice_in_dim(routed.reshape(-1, part), start, share, axis=0)
-    grad_qkv = grad_qkv.T.astype(F32)
-    summed = []
-    start = 0
-    for length in lengths:
-        summed.append(line[start : start + length])
-        start += length
-    summed[0] = summed[0][:width]
-    summed[1] = summed[1][:width]
     return (
         result[None],
         grad_inputs[None],
-        grad_qkv,
-        grad_outw,
+        grad_qkv.T.astype(F32),
+        upright(outw_cells),
         grad_expand,
-        grad_shrink,
-        *summed,
+        upright(shrink_cells),
+        query_sums[0, :width],
+        value_sums[0, :width],
+        row_totals[0],
+        hidden_totals[0],
+        row_totals[1],
+        row_totals[4],
+        row_totals[5],
+        row_totals[2],
+        row_totals[3],
     )
 
 

time: 551 us -> 432 us (0.78)
  the two profiles are of different devices: /device:TPU:23 before, /device:TPU:3 now
where the time goes in v5:
time: 432 us; the launch traced here: 428 us
  Pallas kernels  342 us (79%)
  waiting for transfers between devices  32.4 us (8%)
  local copies, waits for them, and re-layouts  20.9 us (5%)
  other arithmetic  14.1 us (3%)
  starting transfers between devices  10.8 us (2%)
  matrix products  6.93 us (2%)
    pallas_call x1, Pallas kernels, final_part(): pl.pallas_call(functools.partial(final_kernel, axes, sizes, heads, share)...  135 us
    pallas_call x1, Pallas kernels, middle_part(): pl.pallas_call(functools.partial(middle_kernel, every, spec), out_shape=[...  111 us
    pallas_call x1, Pallas kernels, first_gather(): pl.pallas_call(functools.partial(first_kernel, specs, shard_sizes, *every...  52.3 us
    ppermute x1, waiting for transfers between devices, body(): grad_expand = lax.ppermute(expand_whole, axes, routes).astype(F32)  27.2 us
    pallas_call x1, Pallas kernels, attend_back(): pl.pallas_call(functools.partial(attend_back_kernel, heads, block), out_s...  23.4 us
    pallas_call x1, Pallas kernels, attend(): pl.pallas_call(functools.partial(attend_kernel, heads, block), out_shape=...  20 us
  transfers between devices with their start and end apart: 3, of which 2 were waited for; matrix products, arithmetic and copies ran while one was open for 8% of the time, Pallas kernels for 10%

profile of v5, /device:TPU:3, one launch (start us, length us, event | category | flops | bytes accessed | tf_op | source)
XLA Modules:
  0.0 428.2 jit_solution(8221961887046834830)
XLA Ops:
  0.6 2.0 copy.43
  2.6 52.3 %first0.1 = (bf16[4,2,128,1600]{3,2,1,0:T(8,128)(2,1)}, bf16[2,2,400,768]{3,2,1,0:T(8,128)(2,1)}, bf16[4,400,800]{2,1,0:T(8,128)(2,1)}) custom-call(bf16[128,1600]{1,0:T(8,128)(2,1)} %bitcast.31, bf16[400,4800]{1,0:T(8,128)(2,1)} %qkv_weight.1, bf16[400,6400]{1,0:T(8,128)(2,1)} %weight.1), custom_call_target="tpu_custom_call" | custom-call | bytes 82944000 | tf_op jit(solution)/shard_map/first0/pallas_call | solution.py:228
  54.9 1.1 collective-permute-start
  56.0 0.0 copy-start.2
  56.0 0.0 copy-start.5
  56.0 2.5 convert_reduce_fusion
  58.6 1.0 fusion.2
  59.6 0.0 copy-start.8
  59.7 0.0 copy-start.9
  59.7 0.0 copy-start.10
  59.7 0.0 copy-start.11
  59.7 0.0 copy-start.14
  59.7 2.8 fusion.5.normed_low
  62.5 0.8 dynamic_slice.21
  63.3 0.6 broadcast_in_dim.50.expand_bias
  63.9 2.0 copy.44
  65.8 0.6 broadcast_in_dim.49.out_bias
  66.4 0.6 broadcast_in_dim.51.shrink_bias
  67.0 0.6 broadcast_in_dim.52.gain
  67.6 0.6 broadcast_in_dim.53.shift
  68.3 0.6 select_reduce_fusion.inv
  68.9 6.9 %add_convert_fusion.qkv = bf16[1024,768]{1,0:T(8,128)(2,1)} fusion(bf16[1024,1600]{1,0:T(8,128)(2,1)} %fusion.5.normed_low, bf16[1600,768]{1,0:T(8,128)(2,1)} %bitcast.41, f32[768]{0:T(1024)S(1)} %pad_maximum_fusion), kind=kOutput, calls=%fused_computation.8 | convolution fusion | flops 2518155264 | bytes 7310336 | tf_op jit(solution)/shard_map/dot_general | solution.py:1454
  75.8 20.0 %attend.1 = (f32[1024,256]{1,0:T(8,128)}, bf16[1024,256]{1,0:T(8,128)(2,1)}, f32[4,1024]{1,0:T(4,128)}) custom-call(s32[16]{0:T(128)} %select_reduce_fusion.inv, bf16[1024,768]{1,0:T(8,128)(2,1)} %add_convert_fusion.qkv), custom_call_target="tpu_custom_call" | custom-call | flops 2684354560 | bytes 2621440 | tf_op jit(solution)/shard_map/attend/pallas_call | solution.py:1302
  95.8 111.2 %middle1.1 = (bf16[128,1600]{1,0:T(8,128)(2,1)}, bf16[128,1600]{1,0:T(8,128)(2,1)}, f32[128,1600]{1,0:T(8,128)}, bf16[128,1600]{1,0:T(8,128)(2,1)}, f32[4,1600]{...) custom-call(bf16[8,128,256]{2,1,0:T(8,128)(2,1)} %bitcast.45, ...), custom_call_target="tpu_custom_call" | custom-call | flops 10485760000 | bytes 40960000 | tf_op jit(solution)/shard_map/middle1/pallas_call | solution.py:623
  207.0 1.2 dynamic-slice_bitcast_fusion
  208.2 3.0 collective-permute-start.1
  211.2 0.6 broadcast_in_dim.55.gain
  211.8 1.9 copy.48
  213.7 23.4 %attend_back.1.dqkv = bf16[1024,768]{1,0:T(8,128)(2,1)} custom-call(s32[16]{0:T(128)} %select_reduce_fusion.inv, bf16[1024,768]{1,0:T(8,128)(2,1)} %add_convert_fusion.qkv, bf16[1024,256]{1,0:T(8,128)(2,1)} %bitcast.44, f32[1024,256]{1,0:T(8,128)} %get-tuple-element.50.outs, f32[4,1024]{1,0:T(4,128)} %get-tuple-element.51.lse), custom_call_target="tpu_custom_call" | custom-call | flops 6710886400 | bytes 5242880 | tf_op jit(solution)/shard_map/attend_back/pallas_call | solution.py:1412
  237.1 5.2 %collective-permute-done.1 = bf16[400,800]{1,0:T(8,128)(2,1)S(1)} collective-permute-done((bf16[400,800]{1,0:T(8,128)(2,1)S(1)}, bf16[400,800]{1,0:T(8,128)(2,1)S(1)}, u32[]{:S(2)}, u32[]{:S(2)}) %collective-permute-start.1) | collective-permute-done | bytes 640032 | tf_op jit(solution)/shard_map/ppermute | solution.py:1541
  242.3 1.0 fusion.6
  243.4 135.0 %final2.1 = (f32[128,1600]{1,0:T(8,128)}, bf16[11,64,400]{2,1,0:T(8,128)(2,1)}, bf16[2,200,800]{2,1,0:T(8,128)(2,1)}, bf16[2,200,200]{2,1,0:T(8,128)(2,1)}, f32[...) custom-call(bf16[1024,768]{1,0:T(8,128)(2,1)} %attend_back.1.dqkv, ...), custom_call_target="tpu_custom_call" | custom-call | flops 5033164800 | bytes 40960000 | tf_op jit(solution)/shard_map/final2/pallas_call | solution.py:1121
  378.4 1.2 convert_bitcast_fusion
  379.6 1.0 convert_bitcast_fusion.2
  380.6 6.8 %collective-permute-start.2 = (bf16[400,800]{1,0:T(8,128)(2,1)}, bf16[400,800]{1,0:T(8,128)(2,1)}, u32[]{:S(2)}, u32[]{:S(2)}) collective-permute-start(bf16[400,800]{1,0:T(8,128)(2,1)} %fusion.6), channel_id=1, source_target_pairs={{0,0},{1,8},{2,16},{3,24},{4,1},{5,9},{6,17},{7,25},{8,4},{9,12},{... | collective-permute-start | bytes 1920008 | tf_op jit(solution)/shard_map/ppermute | solution.py:1581
  387.3 1.1 constant_dynamic-slice_fusion
  388.5 0.7 copy.47
  389.3 2.0 reshape.84
  391.3 0.3 copy.50
  391.6 0.9 copy.46
  392.5 2.3 copy.49
  394.8 0.7 reduce.3
  395.5 0.6 slice_reduce_fusion.6
  396.1 0.6 slice_reduce_fusion.7
  396.7 0.7 slice_reduce_fusion
  397.5 1.0 convert_bitcast_fusion.1
  398.5 27.2 %collective-permute-done.2 = bf16[400,800]{1,0:T(8,128)(2,1)} collective-permute-done((bf16[400,800]{1,0:T(8,128)(2,1)}, bf16[400,800]{1,0:T(8,128)(2,1)}, u32[]{:S(2)}, u32[]{:S(2)}) %collective-permute-start.2) | collective-permute-done | bytes 640032 | tf_op jit(solution)/shard_map/ppermute | solution.py:1581
  425.7 2.3 convert_element_type.63
  (31 shorter events, 0.1 us)
Async XLA Ops:
  2.6 53.4 %copy-start.6 = (f32[1600]{0:T(1024)S(1)}, f32[1600]{0:T(1024)}, u32[]{:S(2)}) copy-start(f32[1600]{0:T(1024)} %param.19) | copy-start | bytes 19204
  2.6 53.4 %copy-start.7 = (f32[1600]{0:T(1024)S(1)}, f32[1600]{0:T(1024)}, u32[]{:S(2)}) copy-start(f32[1600]{0:T(1024)} %param.20) | copy-start | bytes 19204
  54.9 3.7 copy-start
  54.9 40.9 %collective-permute-start = (bf16[400,1600]{1,0:T(8,128)(2,1)}, bf16[400,1600]{1,0:T(8,128)(2,1)}, u32[]{:S(2)}, u32[]{:S(2)}) collective-permute-start(bf16[400,1600]{1,0:T(8,128)(2,1)} %out_own), channel_id=1, source_target_pairs={{0,2},{2,0},{1,3},{3,1},{4,6},{6,4},{5,7},{7,5},{8,10},{10,8},{9,1... | collective-permute-start | bytes 3840008 | tf_op jit(solution)/shard_map/ppermute | solution.py:1511
  56.0 3.6 copy-start.2
  56.0 3.6 copy-start.5
  59.6 6.2 %copy-start.8 = (f32[1600]{0:T(1024)S(1)}, f32[1600]{0:T(1024)}, u32[]{:S(2)}) copy-start(f32[1600]{0:T(1024)} %param.22) | copy-start | bytes 19204
  59.7 6.8 %copy-start.9 = (f32[1600]{0:T(1024)S(1)}, f32[1600]{0:T(1024)}, u32[]{:S(2)}) copy-start(f32[1600]{0:T(1024)} %param.26) | copy-start | bytes 19204
  59.7 7.4 %copy-start.10 = (f32[1600]{0:T(1024)S(1)}, f32[1600]{0:T(1024)}, u32[]{:S(2)}) copy-start(f32[1600]{0:T(1024)} %param.29) | copy-start | bytes 19204
  59.7 8.0 %copy-start.11 = (f32[1600]{0:T(1024)S(1)}, f32[1600]{0:T(1024)}, u32[]{:S(2)}) copy-start(f32[1600]{0:T(1024)} %param.30) | copy-start | bytes 19204
  59.7 8.6 %copy-start.14 = (s32[1,16]{1,0:T(1,128)S(1)}, s32[1,16]{1,0:T(1,128)}, u32[]{:S(2)}) copy-start(s32[1,16]{1,0:T(1,128)} %param.17) | copy-start | bytes 196
  208.2 34.1 %collective-permute-start.1 = (bf16[400,800]{1,0:T(8,128)(2,1)S(1)}, bf16[400,800]{1,0:T(8,128)(2,1)S(1)}, u32[]{:S(2)}, u32[]{:S(2)}) collective-permute-start(bf16[400,800]{1,0:T(8,128)(2,1)S(1)} %dynamic-slice_bitcast_fusion), channel_id=1, source_target_pairs={{0,16},{16,0},{1,17},{17,1},{2,18},{18,2},{3,19},{19,3},{4,20},{20... | collective-permute-start | bytes 1920008 | tf_op jit(solution)/shard_map/ppermute | solution.py:1541
  213.7 28.6 %copy-start.1 = (bf16[2,400,800]{2,1,0:T(8,128)(2,1)S(1)}, bf16[2,400,800]{2,1,0:T(8,128)(2,1)}, u32[]{:S(2)}) copy-start(bf16[2,400,800]{2,1,0:T(8,128)(2,1)} %get-tuple-element.52) | copy-start | bytes 3840004
  380.6 45.2 %collective-permute-start.2 = (bf16[400,800]{1,0:T(8,128)(2,1)}, bf16[400,800]{1,0:T(8,128)(2,1)}, u32[]{:S(2)}, u32[]{:S(2)}) collective-permute-start(bf16[400,800]{1,0:T(8,128)(2,1)} %fusion.6), channel_id=1, source_target_pairs={{0,0},{1,8},{2,16},{3,24},{4,1},{5,9},{6,17},{7,25},{8,4},{9,12},{... | collective-permute-start | bytes 1920008 | tf_op jit(solution)/shard_map/ppermute | solution.py:1581
  389.2 5.6 %copy-start.4 = (f32[1,6400]{1,0:T(1,128)S(1)}, f32[1,6400]{1,0:T(1,128)}, u32[]{:S(2)}) copy-start(f32[1,6400]{1,0:T(1,128)} %get-tuple-element.68) | copy-start | bytes 76804
  389.2 6.3 %copy-start.13 = (f32[1,2048]{1,0:T(1,128)S(1)}, f32[1,2048]{1,0:T(1,128)}, u32[]{:S(2)}) copy-start(f32[1,2048]{1,0:T(1,128)} %get-tuple-element.66) | copy-start | bytes 24580
  389.2 6.9 %copy-start.12 = (f32[1,2048]{1,0:T(1,128)S(1)}, f32[1,2048]{1,0:T(1,128)}, u32[]{:S(2)}) copy-start(f32[1,2048]{1,0:T(1,128)} %get-tuple-element.65) | copy-start | bytes 24580
  389.2 7.5 %copy-start.3 = (f32[6,1600]{1,0:T(8,128)S(1)}, f32[6,1600]{1,0:T(8,128)}, u32[]{:S(2)}) copy-start(f32[6,1600]{1,0:T(8,128)} %get-tuple-element.67) | copy-start | bytes 115204

commit v6 on v5

--- a/solution.py
+++ b/solution.py
@@ -132,37 +132,115 @@
     return pl.CostEstimate(flops=0, bytes_accessed=20 * size, transcendentals=0)
 
 
+class Line:
+    def __init__(self, sizes, source, out, send, recv, local):
+        self.outer, self.inner = sizes
+        self.count = self.outer * self.inner
+        self.at = lax.axis_index("o") * self.inner + lax.axis_index("i")
+        self.y = lax.axis_index("y")
+        self.mate = {"y": 1 - self.y}
+        self.source, self.out, self.send, self.recv, self.local = source, out, send, recv, local
+
+    def spot(self, at):
+        return {"o": at // self.inner, "i": at % self.inner}
+
+    def copies(self, at, here):
+        block = self.out.at[at, self.y]
+        source = self.source if here else block
+        right, left = lax.rem(self.at + 1, self.count), lax.rem(
+            self.at + self.count - 1, self.count
+        )
+        return [
+            (
+                (at <= self.at) & (self.at + 1 < self.count),
+                remote(source, block, self.send.at[0, at], self.recv.at[0, at], self.spot(right)),
+            ),
+            (
+                (at >= self.at) & (self.at > 0),
+                remote(source, block, self.send.at[1, at], self.recv.at[0, at], self.spot(left)),
+            ),
+            (True, remote(source, block, self.send.at[2, at], self.recv.at[1, at], self.mate)),
+        ]
+
+    def each(self, at, here, act):
+        for needed, copy in self.copies(at, here):
+            if needed is True:
+                act(copy)
+            else:
+
+                @pl.when(needed)
+                def _(copy=copy):
+                    act(copy)
+
+    def start(self):
+        pltpu.make_async_copy(
+            self.source, self.out.at[self.at, self.y], self.local
+        ).start()
+        self.each(self.at, True, lambda copy: copy.start())
+
+    def arrive(self, at):
+        block = self.out.at[at, self.y]
+        remote(self.source, block, self.send.at[0, at], self.recv.at[0, at], self.mate).wait_recv()
+        self.each(at, False, lambda copy: copy.start())
+
+    def across(self, at):
+        block = self.out.at[at, 1 - self.y]
+        remote(self.source, block, self.send.at[2, at], self.recv.at[1, at], self.mate).wait_recv()
+
+    def finish(self):
+        for at in range(self.count):
+            self.each(at, False, lambda copy: copy.wait_send())
+
+
 def first_kernel(
-    specs,
-    shard_sizes,
-    ctx_axes,
-    ctx_sizes,
+    sizes,
     own,
     qkv_weight,
     weight,
-    all_tokens,
+    gain,
+    shift,
+    bias,
+    qkv,
+    normed_out,
     all_columns,
     pieces,
+    sequence,
     qkv_whole,
     columns,
+    columns_in,
     whole,
     cut,
-    *sems,
+    send,
+    recv,
+    local,
+    head_send,
+    head_recv,
+    head_local,
+    read,
+    qkv_read,
+    cut_send,
+    cut_recv,
+    cut_local,
 ):
-    axes = ("x", "k")
+    outer, inner, ys, xs, ks = sizes
+    axes, shard_sizes = ("x", "k"), (xs, ks)
     offs = offsets(shard_sizes)
-    tokens = Gather(*specs[0], own, all_tokens, *sems[0:3])
-    heads = Gather(*specs[1], columns, all_columns, *sems[3:6])
-    read, qkv_read, send, recv, local = sems[6:11]
+    line = Line((outer, inner), own, sequence, send, recv, local)
+    heads = Gather(
+        ("x",), (xs,), "k", columns, all_columns, head_send, head_recv, head_local
+    )
     qkv_fetch = pltpu.make_async_copy(qkv_weight, qkv_whole, qkv_read)
     qkv_fetch.start()
     fetch = pltpu.make_async_copy(weight, whole, read)
     fetch.start()
-    greet(tokens.peers() + heads.peers() + [moved(axes, shard_sizes, o) for o in offs])
-    tokens.start()
+    peers = [moved(axes, shard_sizes, o) for o in offs] + [
+        moved(("o", "i", "y"), (outer, inner, ys), o) for o in offsets((outer, inner, ys))
+    ]
+    greet(peers)
+    line.start()
     qkv_fetch.wait()
-    place = flat(own_place(ctx_axes), ctx_axes, ctx_sizes)
-    rows, span = columns.shape[0], columns.shape[1] // 3
+    place = line.at * ys + line.y
+    part, span = columns.shape[0], columns.shape[1] // 3
     width = qkv_whole.shape[1] // 3
     for spot in range(-(-width // span)):
 
@@ -173,7 +251,7 @@
                 low = section * width + spot * span
                 if size < span:
                     columns[:, section * span : (section + 1) * span] = jnp.zeros(
-                        (rows, span), BF16
+                        (part, span), BF16
                     )
                 columns[:, section * span : section * span + size] = qkv_whole[:, low : low + size]
 
@@ -183,60 +261,107 @@
 
     heads.start()
     fetch.wait()
-    width = cut.shape[2]
-    inner = lax.axis_index("i")
+    cut_width = cut.shape[2]
+    side = lax.axis_index("i")
     for half in range(2):
 
-        @pl.when(inner == half)
+        @pl.when(side == half)
         def _():
             for f in range(cut.shape[0]):
-                low = (2 * f + half) * width
-                cut[f] = whole[:, low : low + width]
+                low = (2 * f + half) * cut_width
+                cut[f] = whole[:, low : low + cut_width]
 
     me = flat(own_place(axes), axes, shard_sizes)
-    here = pltpu.make_async_copy(cut.at[me], pieces.at[me], local)
+    here = pltpu.make_async_copy(cut.at[me], pieces.at[me], cut_local)
     here.start()
     started = []
     for t, off in enumerate(offs):
         peer = moved(axes, shard_sizes, off)
         there = flat(peer, axes, shard_sizes)
-        copy = remote(cut.at[there], pieces.at[me], send.at[t], recv.at[t], peer)
+        copy = remote(cut.at[there], pieces.at[me], cut_send.at[t], cut_recv.at[t], peer)
         copy.start()
         started.append(copy)
-    heads.hand_on()
-    tokens.hand_on()
+    pltpu.make_async_copy(own, sequence.at[line.at, line.y], local).wait()
+    for distance in range(1, line.count):
+        for sign in (-1, 1):
+            at = line.at + sign * distance
+
+            @pl.when((at >= 0) & (at < line.count))
+            def _(at=at):
+                line.arrive(at)
+
+        if distance == 1:
+            heads.hand_on()
+
+    heads.finish()
+    load = pltpu.make_async_copy(all_columns, columns_in, qkv_read)
+    load.start()
+    load.wait()
+    rows = own.shape[0]
+
+    def project(at):
+        values = sequence[at].reshape(ys * rows, width).astype(F32)
+        plain, unused_scale = normed(values)
+        low = (plain * gain[...] + shift[...]).astype(BF16)
+        start = pl.multiple_of(at * ys * rows, ys * rows)
+        normed_out[pl.ds(start, ys * rows), :] = low
+        weights = columns_in[...].reshape(width, 3 * span)
+        qkv[pl.ds(start, ys * rows), :] = (
+            jnp.dot(low, weights, preferred_element_type=F32) + bias[...]
+        ).astype(BF16)
+
+    nearest = [sorted(range(line.count), key=lambda q: abs(q - p)) for p in range(line.count)]
+
+    def step(n, unused):
+        at = line.at
+        for p in range(line.count):
+            for m in range(1, line.count):
+                at = jnp.where((line.at == p) & (n == m), nearest[p][m], at)
+        line.across(at)
+        project(at)
+        return unused
+
+    lax.fori_loop(0, line.count, step, 0)
     here.wait()
     for t, off in enumerate(offs):
         peer = moved(axes, shard_sizes, off, -1)
         came = flat(peer, axes, shard_sizes)
-        remote(cut.at[came], pieces.at[came], send.at[t], recv.at[t], peer).wait_recv()
+        remote(cut.at[came], pieces.at[came], cut_send.at[t], cut_recv.at[t], peer).wait_recv()
     for copy in started:
         copy.wait_send()
-    heads.finish()
-    tokens.finish()
-
-
-def first_gather(own, qkv_weight, weight, span, specs, shard_sizes, every, piece, ident):
-    shards = shard_sizes[0] * shard_sizes[1]
+    line.finish()
+
+
+def first_part(own, qkv_weight, weight, vectors, span, sizes, piece, ident):
+    outer, inner, ys, xs, ks = sizes
+    shards, chips = xs * ks, outer * inner
     part = weight.shape[0]
+    rows, width = own.shape
+    tokens = chips * ys * rows
     columns = jax.ShapeDtypeStruct((part, 3 * span), BF16)
-    shapes = [
-        gather_shape(own, specs[0]),
-        gather_shape(columns, specs[1]),
-        jax.ShapeDtypeStruct((shards, part, piece), BF16),
-    ]
+    spec = (("x",), (xs,), "k")
+    gathered = gather_shape(columns, spec)
     return pl.pallas_call(
-        functools.partial(first_kernel, specs, shard_sizes, *every),
-        out_shape=shapes,
-        in_specs=[VMEM, ANY, ANY],
-        out_specs=[ANY] * 3,
+        functools.partial(first_kernel, sizes),
+        out_shape=[
+            jax.ShapeDtypeStruct((tokens, 3 * span), BF16),
+            jax.ShapeDtypeStruct((tokens, width), BF16),
+            gathered,
+            jax.ShapeDtypeStruct((shards, part, piece), BF16),
+        ],
+        in_specs=[VMEM, ANY, ANY, VMEM, VMEM, VMEM],
+        out_specs=[VMEM, VMEM, ANY, ANY],
         scratch_shapes=[
+            pltpu.VMEM((chips, ys, rows, width), BF16),
             pltpu.VMEM(qkv_weight.shape, BF16),
             pltpu.VMEM(columns.shape, BF16),
+            pltpu.VMEM(gathered.shape, BF16),
             pltpu.VMEM(weight.shape, BF16),
             pltpu.VMEM((shards, part, piece), BF16),
-            *gather_scratch(specs[0]),
-            *gather_scratch(specs[1]),
+            pltpu.SemaphoreType.DMA((3, chips)),
+            pltpu.SemaphoreType.DMA((2, chips)),
+            pltpu.SemaphoreType.DMA,
+            *gather_scratch(spec),
             pltpu.SemaphoreType.DMA,
             pltpu.SemaphoreType.DMA,
             pltpu.SemaphoreType.DMA((shards,)),
@@ -244,9 +369,15 @@
             pltpu.SemaphoreType.DMA,
         ],
         name="first%d" % ident,
-        compiler_params=pltpu.CompilerParams(collective_id=ident, has_side_effects=True),
-        cost_estimate=sent_estimate(sum(s.size for s in shapes)),
-    )(own, qkv_weight, weight)
+        compiler_params=pltpu.CompilerParams(
+            collective_id=ident, has_side_effects=True, vmem_limit_bytes=67_000_000
+        ),
+        cost_estimate=pl.CostEstimate(
+            flops=6 * tokens * width * span,
+            bytes_accessed=40 * tokens * width,
+            transcendentals=0,
+        ),
+    )(own, qkv_weight, weight, *vectors)
 
 
 def pieces_out(axes, sizes, source, out, send, recv):
@@ -288,15 +419,14 @@
     )
 
 
-def by_columns(left, right, out):
+def by_columns(left, right, cell, put):
     tokens = left.shape[0] * left.shape[1] * left.shape[2]
-    cell = out.shape[1]
     wide = 400 // cell
     others = right[...].reshape(tokens, right.shape[-1])
     for c in range(left.shape[3] // 400):
         terms = tn(left[:, :, :, c * 400 : (c + 1) * 400].reshape(tokens, 400), others)
         for n in range(wide):
-            out[c * wide + n] = terms[n * cell : (n + 1) * cell].astype(BF16)
+            put(c * wide + n, terms[n * cell : (n + 1) * cell].astype(BF16))
 
 
 def middle_kernel(
@@ -321,8 +451,20 @@
     sums,
     hidden_sum,
     to_heads,
-    expand_half,
-    shrink_terms,
+    shrink_kept,
+    shrink_sent,
+    *rest,
+):
+    outer = every[1][0]
+    middle_body(every, spec, pieces, own, own_grad, out_own, out_far, expand, shrink, out_bias,
+        expand_bias, shrink_bias, gain, shift, att, result, grad_middle, low_middle, sums,
+        hidden_sum, to_heads, shrink_kept, shrink_sent, rest[:outer], *rest[outer:])
+
+
+def middle_body(
+    every, spec, pieces, own, own_grad, out_own, out_far, expand, shrink, out_bias,
+    expand_bias, shrink_bias, gain, shift, att, result, grad_middle, low_middle, sums,
+    hidden_sum, to_heads, shrink_kept, shrink_sent, expand_half,
     came,
     out_w,
     expand_w,
@@ -572,16 +714,30 @@
     for t in range(1, 4):
         add_and_send(t, part_two, first_two, summed_two, last_two, s_send, s_recv)
     to_heads[here] = cut[here]
-    by_columns(e_all, u_all, shrink_terms)
+
+    def keep_or_send(spot, values):
+        @pl.when(y == spot % 2)
+        def _():
+            shrink_kept[spot // 2] = values
+
+        @pl.when(y != spot % 2)
+        def _():
+            shrink_sent[spot // 2] = values
+
+    by_columns(e_all, u_all, shrink_kept.shape[1], keep_or_send)
     result[...] = (
         mid[...] + gathered_sum(part_two, first_two, last_two, s_send, s_recv) + shrink_bias[...]
     ).astype(BF16)
     pieces_in(axes, sizes, cut, to_heads, h_send, h_recv, head_started)
     for n, copy in enumerate(y_copies):
         copy.wait_recv()
-        expand_half[n] = (
-            expand_terms[n, y].astype(F32) + expand_came[n].astype(F32)
-        ).astype(BF16)
+        half = (expand_terms[n, y].astype(F32) + expand_came[n].astype(F32)).astype(BF16)
+        for step, out in enumerate(expand_half):
+
+            @pl.when(lax.rem(lax.axis_index("o") + step, len(expand_half)) == n)
+            def _(out=out, half=half):
+                out[...] = half
+
 
     for copy in out_sent + c_gather.started:
         copy.wait_send()
@@ -630,11 +786,12 @@
             jax.ShapeDtypeStruct((4, width), F32),
             jax.ShapeDtypeStruct((1, piece), F32),
             jax.ShapeDtypeStruct(pieces.shape, BF16),
-            jax.ShapeDtypeStruct(expand_cut[:1] + expand_cut[2:], BF16),
-            jax.ShapeDtypeStruct((spots, width // spots, piece), BF16),
-        ],
+            jax.ShapeDtypeStruct((spots // 2, width // spots, piece), BF16),
+            jax.ShapeDtypeStruct((spots // 2, width // spots, piece), BF16),
+        ]
+        + [jax.ShapeDtypeStruct(expand_cut[2:], BF16)] * outer,
         in_specs=[VMEM] * 3 + [ANY] * 4 + [VMEM] * 5,
-        out_specs=[VMEM] * 9,
+        out_specs=[VMEM] * (9 + outer),
         scratch_shapes=[
             pltpu.VMEM(pieces.shape, BF16),
             pltpu.VMEM((width, width), BF16),
@@ -688,6 +845,11 @@
         self.y_sems, self.o_sems, self.i_sems = y_sems, o_sems, i_sems
         self.o, self.i, self.y = (lax.axis_index(a) for a in ("o", "i", "y"))
 
+    def come(self, kept, came):
+        self.first = []
+        for n in range(2 * self.outer):
+            self.half[n // 2, n % 2] = (kept[n].astype(F32) + came[n].astype(F32)).astype(BF16)
+
     def start(self):
         mate = {"y": 1 - self.y}
         self.first = [
@@ -709,6 +871,9 @@
             self.half[n // 2, n % 2] = (
                 self.terms[2 * n + self.y].astype(F32) + self.came[n].astype(F32)
             ).astype(BF16)
+        self.send_o()
+
+    def send_o(self):
         self.second = []
         for step in range(1, self.outer):
             there = lax.rem(self.o + step, self.outer)
@@ -744,9 +909,9 @@
             copy.wait_send()
 
 
-def owned_scratch(outer, cell, rows):
+def owned_scratch(outer, cell, rows, first=True):
     return [
-        pltpu.VMEM((2 * outer, cell, rows), BF16),
+        pltpu.VMEM((2 * outer if first else 1, cell, rows), BF16),
         pltpu.VMEM((outer, 2, cell, rows), BF16),
         pltpu.VMEM((max(outer - 1, 1), 2, cell, rows), BF16),
         pltpu.VMEM((2, cell, rows), BF16),
@@ -764,13 +929,27 @@
     dqkv,
     columns,
     normed_low,
-    shrink_terms,
+    shrink_kept,
+    shrink_came,
+    expand_kept,
     low_middle,
     att,
     own,
     grad_middle,
     gain,
     row_sums,
+    hidden_sum,
+    *rest,
+):
+    others = sizes[0] - 1
+    final_body(axes, sizes, heads, share, dqkv, columns, normed_low, shrink_kept, shrink_came,
+        [expand_kept, *rest[:others]], low_middle, att, own, grad_middle, gain, row_sums,
+        hidden_sum, *rest[others:])
+
+
+def final_body(
+    axes, sizes, heads, share, dqkv, columns, normed_low, shrink_kept, shrink_came,
+    expand_parts, low_middle, att, own, grad_middle, gain, row_sums,
     hidden_sum,
     grad_inputs,
     routed,
@@ -780,6 +959,7 @@
     value_out,
     rows_out,
     hidden_out,
+    expand_out,
     part,
     first,
     last,
@@ -810,6 +990,10 @@
     g_recv,
     g_local,
     load_sem,
+    expand_sum,
+    expand_came,
+    e_send,
+    e_recv,
     *owned,
 ):
     outer, inner, ys, xs, ks = sizes
@@ -823,7 +1007,7 @@
     rows, width = own.shape
     span = heads * HEAD_DIM
     y_mate, k_mate, x_mate = {"y": 1 - y}, {"k": 1 - k}, {"x": 1 - x}
-    shrink = Owned(outer, shrink_terms, shrink_out, *owned[:7])
+    shrink = Owned(outer, None, shrink_out, *owned[:7])
     outw = Owned(outer, outw_terms, outw_out, *owned[7:])
 
     def load_normed(n):
@@ -877,7 +1061,41 @@
         return unused
 
     lax.fori_loop(0, chips, terms, 0)
-    shrink.start()
+
+    shards = xs * ks
+    cuts = spots // (2 * shards)
+    total = expand_parts[0][...].astype(F32)
+    for other in expand_parts[1:]:
+        total = total + other[...].astype(F32)
+    expand_sum[...] = total.astype(BF16)
+    index = o * ys + y
+    goal = shard * (spots // shards) + i * cuts + index % cuts
+    goal_shard = index // cuts
+    away = goal * shards + goal_shard != me
+    route = remote(
+        expand_sum,
+        expand_came,
+        e_send,
+        e_recv,
+        {
+            "o": goal // (inner * ys),
+            "i": (goal // ys) % inner,
+            "y": goal % ys,
+            "x": goal_shard // ks,
+            "k": goal_shard % ks,
+        },
+    )
+
+    @pl.when(away)
+    def _():
+        route.start()
+
+    @pl.when(jnp.logical_not(away))
+    def _():
+        expand_came[...] = expand_sum[...]
+
+    shrink.come(shrink_kept, shrink_came)
+    shrink.send_o()
 
     quarter = q_part.shape[3]
     some = normed_part.shape[0]
@@ -922,7 +1140,11 @@
     side.hand_on()
     pieces_in(*group, att_cut, att_all, a_send, a_recv, att_started)
     side.finish()
-    by_columns(gy_all, att_all, outw_terms)
+
+    def put_terms(spot, values):
+        outw_terms[spot] = values
+
+    by_columns(gy_all, att_all, outw_terms.shape[1], put_terms)
     outw.start()
 
     q_copies[1].wait_recv()
@@ -1020,7 +1242,7 @@
         )
         copy.start()
         line_started.append(copy)
-    shrink.over_o()
+    shrink.over_i()
     outw.over_o()
     for copy in line_started:
         copy.wait_recv()
@@ -1038,7 +1260,6 @@
         )
         copy.start()
         line_started.append(copy)
-    shrink.over_i()
     outw.over_i()
 
     base = (share * place) // HEAD_DIM
@@ -1071,6 +1292,12 @@
         take(rows_base + n * w_rows, rows_out, n, 0, width)
     for n in range(xs * ks * inner):
         take(hidden_base + n * p_rows, hidden_out, 0, n * piece, piece)
+
+    @pl.when(away)
+    def _():
+        route.wait()
+
+    expand_out[...] = expand_came[...].astype(F32)
     shrink.finish()
     outw.finish()
     each_sent(sent_block)
@@ -1086,7 +1313,9 @@
     dqkv,
     columns,
     normed_low,
-    shrink_terms,
+    shrink_kept,
+    shrink_came,
+    expand_parts,
     low_middle,
     att,
     own,
@@ -1101,7 +1330,8 @@
     ident,
 ):
     outer, inner, ys, xs, ks = sizes
-    spots, cell, piece = shrink_terms.shape
+    spots = outer * inner * ys
+    cell, piece = shrink_kept.shape[1:]
     rows, width = own.shape
     chips = outer * inner
     devices = spots * xs * ks
@@ -1129,9 +1359,10 @@
             jax.ShapeDtypeStruct((1, spots * span), F32),
             jax.ShapeDtypeStruct((6, width), F32),
             jax.ShapeDtypeStruct((1, group * piece), F32),
+            jax.ShapeDtypeStruct(expand_parts[0].shape, F32),
         ],
-        in_specs=[VMEM] * 2 + [ANY] + [VMEM] * 8,
-        out_specs=[VMEM] * 8,
+        in_specs=[VMEM] * 2 + [ANY] + [VMEM] * (9 + outer),
+        out_specs=[VMEM] * 9,
         scratch_shapes=[
             pltpu.VMEM((chips, ys) + block, BF16),
             pltpu.VMEM((chips,) + block, BF16),
@@ -1161,7 +1392,11 @@
             pltpu.SemaphoreType.DMA((2 * devices,)),
             *gather_scratch((("i", "x"), (inner, xs), "k")),
             pltpu.SemaphoreType.DMA,
-            *owned_scratch(outer, cell, piece),
+            pltpu.VMEM(expand_parts[0].shape, BF16),
+            pltpu.VMEM(expand_parts[0].shape, BF16),
+            pltpu.SemaphoreType.DMA,
+            pltpu.SemaphoreType.DMA,
+            *owned_scratch(outer, cell, piece, False),
             *owned_scratch(outer, cell, out_rows),
         ],
         name="final%d" % ident,
@@ -1177,7 +1412,9 @@
         dqkv,
         columns,
         normed_low,
-        shrink_terms,
+        shrink_kept,
+        shrink_came,
+        expand_parts[0],
         low_middle,
         att,
         own,
@@ -1185,6 +1422,7 @@
         gain,
         row_sums,
         hidden_sum,
+        *expand_parts[1:],
     )
 
 
@@ -1443,17 +1681,6 @@
     )(inv, qkv, grads, outs, lse)
 
 
-def layer_norm(values, gain, shift):
-    center = jnp.mean(values, axis=-1, keepdims=True)
-    centred = values - center
-    spread = jnp.mean(centred * centred, axis=-1, keepdims=True)
-    return centred * lax.rsqrt(spread + EPSILON) * gain + shift
-
-
-def matmul(left, right):
-    return jnp.dot(left, right, preferred_element_type=F32)
-
-
 def body(
     sizes,
     tokens,
@@ -1487,9 +1714,7 @@
     hidden = expand_weight.shape[1]
     piece = hidden // (shards * inner)
     every = (("o", "i", "y"), (outer, inner, ys))
-    ctx = (("o", "i"), (outer, inner), "y")
     group = (("i", "x"), (inner, xs), "k")
-    pair = (("x",), (xs,), "k")
     own = tokens[0]
     own_grad = cotangent[0]
 
@@ -1501,13 +1726,20 @@
     qkv_bias = jnp.concatenate(
         [columns(query_bias, 1)[0], jnp.zeros((span,), F32), columns(value_bias, 1)[0]]
     )
-    gathered, qkv_columns, expand_columns = first_gather(
-        own, qkv_weight, expand_weight, span, [ctx, pair], (xs, ks), every, piece, 0
+    sizes_of = (outer, inner, ys, xs, ks)
+    qkv, normed_low, qkv_columns, expand_columns = first_part(
+        own,
+        qkv_weight,
+        expand_weight,
+        [first_gain[None], first_shift[None], qkv_bias[None]],
+        span,
+        sizes_of,
+        piece,
+        0,
     )
-    sequence = gathered.reshape(spots * rows, width)
     qkv_columns = qkv_columns.reshape(width, 3 * span)
 
-    sequence, out_own = lax.optimization_barrier((sequence, out_weight))
+    qkv, out_own = lax.optimization_barrier((qkv, out_weight))
     out_far = lax.ppermute(out_own, "x", [(0, 1), (1, 0)])
     expand_own_bias = lax.dynamic_slice_in_dim(
         expand_bias, (shard * inner + i) * piece, piece, axis=0
@@ -1523,25 +1755,7 @@
         ),
         axis=0,
     ).astype(jnp.int32)
-    normed_low = layer_norm(sequence.astype(F32), first_gain, first_shift).astype(BF16)
-    qkv = (matmul(normed_low, qkv_columns) + qkv_bias).astype(BF16)
     attended, attended_bf, log_sum = attend(inv, qkv, heads)
-    def cut(values, axis_name, dim):
-        index, size = lax.axis_index(axis_name), sizes[axis_name]
-        return [
-            lax.dynamic_index_in_dim(values, lax.rem(index + s, size), axis=dim, keepdims=False)
-            for s in range(size)
-        ]
-
-    def added(pieces, axis_name):
-        size = sizes[axis_name]
-        total = pieces[0].astype(F32)
-        for step in range(1, size):
-            ring = [(d, (d + step) % size) for d in range(size)]
-            total = total + lax.ppermute(pieces[step], axis_name, ring).astype(F32)
-        return total.astype(BF16)
-
-    cuts = spots // (2 * shards)
     (
         attended_low,
         result,
@@ -1550,8 +1764,9 @@
         row_sums,
         hidden_sums,
         grad_heads,
-        expand_half,
-        shrink_terms,
+        shrink_kept,
+        shrink_sent,
+        *expand_parts,
     ) = middle_part(
         attended_bf.reshape(spots, rows, span),
         own,
@@ -1570,15 +1785,11 @@
     )
     grad_heads = grad_heads.reshape(spots * rows, span)
     dqkv = attend_back(inv, qkv, grad_heads, attended, log_sum, heads)
-    expand_whole = added(cut(expand_half, "o", 0), "o")
-    dqkv, expand_whole = lax.optimization_barrier((dqkv, expand_whole))
+    shrink_came = lax.ppermute(shrink_sent, "y", [(0, 1), (1, 0)])
+    for step in range(1, outer):
+        ring = [(d, (d + step) % outer) for d in range(outer)]
+        expand_parts[step] = lax.ppermute(expand_parts[step], "o", ring)
     axes = ("o", "i", "y", "x", "k")
-    routes = []
-    for so, si, sy, sf in itertools.product(*map(range, (outer, inner, ys, shards))):
-        index = so * ys + sy
-        spot = sf * (spots // shards) + si * cuts + index % cuts
-        routes.append((((so * inner + si) * ys + sy) * shards + sf, spot * shards + index // cuts))
-    grad_expand = lax.ppermute(expand_whole, axes, routes).astype(F32)
     share = 3 * width // spots
     (
         grad_inputs,
@@ -1589,11 +1800,14 @@
         value_sums,
         row_totals,
         hidden_totals,
+        grad_expand,
     ) = final_part(
         dqkv,
         qkv_columns,
         normed_low,
-        shrink_terms,
+        shrink_kept,
+        shrink_came,
+        expand_parts,
         middle_low,
         attended_low,
         own,
@@ -1602,7 +1816,7 @@
         row_sums,
         hidden_sums,
         axes,
-        (outer, inner, ys, xs, ks),
+        sizes_of,
         heads,
         share,
         2,

time: 432 us -> 414 us (0.958)
  the two profiles are of different devices: /device:TPU:3 before, /device:TPU:25 now
where the time goes in v6:
time: 414 us; the launch traced here: 405 us
  Pallas kernels  363 us (88%)
  local copies, waits for them, and re-layouts  24.1 us (6%)
  waiting for transfers between devices  13.2 us (3%)
    pallas_call x1, Pallas kernels, final_part(): pl.pallas_call(functools.partial(final_kernel, axes, sizes, heads, share)...  156 us
    pallas_call x1, Pallas kernels, middle_part(): pl.pallas_call(functools.partial(middle_kernel, every, spec), out_shape=[...  112 us
    pallas_call x1, Pallas kernels, first_part(): pl.pallas_call(functools.partial(first_kernel, sizes), out_shape=[jax.Sha...  52.1 us
    pallas_call x1, Pallas kernels, attend_back(): pl.pallas_call(functools.partial(attend_back_kernel, heads, block), out_s...  23.4 us
    pallas_call x1, Pallas kernels, attend(): pl.pallas_call(functools.partial(attend_kernel, heads, block), out_shape=...  20 us
    unnamed x32, local copies, waits for them, and re-layouts  10 us
    ppermute x1, waiting for transfers between devices, body(): expand_parts[step] = lax.ppermute(expand_parts[step], 'o', ring)  8.58 us
  transfers between devices with their start and end apart: 3, of which 2 were waited for; matrix products, arithmetic and copies ran while one was open for 2% of the time, Pallas kernels for 11%

profile of v6, /device:TPU:25, one launch (start us, length us, event | category | flops | bytes accessed | tf_op | source)
XLA Modules:
  0.0 405.4 jit_solution(12203170506105614498)
XLA Ops:
  0.7 1.3 broadcast_in_dim.50.gain
  2.0 0.7 reshape.55
  2.7 0.7 reshape.56
  3.4 0.6 broadcast_in_dim.53.bias
  4.0 1.3 broadcast_in_dim.51.shift
  5.3 2.0 copy.43
  7.2 0.0 copy-start.12
  7.3 52.1 %first0.1 = (bf16[1024,768]{1,0:T(8,128)(2,1)}, bf16[1024,1600]{1,0:T(8,128)(2,1)}, bf16[2,2,400,768]{3,2,1,0:T(8,128)(2,1)}, bf16[4,400,800]{2,1,0:T(8,128)(2,1)}) custom-call(bf16[128,1600]{1,0:T(8,128)(2,1)} %bitcast.20, bf16[400,4800]{1,0:T(8,128)(2,1)} %qkv_weight.1, bf16[400,6400]{1,0:T(8,128)(2,1)} %weight.1, f32[1,1600]{1,0:T(1,128)} %broadcast_in_dim.50.gain, ...), custom_call_target="tpu_custom_call" | custom-call | flops 2516582400 | bytes 65536000 | tf_op jit(solution)/shard_map/first0/pallas_call | solution.py:344
  59.3 0.3 collective-permute-start
  59.7 0.8 dynamic_slice.14
  60.4 0.6 broadcast_in_dim.55.expand_bias
  61.0 0.0 copy-done.6
  61.0 0.6 broadcast_in_dim.54.out_bias
  61.6 0.0 copy-done.7
  61.6 0.6 broadcast_in_dim.56.shrink_bias
  62.2 0.0 copy-done.8
  62.2 0.6 broadcast_in_dim.57.gain
  62.8 0.0 copy-done.9
  62.8 0.6 broadcast_in_dim.58.shift
  63.4 2.0 copy.44
  65.4 0.6 select_reduce_fusion.inv
  66.0 20.0 %attend.1 = (f32[1024,256]{1,0:T(8,128)}, bf16[1024,256]{1,0:T(8,128)(2,1)}, f32[4,1024]{1,0:T(4,128)}) custom-call(s32[16]{0:T(128)} %select_reduce_fusion.inv, bf16[1024,768]{1,0:T(8,128)(2,1)} %get-tuple-element.45.qkv), custom_call_target="tpu_custom_call" | custom-call | flops 2684354560 | bytes 2621440 | tf_op jit(solution)/shard_map/attend/pallas_call | solution.py:1540
  86.0 4.7 %collective-permute-done.out_far = bf16[400,1600]{1,0:T(8,128)(2,1)} collective-permute-done((bf16[400,1600]{1,0:T(8,128)(2,1)}, bf16[400,1600]{1,0:T(8,128)(2,1)}, u32[]{:S(2)}, u32[]{:S(2)}) %collective-permute-start) | collective-permute-done | bytes 1280032 | tf_op jit(solution)/shard_map/ppermute | solution.py:1743
  90.7 112.2 %middle1.1 = (bf16[128,1600]{1,0:T(8,128)(2,1)}, bf16[128,1600]{1,0:T(8,128)(2,1)}, f32[128,1600]{1,0:T(8,128)}, bf16[128,1600]{1,0:T(8,128)(2,1)}, f32[4,1600]{...) custom-call(bf16[8,128,256]{2,1,0:T(8,128)(2,1)} %bitcast.33, ...), custom_call_target="tpu_custom_call" | custom-call | flops 10485760000 | bytes 40960000 | tf_op jit(solution)/shard_map/middle1/pallas_call | solution.py:779
  202.8 0.8 collective-permute-start.1
  203.6 0.2 collective-permute-start.2
  203.9 1.9 copy.48
  205.8 23.4 %attend_back.1.dqkv = bf16[1024,768]{1,0:T(8,128)(2,1)} custom-call(s32[16]{0:T(128)} %select_reduce_fusion.inv, bf16[1024,768]{1,0:T(8,128)(2,1)} %get-tuple-element.45.qkv, bf16[1024,256]{1,0:T(8,128)(2,1)} %bitcast.32, f32[1024,256]{1,0:T(8,128)} %get-tuple-element.51.outs, f32[4,1024]{1,0:T(4,128)} %get-tuple-element.52.lse), custom_call_target="tpu_custom_call" | custom-call | flops 6710886400 | bytes 5242880 | tf_op jit(solution)/shard_map/attend_back/pallas_call | solution.py:1650
  229.2 8.6 %collective-permute-done.2.rest_0_ = bf16[400,800]{1,0:T(8,128)(2,1)} collective-permute-done((bf16[400,800]{1,0:T(8,128)(2,1)}, bf16[400,800]{1,0:T(8,128)(2,1)}, u32[]{:S(2)}, u32[]{:S(2)}) %collective-permute-start.2) | collective-permute-done | bytes 640032 | tf_op jit(solution)/shard_map/ppermute | solution.py:1791
  237.8 0.0 collective-permute-done.1.shrink_came
  237.8 155.6 %final2.1 = (f32[128,1600]{1,0:T(8,128)}, bf16[11,64,400]{2,1,0:T(8,128)(2,1)}, bf16[2,200,800]{2,1,0:T(8,128)(2,1)}, bf16[2,200,200]{2,1,0:T(8,128)(2,1)}, f32[...) custom-call(bf16[1024,768]{1,0:T(8,128)(2,1)} %attend_back.1.dqkv, ...), custom_call_target="tpu_custom_call" | custom-call | flops 5033164800 | bytes 40960000 | tf_op jit(solution)/shard_map/final2/pallas_call | solution.py:1351
  393.4 2.4 copy.49
  395.9 0.3 copy.50
  396.1 0.3 copy-done.11
  396.5 0.6 slice_reduce_fusion.7
  397.1 0.0 copy-done.10
  397.1 0.6 slice_reduce_fusion.6
  397.7 0.7 slice_reduce_fusion
  398.5 0.9 copy.46
  399.4 1.0 convert_bitcast_fusion.1
  400.4 0.1 convert_bitcast_fusion
  400.5 0.7 copy.47
  401.3 0.0 copy-start.5
  401.3 0.0 copy-start
  401.3 2.0 reshape.62
  403.3 0.0 copy-done.5
  403.3 0.7 reduce.3
  404.0 1.1 copy.52
  (21 shorter events, 0.1 us)
Async XLA Ops:
  7.2 53.8 %copy-start.6 = (f32[1600]{0:T(1024)S(1)}, f32[1600]{0:T(1024)}, u32[]{:S(2)}) copy-start(f32[1600]{0:T(1024)} %param.22) | copy-start | bytes 19204
  7.2 54.4 %copy-start.7 = (f32[1600]{0:T(1024)S(1)}, f32[1600]{0:T(1024)}, u32[]{:S(2)}) copy-start(f32[1600]{0:T(1024)} %param.26) | copy-start | bytes 19204
  7.2 55.0 %copy-start.8 = (f32[1600]{0:T(1024)S(1)}, f32[1600]{0:T(1024)}, u32[]{:S(2)}) copy-start(f32[1600]{0:T(1024)} %param.29) | copy-start | bytes 19204
  7.2 55.6 %copy-start.9 = (f32[1600]{0:T(1024)S(1)}, f32[1600]{0:T(1024)}, u32[]{:S(2)}) copy-start(f32[1600]{0:T(1024)} %param.30) | copy-start | bytes 19204
  7.2 58.1 %copy-start.12 = (s32[1,16]{1,0:T(1,128)S(1)}, s32[1,16]{1,0:T(1,128)}, u32[]{:S(2)}) copy-start(s32[1,16]{1,0:T(1,128)} %param.17) | copy-start | bytes 196
  59.3 31.3 %collective-permute-start = (bf16[400,1600]{1,0:T(8,128)(2,1)}, bf16[400,1600]{1,0:T(8,128)(2,1)}, u32[]{:S(2)}, u32[]{:S(2)}) collective-permute-start(bf16[400,1600]{1,0:T(8,128)(2,1)} %out_own), channel_id=1, source_target_pairs={{0,2},{2,0},{1,3},{3,1},{4,6},{6,4},{5,7},{7,5},{8,10},{10,8},{9,1... | collective-permute-start | bytes 3840008 | tf_op jit(solution)/shard_map/ppermute | solution.py:1743
  202.8 34.9 %collective-permute-start.1 = (bf16[4,200,800]{2,1,0:T(8,128)(2,1)}, bf16[4,200,800]{2,1,0:T(8,128)(2,1)}, u32[]{:S(2)}, u32[]{:S(2)}) collective-permute-start(bf16[4,200,800]{2,1,0:T(8,128)(2,1)} %get-tuple-element.56), channel_id=1, source_target_pairs={{0,4},{4,0},{1,5},{5,1},{2,6},{6,2},{3,7},{7,3},{8,12},{12,8},{9,1... | collective-permute-start | bytes 3840008 | tf_op jit(solution)/shard_map/ppermute | solution.py:1788
  203.6 34.2 %collective-permute-start.2 = (bf16[400,800]{1,0:T(8,128)(2,1)}, bf16[400,800]{1,0:T(8,128)(2,1)}, u32[]{:S(2)}, u32[]{:S(2)}) collective-permute-start(bf16[400,800]{1,0:T(8,128)(2,1)} %get-tuple-element.63), channel_id=1, source_target_pairs={{0,16},{16,0},{1,17},{17,1},{2,18},{18,2},{3,19},{19,3},{4,20},{20... | collective-permute-start | bytes 1920008 | tf_op jit(solution)/shard_map/ppermute | solution.py:1791
  393.4 2.4 copy-start.2
  395.8 0.7 copy-start.11
  395.8 1.3 copy-start.10
  395.8 1.9 copy-start.4
  395.8 2.6 copy-start.3
  398.4 2.0 copy-start.1
  401.3 2.0 copy-start.5
  401.3 2.7 copy-start

commit v7 on v6

--- a/solution.py
+++ b/solution.py
@@ -108,6 +108,89 @@
             ).wait_recv()
         for copy in self.started:
             copy.wait_send()
+
+
+class Quad:
+    def __init__(self, source, out, send, recv, local):
+        self.i, self.x, self.k = (lax.axis_index(a) for a in ("i", "x", "k"))
+        self.source, self.out, self.send, self.recv, self.local = source, out, send, recv, local
+        self.i_mate, self.x_mate, self.k_mate = {"i": 1 - self.i}, {"x": 1 - self.x}, {"k": 1 - self.k}
+        self.half = source.shape[0] // 2
+        self.places = (
+            2 * self.i + self.x,
+            2 * self.i + 1 - self.x,
+            2 * (1 - self.i) + self.x,
+            2 * (1 - self.i) + 1 - self.x,
+        )
+        self.started = []
+
+    def peers(self):
+        return [self.i_mate, self.x_mate, self.k_mate]
+
+    def copy(self, source, target, slot, peer):
+        return remote(source, target, self.send.at[slot], self.recv.at[slot], peer)
+
+    def go(self, source, target, slot, peer):
+        copy = self.copy(source, target, slot, peer)
+        copy.start()
+        self.started.append(copy)
+
+    def start(self):
+        mine = self.out.at[self.places[0], self.k]
+        pltpu.make_async_copy(self.source, mine, self.local).start()
+        self.go(self.source, mine, 0, self.x_mate)
+        self.go(self.source, mine, 1, self.i_mate)
+        self.go(self.source, mine, 2, self.k_mate)
+
+    def x_in(self):
+        block = self.out.at[self.places[1], self.k]
+        self.copy(self.source, block, 0, self.x_mate).wait_recv()
+        part = block.at[pl.ds(0, self.half)]
+        self.go(part, part, 4, self.i_mate)
+        self.go(block, block, 3, self.k_mate)
+
+    def i_in(self):
+        block = self.out.at[self.places[2], self.k]
+        self.copy(self.source, block, 1, self.i_mate).wait_recv()
+        part = block.at[pl.ds(self.half, self.half)]
+        self.go(part, part, 6, self.x_mate)
+        self.go(block, block, 5, self.k_mate)
+
+    def d_in(self):
+        block = self.out.at[self.places[3], self.k]
+        part = block.at[pl.ds(0, self.half)]
+        self.copy(part, part, 4, self.i_mate).wait_recv()
+        part = block.at[pl.ds(self.half, self.half)]
+        self.copy(part, part, 6, self.x_mate).wait_recv()
+        self.go(block, block, 7, self.k_mate)
+
+    def across(self, place, slot):
+        block = self.out.at[place, 1 - self.k]
+        self.copy(self.source, block, slot, self.k_mate).wait_recv()
+
+    def all_across(self):
+        for place, slot in zip(self.places, (2, 3, 5, 7)):
+            self.across(place, slot)
+
+    def local_wait(self):
+        mine = self.out.at[self.places[0], self.k]
+        pltpu.make_async_copy(self.source, mine, self.local).wait()
+
+    def finish(self):
+        for copy in self.started:
+            copy.wait_send()
+
+
+def quad_scratch():
+    return [
+        pltpu.SemaphoreType.DMA((8,)),
+        pltpu.SemaphoreType.DMA((8,)),
+        pltpu.SemaphoreType.DMA,
+    ]
+
+
+def turned(block):
+    return block.astype(F32).T.astype(block.dtype)
 
 
 def gather_shape(block, spec):
@@ -194,17 +277,20 @@
 
 def first_kernel(
     sizes,
-    own,
+    own_turned,
     qkv_weight,
     weight,
     gain,
     shift,
-    bias,
+    query_bias,
+    value_bias,
     qkv,
     normed_out,
     all_columns,
     pieces,
+    own,
     sequence,
+    bias,
     qkv_whole,
     columns,
     columns_in,
@@ -233,6 +319,7 @@
     qkv_fetch.start()
     fetch = pltpu.make_async_copy(weight, whole, read)
     fetch.start()
+    own[...] = turned(own_turned[...])
     peers = [moved(axes, shard_sizes, o) for o in offs] + [
         moved(("o", "i", "y"), (outer, inner, ys), o) for o in offsets((outer, inner, ys))
     ]
@@ -254,10 +341,17 @@
                         (part, span), BF16
                     )
                 columns[:, section * span : section * span + size] = qkv_whole[:, low : low + size]
+            bias[...] = jnp.zeros(bias.shape, F32)
+            low = spot * span
+            bias[:, 0:size] = query_bias[...].reshape(1, width)[:, low : low + size]
+            bias[:, 2 * span : 2 * span + size] = value_bias[...].reshape(1, width)[
+                :, low : low + size
+            ]
 
     @pl.when(place * span >= width)
     def _():
         columns[...] = jnp.zeros(columns.shape, BF16)
+        bias[...] = jnp.zeros(bias.shape, F32)
 
     heads.start()
     fetch.wait()
@@ -302,7 +396,7 @@
     def project(at):
         values = sequence[at].reshape(ys * rows, width).astype(F32)
         plain, unused_scale = normed(values)
-        low = (plain * gain[...] + shift[...]).astype(BF16)
+        low = (plain * gain[...].reshape(1, width) + shift[...].reshape(1, width)).astype(BF16)
         start = pl.multiple_of(at * ys * rows, ys * rows)
         normed_out[pl.ds(start, ys * rows), :] = low
         weights = columns_in[...].reshape(width, 3 * span)
@@ -332,11 +426,11 @@
     line.finish()
 
 
-def first_part(own, qkv_weight, weight, vectors, span, sizes, piece, ident):
+def first_part(own_turned, qkv_weight, weight, vectors, span, sizes, piece, ident):
     outer, inner, ys, xs, ks = sizes
     shards, chips = xs * ks, outer * inner
     part = weight.shape[0]
-    rows, width = own.shape
+    width, rows = own_turned.shape
     tokens = chips * ys * rows
     columns = jax.ShapeDtypeStruct((part, 3 * span), BF16)
     spec = (("x",), (xs,), "k")
@@ -348,11 +442,13 @@
             jax.ShapeDtypeStruct((tokens, width), BF16),
             gathered,
             jax.ShapeDtypeStruct((shards, part, piece), BF16),
+            jax.ShapeDtypeStruct((rows, width), BF16),
         ],
-        in_specs=[VMEM, ANY, ANY, VMEM, VMEM, VMEM],
-        out_specs=[VMEM, VMEM, ANY, ANY],
+        in_specs=[VMEM, ANY, ANY] + [VMEM] * 4,
+        out_specs=[VMEM, VMEM, ANY, ANY, VMEM],
         scratch_shapes=[
             pltpu.VMEM((chips, ys, rows, width), BF16),
+            pltpu.VMEM((1, 3 * span), F32),
             pltpu.VMEM(qkv_weight.shape, BF16),
             pltpu.VMEM(columns.shape, BF16),
             pltpu.VMEM(gathered.shape, BF16),
@@ -377,7 +473,7 @@
             bytes_accessed=40 * tokens * width,
             transcendentals=0,
         ),
-    )(own, qkv_weight, weight, *vectors)
+    )(own_turned, qkv_weight, weight, *vectors)
 
 
 def pieces_out(axes, sizes, source, out, send, recv):
@@ -431,16 +527,15 @@
 
 def middle_kernel(
     every,
-    spec,
     pieces,
     own,
-    own_grad,
+    grad_turned,
     out_own,
     out_far,
     expand,
     shrink,
     out_bias,
-    expand_bias,
+    expand_bias_all,
     shrink_bias,
     gain,
     shift,
@@ -456,15 +551,17 @@
     *rest,
 ):
     outer = every[1][0]
-    middle_body(every, spec, pieces, own, own_grad, out_own, out_far, expand, shrink, out_bias,
-        expand_bias, shrink_bias, gain, shift, att, result, grad_middle, low_middle, sums,
+    middle_body(every, pieces, own, grad_turned, out_own, out_far, expand, shrink, out_bias,
+        expand_bias_all, shrink_bias, gain, shift, att, result, grad_middle, low_middle, sums,
         hidden_sum, to_heads, shrink_kept, shrink_sent, rest[:outer], *rest[outer:])
 
 
 def middle_body(
-    every, spec, pieces, own, own_grad, out_own, out_far, expand, shrink, out_bias,
-    expand_bias, shrink_bias, gain, shift, att, result, grad_middle, low_middle, sums,
+    every, pieces, own, grad_turned, out_own, out_far, expand, shrink, out_bias,
+    expand_bias_all, shrink_bias, gain, shift, att, result, grad_middle, low_middle, sums,
     hidden_sum, to_heads, shrink_kept, shrink_sent, expand_half,
+    own_grad,
+    expand_bias,
     came,
     out_w,
     expand_w,
@@ -536,6 +633,7 @@
         )
     for copy in loads:
         copy.start()
+    own_grad[...] = turned(grad_turned[...])
     greet([moved(axes, sizes, o) for o in offsets(sizes)] + [chip(t)[1] for t in range(1, 4)] + [mate])
 
     started = pieces_out(axes, sizes, pieces, came, send, recv)
@@ -546,10 +644,19 @@
         )
         copy.start()
         out_sent.append(copy)
-    e_gather = Gather(*spec, own_grad, e_all, e_send, e_recv, e_local)
+    e_gather = Quad(own_grad, e_all, e_send, e_recv, e_local)
     e_gather.start()
     here = flat(own_place(axes), axes, sizes)
     came[here] = pieces[here]
+    for n in range(expand_bias_all.shape[0] // piece):
+
+        @pl.when(2 * shard + inner == n)
+        def _(n=n):
+            everything = expand_bias_all[...].reshape(1, expand_bias_all.shape[0])
+            expand_bias[...] = everything[:, n * piece : (n + 1) * piece]
+
+    e_gather.x_in()
+    e_gather.i_in()
     pieces_in(axes, sizes, pieces, came, send, recv, started)
     span = came.shape[2]
     for d in range(came.shape[0]):
@@ -570,14 +677,16 @@
     mid[...] = (
         own[...].astype(F32)
         + jnp.dot(att[...], out_w[...], preferred_element_type=F32)
-        + out_bias[...]
+        + out_bias[...].reshape(1, width)
     )
     plain, scale = normed(mid[...])
-    c_own[...] = (plain * gain[...] + shift[...]).astype(BF16)
-    c_gather = Gather(*spec, c_own, c_all, c_send, c_recv, c_local)
+    gains = gain[...].reshape(1, width)
+    c_own[...] = (plain * gains + shift[...].reshape(1, width)).astype(BF16)
+    c_gather = Quad(c_own, c_all, c_send, c_recv, c_local)
     c_gather.start()
-    e_gather.hand_on()
-    e_gather.finish()
+    e_gather.d_in()
+    e_gather.local_wait()
+    e_gather.all_across()
     for copy in loads[2:]:
         copy.wait()
 
@@ -591,17 +700,6 @@
 
     lax.fori_loop(0, 4, slopes, 0)
     hidden_sum[...] = jnp.zeros(hidden_sum.shape, F32)
-
-    def c_wait(t):
-        place, peer = chip(t)
-        block = c_all.at[place, 1 - k]
-        remote(c_own, block, c_send.at[3 + t], c_recv.at[3 + t], mate).wait_recv()
-
-    def c_hand_on(t):
-        place, peer = chip(t)
-        block = c_all.at[place, k]
-        remote(c_own, block, c_send.at[t - 1], c_recv.at[t - 1], mate).wait_recv()
-        remote(block, block, c_send.at[3 + t], c_recv.at[3 + t], mate).start()
 
     def to_mate(t, source, target, sends, recvs):
         place, peer = chip(t)
@@ -619,11 +717,14 @@
         sums_of[t - 1] = (parts[place, k].astype(F32) + firsts[t].astype(F32)).astype(BF16)
         to_chip(t, sums_of, lasts, sends, recvs).start()
 
-    pltpu.make_async_copy(c_own, c_gather.mine(), c_local).wait()
-
-    def feed(t, unused):
-        c_wait(t)
+    c_gather.x_in()
+    c_gather.i_in()
+    c_gather.local_wait()
+
+    def feed(step, unused):
+        t = lax.rem(step + 1, 4)
         place, peer = chip(t)
+        c_gather.across(place, jnp.where(t == 0, 2, jnp.where(t == 3, 7, 2 * t + 1)))
         expanded = jnp.dot(both(c_all, place), expand_w[...], preferred_element_type=F32)
         expanded = expanded + expand_bias[...]
         square = expanded * expanded
@@ -640,18 +741,17 @@
         part[place] = back.reshape(2, rows, width)
         to_mate(t, part, first, r_send, r_recv).start()
 
-        @pl.when(t < 3)
+        @pl.when(step == 0)
         def _():
-            c_hand_on(t + 1)
-
-        @pl.when(t > 1)
+            c_gather.d_in()
+
+        @pl.when(step > 0)
         def _():
-            add_and_send(t - 1, part, first, summed, last, r_send, r_recv)
+            add_and_send(step, part, first, summed, last, r_send, r_recv)
 
         return unused
 
     lax.fori_loop(0, 4, feed, 0)
-    add_and_send(3, part, first, summed, last, r_send, r_recv)
 
     parts, cuts = expand.shape[0], expand_terms.shape[0] * 2 // expand.shape[0]
     cut_width = expand_terms.shape[3]
@@ -661,7 +761,7 @@
             gz_all[...].reshape(8 * rows, piece),
         )
         for c in range(cuts):
-            index = f * cuts + c
+            index = lax.rem(f + 2 * k, parts) * cuts + c
             expand_terms[index // 2, index % 2] = terms[
                 :, c * cut_width : (c + 1) * cut_width
             ].astype(BF16)
@@ -686,7 +786,7 @@
 
     grad = gathered_sum(part, first, last, r_send, r_recv)
     plain, scale = normed(mid[...])
-    grad_mid = own_grad[...].astype(F32) + norm_back(grad, gain[...], plain, scale)
+    grad_mid = own_grad[...].astype(F32) + norm_back(grad, gains, plain, scale)
     grad_middle[...] = grad_mid
     low = grad_mid.astype(BF16)
     low_middle[...] = low
@@ -725,9 +825,8 @@
             shrink_sent[spot // 2] = values
 
     by_columns(e_all, u_all, shrink_kept.shape[1], keep_or_send)
-    result[...] = (
-        mid[...] + gathered_sum(part_two, first_two, last_two, s_send, s_recv) + shrink_bias[...]
-    ).astype(BF16)
+    values = mid[...] + gathered_sum(part_two, first_two, last_two, s_send, s_recv)
+    result[...] = (values + shrink_bias[...].reshape(1, width)).T.astype(BF16)
     pieces_in(axes, sizes, cut, to_heads, h_send, h_recv, head_started)
     for n, copy in enumerate(y_copies):
         copy.wait_recv()
@@ -739,11 +838,14 @@
                 out[...] = half
 
 
-    for copy in out_sent + c_gather.started:
+    for copy in out_sent:
         copy.wait_send()
-    for t in range(1, 4):
-        place, peer = chip(t)
-        remote(c_own, c_own, c_send.at[3 + t], c_recv.at[3 + t], mate).wait_send()
+    for gather in (e_gather, c_gather):
+        for slot in (0, 1, 2, 3, 5, 7):
+            gather.copy(c_own, c_own, slot, mate).wait_send()
+        for slot in (4, 6):
+            half = c_own.at[pl.ds(0, rows // 2)]
+            gather.copy(half, half, slot, mate).wait_send()
     for t in range(4):
         to_mate(t, part, first, r_send, r_recv).wait_send()
         to_mate(t, part_two, first_two, s_send, s_recv).wait_send()
@@ -755,7 +857,7 @@
 
 
 def middle_part(
-    pieces, own, own_grad, out_own, out_far, expand, shrink, vectors, every, spec, ident
+    pieces, own, grad_turned, out_own, out_far, expand, shrink, vectors, every, ident
 ):
     spots, rows, span = pieces.shape
     width = own.shape[1]
@@ -777,10 +879,10 @@
         ]
 
     return pl.pallas_call(
-        functools.partial(middle_kernel, every, spec),
+        functools.partial(middle_kernel, every),
         out_shape=[
             flat_low,
-            flat_low,
+            jax.ShapeDtypeStruct((width, rows), BF16),
             flat_f32,
             flat_low,
             jax.ShapeDtypeStruct((4, width), F32),
@@ -793,6 +895,8 @@
         in_specs=[VMEM] * 3 + [ANY] * 4 + [VMEM] * 5,
         out_specs=[VMEM] * (9 + outer),
         scratch_shapes=[
+            pltpu.VMEM((rows, width), BF16),
+            pltpu.VMEM((1, piece), F32),
             pltpu.VMEM(pieces.shape, BF16),
             pltpu.VMEM((width, width), BF16),
             pltpu.VMEM((width, piece), BF16),
@@ -811,8 +915,8 @@
             pltpu.VMEM(expand_cut[:1] + expand_cut[2:], BF16),
             pltpu.SemaphoreType.DMA((spots,)),
             pltpu.SemaphoreType.DMA((spots,)),
-            *gather_scratch(spec),
-            *gather_scratch(spec),
+            *quad_scratch(),
+            *quad_scratch(),
             pltpu.SemaphoreType.DMA((7,)),
             pltpu.SemaphoreType.DMA((2,)),
             pltpu.SemaphoreType.DMA((2,)),
@@ -834,12 +938,14 @@
             bytes_accessed=100 * rows * width * 2,
             transcendentals=8 * rows * piece,
         ),
-    )(pieces, own, own_grad, out_own, out_far, expand, shrink, *vectors)
+    )(pieces, own, grad_turned, out_own, out_far, expand, shrink, *vectors)
 
 
 class Owned:
-    def __init__(self, outer, terms, out, came, half, last, whole, y_sems, o_sems, i_sems):
-        self.outer = outer
+    def __init__(
+        self, outer, terms, out, upright, came, half, last, whole, swapped, y_sems, o_sems, i_sems
+    ):
+        self.outer, self.upright, self.swapped = outer, upright, swapped
         self.terms, self.out = terms, out
         self.came, self.half, self.last, self.whole = came, half, last, whole
         self.y_sems, self.o_sems, self.i_sems = y_sems, o_sems, i_sems
@@ -895,16 +1001,23 @@
         self.whole[...] = total.astype(BF16)
         self.third = remote(
             self.whole.at[1 - self.i],
-            self.out.at[self.i],
+            self.swapped.at[self.i],
             self.i_sems.at[0],
             self.i_sems.at[1],
             {"i": 1 - self.i},
         )
         self.third.start()
-        self.out[self.i] = self.whole[self.i]
+        self.swapped[self.i] = self.whole[self.i]
 
     def finish(self):
         self.third.wait_recv()
+        rows = self.swapped.shape[2]
+        for n in range(2):
+            values = self.swapped[n].astype(F32)
+            if self.upright:
+                self.out[n] = values
+            else:
+                self.out[:, n * rows : (n + 1) * rows] = values
         for copy in self.first + self.second + [self.third]:
             copy.wait_send()
 
@@ -914,6 +1027,7 @@
         pltpu.VMEM((2 * outer if first else 1, cell, rows), BF16),
         pltpu.VMEM((outer, 2, cell, rows), BF16),
         pltpu.VMEM((max(outer - 1, 1), 2, cell, rows), BF16),
+        pltpu.VMEM((2, cell, rows), BF16),
         pltpu.VMEM((2, cell, rows), BF16),
         pltpu.SemaphoreType.DMA((2, 2 * outer)),
         pltpu.SemaphoreType.DMA((2, outer)),
@@ -948,8 +1062,8 @@
 
 
 def final_body(
-    axes, sizes, heads, share, dqkv, columns, normed_low, shrink_kept, shrink_came,
-    expand_parts, low_middle, att, own, grad_middle, gain, row_sums,
+    axes, sizes, heads, share, dqkv, columns, normed_low, shrink_kept_far, shrink_came_far,
+    expand_far, low_middle, att, own, grad_middle_far, gain, row_sums,
     hidden_sum,
     grad_inputs,
     routed,
@@ -960,9 +1074,14 @@
     rows_out,
     hidden_out,
     expand_out,
+    shrink_kept,
+    shrink_came,
+    expand_parts,
+    grad_middle,
     part,
     first,
-    last,
+    i_came,
+    o_came,
     normed_part,
     q_part,
     q_first,
@@ -990,6 +1109,7 @@
     g_recv,
     g_local,
     load_sem,
+    late_sem,
     expand_sum,
     expand_came,
     e_send,
@@ -1007,8 +1127,8 @@
     rows, width = own.shape
     span = heads * HEAD_DIM
     y_mate, k_mate, x_mate = {"y": 1 - y}, {"k": 1 - k}, {"x": 1 - x}
-    shrink = Owned(outer, None, shrink_out, *owned[:7])
-    outw = Owned(outer, outw_terms, outw_out, *owned[7:])
+    shrink = Owned(outer, None, shrink_out, False, *owned[:8])
+    outw = Owned(outer, outw_terms, outw_out, True, *owned[8:])
 
     def load_normed(n):
         some = normed_part.shape[0]
@@ -1017,10 +1137,59 @@
         )
 
     load_normed(0).start()
+    late = [
+        pltpu.make_async_copy(source, target, late_sem.at[n])
+        for n, (source, target) in enumerate(
+            [
+                (shrink_kept_far, shrink_kept),
+                (shrink_came_far, shrink_came),
+                (grad_middle_far, grad_middle),
+            ]
+            + [(far, expand_parts.at[n]) for n, far in enumerate(expand_far)]
+        )
+    ]
+    for copy in late:
+        copy.start()
     greet([moved(axes, sizes, off) for off in offs])
 
+    def spot_of(n):
+        to = lax.rem(o + n % outer + 1, outer)
+        ti = lax.rem(i + 1 + n // outer, inner)
+        return to * inner + ti, to
+
+    def to_mate(n):
+        return remote(
+            part.at[spot_of(n)[0], 1 - y], first.at[n], r_send.at[n], r_recv.at[n], y_mate
+        )
+
+    def to_i(s):
+        slot = 2 * outer + s
+        return remote(
+            part.at[spot_of(s)[0], y], i_came.at[s], r_send.at[slot], r_recv.at[slot], {"i": 1 - i}
+        )
+
+    def to_o(s):
+        slot = 3 * outer + s
+        spot, to = spot_of(outer + s)
+        return remote(part.at[spot, y], o_came.at[s], r_send.at[slot], r_recv.at[slot], {"o": to})
+
+    def terms(n, unused):
+        spot = spot_of(n)[0]
+        at = pl.multiple_of(spot * 2 * rows, 2 * rows)
+        values = nt(dqkv[pl.ds(at, 2 * rows), :], columns[...]).astype(BF16)
+        part[spot] = values.reshape(2, rows, width)
+        to_mate(n).start()
+        return unused
+
+    lax.fori_loop(0, chips, terms, 0)
+
+    late[0].wait()
+    late[1].wait()
+    shrink.come(shrink_kept, shrink_came)
+    shrink.send_o()
+
     group = (("i", "x", "k"), (inner, xs, ks))
-    side = Gather(("i", "x"), (inner, xs), "k", low_middle, gy_all, g_send, g_recv, g_local)
+    side = Quad(low_middle, gy_all, g_send, g_recv, g_local)
     side.start()
     cell = att_cut.shape[2]
     for half in range(inner):
@@ -1030,72 +1199,6 @@
     att_started = pieces_out(*group, att_cut, att_all, a_send, a_recv)
     here = (i * xs + x) * ks + k
     att_all[here] = att_cut[here]
-
-    def chip(t):
-        to, ti = lax.rem(o + t // inner, outer), lax.rem(i + t % inner, inner)
-        return to * inner + ti, {"o": to, "i": ti}
-
-    def back_chip(t):
-        to = lax.rem(o + outer - t // inner, outer)
-        ti = lax.rem(i + inner - t % inner, inner)
-        return to * inner + ti
-
-    def to_mate(t):
-        return remote(
-            part.at[chip(t)[0], 1 - y], first.at[t], r_send.at[t], r_recv.at[t], y_mate
-        )
-
-    def to_chip(t):
-        slot = chips + t - 1
-        return remote(
-            part.at[chip(t)[0], y], last.at[t - 1], r_send.at[slot], r_recv.at[slot], chip(t)[1]
-        )
-
-    def terms(step, unused):
-        t = lax.rem(step + 1, chips)
-        spot = chip(t)[0]
-        at = pl.multiple_of(spot * 2 * rows, 2 * rows)
-        values = nt(dqkv[pl.ds(at, 2 * rows), :], columns[...]).astype(BF16)
-        part[spot] = values.reshape(2, rows, width)
-        to_mate(t).start()
-        return unused
-
-    lax.fori_loop(0, chips, terms, 0)
-
-    shards = xs * ks
-    cuts = spots // (2 * shards)
-    total = expand_parts[0][...].astype(F32)
-    for other in expand_parts[1:]:
-        total = total + other[...].astype(F32)
-    expand_sum[...] = total.astype(BF16)
-    index = o * ys + y
-    goal = shard * (spots // shards) + i * cuts + index % cuts
-    goal_shard = index // cuts
-    away = goal * shards + goal_shard != me
-    route = remote(
-        expand_sum,
-        expand_came,
-        e_send,
-        e_recv,
-        {
-            "o": goal // (inner * ys),
-            "i": (goal // ys) % inner,
-            "y": goal % ys,
-            "x": goal_shard // ks,
-            "k": goal_shard % ks,
-        },
-    )
-
-    @pl.when(away)
-    def _():
-        route.start()
-
-    @pl.when(jnp.logical_not(away))
-    def _():
-        expand_came[...] = expand_sum[...]
-
-    shrink.come(shrink_kept, shrink_came)
-    shrink.send_o()
 
     quarter = q_part.shape[3]
     some = normed_part.shape[0]
@@ -1123,23 +1226,69 @@
     for copy in q_copies:
         copy.start()
 
-    def add_and_send(step, unused):
-        t = step + 1
-        to_mate(t).wait_recv()
-        spot = chip(t)[0]
-        part[spot, y] = (part[spot, y].astype(F32) + first[t].astype(F32)).astype(BF16)
-        to_chip(t).start()
-        return unused
-
-    lax.fori_loop(0, chips - 1, add_and_send, 0)
+    for s in range(outer):
+        to_mate(s).wait_recv()
+        spot = spot_of(s)[0]
+        part[spot, y] = (part[spot, y].astype(F32) + first[s].astype(F32)).astype(BF16)
+        to_i(s).start()
+    side.x_in()
+    side.i_in()
     q_copies[0].wait_recv()
     q_sum[...] = (q_part[1 - x, k].astype(F32) + q_first[1].astype(F32)).astype(BF16)
     q_over = remote(q_sum, q_last, q_send.at[2], q_recv.at[2], x_mate)
     q_over.start()
 
-    side.hand_on()
+    def inner_sum(s):
+        to_mate(outer + s).wait_recv()
+        to_i(s).wait_recv()
+        spot = spot_of(outer + s)[0]
+        return spot, (
+            part[spot, y].astype(F32) + first[outer + s].astype(F32) + i_came[s].astype(F32)
+        )
+
+    for s in range(outer - 1):
+        spot, total = inner_sum(s)
+        part[spot, y] = total.astype(BF16)
+        to_o(s).start()
+    side.d_in()
+
+    for copy in late[2:]:
+        copy.wait()
+    shards = xs * ks
+    cuts = spots // (2 * shards)
+    total = expand_parts[0].astype(F32)
+    for n in range(1, outer):
+        total = total + expand_parts[n].astype(F32)
+    expand_sum[...] = total.astype(BF16)
+    index = o * ys + y
+    goal = shard * (spots // shards) + i * cuts + index % cuts
+    goal_shard = lax.rem(index // cuts + 2 * k, shards)
+    away = goal * shards + goal_shard != me
+    route = remote(
+        expand_sum,
+        expand_came,
+        e_send,
+        e_recv,
+        {
+            "o": goal // (inner * ys),
+            "i": (goal // ys) % inner,
+            "y": goal % ys,
+            "x": goal_shard // ks,
+            "k": goal_shard % ks,
+        },
+    )
+
+    @pl.when(away)
+    def _():
+        route.start()
+
+    @pl.when(jnp.logical_not(away))
+    def _():
+        expand_came[...] = expand_sum[...]
+
     pieces_in(*group, att_cut, att_all, a_send, a_recv, att_started)
-    side.finish()
+    side.local_wait()
+    side.all_across()
 
     def put_terms(spot, values):
         outw_terms[spot] = values
@@ -1197,13 +1346,13 @@
 
     each_sent(send_block)
 
-    to_mate(0).wait_recv()
-    grad = part[chip(0)[0], y].astype(F32) + first[0].astype(F32)
-    for t in range(1, chips):
-        to_chip(t).wait_recv()
-        grad = grad + last[t - 1].astype(F32)
+    spot, grad = inner_sum(outer - 1)
+    for s in range(outer - 1):
+        to_o(s).wait_recv()
+        grad = grad + o_came[s].astype(F32)
     plain, scale = normed(own[...].astype(F32))
-    grad_inputs[...] = grad_middle[...] + norm_back(grad, gain[...], plain, scale)
+    gains = gain[...].reshape(1, width)
+    grad_inputs[...] = (grad_middle[...] + norm_back(grad, gains, plain, scale)).T
 
     def fill(base, values):
         size = values.shape[1]
@@ -1303,10 +1452,13 @@
     each_sent(sent_block)
     for copy in line_started + q_copies + [q_over]:
         copy.wait_send()
-    for t in range(chips):
-        to_mate(t).wait_send()
-    for t in range(1, chips):
-        to_chip(t).wait_send()
+    side.finish()
+    for n in range(chips):
+        to_mate(n).wait_send()
+    for s in range(outer):
+        to_i(s).wait_send()
+    for s in range(outer - 1):
+        to_o(s).wait_send()
 
 
 def final_part(
@@ -1351,22 +1503,27 @@
     return pl.pallas_call(
         functools.partial(final_kernel, axes, sizes, heads, share),
         out_shape=[
-            jax.ShapeDtypeStruct(block, F32),
+            jax.ShapeDtypeStruct(block[::-1], F32),
             jax.ShapeDtypeStruct((slots, HEAD_DIM, part_rows), BF16),
-            jax.ShapeDtypeStruct((inner, cell, piece), BF16),
-            jax.ShapeDtypeStruct((inner, cell, out_rows), BF16),
+            jax.ShapeDtypeStruct((cell, inner * piece), F32),
+            jax.ShapeDtypeStruct((inner, cell, out_rows), F32),
             jax.ShapeDtypeStruct((1, spots * span), F32),
             jax.ShapeDtypeStruct((1, spots * span), F32),
             jax.ShapeDtypeStruct((6, width), F32),
             jax.ShapeDtypeStruct((1, group * piece), F32),
             jax.ShapeDtypeStruct(expand_parts[0].shape, F32),
         ],
-        in_specs=[VMEM] * 2 + [ANY] + [VMEM] * (9 + outer),
+        in_specs=[VMEM] * 2 + [ANY] * 4 + [VMEM] * 3 + [ANY] + [VMEM] * 3 + [ANY] * (outer - 1),
         out_specs=[VMEM] * 9,
         scratch_shapes=[
+            pltpu.VMEM(shrink_kept.shape, BF16),
+            pltpu.VMEM(shrink_kept.shape, BF16),
+            pltpu.VMEM((outer,) + expand_parts[0].shape, BF16),
+            pltpu.VMEM(block, F32),
             pltpu.VMEM((chips, ys) + block, BF16),
             pltpu.VMEM((chips,) + block, BF16),
-            pltpu.VMEM((chips - 1,) + block, BF16),
+            pltpu.VMEM((outer,) + block, BF16),
+            pltpu.VMEM((max(outer - 1, 1),) + block, BF16),
             pltpu.VMEM((min(1024, dqkv.shape[0]), width), BF16),
             pltpu.VMEM((xs, ks) + q_block, BF16),
             pltpu.VMEM((2,) + q_block, BF16),
@@ -1380,8 +1537,8 @@
             pltpu.VMEM((devices * line_rows, 128), F32),
             pltpu.VMEM((devices - 1, line_rows, 128), F32),
             pltpu.VMEM((devices * line_rows, 128), F32),
-            pltpu.SemaphoreType.DMA((2 * chips,)),
-            pltpu.SemaphoreType.DMA((2 * chips,)),
+            pltpu.SemaphoreType.DMA((4 * outer,)),
+            pltpu.SemaphoreType.DMA((4 * outer,)),
             pltpu.SemaphoreType.DMA((3,)),
             pltpu.SemaphoreType.DMA((3,)),
             pltpu.SemaphoreType.DMA((6 * heads,)),
@@ -1390,8 +1547,9 @@
             pltpu.SemaphoreType.DMA((group,)),
             pltpu.SemaphoreType.DMA((2 * devices,)),
             pltpu.SemaphoreType.DMA((2 * devices,)),
-            *gather_scratch((("i", "x"), (inner, xs), "k")),
+            *quad_scratch(),
             pltpu.SemaphoreType.DMA,
+            pltpu.SemaphoreType.DMA((3 + outer,)),
             pltpu.VMEM(expand_parts[0].shape, BF16),
             pltpu.VMEM(expand_parts[0].shape, BF16),
             pltpu.SemaphoreType.DMA,
@@ -1715,23 +1873,13 @@
     piece = hidden // (shards * inner)
     every = (("o", "i", "y"), (outer, inner, ys))
     group = (("i", "x"), (inner, xs), "k")
-    own = tokens[0]
-    own_grad = cotangent[0]
-
-    def columns(values, count):
-        wide = values.reshape(values.shape[:-1] + (count, width))
-        wide = jnp.pad(wide, [(0, 0)] * (wide.ndim - 1) + [(0, padded - width)])
-        return lax.dynamic_slice_in_dim(wide, place * span, span, axis=wide.ndim - 1)
-
-    qkv_bias = jnp.concatenate(
-        [columns(query_bias, 1)[0], jnp.zeros((span,), F32), columns(value_bias, 1)[0]]
-    )
+
     sizes_of = (outer, inner, ys, xs, ks)
-    qkv, normed_low, qkv_columns, expand_columns = first_part(
-        own,
+    qkv, normed_low, qkv_columns, expand_columns, own = first_part(
+        tokens[0].T,
         qkv_weight,
         expand_weight,
-        [first_gain[None], first_shift[None], qkv_bias[None]],
+        [first_gain, first_shift, query_bias, value_bias],
         span,
         sizes_of,
         piece,
@@ -1741,9 +1889,6 @@
 
     qkv, out_own = lax.optimization_barrier((qkv, out_weight))
     out_far = lax.ppermute(out_own, "x", [(0, 1), (1, 0)])
-    expand_own_bias = lax.dynamic_slice_in_dim(
-        expand_bias, (shard * inner + i) * piece, piece, axis=0
-    )
 
     order_row = block_order[0]
     blocks = order_row.shape[0]
@@ -1770,17 +1915,13 @@
     ) = middle_part(
         attended_bf.reshape(spots, rows, span),
         own,
-        own_grad,
+        cotangent[0].T,
         out_own,
         out_far,
         expand_columns,
         shrink_weight,
-        [
-            v[None]
-            for v in (out_bias, expand_own_bias, shrink_bias, second_gain, second_shift)
-        ],
+        [out_bias, expand_bias, shrink_bias, second_gain, second_shift],
         every,
-        group,
         1,
     )
     grad_heads = grad_heads.reshape(spots * rows, span)
@@ -1812,7 +1953,7 @@
         attended_low,
         own,
         grad_middle,
-        first_gain[None],
+        first_gain,
         row_sums,
         hidden_sums,
         axes,
@@ -1822,18 +1963,15 @@
         2,
     )
 
-    def upright(cells):
-        return cells.transpose(0, 2, 1).reshape(-1, cells.shape[1]).astype(F32)
-
     start = share * place - HEAD_DIM * ((share * place) // HEAD_DIM)
     grad_qkv = lax.dynamic_slice_in_dim(routed.reshape(-1, part), start, share, axis=0)
     return (
-        result[None],
-        grad_inputs[None],
+        result.T[None],
+        grad_inputs.T[None],
         grad_qkv.T.astype(F32),
-        upright(outw_cells),
+        outw_cells.transpose(0, 2, 1).reshape(part, -1),
         grad_expand,
-        upright(shrink_cells),
+        shrink_cells.T,
         query_sums[0, :width],
         value_sums[0, :width],
         row_totals[0],

time: 414 us -> 387 us (0.935)
  the two profiles are of different devices: /device:TPU:25 before, /device:TPU:23 now
where the time goes in v7:
time: 387 us; the launch traced here: 380 us
  Pallas kernels  346 us (89%)
  waiting for transfers between devices  17.2 us (4%)
  local copies, waits for them, and re-layouts  8.26 us (2%)
  starting transfers between devices  4.96 us (1%)
    pallas_call x1, Pallas kernels, final_part(): pl.pallas_call(functools.partial(final_kernel, axes, sizes, heads, share)...  148 us
    pallas_call x1, Pallas kernels, middle_part(): pl.pallas_call(functools.partial(middle_kernel, every), out_shape=[flat_l...  104 us
    pallas_call x1, Pallas kernels, first_part(): pl.pallas_call(functools.partial(first_kernel, sizes), out_shape=[jax.Sha...  51.5 us
    pallas_call x1, Pallas kernels, attend_back(): pl.pallas_call(functools.partial(attend_back_kernel, heads, block), out_s...  23.3 us
    pallas_call x1, Pallas kernels, attend(): pl.pallas_call(functools.partial(attend_kernel, heads, block), out_shape=...  20 us
    ppermute x1, waiting for transfers between devices, body(): out_far = lax.ppermute(out_own, 'x', [(0, 1), (1, 0)])  9.44 us
    ppermute x1, waiting for transfers between devices, body(): expand_parts[step] = lax.ppermute(expand_parts[step], 'o', ring)  7.79 us
  transfers between devices with their start and end apart: 3, of which 2 were waited for; matrix products, arithmetic and copies ran while one was open for 0% of the time, Pallas kernels for 11%

profile of v7, /device:TPU:23, one launch (start us, length us, event | category | flops | bytes accessed | tf_op | source)
XLA Modules:
  0.0 380.3 jit_solution(17563395745887653248)
XLA Ops:
  0.6 0.0 copy-start.9
  0.7 51.5 %first0.1 = (bf16[1024,768]{1,0:T(8,128)(2,1)}, bf16[1024,1600]{1,0:T(8,128)(2,1)}, bf16[2,2,400,768]{3,2,1,0:T(8,128)(2,1)}, bf16[4,400,800]{2,1,0:T(8,128)(2,1)}, bf16[128,1600]{1,0:T(8,128)(2,1)}) custom-call(bf16[1600,128]{1,0:T(8,128)(2,1)} %bitcast.28, bf16[400,4800]{1,0:T(8,128)(2,1)} %qkv_weight.1, bf16[400,6400]{1,0:T(8,128)(2,1)} %weight.1, ...), custom_call_target="tpu_custom_call" | custom-call | flops 2516582400 | bytes 65536000 | tf_op jit(solution)/shard_map/first0/pallas_call | solution.py:438
  52.1 1.2 collective-permute-start
  53.3 0.0 copy-done.9
  53.3 0.6 select_reduce_fusion.inv
  53.9 20.0 %attend.1 = (f32[1024,256]{1,0:T(8,128)}, bf16[1024,256]{1,0:T(8,128)(2,1)}, f32[4,1024]{1,0:T(4,128)}) custom-call(s32[16]{0:T(128)} %select_reduce_fusion.inv, bf16[1024,768]{1,0:T(8,128)(2,1)} %get-tuple-element.46.qkv), custom_call_target="tpu_custom_call" | custom-call | flops 2684354560 | bytes 2621440 | tf_op jit(solution)/shard_map/attend/pallas_call | solution.py:1698
  73.9 9.4 %collective-permute-done.out_far = bf16[400,1600]{1,0:T(8,128)(2,1)} collective-permute-done((bf16[400,1600]{1,0:T(8,128)(2,1)}, bf16[400,1600]{1,0:T(8,128)(2,1)}, u32[]{:S(2)}, u32[]{:S(2)}) %collective-permute-start) | collective-permute-done | bytes 1280032 | tf_op jit(solution)/shard_map/ppermute | solution.py:1891
  83.3 104.1 %middle1.1 = (bf16[128,1600]{1,0:T(8,128)(2,1)}, bf16[1600,128]{1,0:T(8,128)(2,1)}, f32[128,1600]{1,0:T(8,128)}, bf16[128,1600]{1,0:T(8,128)(2,1)}, f32[4,1600]{...) custom-call(bf16[8,128,256]{2,1,0:T(8,128)(2,1)} %bitcast.33, ...), custom_call_target="tpu_custom_call" | custom-call | flops 10485760000 | bytes 40960000 | tf_op jit(solution)/shard_map/middle1/pallas_call | solution.py:881
  187.5 0.2 collective-permute-start.1
  187.7 3.6 collective-permute-start.2
  191.3 23.3 %attend_back.1.dqkv = bf16[1024,768]{1,0:T(8,128)(2,1)} custom-call(s32[16]{0:T(128)} %select_reduce_fusion.inv, bf16[1024,768]{1,0:T(8,128)(2,1)} %get-tuple-element.46.qkv, bf16[1024,256]{1,0:T(8,128)(2,1)} %bitcast.32, f32[1024,256]{1,0:T(8,128)} %get-tuple-element.53.outs, f32[4,1024]{1,0:T(4,128)} %get-tuple-element.54.lse), custom_call_target="tpu_custom_call" | custom-call | flops 6710886400 | bytes 5242880 | tf_op jit(solution)/shard_map/attend_back/pallas_call | solution.py:1808
  214.6 7.8 %collective-permute-done.2.rest_0_ = bf16[400,800]{1,0:T(8,128)(2,1)} collective-permute-done((bf16[400,800]{1,0:T(8,128)(2,1)}, bf16[400,800]{1,0:T(8,128)(2,1)}, u32[]{:S(2)}, u32[]{:S(2)}) %collective-permute-start.2) | collective-permute-done | bytes 640032 | tf_op jit(solution)/shard_map/ppermute | solution.py:1932
  222.4 0.0 collective-permute-done.1.shrink_came
  222.4 147.5 %final2.1 = (f32[1600,128]{1,0:T(8,128)}, bf16[11,64,400]{2,1,0:T(8,128)(2,1)}, f32[200,1600]{1,0:T(8,128)}, f32[2,200,200]{2,1,0:T(8,128)}, f32[1,2048]{1,0:T(1...) custom-call(bf16[1024,768]{1,0:T(8,128)(2,1)} %attend_back.1.dqkv, ...), custom_call_target="tpu_custom_call" | custom-call | flops 5033164800 | bytes 40960000 | tf_op jit(solution)/shard_map/final2/pallas_call | solution.py:1503
  369.9 1.1 constant_dynamic-slice_fusion
  371.0 0.0 copy-start.4
  371.0 0.3 copy.36
  371.3 0.0 copy-start.8
  371.3 0.0 copy-start.5
  371.3 0.0 copy-start.7
  371.3 0.0 copy-start.6
  371.3 0.0 copy-start.3
  371.3 0.0 copy-start.2
  371.4 1.0 convert_bitcast_fusion
  372.4 0.0 copy-done.4
  372.4 0.9 copy.35
  373.3 0.0 copy-start
  373.3 0.0 copy-done.8
  373.3 0.6 slice_reduce_fusion.7
  373.9 0.0 copy-done.5
  373.9 0.0 copy-done.7
  374.0 0.7 slice_reduce_fusion
  374.7 0.0 copy-done.6
  374.7 0.7 reduce.3
  375.3 0.0 copy-done.3
  375.4 0.8 copy.41
  376.1 0.0 copy-done.2
  376.1 0.9 copy.42
  377.0 0.0 copy-done
  377.0 0.0 copy-start.1
  377.0 1.1 copy.43
  378.1 0.7 copy-done.1
  378.8 1.1 copy.44
Async XLA Ops:
  0.6 52.6 %copy-start.9 = (s32[1,16]{1,0:T(1,128)S(1)}, s32[1,16]{1,0:T(1,128)}, u32[]{:S(2)}) copy-start(s32[1,16]{1,0:T(1,128)} %param.17) | copy-start | bytes 196
  52.1 31.2 %collective-permute-start = (bf16[400,1600]{1,0:T(8,128)(2,1)}, bf16[400,1600]{1,0:T(8,128)(2,1)}, u32[]{:S(2)}, u32[]{:S(2)}) collective-permute-start(bf16[400,1600]{1,0:T(8,128)(2,1)} %out_own), channel_id=1, source_target_pairs={{0,2},{2,0},{1,3},{3,1},{4,6},{6,4},{5,7},{7,5},{8,10},{10,8},{9,1... | collective-permute-start | bytes 3840008 | tf_op jit(solution)/shard_map/ppermute | solution.py:1891
  187.5 34.9 %collective-permute-start.1 = (bf16[4,200,800]{2,1,0:T(8,128)(2,1)}, bf16[4,200,800]{2,1,0:T(8,128)(2,1)}, u32[]{:S(2)}, u32[]{:S(2)}) collective-permute-start(bf16[4,200,800]{2,1,0:T(8,128)(2,1)} %get-tuple-element.58), channel_id=1, source_target_pairs={{0,4},{4,0},{1,5},{5,1},{2,6},{6,2},{3,7},{7,3},{8,12},{12,8},{9,1... | collective-permute-start | bytes 3840008 | tf_op jit(solution)/shard_map/ppermute | solution.py:1929
  187.7 34.7 %collective-permute-start.2 = (bf16[400,800]{1,0:T(8,128)(2,1)}, bf16[400,800]{1,0:T(8,128)(2,1)}, u32[]{:S(2)}, u32[]{:S(2)}) collective-permute-start(bf16[400,800]{1,0:T(8,128)(2,1)} %get-tuple-element.65), channel_id=1, source_target_pairs={{0,16},{16,0},{1,17},{17,1},{2,18},{18,2},{3,19},{19,3},{4,20},{20... | collective-permute-start | bytes 1920008 | tf_op jit(solution)/shard_map/ppermute | solution.py:1932
  371.0 1.4 copy-start.4
  371.3 2.0 copy-start.8
  371.3 2.6 copy-start.5
  371.3 2.6 copy-start.7
  371.3 3.4 copy-start.6
  371.3 4.0 %copy-start.3 = (bf16[1600,128]{1,0:T(8,128)(2,1)S(1)}, bf16[1600,128]{1,0:T(8,128)(2,1)}, u32[]{:S(2)}) copy-start(bf16[1600,128]{1,0:T(8,128)(2,1)} %get-tuple-element.51) | copy-start | bytes 1228804
  371.3 4.8 %copy-start.2 = (f32[1600,128]{1,0:T(8,128)S(1)}, f32[1600,128]{1,0:T(8,128)}, u32[]{:S(2)}) copy-start(f32[1600,128]{1,0:T(8,128)} %get-tuple-element.66) | copy-start | bytes 2457604
  373.3 3.7 copy-start
  377.0 1.8 copy-start.1
